TPU v7x, 8 devices: a whole 2x2x1 slice. The times are simulated.
8 devices in a mesh: dp: 1 (over z), tp: 8 (over y, x, core).
Axes of the slice: x: 2, y: 2, z: 1, core: 2. Of those that a mesh axis runs over, the one named last changes fastest.
Arguments:
- hidden: bfloat16 [12, 768, 2048], P('dp', 'tp')
- grad_out: bfloat16 [12, 768, 2048], P('dp', 'tp')
- prefix_len: int32 [12], P('dp')
- valid_len: int32 [12], P('dp')
- attn_norm: bfloat16 [2048], replicated
- w_query: bfloat16 [2048, 2048], P(None, 'tp')
- w_key: bfloat16 [2048, 256], replicated
- w_value: bfloat16 [2048, 256], replicated
- w_out: bfloat16 [2048, 2048], P('tp')
- mlp_norm: bfloat16 [2048], replicated
- w_gate: bfloat16 [2048, 16384], P(None, 'tp')
- w_up: bfloat16 [2048, 16384], P(None, 'tp')
- w_down: bfloat16 [16384, 2048], P('tp')
Outputs:
- output 1: bfloat16 [12, 768, 2048], P('dp', 'tp')
- output 2: bfloat16 [12, 768, 2048], P('dp', 'tp')
- output 3: float32 [2048], P('dp')
- output 4: float32 [2048, 2048], P('dp', 'tp')
- output 5: float32 [2048, 256], P('dp')
- output 6: float32 [2048, 256], P('dp')
- output 7: float32 [2048, 2048], P(('dp', 'tp'))
- output 8: float32 [2048], P('dp')
- output 9: float32 [2048, 16384], P('dp', 'tp')
- output 10: float32 [2048, 16384], P('dp', 'tp')
- output 11: float32 [16384, 2048], P(('dp', 'tp'))
All inputs are finite; a program needn't handle non-finite values.
Results may differ from a plain program's by a relative error of at most 0.02.
Values are sent between devices in bfloat16 or wider.
A program may use at most 1 GiB of HBM per device.

v0:
```python
import math
import jax
import jax.numpy as jnp
from jax import lax
from jax.sharding import PartitionSpec as P

NORM_EPS = 1e-6


def rms_norm(x_in, gain):
    x_f = x_in.astype(jnp.float32)
    inv_rms = lax.rsqrt(jnp.mean(x_f * x_f, axis=-1, keepdims=True) + NORM_EPS)
    return (x_f * inv_rms * (1.0 + gain)).astype(jnp.bfloat16)


def rope_tables(positions, head_dim):
    half_dim = head_dim // 2
    exponent = jnp.arange(half_dim, dtype=jnp.float32) * (2.0 / head_dim)
    inv_freq = jnp.exp(exponent * (-math.log(10000.0)))
    angles = positions.astype(jnp.float32)[:, None] * inv_freq[None, :]
    return jnp.cos(angles), jnp.sin(angles)


def apply_rope(x_f, cos_t, sin_t):
    half_dim = x_f.shape[-1] // 2
    first = x_f[..., :half_dim]
    second = x_f[..., half_dim:]
    return jnp.concatenate([first * cos_t - second * sin_t, second * cos_t + first * sin_t], axis=-1)


def attend(query, keys, values, prefix_len, valid_len, first_pos):
    scale = query.shape[-1] ** -0.5
    scores = jnp.einsum("crie,cle->cirl", query, keys, preferred_element_type=jnp.float32) * scale
    q_pos = first_pos + jnp.arange(query.shape[1])
    k_pos = jnp.arange(keys.shape[1])
    key_row = k_pos[None, None, :]
    visible = (key_row < valid_len[:, None, None]) & ((key_row < prefix_len[:, None, None]) | (key_row <= q_pos[None, :, None]))
    scores = jnp.where(visible[:, None, :, :], scores, -1e30)
    probs = jax.nn.softmax(scores, axis=-1).astype(jnp.bfloat16)
    return jnp.einsum("cirl,cle->crie", probs, values, preferred_element_type=jnp.float32).astype(jnp.bfloat16)


def gated_act(gate, upper):
    return (jax.nn.gelu(gate, approximate=True) * upper).astype(jnp.bfloat16)


def gather_seq(x_loc):
    return lax.all_gather(x_loc, "tp", axis=1, tiled=True)


def scatter_seq(x_part):
    return lax.psum_scatter(x_part, "tp", scatter_dimension=1, tiled=True)


def solution(mesh):
    tp_size = mesh.shape["tp"]
    act_spec = P("dp", "tp", None)
    in_specs = (act_spec, act_spec, P("dp"), P("dp"), P(None), P(None, "tp"), P(None, None), P(None, None), P("tp", None), P(None), P(None, "tp"), P(None, "tp"), P("tp", None))
    out_specs = (act_spec, act_spec, P("dp"), P("dp", "tp"), P("dp", None), P("dp", None), P(("dp", "tp"), None), P("dp"), P("dp", "tp"), P("dp", "tp"), P(("dp", "tp"), None))

    def local_layer(hidden, grad_out, prefix_len, valid_len, attn_norm, w_query, w_key, w_value, w_out, mlp_norm, w_gate, w_up, w_down):
        batch, shard_len, model_dim = hidden.shape
        head_dim = w_key.shape[1]
        local_heads = w_query.shape[1] // head_dim
        seq_len = shard_len * tp_size
        cos_t, sin_t = rope_tables(jnp.arange(seq_len), head_dim)

        def rope_heads(raw_proj):
            return apply_rope(raw_proj, cos_t[:, None, :], sin_t[:, None, :]).astype(jnp.bfloat16)

        def rope_single(raw_proj):
            return apply_rope(raw_proj, cos_t, sin_t).astype(jnp.bfloat16)

        def attend_here(q_in, k_in, v_in):
            return attend(q_in, k_in, v_in, prefix_len, valid_len, 0)

        normed, norm1_pull = jax.vjp(rms_norm, hidden, attn_norm.astype(jnp.float32))
        normed_all = gather_seq(normed)
        q_raw = jnp.einsum("bld,dn->bln", normed_all, w_query, preferred_element_type=jnp.float32).reshape(batch, seq_len, local_heads, head_dim)
        query, query_pull = jax.vjp(rope_heads, q_raw)
        k_raw = jnp.einsum("bld,de->ble", normed_all, w_key, preferred_element_type=jnp.float32)
        keys, key_pull = jax.vjp(rope_single, k_raw)
        values = jnp.einsum("bld,de->ble", normed_all, w_value, preferred_element_type=jnp.float32).astype(jnp.bfloat16)
        mixed, attn_pull = jax.vjp(attend_here, query, keys, values)
        w_out_heads = w_out.reshape(local_heads, head_dim, model_dim)
        attn_part = jnp.einsum("blhd,hde->ble", mixed, w_out_heads, preferred_element_type=jnp.float32).astype(jnp.bfloat16)
        attn_sum = scatter_seq(attn_part)
        resid = (hidden.astype(jnp.float32) + attn_sum.astype(jnp.float32)).astype(jnp.bfloat16)
        gated_in, norm2_pull = jax.vjp(rms_norm, resid, mlp_norm.astype(jnp.float32))
        gated_all = gather_seq(gated_in)
        gate = jnp.einsum("bld,df->blf", gated_all, w_gate, preferred_element_type=jnp.float32)
        upper = jnp.einsum("bld,df->blf", gated_all, w_up, preferred_element_type=jnp.float32)
        act, act_pull = jax.vjp(gated_act, gate, upper)
        mlp_part = jnp.einsum("blf,fd->bld", act, w_down, preferred_element_type=jnp.float32).astype(jnp.bfloat16)
        mlp_sum = scatter_seq(mlp_part)
        hidden_out = (resid.astype(jnp.float32) + mlp_sum.astype(jnp.float32)).astype(jnp.bfloat16)

        grad_all = gather_seq(grad_out)
        g_down = jnp.einsum("blf,bld->fd", act, grad_all, preferred_element_type=jnp.float32)
        d_act = jnp.einsum("bld,fd->blf", grad_all, w_down, preferred_element_type=jnp.float32).astype(jnp.bfloat16)
        d_gate, d_upper = act_pull(d_act)
        d_gate = d_gate.astype(jnp.bfloat16)
        d_upper = d_upper.astype(jnp.bfloat16)
        g_gate = jnp.einsum("bld,blf->df", gated_all, d_gate, preferred_element_type=jnp.float32)
        g_up = jnp.einsum("bld,blf->df", gated_all, d_upper, preferred_element_type=jnp.float32)
        d_gated_part = (jnp.einsum("blf,df->bld", d_gate, w_gate, preferred_element_type=jnp.float32)
                        + jnp.einsum("blf,df->bld", d_upper, w_up, preferred_element_type=jnp.float32)).astype(jnp.bfloat16)
        d_gated = scatter_seq(d_gated_part)
        d_resid_norm, g_mlp_norm_part = norm2_pull(d_gated)
        g_mlp_norm = lax.psum(g_mlp_norm_part, "tp")
        d_resid = (grad_out.astype(jnp.float32) + d_resid_norm.astype(jnp.float32)).astype(jnp.bfloat16)

        d_resid_all = gather_seq(d_resid)
        g_out = jnp.einsum("blhd,ble->hde", mixed, d_resid_all, preferred_element_type=jnp.float32).reshape(local_heads * head_dim, model_dim)
        d_mixed = jnp.einsum("ble,hde->blhd", d_resid_all, w_out_heads, preferred_element_type=jnp.float32).astype(jnp.bfloat16)
        d_query, d_keys, d_values = attn_pull(d_mixed)
        d_q_raw = query_pull(d_query)[0].astype(jnp.bfloat16).reshape(batch, seq_len, local_heads * head_dim)
        d_k_raw = key_pull(d_keys)[0].astype(jnp.bfloat16)
        g_query = jnp.einsum("bld,bln->dn", normed_all, d_q_raw, preferred_element_type=jnp.float32)
        g_key = lax.psum(jnp.einsum("bld,ble->de", normed_all, d_k_raw, preferred_element_type=jnp.float32), "tp")
        g_value = lax.psum(jnp.einsum("bld,ble->de", normed_all, d_values, preferred_element_type=jnp.float32), "tp")
        d_normed_part = (jnp.einsum("bln,dn->bld", d_q_raw, w_query, preferred_element_type=jnp.float32)
                         + jnp.einsum("ble,de->bld", d_k_raw, w_key, preferred_element_type=jnp.float32)
                         + jnp.einsum("ble,de->bld", d_values, w_value, preferred_element_type=jnp.float32)).astype(jnp.bfloat16)
        d_normed = scatter_seq(d_normed_part)
        d_hidden_norm, g_attn_norm_part = norm1_pull(d_normed)
        g_attn_norm = lax.psum(g_attn_norm_part, "tp")
        grad_hidden = (d_resid.astype(jnp.float32) + d_hidden_norm.astype(jnp.float32)).astype(jnp.bfloat16)
        return (hidden_out, grad_hidden, g_attn_norm, g_query, g_key, g_value, g_out, g_mlp_norm, g_gate, g_up, g_down)

    return jax.shard_map(local_layer, mesh=mesh, in_specs=in_specs, out_specs=out_specs, check_vma=False)
```

profile of v0, /device:TPU:0, one launch (start us, length us, event | category | flops | bytes accessed | tf_op | source)
XLA Modules:
  0.0 2588.3 jit_solution(697227416904107367)
XLA Ops:
  20.5 174.6 %all-gather.5.cloned.1.call-done = bf16[12,768,2048]{2,1,0:T(8,128)(2,1)} async-done(((bf16[12,96,2048]{2,1,0:T(8,128)(2,1)}), bf16[12,768,2048]{2,1,0:T(8,128)(2,1)}) %all-gather.5.cloned.1.call-update) | async-done | bytes 37748752 | tf_op jit(solution)/shard_map/all_gather | solution.py:48
  195.1 19.5 convolution_bitcast_fusion.3
  220.6 19.5 fusion.82
  273.4 18.8 convolution_convert_fusion.5
  309.6 18.0 convolution_convert_fusion.2
  328.6 215.4 %reduce-scatter.5.cloned.1.call-done = bf16[12,96,2048]{2,1,0:T(8,128)(2,1)} async-done(((bf16[12,768,2048]{2,1,0:T(8,128)(2,1)}), bf16[12,96,2048]{2,1,0:T(8,128)(2,1)}) %reduce-scatter.5.cloned.1.call-update) | async-done | bytes 4718608 | tf_op jit(solution)/shard_map/reduce_scatter | solution.py:52
  555.2 164.6 %all-gather.9.cloned.1.call-done = bf16[12,768,2048]{2,1,0:T(8,128)(2,1)} async-done(((bf16[12,96,2048]{2,1,0:T(8,128)(2,1)}), bf16[12,768,2048]{2,1,0:T(8,128)(2,1)}) %all-gather.9.cloned.1.call-update) | async-done | bytes 37748752 | tf_op jit(solution)/shard_map/all_gather | solution.py:48
  719.7 86.5 %convolution_convert_fusion = bf16[12,768,2048]{2,1,0:T(8,128)(2,1)} fusion(bf16[12,768,2048]{2,1,0:T(8,128)(2,1)} %all-gather.9.cloned.1.call-done, bf16[2048,2048]{1,0:T(8,128)(2,1)} %param.25), kind=kOutput, calls=%fused_computation.32 | convolution fusion | flops 77328285696 | bytes 83886080 | tf_op jit(solution)/shard_map/bld,fd->blf/dot_general | solution.py:100
  806.2 89.7 %all-gather.7.cloned.1.call-done = bf16[12,768,2048]{2,1,0:T(8,128)(2,1)} async-done(((bf16[12,96,2048]{2,1,0:T(8,128)(2,1)}), bf16[12,768,2048]{2,1,0:T(8,128)(2,1)}) %all-gather.7.cloned.1.call-update) | async-done | bytes 37748752 | tf_op jit(solution)/shard_map/all_gather | solution.py:48
  895.9 88.4 %fusion.41 = f32[12,768,2048]{2,1,0:T(8,128)} fusion(bf16[12,768,2048]{2,1,0:T(8,128)(2,1)} %all-gather.7.cloned.1.call-done, bf16[2048,2048]{1,0:T(8,128)(2,1)} %param.24), kind=kOutput, calls=%fused_computation.82 | convolution fusion | flops 77309411328 | bytes 121634816 | tf_op jit(solution)/shard_map/bld,df->blf/dot_general | solution.py:92
  984.3 143.0 %fusion.7 = (bf16[12,768,2048]{2,1,0:T(8,128)(2,1)}, bf16[12,768,2048]{2,1,0:T(8,128)(2,1)}, f32[12,768,2048]{2,1,0:T(8,128)}) fusion(f32[12,768,2048]{2,1,0:T(8,128)} %fusion.41, bf16[12,768,2048]{2,1,0:T(8,128)(2,1)} %convolution_convert_fusion, bf16[12,768,2048]{2,1,0:T(8,128)(2,1)} %all-gather.7.cloned.1.call-done, bf16[2048,2048]{1,0:T(8,128)(2,1)} %param.23), kind=kOutput, calls=%fused_computation.11 | convolution fusion | flops 77781270528 | bytes 310378496 | tf_op jit(solution)/shard_map/bld,df->blf/dot_general | solution.py:91
  1127.3 89.1 %fusion.43 = f32[12,768,2048]{2,1,0:T(8,128)} fusion(bf16[12,768,2048]{2,1,0:T(8,128)(2,1)} %get-tuple-element.21, bf16[2048,2048]{1,0:T(8,128)(2,1)} %param.23), kind=kOutput, calls=%fused_computation.84 | convolution fusion | flops 77309411328 | bytes 121634816 | tf_op jit(solution)/shard_map/blf,df->bld/dot_general | solution.py:106
  1216.4 100.7 %add_convert_fusion.1 = bf16[12,768,2048]{2,1,0:T(8,128)(2,1)} fusion(f32[12,768,2048]{2,1,0:T(8,128)} %fusion.43, bf16[2048,2048]{1,0:T(8,128)(2,1)} %param.24, bf16[12,768,2048]{2,1,0:T(8,128)(2,1)} %convolution_convert_fusion, f32[12,768,2048]{2,1,0:T(8,128)} %get-tuple-element.37), kind=kOutput, calls=%fused_computation.13 | convolution fusion | flops 77554778112 | bytes 234881024 | tf_op jit(solution)/shard_map/blf,df->bld/dot_general | solution.py:107
  1317.2 86.1 %convolution_convert_fusion.1 = bf16[12,768,2048]{2,1,0:T(8,128)(2,1)} fusion(bf16[12,768,2048]{2,1,0:T(8,128)(2,1)} %get-tuple-element.22, bf16[2048,2048]{1,0:T(8,128)(2,1)} %param.25), kind=kOutput, calls=%fused_computation.33 | convolution fusion | flops 77328285696 | bytes 83886080 | tf_op jit(solution)/shard_map/blf,fd->bld/dot_general | solution.py:94
  1403.3 130.2 %reduce-scatter.9.cloned.1.call-done = bf16[12,96,2048]{2,1,0:T(8,128)(2,1)} async-done(((bf16[12,768,2048]{2,1,0:T(8,128)(2,1)}), bf16[12,96,2048]{2,1,0:T(8,128)(2,1)}) %reduce-scatter.9.cloned.1.call-update) | async-done | bytes 4718608 | tf_op jit(solution)/shard_map/reduce_scatter | solution.py:52
  1541.0 212.3 %reduce-scatter.7.cloned.1.call-done = bf16[12,96,2048]{2,1,0:T(8,128)(2,1)} async-done(((bf16[12,768,2048]{2,1,0:T(8,128)(2,1)}), bf16[12,96,2048]{2,1,0:T(8,128)(2,1)}) %reduce-scatter.7.cloned.1.call-update) | async-done | bytes 4718608 | tf_op jit(solution)/shard_map/reduce_scatter | solution.py:52
  1766.9 173.9 %all-gather.11.cloned.1.call-done = bf16[12,768,2048]{2,1,0:T(8,128)(2,1)} async-done(((bf16[12,96,2048]{2,1,0:T(8,128)(2,1)}), bf16[12,768,2048]{2,1,0:T(8,128)(2,1)}) %all-gather.11.cloned.1.call-update) | async-done | bytes 37748752 | tf_op jit(solution)/shard_map/all_gather | solution.py:48
  1940.8 18.3 convolution_convert_fusion.4
  1959.1 18.7 fusion.62
  1977.8 21.4 fusion.16
  1999.3 23.6 convert_convert_fusion
  2023.0 23.0 bitcast_convert_fusion
  2063.5 29.8 %fusion.80 = f32[12,768,2048]{2,1,0:T(8,128)} fusion(bf16[2048,256]{1,0:T(8,128)(2,1)S(1)} %copy-done.19, f32[12,768,128]{1,2,0:T(8,128)} %get-tuple-element.24, f32[12,768,128]{1,2,0:T(8,128)} %get-tuple-element.23), kind=kOutput, calls=%fused_computation.126 | convolution fusion | flops 9668395008 | bytes 85983232 | tf_op jit(solution)/shard_map/ble,de->bld/dot_general | solution.py:123
  2093.3 28.7 %fusion.77 = f32[12,768,2048]{2,1,0:T(8,128)} fusion(bf16[2048,256]{1,0:T(8,128)(2,1)S(1)} %copy-done.21, f32[12,768,1,128]{1,3,0,2:T(8,128)} %get-tuple-element.26, f32[12,768,1,128]{1,3,0,2:T(8,128)S(1)} %get-tuple-element.25), kind=kOutput, calls=%fused_computation.123 | convolution fusion | flops 9668395008 | bytes 85983232 | tf_op jit(solution)/shard_map/bln,dn->bld/dot_general | solution.py:122
  2122.0 61.4 %add_convert_fusion = bf16[12,768,2048]{2,1,0:T(8,128)(2,1)} fusion(f32[12,768,2048]{2,1,0:T(8,128)} %fusion.77, f32[12,768,2048]{2,1,0:T(8,128)} %fusion.80, bf16[12,768,256]{2,1,0:T(8,128)(2,1)} %fusion.62, bf16[2048,256]{1,0:T(8,128)(2,1)} %param.20), kind=kOutput, calls=%fused_computation.12 | convolution fusion | flops 9720299520 | bytes 194510848 | tf_op jit(solution)/shard_map/ble,de->bld/dot_general | solution.py:124
  2183.5 97.3 %convolution_bitcast_fusion.1 = f32[2048,2048]{1,0:T(8,128)} fusion(bf16[12,768,2048]{2,1,0:T(8,128)(2,1)} %all-gather.7.cloned.1.call-done, bf16[12,768,2048]{2,1,0:T(8,128)(2,1)} %convolution_convert_fusion, f32[12,768,2048]{2,1,0:T(8,128)} %get-tuple-element.37), kind=kOutput, calls=%fused_computation.77 | convolution fusion | flops 77517029376 | bytes 167772160 | tf_op jit(solution)/shard_map/bld,blf->df/dot_general | solution.py:105
  2280.8 89.5 %convolution_bitcast_fusion = f32[2048,2048]{1,0:T(8,128)} fusion(bf16[12,768,2048]{2,1,0:T(8,128)(2,1)} %get-tuple-element.22, bf16[12,768,2048]{2,1,0:T(8,128)(2,1)} %all-gather.9.cloned.1.call-done), kind=kOutput, calls=%fused_computation.76 | convolution fusion | flops 77309411328 | bytes 92274688 | tf_op jit(solution)/shard_map/blf,bld->fd/dot_general | solution.py:99
  2370.3 89.9 %convolution_bitcast_fusion.2 = f32[2048,2048]{1,0:T(8,128)} fusion(bf16[12,768,2048]{2,1,0:T(8,128)(2,1)} %all-gather.7.cloned.1.call-done, bf16[12,768,2048]{2,1,0:T(8,128)(2,1)} %get-tuple-element.21), kind=kOutput, calls=%fused_computation.78 | convolution fusion | flops 77309411328 | bytes 92274688 | tf_op jit(solution)/shard_map/bld,blf->df/dot_general | solution.py:104
  2460.2 19.1 convolution_bitcast_fusion.5
  2479.3 19.2 convolution_bitcast_fusion.4
  2498.5 20.4 convolution_bitcast_fusion.6
  2543.2 23.0 all-reduce.4
  (152 shorter events, 160.2 us)
Async XLA Ops:
  7.2 302.4 %copy-start = (bf16[256,2048]{1,0:T(8,128)(2,1)S(1)}, bf16[256,2048]{1,0:T(8,128)(2,1)}, u32[]{:S(2)}) copy-start(bf16[256,2048]{1,0:T(8,128)(2,1)} %param.21) | copy-start | bytes 3145732
  7.2 187.9 %all-gather.5.cloned.1.call-start = ((), (), s32[]{:S(2)}) async-start(), calls=%async_computation.4 | async-start | bytes 42467328 | tf_op jit(solution)/shard_map/all_gather | solution.py:48
  8.0 187.1 %copy-start.20 = (bf16[2048,256]{1,0:T(8,128)(2,1)S(1)}, bf16[2048,256]{1,0:T(8,128)(2,1)}, u32[]{:S(2)}) copy-start(bf16[2048,256]{1,0:T(8,128)(2,1)} %param.18) | copy-start | bytes 3145732
  18.3 525.7 %reduce-scatter.5.cloned.1.call-start = ((), (), s32[]{:S(2)}) async-start(), calls=%async_computation.5 | async-start | bytes 42467328 | tf_op jit(solution)/shard_map/reduce_scatter | solution.py:52
  18.9 273.3 %copy-start.16 = (pred[768,768]{0,1:T(8,128)(4,1)}, pred[768,768]{0,1:T(8,128)(4,1)S(1)}, u32[]{:S(2)}) copy-start(pred[768,768]{0,1:T(8,128)(4,1)S(1)} %iota_compare_fusion) | copy-start | bytes 1769476
  19.0 273.2 %copy-start.39 = (pred[12,768]{1,0:T(8,128)(4,1)}, pred[12,768]{1,0:T(8,128)(4,1)S(1)}, u32[]{:S(2)}) copy-start(pred[12,768]{1,0:T(8,128)(4,1)S(1)} %get-tuple-element.40) | copy-start | bytes 27652
  19.0 273.2 %copy-start.41 = (pred[12,768]{1,0:T(8,128)(4,1)}, pred[12,768]{1,0:T(8,128)(4,1)S(1)}, u32[]{:S(2)}) copy-start(pred[12,768]{1,0:T(8,128)(4,1)S(1)} %get-tuple-element.41) | copy-start | bytes 27652
  20.5 219.6 %copy-start.4 = (f32[768,128]{0,1:T(8,128)}, f32[768,128]{0,1:T(8,128)S(1)}, u32[]{:S(2)}) copy-start(f32[768,128]{0,1:T(8,128)S(1)} %get-tuple-element.33) | copy-start | bytes 1179652
  20.5 219.6 %copy-start.6 = (f32[768,128]{0,1:T(8,128)}, f32[768,128]{0,1:T(8,128)S(1)}, u32[]{:S(2)}) copy-start(f32[768,128]{0,1:T(8,128)S(1)} %get-tuple-element.34) | copy-start | bytes 1179652
  258.2 34.0 %copy-start.37 = (f32[12,768]{1,0:T(8,128)}, f32[12,768]{1,0:T(8,128)S(1)}, u32[]{:S(2)}) copy-start(f32[12,768]{1,0:T(8,128)S(1)} %get-tuple-element.35) | copy-start | bytes 110596
  327.6 392.1 %all-gather.9.cloned.1.call-start = ((), (), s32[]{:S(2)}) async-start(), calls=%async_computation.8 | async-start | bytes 42467328 | tf_op jit(solution)/shard_map/all_gather | solution.py:48
  328.3 567.5 %all-gather.7.cloned.1.call-start = ((), (), s32[]{:S(2)}) async-start(), calls=%async_computation.6 | async-start | bytes 42467328 | tf_op jit(solution)/shard_map/all_gather | solution.py:48
  328.6 226.5 %copy-start.29 = (f32[2048]{0:T(1024)}, f32[2048]{0:T(1024)S(1)}, u32[]{:S(2)}) copy-start(f32[2048]{0:T(1024)S(1)} %convert_add_fusion.2) | copy-start | bytes 24580
  555.1 978.4 %reduce-scatter.9.cloned.1.call-start = ((), (), s32[]{:S(2)}) async-start(), calls=%async_computation.9 | async-start | bytes 42467328 | tf_op jit(solution)/shard_map/reduce_scatter | solution.py:52
  1317.1 436.1 %reduce-scatter.7.cloned.1.call-start = ((), (), s32[]{:S(2)}) async-start(), calls=%async_computation.7 | async-start | bytes 42467328 | tf_op jit(solution)/shard_map/reduce_scatter | solution.py:52
  1403.3 130.3 %copy-start.30 = (f32[2048]{0:T(1024)S(1)}, f32[2048]{0:T(1024)}, u32[]{:S(2)}) copy-start(f32[2048]{0:T(1024)} %copy-done.29) | copy-start | bytes 24580
  1403.3 130.3 %copy-start.32 = (f32[12,96]{1,0:T(8,128)S(1)}, f32[12,96]{1,0:T(8,128)}, u32[]{:S(2)}) copy-start(f32[12,96]{1,0:T(8,128)} %copy-done.31) | copy-start | bytes 13828
  1403.3 137.6 %copy-start.36 = (f32[12,96]{1,0:T(8,128)S(1)}, f32[12,96]{1,0:T(8,128)}, u32[]{:S(2)}) copy-start(f32[12,96]{1,0:T(8,128)} %copy-done.35) | copy-start | bytes 13828
  1403.3 537.5 %all-gather.11.cloned.1.call-start = ((), (), s32[]{:S(2)}) async-start(), calls=%async_computation.10 | async-start | bytes 42467328 | tf_op jit(solution)/shard_map/all_gather | solution.py:48
  1540.9 225.9 %copy-start.24 = (f32[12,768]{1,0:T(8,128)S(1)}, f32[12,768]{1,0:T(8,128)}, u32[]{:S(2)}) copy-start(f32[12,768]{1,0:T(8,128)} %copy-done.23) | copy-start | bytes 110596
  1766.8 769.8 %reduce-scatter.11.cloned.1.call-start = ((), (), s32[]{:S(2)}) async-start(), calls=%async_computation.11 | async-start | bytes 42467328 | tf_op jit(solution)/shard_map/reduce_scatter | solution.py:52
  1766.9 192.2 %copy-start.17 = (pred[768,768]{0,1:T(8,128)(4,1)S(1)}, pred[768,768]{0,1:T(8,128)(4,1)}, u32[]{:S(2)}) copy-start(pred[768,768]{0,1:T(8,128)(4,1)} %copy-done.16) | copy-start | bytes 1769476
  1766.9 192.2 %copy-start.38 = (f32[12,768]{1,0:T(8,128)S(1)}, f32[12,768]{1,0:T(8,128)}, u32[]{:S(2)}) copy-start(f32[12,768]{1,0:T(8,128)} %copy-done.37) | copy-start | bytes 110596
  1766.9 192.2 %copy-start.40 = (pred[12,768]{1,0:T(8,128)(4,1)S(1)}, pred[12,768]{1,0:T(8,128)(4,1)}, u32[]{:S(2)}) copy-start(pred[12,768]{1,0:T(8,128)(4,1)} %copy-done.39) | copy-start | bytes 27652
  1766.9 192.2 %copy-start.42 = (pred[12,768]{1,0:T(8,128)(4,1)S(1)}, pred[12,768]{1,0:T(8,128)(4,1)}, u32[]{:S(2)}) copy-start(pred[12,768]{1,0:T(8,128)(4,1)} %copy-done.41) | copy-start | bytes 27652
  1999.3 23.7 copy-start.9
  2053.0 40.3 %copy-start.2 = (f32[12,768,1,128]{1,3,0,2:T(8,128)}, f32[12,768,1,128]{1,3,0,2:T(8,128)S(1)}, u32[]{:S(2)}) copy-start(f32[12,768,1,128]{1,3,0,2:T(8,128)S(1)} %get-tuple-element.25) | copy-start | bytes 14155780
  2063.5 29.8 %copy-start.21 = (bf16[2048,256]{1,0:T(8,128)(2,1)S(1)}, bf16[2048,256]{1,0:T(8,128)(2,1)}, u32[]{:S(2)}) copy-start(bf16[2048,256]{1,0:T(8,128)(2,1)} %param.18) | copy-start | bytes 3145732
  2183.4 392.0 %all-reduce.8.cloned.1.call-start = ((), (), s32[]{:S(2)}) async-start(), calls=%async_computation.12 | async-start | bytes 8388608 | tf_op jit(solution)/shard_map/psum | solution.py:120
  2370.3 89.9 %copy-start.3 = (f32[12,768,128]{1,2,0:T(8,128)S(1)}, f32[12,768,128]{1,2,0:T(8,128)}, u32[]{:S(2)}) copy-start(f32[12,768,128]{1,2,0:T(8,128)} %get-tuple-element.23) | copy-start | bytes 14155780
  2479.3 39.6 %slice-start = ((s8[4718592]{0:T(1024)(128)(4,1)}), s8[524288]{0:T(1024)(128)(4,1)S(1)}, s32[]{:S(2)}) async-start(s8[4718592]{0:T(1024)(128)(4,1)} %bitcast.180), calls=%async_computation.13 | async-start | bytes 1048576
  2536.6 29.6 %copy-start.34 = (f32[12,96]{1,0:T(8,128)S(1)}, f32[12,96]{1,0:T(8,128)}, u32[]{:S(2)}) copy-start(f32[12,96]{1,0:T(8,128)} %copy-done.33) | copy-start | bytes 13828
  (27 other events, 313.2 us)
Sparse Core Ops, SparseCore 0:
  18.5 176.6 all-gather.4
  327.7 216.2 reduce-scatter.4
  545.9 173.7 all-gather.8
  722.0 173.8 all-gather.6
  1317.2 216.2 reduce-scatter.8
  1536.9 216.2 reduce-scatter.6
  1766.9 173.8 all-gather.10
  2183.6 216.2 reduce-scatter.10
  2498.6 70.1 all-reduce.7
where the time goes:
time: 2590 us
  matrix products  1280 us (49%)
  waiting for transfers between devices  1160 us (45%)
  other arithmetic  100 us (4%)
    all_gather x4, waiting for transfers between devices, gather_seq(): return lax.all_gather(x_loc, 'tp', axis=1, tiled=True)  603 us
    reduce_scatter x4, waiting for transfers between devices, scatter_seq(): return lax.psum_scatter(x_part, 'tp', scatter_dimension=1, tiled=True)  558 us
    dot_general x1, matrix products, local_layer(): jnp.einsum('bld,df->blf', gated_all, w_gate, preferred_element_type=jnp.f...  143 us
    dot_general x1, matrix products, local_layer(): jnp.einsum('blf,df->bld', d_upper, w_up, preferred_element_type=jnp.float32)  101 us
    dot_general x1, matrix products, local_layer(): jnp.einsum('bld,blf->df', gated_all, d_upper, preferred_element_type=jnp....  97.3 us
    dot_general x1, matrix products, local_layer(): jnp.einsum('bld,blf->df', gated_all, d_gate, preferred_element_type=jnp.f...  89.9 us
    dot_general x1, matrix products, local_layer(): jnp.einsum('blf,bld->fd', act, grad_all, preferred_element_type=jnp.float32)  89.5 us
    dot_general x1, matrix products, local_layer(): jnp.einsum('blf,df->bld', d_gate, w_gate, preferred_element_type=jnp.floa...  89.1 us
  transfers between devices with their start and end apart: 9, of which 7 were waited for; matrix products, arithmetic and copies ran while one was open for 22% of the time, Pallas kernels for 0%

commit v1 on v0

v1 whole, which is shorter than its diff:
```python
import functools
import math
import jax
import jax.numpy as jnp
from jax import lax
from jax.experimental import pallas as pl
from jax.experimental.pallas import tpu as pltpu
from jax.sharding import PartitionSpec as P

NORM_EPS = 1e-6
CHUNKS = 2
F32 = jnp.float32
BF16 = jnp.bfloat16
MASKED = -1e30


def rms_norm(x_in, gain):
    x_f = x_in.astype(F32)
    inv_rms = lax.rsqrt(jnp.mean(x_f * x_f, axis=-1, keepdims=True) + NORM_EPS)
    return (x_f * inv_rms * (1.0 + gain)).astype(BF16)


def rope_tables(positions, head_dim):
    half_dim = head_dim // 2
    exponent = jnp.arange(half_dim, dtype=F32) * (2.0 / head_dim)
    inv_freq = jnp.exp(exponent * (-math.log(10000.0)))
    angles = positions.astype(F32)[:, None] * inv_freq[None, :]
    return jnp.cos(angles), jnp.sin(angles)


def apply_rope(x_f, cos_t, sin_t):
    half_dim = x_f.shape[-1] // 2
    first = x_f[..., :half_dim]
    second = x_f[..., half_dim:]
    return jnp.concatenate([first * cos_t - second * sin_t, second * cos_t + first * sin_t], axis=-1)


def gated_act(gate, upper):
    return (jax.nn.gelu(gate, approximate=True) * upper).astype(BF16)


def dot_f32(lhs, rhs, lhs_dim, rhs_dim):
    return lax.dot_general(lhs, rhs, (((lhs_dim,), (rhs_dim,)), ((), ())), preferred_element_type=F32)


def attn_fwd_kernel(prefix_s, valid_s, q_own_ref, q_oth_ref, kv_own_ref, kv_oth_ref, cos_ref, sin_ref, qpos_ref, kpos_ref,
                    o_own_ref, o_oth_ref, r_own_ref, r_oth_ref):
    b = pl.program_id(0)
    rows, width = q_own_ref.shape[1:]
    hd = kv_own_ref.shape[-1] // 2
    half = hd // 2
    heads = width // hd
    scale = hd ** -0.5
    cos_t, sin_t = cos_ref[...], sin_ref[...]
    queries = []
    for src, dst in ((q_own_ref, r_own_ref), (q_oth_ref, r_oth_ref)):
        for n in range(heads):
            first = src[0, :, n * hd:n * hd + half]
            second = src[0, :, n * hd + half:(n + 1) * hd]
            q_1 = ((first * cos_t - second * sin_t).astype(BF16) * scale).astype(BF16)
            q_2 = ((second * cos_t + first * sin_t).astype(BF16) * scale).astype(BF16)
            dst[0, :, n * hd:n * hd + half] = q_1
            dst[0, :, n * hd + half:(n + 1) * hd] = q_2
            queries.append(jnp.concatenate([q_1, q_2], axis=1))
    n_keys = kv_own_ref.shape[0] * kv_own_ref.shape[2]
    keys = jnp.concatenate([kv_own_ref[:, 0, :, :hd].reshape(n_keys, hd), kv_oth_ref[:, 0, :, :hd].reshape(n_keys, hd)], axis=0)
    values = jnp.concatenate([kv_own_ref[:, 0, :, hd:].reshape(n_keys, hd), kv_oth_ref[:, 0, :, hd:].reshape(n_keys, hd)], axis=0)
    limit = jnp.minimum(valid_s[b], jnp.maximum(prefix_s[b], qpos_ref[...] + 1))
    visible = kpos_ref[...] < limit
    for side, dst in ((0, o_own_ref), (1, o_oth_ref)):
        query = jnp.concatenate(queries[side * heads:(side + 1) * heads], axis=0)
        scores = dot_f32(query, keys, 1, 1)
        scores = jnp.where(visible, scores, MASKED)
        top = jnp.max(scores, axis=-1, keepdims=True)
        expo = jnp.exp(scores - top)
        inv = 1.0 / jnp.sum(expo, axis=-1, keepdims=True)
        probs = (expo * inv).astype(BF16)
        mixed = dot_f32(probs, values, 1, 0).astype(BF16)
        for n in range(heads):
            dst[0, :, n * hd:(n + 1) * hd] = mixed[n * rows:(n + 1) * rows]


def attn_bwd_kernel(prefix_s, valid_s, q_own_ref, q_oth_ref, g_own_ref, g_oth_ref, kv_own_ref, kv_oth_ref, cos_ref, sin_ref,
                    qpos_ref, kpos_ref, dq_own_ref, dq_oth_ref, dkv_own_ref, dkv_oth_ref):
    b = pl.program_id(0)
    rows, width = q_own_ref.shape[1:]
    hd = kv_own_ref.shape[-1] // 2
    half = hd // 2
    heads = width // hd
    scale = hd ** -0.5
    cos_t, sin_t = cos_ref[...], sin_ref[...]
    shards = kv_own_ref.shape[0]
    n_keys = shards * kv_own_ref.shape[2]
    keys = jnp.concatenate([kv_own_ref[:, 0, :, :hd].reshape(n_keys, hd), kv_oth_ref[:, 0, :, :hd].reshape(n_keys, hd)], axis=0)
    values = jnp.concatenate([kv_own_ref[:, 0, :, hd:].reshape(n_keys, hd), kv_oth_ref[:, 0, :, hd:].reshape(n_keys, hd)], axis=0)
    limit = jnp.minimum(valid_s[b], jnp.maximum(prefix_s[b], qpos_ref[...] + 1))
    visible = kpos_ref[...] < limit
    d_keys, d_values = 0.0, 0.0
    for q_ref, g_ref, dst in ((q_own_ref, g_own_ref, dq_own_ref), (q_oth_ref, g_oth_ref, dq_oth_ref)):
        query = jnp.concatenate([q_ref[0, :, n * hd:(n + 1) * hd] for n in range(heads)], axis=0)
        grad = jnp.concatenate([g_ref[0, :, n * hd:(n + 1) * hd] for n in range(heads)], axis=0)
        scores = dot_f32(keys, query, 1, 1)
        scores = jnp.where(visible, scores, MASKED)
        top = jnp.max(scores, axis=0, keepdims=True)
        expo = jnp.exp(scores - top)
        inv = 1.0 / jnp.sum(expo, axis=0, keepdims=True)
        probs = expo * inv
        d_probs = dot_f32(values, grad, 1, 1)
        delta = jnp.sum(probs * d_probs, axis=0, keepdims=True)
        d_scores = (probs * (d_probs - delta)).astype(BF16)
        d_values = d_values + dot_f32(probs.astype(BF16), grad, 1, 0)
        d_keys = d_keys + dot_f32(d_scores, query, 1, 0)
        d_query = dot_f32(d_scores, keys, 0, 0) * scale
        for n in range(heads):
            g_1 = d_query[n * rows:(n + 1) * rows, :half]
            g_2 = d_query[n * rows:(n + 1) * rows, half:]
            dst[0, :, n * hd:n * hd + half] = (g_1 * cos_t + g_2 * sin_t).astype(BF16)
            dst[0, :, n * hd + half:(n + 1) * hd] = (g_2 * cos_t - g_1 * sin_t).astype(BF16)
    d_keys = d_keys.astype(BF16)
    d_values = d_values.astype(BF16)
    span = n_keys // shards
    for side, dst in ((0, dkv_own_ref), (1, dkv_oth_ref)):
        for c in range(shards):
            at = side * n_keys + c * span
            dst[c, 0, :, :hd] = d_keys[at:at + span]
            dst[c, 0, :, hd:] = d_values[at:at + span]


def attn_specs(batch, rows, width, shards, two_hd, half):
    q_spec = pl.BlockSpec((1, rows, width), lambda b, *_: (b, 0, 0))
    kv_spec = pl.BlockSpec((shards, 1, rows, two_hd), lambda b, *_: (0, b, 0, 0))
    tab_spec = pl.BlockSpec((rows, half), lambda b, *_: (0, 0))
    return q_spec, kv_spec, tab_spec


def whole(shape):
    return pl.BlockSpec(shape, lambda b, *_: tuple(0 for _ in shape))


def attn_fwd(q_own, q_oth, kv_own, kv_oth, cos_t, sin_t, qpos, kpos, prefix_len, valid_len):
    batch, rows, width = q_own.shape
    shards, two_hd = kv_own.shape[0], kv_own.shape[3]
    q_spec, kv_spec, tab_spec = attn_specs(batch, rows, width, shards, two_hd, two_hd // 4)
    heads = width * 2 // two_hd
    out = jax.ShapeDtypeStruct((batch, rows, width), BF16)
    qpos_col = jnp.tile(qpos, heads)[:, None]
    n_keys = kpos.shape[0]
    flops = 2 * 2 * batch * rows * 2 * width * n_keys
    return pl.pallas_call(
        attn_fwd_kernel,
        out_shape=(out, out, out, out),
        grid_spec=pltpu.PrefetchScalarGridSpec(
            num_scalar_prefetch=2, grid=(batch,),
            in_specs=[q_spec, q_spec, kv_spec, kv_spec, tab_spec, tab_spec, whole((heads * rows, 1)), whole((1, n_keys))],
            out_specs=[q_spec] * 4),
        compiler_params=pltpu.CompilerParams(dimension_semantics=("arbitrary",), vmem_limit_bytes=48 << 20),
        cost_estimate=pl.CostEstimate(flops=flops, bytes_accessed=batch * rows * width * 16 + kv_own.size * 4, transcendentals=batch * rows * heads * 2 * n_keys),
        name="attn_fwd",
    )(prefix_len, valid_len, q_own, q_oth, kv_own, kv_oth, cos_t, sin_t, qpos_col, kpos[None, :])


def attn_bwd(q_own, q_oth, g_own, g_oth, kv_own, kv_oth, cos_t, sin_t, qpos, kpos, prefix_len, valid_len):
    batch, rows, width = q_own.shape
    shards, two_hd = kv_own.shape[0], kv_own.shape[3]
    q_spec, kv_spec, tab_spec = attn_specs(batch, rows, width, shards, two_hd, two_hd // 4)
    heads = width * 2 // two_hd
    out = jax.ShapeDtypeStruct((batch, rows, width), BF16)
    kv_out = jax.ShapeDtypeStruct(kv_own.shape, BF16)
    qpos_row = jnp.tile(qpos, heads)[None, :]
    n_keys = kpos.shape[0]
    flops = 2 * 5 * batch * rows * 2 * width * n_keys
    return pl.pallas_call(
        attn_bwd_kernel,
        out_shape=(out, out, kv_out, kv_out),
        grid_spec=pltpu.PrefetchScalarGridSpec(
            num_scalar_prefetch=2, grid=(batch,),
            in_specs=[q_spec, q_spec, q_spec, q_spec, kv_spec, kv_spec, tab_spec, tab_spec, whole((1, heads * rows)), whole((n_keys, 1))],
            out_specs=[q_spec, q_spec, kv_spec, kv_spec]),
        compiler_params=pltpu.CompilerParams(dimension_semantics=("arbitrary",), vmem_limit_bytes=48 << 20),
        cost_estimate=pl.CostEstimate(flops=flops, bytes_accessed=batch * rows * width * 12 + kv_own.size * 8, transcendentals=batch * rows * heads * 2 * n_keys),
        name="attn_bwd",
    )(prefix_len, valid_len, q_own, q_oth, g_own, g_oth, kv_own, kv_oth, cos_t, sin_t, qpos_row, kpos[:, None])


def solution(mesh):
    tp_size = mesh.shape["tp"]
    chips = tp_size // 2
    act_spec = P("dp", "tp", None)
    in_specs = (act_spec, act_spec, P("dp"), P("dp"), P(None), P(None, "tp"), P(None, None), P(None, None), P("tp", None), P(None), P(None, "tp"), P(None, "tp"), P("tp", None))
    out_specs = (act_spec, act_spec, P("dp"), P("dp", "tp"), P("dp", None), P("dp", None), P(("dp", "tp"), None), P("dp"), P("dp", "tp"), P("dp", "tp"), P(("dp", "tp"), None))
    same_core = [[2 * c + k for c in range(chips)] for k in range(2)]
    partner = [(i, i ^ 1) for i in range(tp_size)]

    def gather4(x_loc):
        return lax.all_gather(x_loc, "tp", axis=0, tiled=False, axis_index_groups=same_core)

    def scatter4(x_part):
        return lax.psum_scatter(x_part, "tp", scatter_dimension=0, tiled=False, axis_index_groups=same_core)

    def swap(x_loc):
        return lax.ppermute(x_loc, "tp", partner)

    def local_layer(hidden, grad_out, prefix_len, valid_len, attn_norm, w_query, w_key, w_value, w_out, mlp_norm, w_gate, w_up, w_down):
        batch, rows, dim = hidden.shape
        hd = w_key.shape[1]
        tokens = batch * rows
        me = lax.axis_index("tp")
        core = lax.rem(me, 2)
        qpos = me * rows + jnp.arange(rows, dtype=jnp.int32)
        shard_pos = jnp.arange(rows, dtype=jnp.int32)[None, :] + (jnp.arange(chips, dtype=jnp.int32) * 2 * rows)[:, None]
        kpos = jnp.concatenate([(shard_pos + core * rows).reshape(-1), (shard_pos + (1 - core) * rows).reshape(-1)])
        cos_t, sin_t = rope_tables(qpos, hd)

        def rope_single(raw_proj):
            return apply_rope(raw_proj, cos_t, sin_t).astype(BF16)

        wq_own = gather4(w_query.T).reshape(chips * hd, dim)
        normed, norm1_pull = jax.vjp(rms_norm, hidden, attn_norm.astype(F32))
        normed_flat = normed.reshape(tokens, dim)
        k_raw = dot_f32(normed_flat, w_key, 1, 0).reshape(batch, rows, hd)
        keys, key_pull = jax.vjp(rope_single, k_raw)
        values = dot_f32(normed_flat, w_value, 1, 0).astype(BF16).reshape(batch, rows, hd)
        kv_own = gather4(jnp.concatenate([keys, values], axis=-1))
        wo_own = gather4(w_out).reshape(chips * hd, dim)
        wq_oth = swap(wq_own)
        kv_oth = swap(kv_own)
        wo_oth = swap(wo_own)
        q_own = dot_f32(normed_flat, wq_own, 1, 1).reshape(batch, rows, chips * hd)
        q_oth = dot_f32(normed_flat, wq_oth, 1, 1).reshape(batch, rows, chips * hd)
        mix_own, mix_oth, q_own, q_oth = attn_fwd(q_own, q_oth, kv_own, kv_oth, cos_t, sin_t, qpos, kpos, prefix_len, valid_len)
        mix_own = mix_own.reshape(tokens, chips * hd)
        mix_oth = mix_oth.reshape(tokens, chips * hd)
        attn_sum = dot_f32(mix_own, wo_own, 1, 0) + dot_f32(mix_oth, wo_oth, 1, 0)
        resid = (hidden.astype(F32) + attn_sum.reshape(batch, rows, dim)).astype(BF16)
        gated_in, norm2_pull = jax.vjp(rms_norm, resid, mlp_norm.astype(F32))

        step = batch // CHUNKS
        g_down = g_gate = g_up = 0.0
        mlp_sums, d_gated = [], []
        for c in range(CHUNKS):
            sl = slice(c * step, (c + 1) * step)
            g_own = gather4(grad_out[sl].reshape(step * rows, dim)).reshape(-1, dim)
            g_oth = swap(g_own)
            z_own = gather4(gated_in[sl].reshape(step * rows, dim)).reshape(-1, dim)
            z_oth = swap(z_own)
            outs, backs = [], []
            for z_all, g_all in ((z_own, g_own), (z_oth, g_oth)):
                d_act = dot_f32(g_all, w_down, 1, 1).astype(BF16)
                gate = dot_f32(z_all, w_gate, 1, 0)
                upper = dot_f32(z_all, w_up, 1, 0)
                act, act_pull = jax.vjp(gated_act, gate, upper)
                d_gate, d_upper = act_pull(d_act)
                d_gate = d_gate.astype(BF16)
                d_upper = d_upper.astype(BF16)
                outs.append(dot_f32(act, w_down, 1, 0))
                backs.append(dot_f32(d_gate, w_gate, 1, 1) + dot_f32(d_upper, w_up, 1, 1))
                g_down = g_down + dot_f32(act, g_all, 0, 0)
                g_gate = g_gate + dot_f32(z_all, d_gate, 0, 0)
                g_up = g_up + dot_f32(z_all, d_upper, 0, 0)
            for (own, oth), dest in ((outs, mlp_sums), (backs, d_gated)):
                part = (own + swap(oth.astype(BF16)).astype(F32)).astype(BF16)
                dest.append(scatter4(part.reshape(chips, step * rows, dim)).reshape(step, rows, dim))
        mlp_sum = jnp.concatenate(mlp_sums, axis=0)
        hidden_out = (resid.astype(F32) + mlp_sum.astype(F32)).astype(BF16)
        d_resid_norm, g_mlp_norm_part = norm2_pull(jnp.concatenate(d_gated, axis=0))
        d_resid = (grad_out.astype(F32) + d_resid_norm.astype(F32)).astype(BF16)

        d_resid_flat = d_resid.reshape(tokens, dim)
        d_mix_own = dot_f32(d_resid_flat, wo_own, 1, 1).astype(BF16).reshape(batch, rows, chips * hd)
        d_mix_oth = dot_f32(d_resid_flat, wo_oth, 1, 1).astype(BF16).reshape(batch, rows, chips * hd)
        dq_own, dq_oth, dkv_own, dkv_oth = attn_bwd(q_own, q_oth, d_mix_own, d_mix_oth, kv_own, kv_oth, cos_t, sin_t, qpos, kpos, prefix_len, valid_len)
        dkv = scatter4((dkv_own.astype(F32) + swap(dkv_oth).astype(F32)).astype(BF16))
        d_k_raw = key_pull(dkv[..., :hd])[0].astype(BF16).reshape(tokens, hd)
        d_values = dkv[..., hd:].reshape(tokens, hd)
        dq_own = dq_own.reshape(tokens, chips * hd)
        dq_oth = dq_oth.reshape(tokens, chips * hd)

        def weight_sum(own, oth):
            return scatter4((own + swap(oth)).reshape(chips, hd, dim))

        g_out = weight_sum(dot_f32(mix_own, d_resid_flat, 0, 0), dot_f32(mix_oth, d_resid_flat, 0, 0))
        g_query = weight_sum(dot_f32(dq_own, normed_flat, 0, 0), dot_f32(dq_oth, normed_flat, 0, 0)).T
        d_normed = (dot_f32(dq_own, wq_own, 1, 0) + dot_f32(dq_oth, wq_oth, 1, 0)
                    + dot_f32(d_k_raw, w_key, 1, 1) + dot_f32(d_values, w_value, 1, 1)).astype(BF16)
        d_hidden_norm, g_attn_norm_part = norm1_pull(d_normed.reshape(batch, rows, dim))
        grad_hidden = (d_resid.astype(F32) + d_hidden_norm.astype(F32)).astype(BF16)
        g_key = lax.psum(dot_f32(normed_flat, d_k_raw, 0, 0), "tp")
        g_value = lax.psum(dot_f32(normed_flat, d_values, 0, 0), "tp")
        g_attn_norm = lax.psum(g_attn_norm_part, "tp")
        g_mlp_norm = lax.psum(g_mlp_norm_part, "tp")
        return (hidden_out, grad_hidden, g_attn_norm, g_query, g_key, g_value, g_out, g_mlp_norm, g_gate, g_up, g_down)

    return jax.shard_map(local_layer, mesh=mesh, in_specs=in_specs, out_specs=out_specs, check_vma=False)
```

time: 2590 us -> 1860 us (0.72)
  waiting for transfers between devices: 1160 us -> 408 us
  Pallas kernels: 0 us -> 58.9 us
  matrix products: 1280 us -> 1230 us
    reduce_scatter x4 -> x0, waiting for transfers between devices: 558 us -> none  [scatter_seq(): return lax.psum_scatter(x_part, 'tp', scatter_dimension=1, tiled=True)]
    all_gather x4 -> x7, waiting for transfers between devices: 603 us -> 297 us  [gather4(): lax.all_gather(x_loc, 'tp', axis=0, tiled=False, axis_index_groups=same_c...]
    unnamed x9 -> x22, waiting for transfers between devices: 0.81 us -> 82.3 us
    pallas_call x0 -> x2, Pallas kernels: none -> 58.9 us  [the longest x1 37.8 us: attn_bwd(): pl.pallas_call(attn_bwd_kernel, out_shape=(out, out, kv_out, kv_out), gri...]
    dot_general x27 -> x54, matrix products: 1280 us -> 1230 us  [dot_f32(): lax.dot_general(lhs, rhs, (((lhs_dim,), (rhs_dim,)), ((), ())), preferred...]
    ppermute x0 -> x14, waiting for transfers between devices: none -> 28.6 us  [swap(): return lax.ppermute(x_loc, 'tp', partner)]
  transfers between devices with their start and end apart: 9 -> 29, of which waited for: 7 -> 9; matrix products, arithmetic and copies ran while one was open for 22% -> 68% of each run, Pallas kernels for 0% -> 1%
where the time goes in v1:
time: 1860 us; the launch traced here: 1850 us
  matrix products  1230 us (66%)
  waiting for transfers between devices  408 us (22%)
  other arithmetic  86.7 us (5%)
  Pallas kernels  58.9 us (3%)
  local copies, waits for them, and re-layouts  32.8 us (2%)
  blocking collectives  22.4 us (1%)
    dot_general x54, matrix products, dot_f32(): lax.dot_general(lhs, rhs, (((lhs_dim,), (rhs_dim,)), ((), ())), preferred...  1230 us
    all_gather x7, waiting for transfers between devices, gather4(): lax.all_gather(x_loc, 'tp', axis=0, tiled=False, axis_index_groups=same_c...  297 us
    unnamed x22, waiting for transfers between devices  82.3 us
    pallas_call x1, Pallas kernels, attn_bwd(): pl.pallas_call(attn_bwd_kernel, out_shape=(out, out, kv_out, kv_out), gri...  37.8 us
  transfers between devices with their start and end apart: 29, of which 9 were waited for; matrix products, arithmetic and copies ran while one was open for 68% of the time, Pallas kernels for 1%

profile of v1, /device:TPU:0, one launch (start us, length us, event | category | flops | bytes accessed | tf_op | source)
XLA Modules:
  0.0 1854.5 jit_solution(1190847511621107094)
XLA Ops:
  29.9 30.0 %all-gather.19.cloned.1.call-done = bf16[1024,2048]{1,0:T(8,128)(2,1)} async-done(((bf16[256,2048]{1,0:T(8,128)(2,1)}), bf16[1024,2048]{1,0:T(8,128)(2,1)}) %all-gather.19.cloned.1.call-update) | async-done | bytes 4194320 | tf_op jit(solution)/shard_map/all_gather | solution.py:195
  59.9 53.6 %all-gather.21.cloned.1.call-done = bf16[48,96,512]{2,1,0:T(8,128)(2,1)} async-done(((bf16[12,96,512]{2,1,0:T(8,128)(2,1)}), bf16[48,96,512]{2,1,0:T(8,128)(2,1)}) %all-gather.21.cloned.1.call-update) | async-done | bytes 4718608 | tf_op jit(solution)/shard_map/all_gather | solution.py:195
  113.4 48.5 %all-gather.23.cloned.1.call-done = bf16[1024,2048]{1,0:T(8,128)(2,1)} async-done(((bf16[256,2048]{1,0:T(8,128)(2,1)}), bf16[1024,2048]{1,0:T(8,128)(2,1)}) %all-gather.23.cloned.1.call-update) | async-done | bytes 4194320 | tf_op jit(solution)/shard_map/all_gather | solution.py:195
  254.8 92.1 %all-gather.17.cloned.1.call-done = bf16[4,576,2048]{2,1,0:T(8,128)(2,1)} async-done(((bf16[1,576,2048]{2,1,0:T(8,128)(2,1)}), bf16[4,576,2048]{2,1,0:T(8,128)(2,1)}) %all-gather.17.cloned.1.call-update) | async-done | bytes 9437200 | tf_op jit(solution)/shard_map/all_gather | solution.py:195
  453.3 26.8 %fusion.76 = f32[2304,2048]{1,0:T(8,128)} fusion(bf16[2304,2048]{1,0:T(8,128)(2,1)} %bitcast.204, bf16[2048,2048]{1,0:T(8,128)(2,1)} %param.24), kind=kOutput, calls=%fused_computation.158 | convolution fusion | flops 19327352832 | bytes 36700160 | tf_op jit(solution)/shard_map/dot_general | solution.py:43
  480.1 52.6 %all-gather.13.cloned.1.call-done = bf16[4,576,2048]{2,1,0:T(8,128)(2,1)} async-done(((bf16[1,576,2048]{2,1,0:T(8,128)(2,1)}), bf16[4,576,2048]{2,1,0:T(8,128)(2,1)}) %all-gather.13.cloned.1.call-update) | async-done | bytes 9437200 | tf_op jit(solution)/shard_map/all_gather | solution.py:195
  532.7 45.9 %fusion.10 = (bf16[2304,2048]{1,0:T(8,128)(2,1)}, bf16[2304,2048]{1,0:T(8,128)(2,1)}, f32[2304,2048]{1,0:T(8,128)}) fusion(f32[2304,2048]{1,0:T(8,128)} %fusion.76, bf16[2304,2048]{1,0:T(8,128)(2,1)} %convolution_convert_fusion.3, bf16[2304,2048]{1,0:T(8,128)(2,1)} %bitcast.205, bf16[2048,2048]{1,0:T(8,128)(2,1)} %param.23), kind=kOutput, calls=%fused_computation.26 | convolution fusion | flops 19445317632 | bytes 83886080 | tf_op jit(solution)/shard_map/dot_general | solution.py:43
  578.6 27.1 %fusion.80 = f32[2304,2048]{1,0:T(8,128)} fusion(bf16[2304,2048]{1,0:T(8,128)(2,1)} %get-tuple-element.37, bf16[2048,2048]{1,0:T(8,128)(2,1)} %param.23), kind=kOutput, calls=%fused_computation.162 | convolution fusion | flops 19327352832 | bytes 36700160 | tf_op jit(solution)/shard_map/dot_general | solution.py:43
  630.3 43.8 %fusion.17 = (bf16[2304,2048]{1,0:T(8,128)(2,1)}, bf16[2304,2048]{1,0:T(8,128)(2,1)}) fusion(f32[2304,2048]{1,0:T(8,128)} %fusion.77, bf16[2304,2048]{1,0:T(8,128)(2,1)} %convolution_convert_fusion.2, bf16[2304,2048]{1,0:T(8,128)(2,1)} %collective-permute-done.3, bf16[2048,2048]{1,0:T(8,128)(2,1)} %param.24), kind=kOutput, calls=%fused_computation.33 | convolution fusion | flops 19445317632 | bytes 65011712 | tf_op jit(solution)/shard_map/dot_general | solution.py:43
  674.0 26.9 %fusion.81 = f32[2304,2048]{1,0:T(8,128)} fusion(bf16[2304,2048]{1,0:T(8,128)(2,1)} %get-tuple-element.39, bf16[2048,2048]{1,0:T(8,128)(2,1)} %param.23), kind=kOutput, calls=%fused_computation.163 | convolution fusion | flops 19327352832 | bytes 36700160 | tf_op jit(solution)/shard_map/dot_general | solution.py:43
  701.0 32.6 %add_convert_fusion.3 = bf16[2304,2048]{1,0:T(8,128)(2,1)} fusion(f32[2304,2048]{1,0:T(8,128)} %fusion.81, bf16[2048,2048]{1,0:T(8,128)(2,1)} %param.24, bf16[2304,2048]{1,0:T(8,128)(2,1)} %convolution_convert_fusion.2, f32[2304,2048]{1,0:T(8,128)} %fusion.77), kind=kOutput, calls=%fused_computation.51 | convolution fusion | flops 19388694528 | bytes 65011712 | tf_op jit(solution)/shard_map/dot_general | solution.py:43
  734.0 26.4 %fusion.79 = f32[2304,2048]{1,0:T(8,128)} fusion(bf16[2304,2048]{1,0:T(8,128)(2,1)} %collective-permute-done.5, bf16[2048,2048]{1,0:T(8,128)(2,1)} %param.23), kind=kOutput, calls=%fused_computation.161 | convolution fusion | flops 19327352832 | bytes 36700160 | tf_op jit(solution)/shard_map/dot_general | solution.py:43
  760.4 43.7 %fusion.31 = (bf16[2304,2048]{1,0:T(8,128)(2,1)}, bf16[2304,2048]{1,0:T(8,128)(2,1)}) fusion(f32[2304,2048]{1,0:T(8,128)} %fusion.79, bf16[2304,2048]{1,0:T(8,128)(2,1)} %convolution_convert_fusion, bf16[2304,2048]{1,0:T(8,128)(2,1)} %collective-permute-done.5, bf16[2048,2048]{1,0:T(8,128)(2,1)} %param.24), kind=kOutput, calls=%fused_computation.47 | convolution fusion | flops 19445317632 | bytes 65011712 | tf_op jit(solution)/shard_map/dot_general | solution.py:43
  804.1 26.8 %fusion.83 = f32[2304,2048]{1,0:T(8,128)} fusion(bf16[2304,2048]{1,0:T(8,128)(2,1)} %get-tuple-element.43, bf16[2048,2048]{1,0:T(8,128)(2,1)} %param.23), kind=kOutput, calls=%fused_computation.165 | convolution fusion | flops 19327352832 | bytes 36700160 | tf_op jit(solution)/shard_map/dot_general | solution.py:43
  830.9 31.9 %add_convert_fusion.2 = bf16[2304,2048]{1,0:T(8,128)(2,1)} fusion(bf16[2304,2048]{1,0:T(8,128)(2,1)} %collective-permute-done.8, f32[2304,2048]{1,0:T(8,128)} %fusion.80, bf16[2048,2048]{1,0:T(8,128)(2,1)} %param.24, bf16[2304,2048]{1,0:T(8,128)(2,1)} %convolution_convert_fusion.3, f32[2304,2048]{1,0:T(8,128)} %get-tuple-element.62), kind=kOutput, calls=%fused_computation.50 | convolution fusion | flops 19398131712 | bytes 74448896 | tf_op jit(solution)/shard_map/dot_general | solution.py:43
  862.9 32.8 %add_convert_fusion.1 = bf16[2304,2048]{1,0:T(8,128)(2,1)} fusion(f32[2304,2048]{1,0:T(8,128)} %fusion.83, bf16[2048,2048]{1,0:T(8,128)(2,1)} %param.24, bf16[2304,2048]{1,0:T(8,128)(2,1)} %convolution_convert_fusion, f32[2304,2048]{1,0:T(8,128)} %fusion.79), kind=kOutput, calls=%fused_computation.49 | convolution fusion | flops 19388694528 | bytes 65011712 | tf_op jit(solution)/shard_map/dot_general | solution.py:43
  895.8 26.4 %fusion.78 = f32[2304,2048]{1,0:T(8,128)} fusion(bf16[2304,2048]{1,0:T(8,128)(2,1)} %bitcast.209, bf16[2048,2048]{1,0:T(8,128)(2,1)} %param.24), kind=kOutput, calls=%fused_computation.160 | convolution fusion | flops 19327352832 | bytes 36700160 | tf_op jit(solution)/shard_map/dot_general | solution.py:43
  922.2 46.5 %fusion.24 = (bf16[2304,2048]{1,0:T(8,128)(2,1)}, bf16[2304,2048]{1,0:T(8,128)(2,1)}, f32[2304,2048]{1,0:T(8,128)}) fusion(f32[2304,2048]{1,0:T(8,128)} %fusion.78, bf16[2304,2048]{1,0:T(8,128)(2,1)} %convolution_convert_fusion.1, bf16[2304,2048]{1,0:T(8,128)(2,1)} %bitcast.210, bf16[2048,2048]{1,0:T(8,128)(2,1)} %param.23), kind=kOutput, calls=%fused_computation.40 | convolution fusion | flops 19445317632 | bytes 83886080 | tf_op jit(solution)/shard_map/dot_general | solution.py:43
  968.7 26.8 %fusion.82 = f32[2304,2048]{1,0:T(8,128)} fusion(bf16[2304,2048]{1,0:T(8,128)(2,1)} %get-tuple-element.41, bf16[2048,2048]{1,0:T(8,128)(2,1)} %param.23), kind=kOutput, calls=%fused_computation.164 | convolution fusion | flops 19327352832 | bytes 36700160 | tf_op jit(solution)/shard_map/dot_general | solution.py:43
  995.5 31.8 %add_convert_fusion = bf16[2304,2048]{1,0:T(8,128)(2,1)} fusion(bf16[2304,2048]{1,0:T(8,128)(2,1)} %collective-permute-done.10, f32[2304,2048]{1,0:T(8,128)} %fusion.82, bf16[2048,2048]{1,0:T(8,128)(2,1)} %param.24, bf16[2304,2048]{1,0:T(8,128)(2,1)} %convolution_convert_fusion.1, f32[2304,2048]{1,0:T(8,128)} %get-tuple-element.61), kind=kOutput, calls=%fused_computation.48 | convolution fusion | flops 19398131712 | bytes 74448896 | tf_op jit(solution)/shard_map/dot_general | solution.py:43
  1158.6 27.3 %fusion.92 = f32[2048,2048]{1,0:T(8,128)} fusion(bf16[2304,2048]{1,0:T(8,128)(2,1)} %get-tuple-element.38, bf16[2304,2048]{1,0:T(8,128)(2,1)} %bitcast.199), kind=kOutput, calls=%fused_computation.174 | convolution fusion | flops 19327352832 | bytes 35651584 | tf_op jit(solution)/shard_map/dot_general | solution.py:43
  1185.9 26.9 %fusion.94 = f32[2048,2048]{1,0:T(8,128)} fusion(bf16[2304,2048]{1,0:T(8,128)(2,1)} %get-tuple-element.42, bf16[2304,2048]{1,0:T(8,128)(2,1)} %bitcast.202), kind=kOutput, calls=%fused_computation.176 | convolution fusion | flops 19327352832 | bytes 35651584 | tf_op jit(solution)/shard_map/dot_general | solution.py:43
  1220.2 80.8 %reduce-scatter.24.cloned.1.call-done = bf16[1,576,2048]{2,1,0:T(8,128)(2,1)} async-done(((bf16[4,576,2048]{2,1,0:T(8,128)(2,1)}), bf16[1,576,2048]{2,1,0:T(8,128)(2,1)}) %reduce-scatter.24.cloned.1.call-update) | async-done | bytes 2359312
  1329.3 37.8 %attn_bwd.1 = (bf16[12,96,1024]{2,1,0:T(8,128)(2,1)S(1)}, bf16[12,96,1024]{2,1,0:T(8,128)(2,1)S(1)}, bf16[4,12,96,512]{3,2,1,0:T(8,128)(2,1)}, bf16[4,12,96,512]{3,2,1,0:T(8,128)(2,1)}) custom-call(s32[12]{0:T(128)S(1)} %copy-done.2, s32[12]{0:T(128)S(1)} %copy-done.4, bf16[12,96,1024]{2,1,0:T(8,128)(2,1)} %get-tuple-element.21.q_own_ref, ...), custom_call_target="tpu_custom_call" | custom-call | flops 18119393280 | bytes 33030144 | tf_op jit(solution)/shard_map/attn_bwd/pallas_call | solution.py:172
  1367.2 29.0 %fusion.89 = f32[2048,2048]{1,0:T(8,128)} fusion(bf16[2304,2048]{1,0:T(8,128)(2,1)} %bitcast.206, bf16[2304,2048]{1,0:T(8,128)(2,1)} %get-tuple-element.37), kind=kOutput, calls=%fused_computation.171 | convolution fusion | flops 19327352832 | bytes 35651584 | tf_op jit(solution)/shard_map/dot_general | solution.py:43
  1427.9 29.6 %fusion.63 = f32[2048,2048]{1,0:T(8,128)} fusion(bf16[2304,2048]{1,0:T(8,128)(2,1)} %bitcast.211, bf16[2304,2048]{1,0:T(8,128)(2,1)} %convolution_convert_fusion.1, f32[2304,2048]{1,0:T(8,128)} %get-tuple-element.61), kind=kOutput, calls=%fused_computation.152 | convolution fusion | flops 19379257344 | bytes 54525952 | tf_op jit(solution)/shard_map/dot_general | solution.py:43
  1468.1 29.3 %fusion.69 = f32[2048,2048]{1,0:T(8,128)} fusion(bf16[2304,2048]{1,0:T(8,128)(2,1)} %bitcast.207, bf16[2304,2048]{1,0:T(8,128)(2,1)} %convolution_convert_fusion.3, f32[2304,2048]{1,0:T(8,128)} %get-tuple-element.62), kind=kOutput, calls=%fused_computation.154 | convolution fusion | flops 19379257344 | bytes 54525952 | tf_op jit(solution)/shard_map/dot_general | solution.py:43
  1557.1 27.2 %fusion.90 = f32[2048,2048]{1,0:T(8,128)} fusion(bf16[2304,2048]{1,0:T(8,128)(2,1)} %collective-permute-done.3, bf16[2304,2048]{1,0:T(8,128)(2,1)} %get-tuple-element.39), kind=kOutput, calls=%fused_computation.172 | convolution fusion | flops 19327352832 | bytes 35651584 | tf_op jit(solution)/shard_map/dot_general | solution.py:43
  1584.3 36.4 %add_add_fusion = f32[2048,2048]{1,0:T(8,128)} fusion(f32[2048,2048]{1,0:T(8,128)} %fusion.94, f32[2048,2048]{1,0:T(8,128)} %fusion.92, f32[2048,2048]{1,0:T(8,128)} %fusion.93, bf16[2304,2048]{1,0:T(8,128)(2,1)} %get-tuple-element.44, bf16[2304,2048]{1,0:T(8,128)(2,1)} %copy-done.39), kind=kOutput, calls=%fused_computation.72 | convolution fusion | flops 19339935744 | bytes 85983232 | tf_op jit(solution)/shard_map/dot_general | solution.py:43
  1631.6 28.9 %fusion.66 = f32[2048,2048]{1,0:T(8,128)} fusion(bf16[2304,2048]{1,0:T(8,128)(2,1)} %collective-permute-done.3, bf16[2304,2048]{1,0:T(8,128)(2,1)} %convolution_convert_fusion.2, f32[2304,2048]{1,0:T(8,128)} %fusion.77), kind=kOutput, calls=%fused_computation.153 | convolution fusion | flops 19379257344 | bytes 54525952 | tf_op jit(solution)/shard_map/dot_general | solution.py:43
  1660.6 36.5 %add_add_fusion.2 = f32[2048,2048]{1,0:T(8,128)} fusion(f32[2048,2048]{1,0:T(8,128)} %fusion.91, f32[2048,2048]{1,0:T(8,128)} %fusion.89, f32[2048,2048]{1,0:T(8,128)} %fusion.90, bf16[2304,2048]{1,0:T(8,128)(2,1)} %collective-permute-done.5, bf16[2304,2048]{1,0:T(8,128)(2,1)} %get-tuple-element.43), kind=kOutput, calls=%fused_computation.74 | convolution fusion | flops 19339935744 | bytes 85983232 | tf_op jit(solution)/shard_map/dot_general | solution.py:43
  1728.1 40.9 %add_add_fusion.1 = f32[2048,2048]{1,0:T(8,128)} fusion(f32[2048,2048]{1,0:T(8,128)} %fusion.63, f32[2048,2048]{1,0:T(8,128)} %fusion.69, f32[2048,2048]{1,0:T(8,128)} %fusion.66, bf16[2304,2048]{1,0:T(8,128)(2,1)} %collective-permute-done.5, bf16[2304,2048]{1,0:T(8,128)(2,1)} %convolution_convert_fusion, f32[2304,2048]{1,0:T(8,128)} %fusion.79), kind=kOutput, calls=%fused_computation.73 | convolution fusion | flops 19391840256 | bytes 104857600 | tf_op jit(solution)/shard_map/dot_general | solution.py:43
  (263 shorter events, 635.9 us)
Async XLA Ops:
  7.2 52.7 %all-gather.19.cloned.1.call-start = ((), (), s32[]{:S(2)}) async-start(), calls=%async_computation.11 | async-start | bytes 5242880 | tf_op jit(solution)/shard_map/all_gather | solution.py:195
  9.6 103.8 %all-gather.21.cloned.1.call-start = ((), (), s32[]{:S(2)}) async-start(), calls=%async_computation.12 | async-start | bytes 5898240 | tf_op jit(solution)/shard_map/all_gather | solution.py:195
  21.5 141.4 %copy-start.38 = (bf16[2048]{0:T(1024)(128)(2,1)S(1)}, bf16[2048]{0:T(1024)(128)(2,1)}, u32[]{:S(2)}) copy-start(bf16[2048]{0:T(1024)(128)(2,1)} %param.22) | copy-start | bytes 12292
  22.7 139.2 %all-gather.23.cloned.1.call-start = ((), (), s32[]{:S(2)}) async-start(), calls=%async_computation.13 | async-start | bytes 5242880 | tf_op jit(solution)/shard_map/all_gather | solution.py:195
  23.4 231.3 %all-gather.15.cloned.1.call-start = ((), (), s32[]{:S(2)}) async-start(), calls=%async_computation.9 | async-start | bytes 11796480 | tf_op jit(solution)/shard_map/all_gather | solution.py:195
  28.7 318.2 %all-gather.17.cloned.1.call-start = ((), (), s32[]{:S(2)}) async-start(), calls=%async_computation.10 | async-start | bytes 11796480 | tf_op jit(solution)/shard_map/all_gather | solution.py:195
  29.3 423.5 %all-gather.11.cloned.1.call-start = ((), (), s32[]{:S(2)}) async-start(), calls=%async_computation.7 | async-start | bytes 11796480 | tf_op jit(solution)/shard_map/all_gather | solution.py:195
  59.9 112.8 %collective-permute-start = (bf16[1024,2048]{1,0:T(8,128)(2,1)}, bf16[1024,2048]{1,0:T(8,128)(2,1)}, u32[]{:S(2)}, u32[]{:S(2)}) collective-permute-start(bf16[1024,2048]{1,0:T(8,128)(2,1)} %all-gather.19.cloned.1.call-done), channel_id=1, source_target_pairs={{0,1},{1,0},{2,3},{3,2},{4,5},{5,4},{6,7},{7,6}} | collective-permute-start | bytes 12582920 | tf_op jit(solution)/shard_map/ppermute | solution.py:201
  113.4 69.0 %collective-permute-start.1 = (bf16[4,12,96,512]{3,2,1,0:T(8,128)(2,1)}, bf16[4,12,96,512]{3,2,1,0:T(8,128)(2,1)}, u32[]{:S(2)}, u32[]{:S(2)}) collective-permute-start(bf16[4,12,96,512]{3,2,1,0:T(8,128)(2,1)} %bitcast.215), channel_id=1, source_target_pairs={{0,1},{1,0},{2,3},{3,2},{4,5},{5,4},{6,7},{7,6}} | collective-permute-start | bytes 14155784 | tf_op jit(solution)/shard_map/ppermute | solution.py:201
  161.9 41.7 %collective-permute-start.2 = (bf16[1024,2048]{1,0:T(8,128)(2,1)}, bf16[1024,2048]{1,0:T(8,128)(2,1)}, u32[]{:S(2)}, u32[]{:S(2)}) collective-permute-start(bf16[1024,2048]{1,0:T(8,128)(2,1)} %all-gather.23.cloned.1.call-done), channel_id=1, source_target_pairs={{0,1},{1,0},{2,3},{3,2},{4,5},{5,4},{6,7},{7,6}} | collective-permute-start | bytes 12582920 | tf_op jit(solution)/shard_map/ppermute | solution.py:201
  163.0 64.6 %copy-start.25 = (f32[2048]{0:T(1024)}, f32[2048]{0:T(1024)S(1)}, u32[]{:S(2)}) copy-start(f32[2048]{0:T(1024)S(1)} %convert_add_fusion.2) | copy-start | bytes 24580
  234.0 298.7 %all-gather.13.cloned.1.call-start = ((), (), s32[]{:S(2)}) async-start(), calls=%async_computation.8 | async-start | bytes 11796480 | tf_op jit(solution)/shard_map/all_gather | solution.py:195
  254.7 143.9 %collective-permute-start.7 = (bf16[2304,2048]{1,0:T(8,128)(2,1)}, bf16[2304,2048]{1,0:T(8,128)(2,1)}, u32[]{:S(2)}, u32[]{:S(2)}) collective-permute-start(bf16[2304,2048]{1,0:T(8,128)(2,1)} %bitcast.197), channel_id=1, source_target_pairs={{0,1},{1,0},{2,3},{3,2},{4,5},{5,4},{6,7},{7,6}} | collective-permute-start | bytes 28311560 | tf_op jit(solution)/shard_map/ppermute | solution.py:201
  254.7 958.1 %reduce-scatter.26.cloned.1.call-start = ((), (), s32[]{:S(2)}) async-start(), calls=%async_computation.16 | async-start | bytes 11796480
  346.9 77.8 %collective-permute-start.9 = (bf16[2304,2048]{1,0:T(8,128)(2,1)}, bf16[2304,2048]{1,0:T(8,128)(2,1)S(1)}, u32[]{:S(2)}, u32[]{:S(2)}) collective-permute-start(bf16[2304,2048]{1,0:T(8,128)(2,1)} %bitcast.200), channel_id=1, source_target_pairs={{0,1},{1,0},{2,3},{3,2},{4,5},{5,4},{6,7},{7,6}} | collective-permute-start | bytes 28311560 | tf_op jit(solution)/shard_map/ppermute | solution.py:201
  452.8 152.9 %collective-permute-start.3 = (bf16[2304,2048]{1,0:T(8,128)(2,1)}, bf16[2304,2048]{1,0:T(8,128)(2,1)}, u32[]{:S(2)}, u32[]{:S(2)}) collective-permute-start(bf16[2304,2048]{1,0:T(8,128)(2,1)} %bitcast.203), channel_id=1, source_target_pairs={{0,1},{1,0},{2,3},{3,2},{4,5},{5,4},{6,7},{7,6}} | collective-permute-start | bytes 28311560 | tf_op jit(solution)/shard_map/ppermute | solution.py:201
  532.7 201.3 %collective-permute-start.5 = (bf16[2304,2048]{1,0:T(8,128)(2,1)}, bf16[2304,2048]{1,0:T(8,128)(2,1)}, u32[]{:S(2)}, u32[]{:S(2)}) collective-permute-start(bf16[2304,2048]{1,0:T(8,128)(2,1)} %bitcast.208), channel_id=1, source_target_pairs={{0,1},{1,0},{2,3},{3,2},{4,5},{5,4},{6,7},{7,6}} | collective-permute-start | bytes 28311560 | tf_op jit(solution)/shard_map/ppermute | solution.py:201
  733.5 97.4 %collective-permute-start.8 = (bf16[2304,2048]{1,0:T(8,128)(2,1)}, bf16[2304,2048]{1,0:T(8,128)(2,1)}, u32[]{:S(2)}, u32[]{:S(2)}) collective-permute-start(bf16[2304,2048]{1,0:T(8,128)(2,1)} %add_convert_fusion.3), channel_id=1, source_target_pairs={{0,1},{1,0},{2,3},{3,2},{4,5},{5,4},{6,7},{7,6}} | collective-permute-start | bytes 28311560 | tf_op jit(solution)/shard_map/ppermute | solution.py:201
  862.8 350.0 %reduce-scatter.28.cloned.1.call-start = ((), (), s32[]{:S(2)}) async-start(), calls=%async_computation.17 | async-start | bytes 11796480
  895.7 99.8 %collective-permute-start.10 = (bf16[2304,2048]{1,0:T(8,128)(2,1)}, bf16[2304,2048]{1,0:T(8,128)(2,1)}, u32[]{:S(2)}, u32[]{:S(2)}) collective-permute-start(bf16[2304,2048]{1,0:T(8,128)(2,1)} %add_convert_fusion.1), channel_id=1, source_target_pairs={{0,1},{1,0},{2,3},{3,2},{4,5},{5,4},{6,7},{7,6}} | collective-permute-start | bytes 28311560 | tf_op jit(solution)/shard_map/ppermute | solution.py:201
  1027.4 192.8 %reduce-scatter.22.cloned.1.call-start = ((), (), s32[]{:S(2)}) async-start(), calls=%async_computation.14 | async-start | bytes 11796480
  1051.9 14.8 collective-permute-start.4
  1092.6 208.5 %reduce-scatter.24.cloned.1.call-start = ((), (), s32[]{:S(2)}) async-start(), calls=%async_computation.15 | async-start | bytes 11796480
  1117.2 14.7 collective-permute-start.6
  1157.7 365.0 %reduce-scatter.30.cloned.1.call-start = ((), (), s32[]{:S(2)}) async-start(), calls=%async_computation.18 | async-start | bytes 5898240
  1367.1 54.4 %collective-permute-start.11 = (bf16[4,12,96,512]{3,2,1,0:T(8,128)(2,1)}, bf16[4,12,96,512]{3,2,1,0:T(8,128)(2,1)}, u32[]{:S(2)}, u32[]{:S(2)}) collective-permute-start(bf16[4,12,96,512]{3,2,1,0:T(8,128)(2,1)} %get-tuple-element.26), channel_id=1, source_target_pairs={{0,1},{1,0},{2,3},{3,2},{4,5},{5,4},{6,7},{7,6}} | collective-permute-start | bytes 14155784 | tf_op jit(solution)/shard_map/ppermute | solution.py:201
  1367.2 54.4 %slice-start.4 = ((s8[4718592]{0:T(1024)(128)(4,1)}), s8[4194304]{0:T(1024)(128)(4,1)S(1)}, s32[]{:S(2)}) async-start(s8[4718592]{0:T(1024)(128)(4,1)} %bitcast.184), calls=%async_computation.26 | async-start | bytes 8388608
  1427.9 413.7 %all-reduce.13.cloned.1.call-start = ((), (), s32[]{:S(2)}) async-start(), calls=%async_computation.21 | async-start | bytes 8388608 | tf_op jit(solution)/shard_map/psum | solution.py:287
  1467.8 77.4 %collective-permute-start.13 = (f32[1024,2048]{1,0:T(8,128)}, f32[1024,2048]{1,0:T(8,128)}, u32[]{:S(2)}, u32[]{:S(2)}) collective-permute-start(f32[1024,2048]{1,0:T(8,128)} %convolution_bitcast_fusion), channel_id=1, source_target_pairs={{0,1},{1,0},{2,3},{3,2},{4,5},{5,4},{6,7},{7,6}} | collective-permute-start | bytes 25165832 | tf_op jit(solution)/shard_map/ppermute | solution.py:201
  1535.0 306.6 %reduce-scatter.34.cloned.1.call-start = ((), (), s32[]{:S(2)}) async-start(), calls=%async_computation.20 | async-start | bytes 10485760
  1557.1 284.5 %reduce-scatter.32.cloned.1.call-start = ((), (), s32[]{:S(2)}) async-start(), calls=%async_computation.19 | async-start | bytes 10485760
  1631.4 76.0 %collective-permute-start.12 = (f32[1024,2048]{1,0:T(8,128)}, f32[1024,2048]{1,0:T(8,128)}, u32[]{:S(2)}, u32[]{:S(2)}) collective-permute-start(f32[1024,2048]{1,0:T(8,128)} %convolution_bitcast_fusion.1), channel_id=1, source_target_pairs={{0,1},{1,0},{2,3},{3,2},{4,5},{5,4},{6,7},{7,6}} | collective-permute-start | bytes 25165832 | tf_op jit(solution)/shard_map/ppermute | solution.py:201
  (55 other events, 765.2 us)
Sparse Core Ops, SparseCore 0:
  10.3 49.4 all-gather.18
  62.2 51.1 all-gather.20
  115.2 46.6 all-gather.22
  164.1 90.5 all-gather.14
  256.3 90.5 all-gather.16
  349.1 90.5 all-gather.10
  442.1 90.5 all-gather.12
  863.0 89.1 reduce-scatter.25
  1027.5 89.2 reduce-scatter.27
  1119.7 89.1 reduce-scatter.21
  1211.9 89.1 reduce-scatter.23
  1428.0 51.1 reduce-scatter.29
  1535.1 69.2 all-reduce.12
  1607.8 80.6 reduce-scatter.33
  1728.2 80.5 reduce-scatter.31

commit v2 on v1

--- a/solution.py
+++ b/solution.py
@@ -8,7 +8,7 @@
 from jax.sharding import PartitionSpec as P
 
 NORM_EPS = 1e-6
-CHUNKS = 2
+SIZES = (4, 4, 4)
 F32 = jnp.float32
 BF16 = jnp.bfloat16
 MASKED = -1e30
@@ -33,10 +33,6 @@
     first = x_f[..., :half_dim]
     second = x_f[..., half_dim:]
     return jnp.concatenate([first * cos_t - second * sin_t, second * cos_t + first * sin_t], axis=-1)
-
-
-def gated_act(gate, upper):
-    return (jax.nn.gelu(gate, approximate=True) * upper).astype(BF16)
 
 
 def dot_f32(lhs, rhs, lhs_dim, rhs_dim):
@@ -80,9 +76,9 @@
             dst[0, :, n * hd:(n + 1) * hd] = mixed[n * rows:(n + 1) * rows]
 
 
-def attn_bwd_kernel(prefix_s, valid_s, q_own_ref, q_oth_ref, g_own_ref, g_oth_ref, kv_own_ref, kv_oth_ref, cos_ref, sin_ref,
+def attn_bwd_kernel(first, prefix_s, valid_s, q_own_ref, q_oth_ref, g_own_ref, g_oth_ref, kv_own_ref, kv_oth_ref, cos_ref, sin_ref,
                     qpos_ref, kpos_ref, dq_own_ref, dq_oth_ref, dkv_own_ref, dkv_oth_ref):
-    b = pl.program_id(0)
+    b = pl.program_id(0) + first
     rows, width = q_own_ref.shape[1:]
     hd = kv_own_ref.shape[-1] // 2
     half = hd // 2
@@ -126,7 +122,7 @@
             dst[c, 0, :, hd:] = d_values[at:at + span]
 
 
-def attn_specs(batch, rows, width, shards, two_hd, half):
+def attn_specs(rows, width, shards, two_hd, half):
     q_spec = pl.BlockSpec((1, rows, width), lambda b, *_: (b, 0, 0))
     kv_spec = pl.BlockSpec((shards, 1, rows, two_hd), lambda b, *_: (0, b, 0, 0))
     tab_spec = pl.BlockSpec((rows, half), lambda b, *_: (0, 0))
@@ -140,7 +136,7 @@
 def attn_fwd(q_own, q_oth, kv_own, kv_oth, cos_t, sin_t, qpos, kpos, prefix_len, valid_len):
     batch, rows, width = q_own.shape
     shards, two_hd = kv_own.shape[0], kv_own.shape[3]
-    q_spec, kv_spec, tab_spec = attn_specs(batch, rows, width, shards, two_hd, two_hd // 4)
+    q_spec, kv_spec, tab_spec = attn_specs(rows, width, shards, two_hd, two_hd // 4)
     heads = width * 2 // two_hd
     out = jax.ShapeDtypeStruct((batch, rows, width), BF16)
     qpos_col = jnp.tile(qpos, heads)[:, None]
@@ -159,27 +155,292 @@
     )(prefix_len, valid_len, q_own, q_oth, kv_own, kv_oth, cos_t, sin_t, qpos_col, kpos[None, :])
 
 
-def attn_bwd(q_own, q_oth, g_own, g_oth, kv_own, kv_oth, cos_t, sin_t, qpos, kpos, prefix_len, valid_len):
-    batch, rows, width = q_own.shape
+def attn_bwd(order, q_own, q_oth, g_own, g_oth, kv_own, kv_oth, cos_t, sin_t, qpos, kpos, prefix_len, valid_len, first):
+    batch, rows, width = g_own.shape
     shards, two_hd = kv_own.shape[0], kv_own.shape[3]
-    q_spec, kv_spec, tab_spec = attn_specs(batch, rows, width, shards, two_hd, two_hd // 4)
+    g_spec, kv_out_spec, tab_spec = attn_specs(rows, width, shards, two_hd, two_hd // 4)
+    q_spec = pl.BlockSpec((1, rows, width), lambda b, *_: (b + first, 0, 0))
+    kv_spec = pl.BlockSpec((shards, 1, rows, two_hd), lambda b, *_: (0, b + first, 0, 0))
     heads = width * 2 // two_hd
     out = jax.ShapeDtypeStruct((batch, rows, width), BF16)
-    kv_out = jax.ShapeDtypeStruct(kv_own.shape, BF16)
+    kv_out = jax.ShapeDtypeStruct((shards, batch, rows, two_hd), BF16)
     qpos_row = jnp.tile(qpos, heads)[None, :]
     n_keys = kpos.shape[0]
     flops = 2 * 5 * batch * rows * 2 * width * n_keys
-    return pl.pallas_call(
-        attn_bwd_kernel,
+
+    def body(*refs):
+        attn_bwd_kernel(first, *refs[:12], *refs[13:])
+
+    out = pl.pallas_call(
+        body,
         out_shape=(out, out, kv_out, kv_out),
         grid_spec=pltpu.PrefetchScalarGridSpec(
             num_scalar_prefetch=2, grid=(batch,),
-            in_specs=[q_spec, q_spec, q_spec, q_spec, kv_spec, kv_spec, tab_spec, tab_spec, whole((1, heads * rows)), whole((n_keys, 1))],
-            out_specs=[q_spec, q_spec, kv_spec, kv_spec]),
+            in_specs=[q_spec, q_spec, g_spec, g_spec, kv_spec, kv_spec, tab_spec, tab_spec, whole((1, heads * rows)), whole((n_keys, 1)), pl.BlockSpec(memory_space=pl.ANY)],
+            out_specs=[g_spec, g_spec, kv_out_spec, kv_out_spec]),
         compiler_params=pltpu.CompilerParams(dimension_semantics=("arbitrary",), vmem_limit_bytes=48 << 20),
-        cost_estimate=pl.CostEstimate(flops=flops, bytes_accessed=batch * rows * width * 12 + kv_own.size * 8, transcendentals=batch * rows * heads * 2 * n_keys),
+        cost_estimate=pl.CostEstimate(flops=flops, bytes_accessed=batch * rows * width * 12 + kv_out.size * 8, transcendentals=batch * rows * heads * 2 * n_keys),
         name="attn_bwd",
-    )(prefix_len, valid_len, q_own, q_oth, g_own, g_oth, kv_own, kv_oth, cos_t, sin_t, qpos_row, kpos[:, None])
+    )(prefix_len, valid_len, q_own, q_oth, g_own, g_oth, kv_own, kv_oth, cos_t, sin_t, qpos_row, kpos[:, None], order.last)
+    order.last = out[0]
+    return out
+
+
+class Order:
+    def __init__(self):
+        self.last = None
+
+    def call(self, kernel, n_in, *, in_specs, **options):
+        def run(*args):
+            deps = () if self.last is None or any(self.last is a for a in args) else (self.last,)
+
+            def body(*refs):
+                kernel(*refs[:n_in], *refs[n_in + len(deps):])
+
+            out = pl.pallas_call(body, in_specs=in_specs + [pl.BlockSpec(memory_space=pl.ANY)] * len(deps), **options)(*args, *deps)
+            self.last = out[0] if isinstance(out, (tuple, list)) else out
+            return out
+
+        return run
+
+
+def params(steps, limit=56):
+    return pltpu.CompilerParams(dimension_semantics=("arbitrary",) * steps, vmem_limit_bytes=limit << 20)
+
+
+def cost(flops, *arrays):
+    return pl.CostEstimate(flops=flops, bytes_accessed=sum(a.size * a.dtype.itemsize for a in arrays), transcendentals=0)
+
+
+def act_kernel(z_ref, g_ref, wg_ref, wu_ref, *refs, sub):
+    act_ref, dg_ref, du_ref = refs[-3:]
+    c_1 = math.sqrt(2.0 / math.pi)
+    c_3 = 0.044715 * c_1
+    for j in range(0, wg_ref.shape[1], sub):
+        gate = dot_f32(z_ref[...], wg_ref[:, j:j + sub], 1, 0)
+        upper = dot_f32(z_ref[...], wu_ref[:, j:j + sub], 1, 0)
+        if len(refs) == 4:
+            d_act = dot_f32(g_ref[...], refs[0][j:j + sub, :], 1, 1).astype(BF16).astype(F32)
+        else:
+            d_act = g_ref[:, j:j + sub].astype(F32)
+        square = gate * gate
+        half = 0.5 * jnp.tanh(gate * (c_3 * square + c_1)) + 0.5
+        gelu = gate * half
+        act_ref[:, j:j + sub] = (gelu * upper).astype(BF16)
+        du_ref[:, j:j + sub] = (d_act * gelu).astype(BF16)
+        slope = half + gelu * (1.0 - half) * (6.0 * c_3 * square + 2.0 * c_1)
+        dg_ref[:, j:j + sub] = (d_act * upper * slope).astype(BF16)
+
+
+def act_call(order, z_all, g_all, w_gate, w_up, w_down, tm=768, tn=512, sub=256):
+    tokens, dim = z_all.shape
+    width = w_gate.shape[1]
+    out = jax.ShapeDtypeStruct((tokens, width), BF16)
+    row = pl.BlockSpec((tm, dim), lambda j, i: (i, 0))
+    col = pl.BlockSpec((dim, tn), lambda j, i: (0, j))
+    tile = pl.BlockSpec((tm, tn), lambda j, i: (i, j))
+    args = (z_all, g_all, w_gate, w_up) + (() if w_down is None else (w_down,))
+    specs = [row, tile if w_down is None else row, col, col] + ([] if w_down is None else [pl.BlockSpec((tn, dim), lambda j, i: (j, 0))])
+    return order.call(
+        functools.partial(act_kernel, sub=sub), len(args), out_shape=(out, out, out), grid=(width // tn, tokens // tm),
+        in_specs=specs, out_specs=[tile] * 3, compiler_params=params(2),
+        cost_estimate=cost(2 * (len(args) - 2) * tokens * dim * width, *args, out, out, out), name="mlp_act",
+    )(*args)
+
+
+def mm_kernel(*refs, n, rhs_dim):
+    total = dot_f32(refs[0][...], refs[n][...], 1, rhs_dim)
+    for p in range(1, n):
+        total += dot_f32(refs[p][...], refs[n + p][...], 1, rhs_dim)
+    for extra in refs[2 * n:-1]:
+        total += extra[...].astype(F32)
+    refs[-1][...] = total.astype(refs[-1].dtype)
+
+
+def mm_call(order, lhs, rhs, rhs_dim, extra=(), tm=1152, tn=512, out_dtype=BF16, name="mm"):
+    n = len(lhs)
+    tokens, depth = lhs[0].shape
+    width = rhs[0].shape[1 - rhs_dim]
+    w_shape, w_map = ((depth, tn), lambda j, i: (0, j)) if rhs_dim == 0 else ((tn, depth), lambda j, i: (j, 0))
+    out = jax.ShapeDtypeStruct((tokens, width), out_dtype)
+    tile = pl.BlockSpec((tm, tn), lambda j, i: (i, j))
+    return order.call(
+        functools.partial(mm_kernel, n=n, rhs_dim=rhs_dim), 2 * n + len(extra), out_shape=out, grid=(width // tn, tokens // tm),
+        in_specs=[pl.BlockSpec((tm, depth), lambda j, i: (i, 0))] * n + [pl.BlockSpec(w_shape, w_map)] * n + [tile] * len(extra),
+        out_specs=tile, compiler_params=params(2),
+        cost_estimate=cost(2 * n * tokens * depth * width, *lhs, *rhs, *extra, out), name=name,
+    )(*lhs, *rhs, *extra)
+
+
+def wgrad_kernel(*refs, n, tf, tn, cols):
+    lhs, rhs, out, l_buf, r_buf, sems = refs[:n], refs[n:2 * n], *refs[2 * n:]
+    i, j, k = pl.program_id(0), pl.program_id(1), pl.program_id(2)
+    step = (i * cols + j) * n + k
+    slot = lax.rem(step, 2)
+
+    def copies(s, at, p):
+        row = lax.div(s, cols * n)
+        col = lax.rem(lax.div(s, n), cols)
+        return (pltpu.make_async_copy(lhs[p].at[:, pl.ds(pl.multiple_of(row * tf, tf), tf)], l_buf.at[at], sems.at[0, at]),
+                pltpu.make_async_copy(rhs[p].at[:, pl.ds(pl.multiple_of(col * tn, tn), tn)], r_buf.at[at], sems.at[1, at]))
+
+    def fetch(s, at):
+        for p in range(n):
+            @pl.when(lax.rem(s, n) == p)
+            def _(p=p):
+                for copy in copies(s, at, p):
+                    copy.start()
+
+    @pl.when(step == 0)
+    def _():
+        fetch(step, slot)
+
+    @pl.when(step + 1 < pl.num_programs(0) * cols * n)
+    def _():
+        fetch(step + 1, 1 - slot)
+
+    for copy in copies(step, slot, 0):
+        copy.wait()
+    part = dot_f32(l_buf[slot], r_buf[slot], 0, 0)
+    out[...] = jnp.where(k == 0, part, out[...] + part)
+
+
+def wgrad_call(order, lhs, rhs, tf=1024, tn=1024):
+    n = len(lhs)
+    tokens, rows = lhs[0].shape
+    width = rhs[0].shape[1]
+    cols = width // tn
+    out = jax.ShapeDtypeStruct((rows, width), F32)
+    return order.call(
+        functools.partial(wgrad_kernel, n=n, tf=tf, tn=tn, cols=cols), 2 * n, out_shape=out, grid=(rows // tf, cols, n),
+        in_specs=[pl.BlockSpec(memory_space=pl.ANY)] * (2 * n), out_specs=pl.BlockSpec((tf, tn), lambda i, j, k: (i, j)),
+        scratch_shapes=[pltpu.VMEM((2, tokens, tf), BF16), pltpu.VMEM((2, tokens, tn), BF16), pltpu.SemaphoreType.DMA((2, 2))],
+        compiler_params=params(3), cost_estimate=cost(2 * n * tokens * rows * width, *lhs, *rhs, out), name="wgrad",
+    )(*lhs, *rhs)
+
+
+def small_wgrad_kernel(l_ref, r_ref, *refs):
+    total = dot_f32(l_ref[...], r_ref[...], 0, 0)
+    for extra in refs[:-1]:
+        total += extra[...]
+    refs[-1][...] = total
+
+
+def small_wgrad(order, lhs, rhs, extra=(), tf=512, tn=1024):
+    tokens, rows = lhs.shape
+    width = rhs.shape[1]
+    out = jax.ShapeDtypeStruct((rows, width), F32)
+    tile = pl.BlockSpec((tf, tn), lambda j, i: (i, j))
+    return order.call(
+        small_wgrad_kernel, 2 + len(extra), out_shape=out, grid=(width // tn, rows // tf),
+        in_specs=[pl.BlockSpec((tokens, tf), lambda j, i: (0, i)), pl.BlockSpec((tokens, tn), lambda j, i: (0, j))] + [tile] * len(extra),
+        out_specs=tile, compiler_params=params(2), cost_estimate=cost(2 * tokens * rows * width, lhs, rhs, *extra, out), name="small_wgrad",
+    )(lhs, rhs, *extra)
+
+
+def resid_kernel(h_ref, a_own_ref, a_oth_ref, w_own_ref, w_oth_ref, gain_ref, resid_ref, *z_refs, edges):
+    i = pl.program_id(0)
+    total = dot_f32(a_own_ref[...], w_own_ref[...], 1, 0) + dot_f32(a_oth_ref[...], w_oth_ref[...], 1, 0)
+    resid = (h_ref[...].astype(F32) + total).astype(BF16)
+    resid_ref[...] = resid
+    x_f = resid.astype(F32)
+    inv = lax.rsqrt(jnp.mean(x_f * x_f, axis=-1, keepdims=True) + NORM_EPS)
+    z = (x_f * inv * (1.0 + gain_ref[...])).astype(BF16)
+    for z_ref, lo, hi in zip(z_refs, edges[:-1], edges[1:]):
+        @pl.when((i >= lo) & (i < hi))
+        def _(z_ref=z_ref):
+            z_ref[...] = z
+
+
+def resid_call(order, hidden, mix_own, mix_oth, wo_own, wo_oth, gain, sizes, tm):
+    tokens, dim = hidden.shape
+    width = mix_own.shape[1]
+    edges = [0]
+    for size in sizes:
+        edges.append(edges[-1] + size // tm)
+    row = pl.BlockSpec((tm, dim), lambda i: (i, 0))
+    mix = pl.BlockSpec((tm, width), lambda i: (i, 0))
+    whole_w = pl.BlockSpec((width, dim), lambda i: (0, 0))
+    z_specs = [pl.BlockSpec((tm, dim), lambda i, lo=lo, hi=hi: (jnp.clip(i - lo, 0, hi - lo - 1), 0)) for lo, hi in zip(edges[:-1], edges[1:])]
+    outs = (jax.ShapeDtypeStruct((tokens, dim), BF16),) + tuple(jax.ShapeDtypeStruct((size, dim), BF16) for size in sizes)
+    return order.call(
+        functools.partial(resid_kernel, edges=tuple(edges)), 6, out_shape=outs, grid=(tokens // tm,),
+        in_specs=[row, mix, mix, whole_w, whole_w, pl.BlockSpec((1, dim), lambda i: (0, 0))], out_specs=[row] + z_specs,
+        compiler_params=params(1), cost_estimate=cost(4 * tokens * dim * width, hidden, mix_own, mix_oth, wo_own, wo_oth, *outs), name="resid",
+    )(hidden, mix_own, mix_oth, wo_own, wo_oth, gain)
+
+
+def norm_back(x_f, gain_1, d_out):
+    inv = lax.rsqrt(jnp.mean(x_f * x_f, axis=-1, keepdims=True) + NORM_EPS)
+    unit = x_f * inv
+    scaled = d_out * gain_1
+    d_x = inv * (scaled - unit * jnp.mean(scaled * unit, axis=-1, keepdims=True))
+    return d_x, d_out * unit
+
+
+def fold_rows(terms):
+    rows, dim = terms.shape
+    return jnp.sum(terms.reshape(rows // 8, 8, dim), axis=0)
+
+
+def d_resid_kernel(dz_ref, x_ref, g_ref, gain_ref, w_own_ref, w_oth_ref, d_ref, own_ref, oth_ref, norm_ref):
+    @pl.when(pl.program_id(0) == 0)
+    def _():
+        norm_ref[...] = jnp.zeros_like(norm_ref)
+
+    d_x, terms = norm_back(x_ref[...].astype(F32), 1.0 + gain_ref[...], dz_ref[...].astype(F32))
+    norm_ref[...] += fold_rows(terms)
+    d_resid = (g_ref[...].astype(F32) + d_x).astype(BF16)
+    d_ref[...] = d_resid
+    own_ref[...] = dot_f32(d_resid, w_own_ref[...], 1, 1).astype(BF16)
+    oth_ref[...] = dot_f32(d_resid, w_oth_ref[...], 1, 1).astype(BF16)
+
+
+def d_resid_call(order, dz, resid, grad_out, gain, wo_own, wo_oth, first, tm):
+    tokens, dim = dz.shape
+    width = wo_own.shape[0]
+    base = first // tm
+    row = pl.BlockSpec((tm, dim), lambda i: (i, 0))
+    far = pl.BlockSpec((tm, dim), lambda i: (i + base, 0))
+    mix = pl.BlockSpec((tm, width), lambda i: (i, 0))
+    whole_w = pl.BlockSpec((width, dim), lambda i: (0, 0))
+    outs = (jax.ShapeDtypeStruct((tokens, dim), BF16), jax.ShapeDtypeStruct((tokens, width), BF16),
+            jax.ShapeDtypeStruct((tokens, width), BF16), jax.ShapeDtypeStruct((8, dim), F32))
+    return order.call(
+        d_resid_kernel, 6, out_shape=outs, grid=(tokens // tm,),
+        in_specs=[row, far, far, pl.BlockSpec((1, dim), lambda i: (0, 0)), whole_w, whole_w],
+        out_specs=[row, mix, mix, pl.BlockSpec((8, dim), lambda i: (0, 0))],
+        compiler_params=params(1), cost_estimate=cost(4 * tokens * dim * width, dz, dz, dz, wo_own, wo_oth, *outs), name="d_resid",
+    )(dz, resid, grad_out, gain, wo_own, wo_oth)
+
+
+def d_hidden_kernel(q_own_ref, q_oth_ref, dk_ref, dv_ref, x_ref, d_ref, gain_ref, wq_own_ref, wq_oth_ref, wk_ref, wv_ref, out_ref, norm_ref):
+    @pl.when(pl.program_id(0) == 0)
+    def _():
+        norm_ref[...] = jnp.zeros_like(norm_ref)
+
+    d_normed = (dot_f32(q_own_ref[...], wq_own_ref[...], 1, 0) + dot_f32(q_oth_ref[...], wq_oth_ref[...], 1, 0)
+                + dot_f32(dk_ref[...], wk_ref[...], 1, 1) + dot_f32(dv_ref[...], wv_ref[...], 1, 1)).astype(BF16).astype(F32)
+    d_x, terms = norm_back(x_ref[...].astype(F32), 1.0 + gain_ref[...], d_normed)
+    norm_ref[...] += fold_rows(terms)
+    out_ref[...] = (d_ref[...].astype(F32) + d_x).astype(BF16)
+
+
+def d_hidden_call(order, dq_own, dq_oth, d_k, d_v, hidden, d_resid, gain, wq_own, wq_oth, w_key, w_value, tm):
+    tokens, dim = hidden.shape
+    width, hd = dq_own.shape[1], d_k.shape[1]
+    row = pl.BlockSpec((tm, dim), lambda i: (i, 0))
+    mix = pl.BlockSpec((tm, width), lambda i: (i, 0))
+    one = pl.BlockSpec((tm, hd), lambda i: (i, 0))
+    whole_w = pl.BlockSpec((width, dim), lambda i: (0, 0))
+    whole_k = pl.BlockSpec((dim, hd), lambda i: (0, 0))
+    outs = (jax.ShapeDtypeStruct((tokens, dim), BF16), jax.ShapeDtypeStruct((8, dim), F32))
+    return order.call(
+        d_hidden_kernel, 11, out_shape=outs, grid=(tokens // tm,),
+        in_specs=[mix, mix, one, one, row, row, pl.BlockSpec((1, dim), lambda i: (0, 0)), whole_w, whole_w, whole_k, whole_k],
+        out_specs=[row, pl.BlockSpec((8, dim), lambda i: (0, 0))],
+        compiler_params=params(1), cost_estimate=cost(4 * tokens * dim * (width + hd), dq_own, dq_oth, hidden, d_resid, wq_own, wq_oth, *outs), name="d_hidden",
+    )(dq_own, dq_oth, d_k, d_v, hidden, d_resid, gain, wq_own, wq_oth, w_key, w_value)
 
 
 def solution(mesh):
@@ -195,15 +456,31 @@
         return lax.all_gather(x_loc, "tp", axis=0, tiled=False, axis_index_groups=same_core)
 
     def scatter4(x_part):
-        return lax.psum_scatter(x_part, "tp", scatter_dimension=0, tiled=False, axis_index_groups=same_core)
+        flat = x_part.reshape((-1,) + x_part.shape[2:])
+        return lax.psum_scatter(flat, "tp", scatter_dimension=0, tiled=True, axis_index_groups=same_core)
 
     def swap(x_loc):
         return lax.ppermute(x_loc, "tp", partner)
+
+    def flip(x_loc, bits):
+        return lax.ppermute(x_loc, "tp", [(i, i ^ bits) for i in range(tp_size)])
+
+    def gather4_direct(x_loc):
+        chip = lax.axis_index("tp") // 2
+        half = x_loc.shape[0] // 2
+        near, far = flip(x_loc, 2), flip(x_loc, 4)
+        low, high = flip(near[:half], 4), flip(far[half:], 2)
+        out = jnp.zeros((chips,) + x_loc.shape, x_loc.dtype)
+        for k, block in ((0, x_loc), (1, near), (2, far)):
+            out = lax.dynamic_update_slice(out, block[None], (chip ^ k, 0, 0))
+        out = lax.dynamic_update_slice(out, low[None], (chip ^ 3, 0, 0))
+        return lax.dynamic_update_slice(out, high[None], (chip ^ 3, half, 0))
 
     def local_layer(hidden, grad_out, prefix_len, valid_len, attn_norm, w_query, w_key, w_value, w_out, mlp_norm, w_gate, w_up, w_down):
         batch, rows, dim = hidden.shape
         hd = w_key.shape[1]
         tokens = batch * rows
+        assert sum(SIZES) == batch
         me = lax.axis_index("tp")
         core = lax.rem(me, 2)
         qpos = me * rows + jnp.arange(rows, dtype=jnp.int32)
@@ -214,14 +491,16 @@
         def rope_single(raw_proj):
             return apply_rope(raw_proj, cos_t, sin_t).astype(BF16)
 
-        wq_own = gather4(w_query.T).reshape(chips * hd, dim)
-        normed, norm1_pull = jax.vjp(rms_norm, hidden, attn_norm.astype(F32))
-        normed_flat = normed.reshape(tokens, dim)
+        attn_gain = attn_norm.astype(F32)
+        mlp_gain = mlp_norm.astype(F32)
+        order = Order()
+        wq_own = gather4_direct(w_query.T).reshape(chips * hd, dim)
+        normed_flat = rms_norm(hidden, attn_gain).reshape(tokens, dim)
         k_raw = dot_f32(normed_flat, w_key, 1, 0).reshape(batch, rows, hd)
         keys, key_pull = jax.vjp(rope_single, k_raw)
         values = dot_f32(normed_flat, w_value, 1, 0).astype(BF16).reshape(batch, rows, hd)
         kv_own = gather4(jnp.concatenate([keys, values], axis=-1))
-        wo_own = gather4(w_out).reshape(chips * hd, dim)
+        wo_own = gather4_direct(w_out).reshape(chips * hd, dim)
         wq_oth = swap(wq_own)
         kv_oth = swap(kv_own)
         wo_oth = swap(wo_own)
@@ -230,64 +509,74 @@
         mix_own, mix_oth, q_own, q_oth = attn_fwd(q_own, q_oth, kv_own, kv_oth, cos_t, sin_t, qpos, kpos, prefix_len, valid_len)
         mix_own = mix_own.reshape(tokens, chips * hd)
         mix_oth = mix_oth.reshape(tokens, chips * hd)
-        attn_sum = dot_f32(mix_own, wo_own, 1, 0) + dot_f32(mix_oth, wo_oth, 1, 0)
-        resid = (hidden.astype(F32) + attn_sum.reshape(batch, rows, dim)).astype(BF16)
-        gated_in, norm2_pull = jax.vjp(rms_norm, resid, mlp_norm.astype(F32))
-
-        step = batch // CHUNKS
-        g_down = g_gate = g_up = 0.0
+        hidden_flat = hidden.reshape(tokens, dim)
+        grad_flat = grad_out.reshape(tokens, dim)
+        sizes = [n * rows for n in SIZES]
+        firsts = [sum(SIZES[:c]) for c in range(len(SIZES))]
+        resid, *z_parts = resid_call(order, hidden_flat, mix_own, mix_oth, wo_own, wo_oth, mlp_gain[None, :], sizes, 2 * rows)
+
+        z_pieces, g_pieces, act_pieces, dg_pieces, du_pieces = [], [], [], [], []
         mlp_sums, d_gated = [], []
-        for c in range(CHUNKS):
-            sl = slice(c * step, (c + 1) * step)
-            g_own = gather4(grad_out[sl].reshape(step * rows, dim)).reshape(-1, dim)
+        for c, (first, size, z_part) in enumerate(zip(firsts, sizes, z_parts)):
+            g_own = gather4(grad_flat[first * rows:first * rows + size]).reshape(-1, dim)
             g_oth = swap(g_own)
-            z_own = gather4(gated_in[sl].reshape(step * rows, dim)).reshape(-1, dim)
+            z_own = gather4(z_part).reshape(-1, dim)
             z_oth = swap(z_own)
-            outs, backs = [], []
-            for z_all, g_all in ((z_own, g_own), (z_oth, g_oth)):
-                d_act = dot_f32(g_all, w_down, 1, 1).astype(BF16)
-                gate = dot_f32(z_all, w_gate, 1, 0)
-                upper = dot_f32(z_all, w_up, 1, 0)
-                act, act_pull = jax.vjp(gated_act, gate, upper)
-                d_gate, d_upper = act_pull(d_act)
-                d_gate = d_gate.astype(BF16)
-                d_upper = d_upper.astype(BF16)
-                outs.append(dot_f32(act, w_down, 1, 0))
-                backs.append(dot_f32(d_gate, w_gate, 1, 1) + dot_f32(d_upper, w_up, 1, 1))
-                g_down = g_down + dot_f32(act, g_all, 0, 0)
-                g_gate = g_gate + dot_f32(z_all, d_gate, 0, 0)
-                g_up = g_up + dot_f32(z_all, d_upper, 0, 0)
-            for (own, oth), dest in ((outs, mlp_sums), (backs, d_gated)):
-                part = (own + swap(oth.astype(BF16)).astype(F32)).astype(BF16)
-                dest.append(scatter4(part.reshape(chips, step * rows, dim)).reshape(step, rows, dim))
-        mlp_sum = jnp.concatenate(mlp_sums, axis=0)
-        hidden_out = (resid.astype(F32) + mlp_sum.astype(F32)).astype(BF16)
-        d_resid_norm, g_mlp_norm_part = norm2_pull(jnp.concatenate(d_gated, axis=0))
-        d_resid = (grad_out.astype(F32) + d_resid_norm.astype(F32)).astype(BF16)
-
-        d_resid_flat = d_resid.reshape(tokens, dim)
-        d_mix_own = dot_f32(d_resid_flat, wo_own, 1, 1).astype(BF16).reshape(batch, rows, chips * hd)
-        d_mix_oth = dot_f32(d_resid_flat, wo_oth, 1, 1).astype(BF16).reshape(batch, rows, chips * hd)
-        dq_own, dq_oth, dkv_own, dkv_oth = attn_bwd(q_own, q_oth, d_mix_own, d_mix_oth, kv_own, kv_oth, cos_t, sin_t, qpos, kpos, prefix_len, valid_len)
-        dkv = scatter4((dkv_own.astype(F32) + swap(dkv_oth).astype(F32)).astype(BF16))
-        d_k_raw = key_pull(dkv[..., :hd])[0].astype(BF16).reshape(tokens, hd)
+            tm = 1152 if (chips * size) % 1152 == 0 else 768
+            if c == 0:
+                d_acts = [mm_call(order, (g,), (w_down,), 1, tm=tm, name="d_act") for g in (g_own, g_oth)]
+                acts = [act_call(order, z, d, w_gate, w_up, None) for z, d in zip((z_own, z_oth), d_acts)]
+            else:
+                acts = [act_call(order, z, g, w_gate, w_up, w_down) for z, g in ((z_own, g_own), (z_oth, g_oth))]
+            (act_own, dg_own, du_own), (act_oth, dg_oth, du_oth) = acts
+            back_oth = swap(mm_call(order, (dg_oth, du_oth), (w_gate, w_up), 1, tm=tm, name="d_gated"))
+            out_oth = swap(mm_call(order, (act_oth,), (w_down,), 0, tm=tm, name="mlp_out"))
+            back = mm_call(order, (dg_own, du_own), (w_gate, w_up), 1, (back_oth,), tm=tm, name="d_gated")
+            d_gated.append(scatter4(back.reshape(chips, size, dim)).reshape(size, dim))
+            out = mm_call(order, (act_own,), (w_down,), 0, (out_oth,), tm=tm, name="mlp_out")
+            mlp_sums.append(scatter4(out.reshape(chips, size, dim)).reshape(size, dim))
+            z_pieces += [z_own, z_oth]
+            g_pieces += [g_own, g_oth]
+            act_pieces += [act_own, act_oth]
+            dg_pieces += [dg_own, dg_oth]
+            du_pieces += [du_own, du_oth]
+        hidden_out = (resid.astype(F32) + jnp.concatenate(mlp_sums, axis=0).astype(F32)).astype(BF16).reshape(batch, rows, dim)
+
+        d_resids, dq_owns, dq_oths, dkv_owns, dkv_oths = [], [], [], [], []
+        norm_terms = 0.0
+        for c, (first, n, size, dz) in enumerate(zip(firsts, SIZES, sizes, d_gated)):
+            if c == len(SIZES) - 1:
+                g_gate = wgrad_call(order, z_pieces, dg_pieces)
+            d_resid, d_own, d_oth, terms = d_resid_call(order, dz, resid, grad_flat, mlp_gain[None, :], wo_own, wo_oth, first * rows, 2 * rows)
+            dq_own, dq_oth, dkv_own, dkv_oth = attn_bwd(
+                order, q_own, q_oth, d_own.reshape(n, rows, -1), d_oth.reshape(n, rows, -1), kv_own, kv_oth, cos_t, sin_t, qpos, kpos, prefix_len, valid_len, first)
+            norm_terms = norm_terms + terms
+            d_resids.append(d_resid)
+            dq_owns.append(dq_own.reshape(size, -1))
+            dq_oths.append(dq_oth.reshape(size, -1))
+            dkv_owns.append(dkv_own)
+            dkv_oths.append(swap(dkv_oth))
+        d_resid = jnp.concatenate(d_resids, axis=0)
+        dq_own = jnp.concatenate(dq_owns, axis=0)
+        dq_oth = jnp.concatenate(dq_oths, axis=0)
+        dkv_parts = [(own.astype(F32) + oth.astype(F32)).astype(BF16) for own, oth in zip(dkv_owns, dkv_oths)]
+        dkv = scatter4(jnp.concatenate(dkv_parts, axis=1))
+        d_k_raw = key_pull(dkv[..., :hd].astype(BF16))[0].astype(BF16).reshape(tokens, hd)
         d_values = dkv[..., hd:].reshape(tokens, hd)
-        dq_own = dq_own.reshape(tokens, chips * hd)
-        dq_oth = dq_oth.reshape(tokens, chips * hd)
-
-        def weight_sum(own, oth):
-            return scatter4((own + swap(oth)).reshape(chips, hd, dim))
-
-        g_out = weight_sum(dot_f32(mix_own, d_resid_flat, 0, 0), dot_f32(mix_oth, d_resid_flat, 0, 0))
-        g_query = weight_sum(dot_f32(dq_own, normed_flat, 0, 0), dot_f32(dq_oth, normed_flat, 0, 0)).T
-        d_normed = (dot_f32(dq_own, wq_own, 1, 0) + dot_f32(dq_oth, wq_oth, 1, 0)
-                    + dot_f32(d_k_raw, w_key, 1, 1) + dot_f32(d_values, w_value, 1, 1)).astype(BF16)
-        d_hidden_norm, g_attn_norm_part = norm1_pull(d_normed.reshape(batch, rows, dim))
-        grad_hidden = (d_resid.astype(F32) + d_hidden_norm.astype(F32)).astype(BF16)
+
+        g_out_far = swap(small_wgrad(order, mix_oth, d_resid))
+        g_query_far = swap(small_wgrad(order, dq_oth, normed_flat))
+        g_out_part = small_wgrad(order, mix_own, d_resid, (g_out_far,))
+        g_query_part = small_wgrad(order, dq_own, normed_flat, (g_query_far,))
+        g_out = scatter4(g_out_part.reshape(chips, hd, dim))
+        g_query = scatter4(g_query_part.reshape(chips, hd, dim)).reshape(hd, dim).T
+        g_up = wgrad_call(order, z_pieces, du_pieces)
         g_key = lax.psum(dot_f32(normed_flat, d_k_raw, 0, 0), "tp")
         g_value = lax.psum(dot_f32(normed_flat, d_values, 0, 0), "tp")
-        g_attn_norm = lax.psum(g_attn_norm_part, "tp")
-        g_mlp_norm = lax.psum(g_mlp_norm_part, "tp")
-        return (hidden_out, grad_hidden, g_attn_norm, g_query, g_key, g_value, g_out, g_mlp_norm, g_gate, g_up, g_down)
+        grad_hidden, attn_terms = d_hidden_call(order, dq_own, dq_oth, d_k_raw, d_values, hidden_flat, d_resid, attn_gain[None, :], wq_own, wq_oth, w_key, w_value, 2 * rows)
+        g_attn_norm = lax.psum(jnp.sum(attn_terms, axis=0), "tp")
+        g_mlp_norm = lax.psum(jnp.sum(norm_terms, axis=0), "tp")
+        g_down = wgrad_call(order, act_pieces, g_pieces)
+        return (hidden_out, grad_hidden.reshape(batch, rows, dim), g_attn_norm, g_query, g_key, g_value, g_out.reshape(hd, dim), g_mlp_norm, g_gate, g_up, g_down)
 
     return jax.shard_map(local_layer, mesh=mesh, in_specs=in_specs, out_specs=out_specs, check_vma=False)

time: 1860 us -> 1660 us (0.89)
  matrix products: 1230 us -> 31.8 us
  Pallas kernels: 58.9 us -> 1140 us
  waiting for transfers between devices: 408 us -> 334 us
  other arithmetic: 86.7 us -> 28.3 us
  local copies, waits for them, and re-layouts: 32.8 us -> 66.5 us
    dot_general x54 -> x6, matrix products: 1230 us -> 31.8 us  [dot_f32(): lax.dot_general(lhs, rhs, (((lhs_dim,), (rhs_dim,)), ((), ())), preferred...]
    pallas_call x1 -> x35, Pallas kernels: 37.8 us -> 1120 us  [the longest x32 1080 us: run(): pl.pallas_call(body, in_specs=in_specs + [pl.BlockSpec(memory_space=pl.AN...]
    all_gather x7, waiting for transfers between devices: 297 us -> 62 us  [gather4(): lax.all_gather(x_loc, 'tp', axis=0, tiled=False, axis_index_groups=same_c...]
    reduce_scatter x0 -> x9, waiting for transfers between devices: none -> 182 us  [scatter4(): lax.psum_scatter(flat, 'tp', scatter_dimension=0, tiled=True, axis_index_...]
    ppermute x0 -> x8, waiting for transfers between devices: none -> 85.9 us  [flip(): return lax.ppermute(x_loc, 'tp', [(i, i ^ bits) for i in range(tp_size)])]
    unnamed x22 -> x17, waiting for transfers between devices: 82.3 us -> 3.5 us
    ppermute x14 -> x20, waiting for transfers between devices: 28.6 us -> 0.05 us  [swap(): return lax.ppermute(x_loc, 'tp', partner)]
    add x2 -> x0, other arithmetic: 23.7 us -> none  [weight_sum(): return scatter4((own + swap(oth)).reshape(chips, hd, dim))]
  transfers between devices with their start and end apart: 29 -> 45, of which waited for: 9 -> 9; matrix products, arithmetic and copies ran while one was open for 68% -> 5% of each run, Pallas kernels for 1% -> 69%
where the time goes in v2:
time: 1660 us
  Pallas kernels  1140 us (69%)
  waiting for transfers between devices  334 us (20%)
  local copies, waits for them, and re-layouts  66.5 us (4%)
  matrix products  31.8 us (2%)
  other arithmetic  28.3 us (2%)
  blocking collectives  23.7 us (1%)
  starting transfers between devices  17.2 us (1%)
    pallas_call x32, Pallas kernels, run(): pl.pallas_call(body, in_specs=in_specs + [pl.BlockSpec(memory_space=pl.AN...  1080 us
    reduce_scatter x9, waiting for transfers between devices, scatter4(): lax.psum_scatter(flat, 'tp', scatter_dimension=0, tiled=True, axis_index_...  182 us
    ppermute x8, waiting for transfers between devices, flip(): return lax.ppermute(x_loc, 'tp', [(i, i ^ bits) for i in range(tp_size)])  85.9 us
    all_gather x7, waiting for transfers between devices, gather4(): lax.all_gather(x_loc, 'tp', axis=0, tiled=False, axis_index_groups=same_c...  62 us
    pallas_call x3, Pallas kernels, attn_bwd(): pl.pallas_call(body, out_shape=(out, out, kv_out, kv_out), grid_spec=pltp...  42.8 us
  transfers between devices with their start and end apart: 45, of which 9 were waited for; matrix products, arithmetic and copies ran while one was open for 5% of the time, Pallas kernels for 69%

profile of v2, /device:TPU:0, one launch (start us, length us, event | category | flops | bytes accessed | tf_op | source)
XLA Modules:
  0.0 1658.0 jit_solution(4080279819326346423)
XLA Ops:
  35.3 32.5 %collective-permute-done = bf16[256,2048]{0,1:T(8,128)(2,1)S(1)} collective-permute-done((bf16[256,2048]{0,1:T(8,128)(2,1)}, bf16[256,2048]{0,1:T(8,128)(2,1)S(1)}, u32[]{:S(2)}, u32[]{:S(2)}) %collective-permute-start) | collective-permute-done | bytes 1048608 | tf_op jit(solution)/shard_map/ppermute | solution.py:466
  79.6 33.1 %collective-permute-done.7 = bf16[256,2048]{1,0:T(8,128)(2,1)S(1)} collective-permute-done((bf16[256,2048]{1,0:T(8,128)(2,1)}, bf16[256,2048]{1,0:T(8,128)(2,1)S(1)}, u32[]{:S(2)}, u32[]{:S(2)}) %collective-permute-start.7) | collective-permute-done | bytes 1048608 | tf_op jit(solution)/shard_map/ppermute | solution.py:466
  173.4 21.1 %attn_fwd.1 = (bf16[12,96,1024]{2,1,0:T(8,128)(2,1)S(1)}, bf16[12,96,1024]{2,1,0:T(8,128)(2,1)S(1)}, bf16[12,96,1024]{2,1,0:T(8,128)(2,1)}, bf16[12,96,1024]{2,1,0:T(8,128)(2,1)}) custom-call(s32[12]{0:T(128)S(1)} %copy-done.26, s32[12]{0:T(128)S(1)} %copy-done.28, f32[12,96,1024]{2,1,0:T(8,128)} %fusion.13.q_own_ref, f32[12,96,1024]{2,1,0:T(8,128)} %fusion.3.q_oth_ref, ...), custom_call_target="tpu_custom_call" | custom-call | flops 7247757312 | bytes 28311552 | tf_op jit(solution)/shard_map/attn_fwd/pallas_call | solution.py:145
  218.9 62.0 %all-gather.20.cloned.1.call-done.refs_0_ = bf16[1536,2048]{1,0:T(8,128)(2,1)} async-done(((bf16[384,2048]{1,0:T(8,128)(2,1)}), bf16[1536,2048]{1,0:T(8,128)(2,1)}) %all-gather.20.cloned.1.call-update) | async-done | bytes 6291472 | tf_op jit(solution)/shard_map/all_gather | solution.py:456
  281.1 22.1 %d_act.2.refs_2_.refs_1_ = bf16[1536,2048]{1,0:T(8,128)(2,1)} custom-call(bf16[1536,2048]{1,0:T(8,128)(2,1)} %bitcast.115, bf16[2048,2048]{1,0:T(8,128)(2,1)} %refs_1_.18, bf16[1152,2048]{1,0:T(8,128)(2,1)} %get-tuple-element.65.refs_2_.refs_1_), custom_call_target="tpu_custom_call" | custom-call | flops 12884901888 | bytes 20971520 | tf_op jit(solution)/shard_map/d_act/pallas_call | solution.py:200
  303.2 21.1 %d_act.3.refs_4_.refs_1_ = bf16[1536,2048]{1,0:T(8,128)(2,1)} custom-call(bf16[1536,2048]{1,0:T(8,128)(2,1)} %collective-permute-done.11.refs_0_.refs_7_, bf16[2048,2048]{1,0:T(8,128)(2,1)} %refs_1_.18, bf16[1536,2048]{1,0:T(8,128)(2,1)} %d_act.2.refs_2_.refs_1_), custom_call_target="tpu_custom_call" | custom-call | flops 12884901888 | bytes 20971520 | tf_op jit(solution)/shard_map/d_act/pallas_call | solution.py:200
  324.3 38.5 %mlp_act.6 = (bf16[1536,2048]{1,0:T(8,128)(2,1)}, bf16[1536,2048]{1,0:T(8,128)(2,1)}, bf16[1536,2048]{1,0:T(8,128)(2,1)}) custom-call(bf16[1536,2048]{1,0:T(8,128)(2,1)} %all-gather.20.cloned.1.call-done.refs_0_, bf16[1536,2048]{1,0:T(8,128)(2,1)} %d_act.2.refs_2_.refs_1_, bf16[2048,2048]{1,0:T(8,128)(2,1)} %refs_2_.23, bf16[2048,2048]{1,0:T(8,128)(2,1)} %refs_3_.23, ...), custom_call_target="tpu_custom_call" | custom-call | flops 25769803776 | bytes 48234496 | tf_op jit(solution)/shard_map/mlp_act/pallas_call | solution.py:200
  362.7 38.4 %mlp_act.7 = (bf16[1536,2048]{1,0:T(8,128)(2,1)}, bf16[1536,2048]{1,0:T(8,128)(2,1)}, bf16[1536,2048]{1,0:T(8,128)(2,1)}) custom-call(bf16[1536,2048]{1,0:T(8,128)(2,1)} %collective-permute-done.12.refs_0_.refs_1_, bf16[1536,2048]{1,0:T(8,128)(2,1)} %d_act.3.refs_4_.refs_1_, bf16[2048,2048]{1,0:T(8,128)(2,1)} %refs_2_.23, bf16[2048,2048]{1,0:T(8,128)(2,1)} %refs_3_.23, ...), custom_call_target="tpu_custom_call" | custom-call | flops 25769803776 | bytes 48234496 | tf_op jit(solution)/shard_map/mlp_act/pallas_call | solution.py:200
  401.1 36.4 %d_gated.6.refs_2_ = bf16[1536,2048]{1,0:T(8,128)(2,1)} custom-call(bf16[1536,2048]{1,0:T(8,128)(2,1)} %get-tuple-element.69.refs_0_.refs_7_, bf16[1536,2048]{1,0:T(8,128)(2,1)} %get-tuple-element.70.refs_1_.refs_7_, bf16[2048,2048]{1,0:T(8,128)(2,1)} %refs_2_.23, bf16[2048,2048]{1,0:T(8,128)(2,1)} %refs_3_.23, ...), custom_call_target="tpu_custom_call" | custom-call | flops 25769803776 | bytes 35651584 | tf_op jit(solution)/shard_map/d_gated/pallas_call | solution.py:200
  438.1 22.3 %mlp_out.6.refs_5_ = bf16[1536,2048]{1,0:T(8,128)(2,1)} custom-call(bf16[1536,2048]{1,0:T(8,128)(2,1)} %get-tuple-element.68.refs_4_.refs_0_.refs_1_, bf16[2048,2048]{1,0:T(8,128)(2,1)} %refs_1_.18, bf16[1536,2048]{1,0:T(8,128)(2,1)} %d_gated.6.refs_2_), custom_call_target="tpu_custom_call" | custom-call | flops 12884901888 | bytes 20971520 | tf_op jit(solution)/shard_map/mlp_out/pallas_call | solution.py:200
  461.0 37.8 %d_gated.7.refs_3_ = bf16[1536,2048]{1,0:T(8,128)(2,1)} custom-call(bf16[1536,2048]{1,0:T(8,128)(2,1)} %get-tuple-element.71.refs_0_.refs_6_, bf16[1536,2048]{1,0:T(8,128)(2,1)} %get-tuple-element.72.refs_1_.refs_6_, bf16[2048,2048]{1,0:T(8,128)(2,1)} %refs_2_.23, bf16[2048,2048]{1,0:T(8,128)(2,1)} %refs_3_.23, ...), custom_call_target="tpu_custom_call" | custom-call | flops 25769803776 | bytes 41943040 | tf_op jit(solution)/shard_map/d_gated/pallas_call | solution.py:200
  498.9 23.8 %mlp_out.7.refs_5_ = bf16[1536,2048]{1,0:T(8,128)(2,1)} custom-call(bf16[1536,2048]{1,0:T(8,128)(2,1)} %get-tuple-element.67.refs_4_.refs_0_, bf16[2048,2048]{1,0:T(8,128)(2,1)} %refs_1_.18, bf16[1536,2048]{1,0:T(8,128)(2,1)} %collective-permute-done.13.refs_2_, bf16[1536,2048]{1,0:T(8,128)(2,1)} %d_gated.7.refs_3_), custom_call_target="tpu_custom_call" | custom-call | flops 12884901888 | bytes 27262976 | tf_op jit(solution)/shard_map/mlp_out/pallas_call | solution.py:200
  522.7 48.8 %mlp_act.8 = (bf16[1536,2048]{1,0:T(8,128)(2,1)}, bf16[1536,2048]{1,0:T(8,128)(2,1)}, bf16[1536,2048]{1,0:T(8,128)(2,1)}) custom-call(bf16[1536,2048]{1,0:T(8,128)(2,1)} %all-gather.22.cloned.1.call-done.refs_0_.refs_2_, bf16[1536,2048]{1,0:T(8,128)(2,1)} %bitcast.118, bf16[2048,2048]{1,0:T(8,128)(2,1)} %refs_2_.23, bf16[2048,2048]{1,0:T(8,128)(2,1)} %refs_3_.23, ...), custom_call_target="tpu_custom_call" | custom-call | flops 38654705664 | bytes 56623104 | tf_op jit(solution)/shard_map/mlp_act/pallas_call | solution.py:200
  571.6 50.0 %mlp_act.9 = (bf16[1536,2048]{1,0:T(8,128)(2,1)}, bf16[1536,2048]{1,0:T(8,128)(2,1)}, bf16[1536,2048]{1,0:T(8,128)(2,1)}) custom-call(bf16[1536,2048]{1,0:T(8,128)(2,1)} %collective-permute-done.15.refs_0_.refs_3_, bf16[1536,2048]{1,0:T(8,128)(2,1)} %collective-permute-done.16.refs_1_.refs_9_, bf16[2048,2048]{1,0:T(8,128)(2,1)} %refs_2_.23, ...), custom_call_target="tpu_custom_call" | custom-call | flops 38654705664 | bytes 56623104 | tf_op jit(solution)/shard_map/mlp_act/pallas_call | solution.py:200
  621.5 35.2 %d_gated.8.refs_2_ = bf16[1536,2048]{1,0:T(8,128)(2,1)} custom-call(bf16[1536,2048]{1,0:T(8,128)(2,1)} %get-tuple-element.76.refs_0_.refs_9_, bf16[1536,2048]{1,0:T(8,128)(2,1)} %get-tuple-element.77.refs_1_.refs_9_, bf16[2048,2048]{1,0:T(8,128)(2,1)} %refs_2_.23, bf16[2048,2048]{1,0:T(8,128)(2,1)} %refs_3_.23, ...), custom_call_target="tpu_custom_call" | custom-call | flops 25769803776 | bytes 35651584 | tf_op jit(solution)/shard_map/d_gated/pallas_call | solution.py:200
  657.2 21.6 %mlp_out.8.refs_5_ = bf16[1536,2048]{1,0:T(8,128)(2,1)} custom-call(bf16[1536,2048]{1,0:T(8,128)(2,1)} %get-tuple-element.75.refs_4_.refs_0_.refs_3_, bf16[2048,2048]{1,0:T(8,128)(2,1)} %refs_1_.18, bf16[1536,2048]{1,0:T(8,128)(2,1)} %d_gated.8.refs_2_), custom_call_target="tpu_custom_call" | custom-call | flops 12884901888 | bytes 20971520 | tf_op jit(solution)/shard_map/mlp_out/pallas_call | solution.py:200
  679.4 36.4 %d_gated.9.refs_3_ = bf16[1536,2048]{1,0:T(8,128)(2,1)} custom-call(bf16[1536,2048]{1,0:T(8,128)(2,1)} %get-tuple-element.78.refs_0_.refs_8_, bf16[1536,2048]{1,0:T(8,128)(2,1)} %get-tuple-element.79.refs_1_.refs_8_, bf16[2048,2048]{1,0:T(8,128)(2,1)} %refs_2_.23, bf16[2048,2048]{1,0:T(8,128)(2,1)} %refs_3_.23, ...), custom_call_target="tpu_custom_call" | custom-call | flops 25769803776 | bytes 41943040 | tf_op jit(solution)/shard_map/d_gated/pallas_call | solution.py:200
  715.9 23.3 %mlp_out.9.refs_5_ = bf16[1536,2048]{1,0:T(8,128)(2,1)} custom-call(bf16[1536,2048]{1,0:T(8,128)(2,1)} %get-tuple-element.74.refs_5_.refs_0_.refs_2_, bf16[2048,2048]{1,0:T(8,128)(2,1)} %refs_1_.18, bf16[1536,2048]{1,0:T(8,128)(2,1)} %collective-permute-done.17.refs_2_, bf16[1536,2048]{1,0:T(8,128)(2,1)} %d_gated.9.refs_3_), custom_call_target="tpu_custom_call" | custom-call | flops 12884901888 | bytes 27262976 | tf_op jit(solution)/shard_map/mlp_out/pallas_call | solution.py:200
  739.2 49.6 %mlp_act.10 = (bf16[1536,2048]{1,0:T(8,128)(2,1)}, bf16[1536,2048]{1,0:T(8,128)(2,1)}, bf16[1536,2048]{1,0:T(8,128)(2,1)}) custom-call(bf16[1536,2048]{1,0:T(8,128)(2,1)} %all-gather.24.cloned.1.call-done.refs_0_.refs_4_, bf16[1536,2048]{1,0:T(8,128)(2,1)} %bitcast.121, bf16[2048,2048]{1,0:T(8,128)(2,1)} %refs_2_.23, bf16[2048,2048]{1,0:T(8,128)(2,1)} %refs_3_.23, ...), custom_call_target="tpu_custom_call" | custom-call | flops 38654705664 | bytes 56623104 | tf_op jit(solution)/shard_map/mlp_act/pallas_call | solution.py:200
  788.8 48.8 %mlp_act.11 = (bf16[1536,2048]{1,0:T(8,128)(2,1)}, bf16[1536,2048]{1,0:T(8,128)(2,1)}, bf16[1536,2048]{1,0:T(8,128)(2,1)}) custom-call(bf16[1536,2048]{1,0:T(8,128)(2,1)} %collective-permute-done.19.refs_0_.refs_5_, bf16[1536,2048]{1,0:T(8,128)(2,1)} %collective-permute-done.20.refs_1_.refs_11_, bf16[2048,2048]{1,0:T(8,128)(2,1)} %refs_2_.23, ...), custom_call_target="tpu_custom_call" | custom-call | flops 38654705664 | bytes 56623104 | tf_op jit(solution)/shard_map/mlp_act/pallas_call | solution.py:200
  837.6 35.3 %d_gated.10.refs_2_ = bf16[1536,2048]{1,0:T(8,128)(2,1)} custom-call(bf16[1536,2048]{1,0:T(8,128)(2,1)} %get-tuple-element.83.refs_0_.refs_11_, bf16[1536,2048]{1,0:T(8,128)(2,1)} %get-tuple-element.84.refs_1_.refs_11_, bf16[2048,2048]{1,0:T(8,128)(2,1)} %refs_2_.23, bf16[2048,2048]{1,0:T(8,128)(2,1)} %refs_3_.23, ...), custom_call_target="tpu_custom_call" | custom-call | flops 25769803776 | bytes 35651584 | tf_op jit(solution)/shard_map/d_gated/pallas_call | solution.py:200
  873.4 21.8 %mlp_out.10.refs_5_ = bf16[1536,2048]{1,0:T(8,128)(2,1)} custom-call(bf16[1536,2048]{1,0:T(8,128)(2,1)} %get-tuple-element.82.refs_4_.refs_0_.refs_5_, bf16[2048,2048]{1,0:T(8,128)(2,1)} %refs_1_.18, bf16[1536,2048]{1,0:T(8,128)(2,1)} %d_gated.10.refs_2_), custom_call_target="tpu_custom_call" | custom-call | flops 12884901888 | bytes 20971520 | tf_op jit(solution)/shard_map/mlp_out/pallas_call | solution.py:200
  897.9 36.4 %d_gated.11.refs_3_ = bf16[1536,2048]{1,0:T(8,128)(2,1)} custom-call(bf16[1536,2048]{1,0:T(8,128)(2,1)} %get-tuple-element.85.refs_0_.refs_10_, bf16[1536,2048]{1,0:T(8,128)(2,1)} %get-tuple-element.86.refs_1_.refs_10_, bf16[2048,2048]{1,0:T(8,128)(2,1)} %refs_2_.23, bf16[2048,2048]{1,0:T(8,128)(2,1)} %refs_3_.23, bf16[1536,2048]{1,0:T(8,128)(2,1)} %copy-done.49, ...), custom_call_target="tpu_custom_call" | custom-call | flops 25769803776 | bytes 41943040 | tf_op jit(solution)/shard_map/d_gated/pallas_call | solution.py:200
  935.2 23.2 %mlp_out.11.refs_6_ = bf16[1536,2048]{1,0:T(8,128)(2,1)} custom-call(bf16[1536,2048]{1,0:T(8,128)(2,1)} %get-tuple-element.81.refs_5_.refs_0_.refs_4_, bf16[2048,2048]{1,0:T(8,128)(2,1)} %refs_1_.18, bf16[1536,2048]{1,0:T(8,128)(2,1)} %collective-permute-done.21.refs_2_, bf16[1536,2048]{1,0:T(8,128)(2,1)} %d_gated.11.refs_3_), custom_call_target="tpu_custom_call" | custom-call | flops 12884901888 | bytes 27262976 | tf_op jit(solution)/shard_map/mlp_out/pallas_call | solution.py:200
  1021.3 91.6 %wgrad.3.refs_6_ = f32[2048,2048]{1,0:T(8,128)} custom-call(bf16[1536,2048]{1,0:T(8,128)(2,1)} %all-gather.20.cloned.1.call-done.refs_0_, bf16[1536,2048]{1,0:T(8,128)(2,1)} %collective-permute-done.12.refs_0_.refs_1_, bf16[1536,2048]{1,0:T(8,128)(2,1)} %all-gather.22.cloned.1.call-done.refs_0_.refs_2_, ...), custom_call_target="tpu_custom_call" | custom-call | flops 77309411328 | bytes 92274688 | tf_op jit(solution)/shard_map/wgrad/pallas_call | solution.py:200
  1222.2 47.2 %reduce-scatter.10.cloned.1.call-done = bf16[384,2048]{1,0:T(8,128)(2,1)} async-done(((bf16[1536,2048]{1,0:T(8,128)(2,1)}), bf16[384,2048]{1,0:T(8,128)(2,1)}) %reduce-scatter.10.cloned.1.call-update) | async-done | bytes 1572880 | tf_op jit(solution)/shard_map/reduce_scatter | solution.py:460
  1269.3 67.4 %reduce-scatter.12.cloned.1.call-done = bf16[384,2048]{1,0:T(8,128)(2,1)} async-done(((bf16[1536,2048]{1,0:T(8,128)(2,1)}), bf16[384,2048]{1,0:T(8,128)(2,1)}) %reduce-scatter.12.cloned.1.call-update) | async-done | bytes 1572880 | tf_op jit(solution)/shard_map/reduce_scatter | solution.py:460
  1336.8 67.3 %reduce-scatter.14.cloned.1.call-done = bf16[384,2048]{1,0:T(8,128)(2,1)} async-done(((bf16[1536,2048]{1,0:T(8,128)(2,1)}), bf16[384,2048]{1,0:T(8,128)(2,1)}) %reduce-scatter.14.cloned.1.call-update) | async-done | bytes 1572880 | tf_op jit(solution)/shard_map/reduce_scatter | solution.py:460
  1410.6 91.8 %wgrad.4.refs_11_ = f32[2048,2048]{1,0:T(8,128)} custom-call(bf16[1536,2048]{1,0:T(8,128)(2,1)} %all-gather.20.cloned.1.call-done.refs_0_, bf16[1536,2048]{1,0:T(8,128)(2,1)} %collective-permute-done.12.refs_0_.refs_1_, bf16[1536,2048]{1,0:T(8,128)(2,1)} %all-gather.22.cloned.1.call-done.refs_0_.refs_2_, ...), custom_call_target="tpu_custom_call" | custom-call | flops 77309411328 | bytes 92274688 | tf_op jit(solution)/shard_map/wgrad/pallas_call | solution.py:200
  1502.4 24.2 %d_hidden.1 = (bf16[1152,2048]{1,0:T(8,128)(2,1)}, f32[8,2048]{1,0:T(8,128)}) custom-call(bf16[1152,1024]{1,0:T(8,128)(2,1)} %pad_maximum_fusion.1.refs_0_, bf16[1152,1024]{1,0:T(8,128)(2,1)} %pad_maximum_fusion.2.refs_0_.refs_1_, bf16[1152,256]{1,0:T(8,128)(2,1)} %bitcast.106, bf16[1152,256]{1,0:T(8,128)(2,1)} %bitcast.107, bf16[1152,2048]{1,0:T(8,128)(2,1)} %bitcast.98, ...), custom_call_target="tpu_custom_call" | custom-call | flops 12079595520 | bytes 27328512 | tf_op jit(solution)/shard_map/d_hidden/pallas_call | solution.py:200
  1527.4 23.7 %all-reduce.2 = (f32[2048]{0:T(1024)}, f32[2048]{0:T(1024)}) all-reduce(f32[2048]{0:T(1024)S(1)} %reduce_sum.28, f32[2048]{0:T(1024)S(1)} %add_reduce_fusion), channel_id=1, replica_groups=mesh['dp'=1,'tp'=8] {'tp'}, use_global_device_ids=true, to_apply=%region_9.10 | all-reduce | flops 4096 | bytes 32768 | tf_op jit(solution)/shard_map/psum | solution.py:577
  1551.2 92.1 %wgrad.5 = f32[2048,2048]{1,0:T(8,128)} custom-call(bf16[1536,2048]{1,0:T(8,128)(2,1)} %get-tuple-element.67.refs_4_.refs_0_, bf16[1536,2048]{1,0:T(8,128)(2,1)} %get-tuple-element.68.refs_4_.refs_0_.refs_1_, bf16[1536,2048]{1,0:T(8,128)(2,1)} %get-tuple-element.74.refs_5_.refs_0_.refs_2_, bf16[1536,2048]{1,0:T(8,128)(2,1)} %get-tuple-element.75.refs_4_.refs_0_.refs_3_, ...), custom_call_target="tpu_custom_call" | custom-call | flops 77309411328 | bytes 92274688 | tf_op jit(solution)/shard_map/wgrad/pallas_call | solution.py:200
  (290 shorter events, 318.3 us)
Async XLA Ops:
  7.2 125.5 %all-gather.18.cloned.1.call-start = ((), (), s32[]{:S(2)}) async-start(), calls=%async_computation.21 | async-start | bytes 5898240 | tf_op jit(solution)/shard_map/all_gather | solution.py:456
  18.1 200.2 %all-gather.12.cloned.1.call-start = ((), (), s32[]{:S(2)}) async-start(), calls=%async_computation.9 | async-start | bytes 7864320 | tf_op jit(solution)/shard_map/all_gather | solution.py:456
  23.0 257.8 %all-gather.20.cloned.1.call-start = ((), (), s32[]{:S(2)}) async-start(), calls=%async_computation.22 | async-start | bytes 7864320 | tf_op jit(solution)/shard_map/all_gather | solution.py:456
  23.5 44.2 %collective-permute-start = (bf16[256,2048]{0,1:T(8,128)(2,1)}, bf16[256,2048]{0,1:T(8,128)(2,1)S(1)}, u32[]{:S(2)}, u32[]{:S(2)}) collective-permute-start(bf16[256,2048]{0,1:T(8,128)(2,1)} %bitcast.1), channel_id=1, source_target_pairs={{0,2},{1,3},{2,0},{3,1},{4,6},{5,7},{6,4},{7,5}} | collective-permute-start | bytes 3145736 | tf_op jit(solution)/shard_map/ppermute | solution.py:466
  26.9 43.9 %collective-permute-start.1 = (bf16[256,2048]{0,1:T(8,128)(2,1)}, bf16[256,2048]{0,1:T(8,128)(2,1)}, u32[]{:S(2)}, u32[]{:S(2)}) collective-permute-start(bf16[256,2048]{0,1:T(8,128)(2,1)} %bitcast.1), channel_id=1, source_target_pairs={{0,4},{1,5},{2,6},{3,7},{4,0},{5,1},{6,2},{7,3}} | collective-permute-start | bytes 3145736 | tf_op jit(solution)/shard_map/ppermute | solution.py:466
  28.4 84.3 %collective-permute-start.7 = (bf16[256,2048]{1,0:T(8,128)(2,1)}, bf16[256,2048]{1,0:T(8,128)(2,1)S(1)}, u32[]{:S(2)}, u32[]{:S(2)}) collective-permute-start(bf16[256,2048]{1,0:T(8,128)(2,1)} %param.21), channel_id=1, source_target_pairs={{0,4},{1,5},{2,6},{3,7},{4,0},{5,1},{6,2},{7,3}} | collective-permute-start | bytes 3145736 | tf_op jit(solution)/shard_map/ppermute | solution.py:466
  28.9 85.5 %collective-permute-start.6 = (bf16[256,2048]{1,0:T(8,128)(2,1)}, bf16[256,2048]{1,0:T(8,128)(2,1)}, u32[]{:S(2)}, u32[]{:S(2)}) collective-permute-start(bf16[256,2048]{1,0:T(8,128)(2,1)} %param.21), channel_id=1, source_target_pairs={{0,2},{1,3},{2,0},{3,1},{4,6},{5,7},{6,4},{7,5}} | collective-permute-start | bytes 3145736 | tf_op jit(solution)/shard_map/ppermute | solution.py:466
  68.6 57.6 %collective-permute-start.2 = (bf16[128,2048]{0,1:T(8,128)(2,1)}, bf16[128,2048]{0,1:T(8,128)(2,1)}, u32[]{:S(2)}, u32[]{:S(2)}) collective-permute-start(bf16[128,2048]{0,1:T(8,128)(2,1)} %slice.47), channel_id=1, source_target_pairs={{0,4},{1,5},{2,6},{3,7},{4,0},{5,1},{6,2},{7,3}} | collective-permute-start | bytes 1572872 | tf_op jit(solution)/shard_map/ppermute | solution.py:466
  72.6 54.8 %collective-permute-start.3 = (bf16[128,2048]{0,1:T(8,128)(2,1)}, bf16[128,2048]{0,1:T(8,128)(2,1)}, u32[]{:S(2)}, u32[]{:S(2)}) collective-permute-start(bf16[128,2048]{0,1:T(8,128)(2,1)} %slice.48), channel_id=1, source_target_pairs={{0,2},{1,3},{2,0},{3,1},{4,6},{5,7},{6,4},{7,5}} | collective-permute-start | bytes 1572872 | tf_op jit(solution)/shard_map/ppermute | solution.py:466
  151.8 45.6 %collective-permute-start.10 = (bf16[1024,2048]{1,0:T(8,128)(2,1)}, bf16[1024,2048]{1,0:T(8,128)(2,1)}, u32[]{:S(2)}, u32[]{:S(2)}) collective-permute-start(bf16[1024,2048]{1,0:T(8,128)(2,1)} %bitcast.21.refs_3_.refs_4_), channel_id=1, source_target_pairs={{0,1},{1,0},{2,3},{3,2},{4,5},{5,4},{6,7},{7,6}} | collective-permute-start | bytes 12582920 | tf_op jit(solution)/shard_map/ppermute | solution.py:463
  216.6 243.9 %all-gather.14.cloned.1.call-start = ((), (), s32[]{:S(2)}) async-start(), calls=%async_computation.11 | async-start | bytes 7864320 | tf_op jit(solution)/shard_map/all_gather | solution.py:456
  217.1 243.8 %all-gather.22.cloned.1.call-start = ((), (), s32[]{:S(2)}) async-start(), calls=%async_computation.23 | async-start | bytes 7864320 | tf_op jit(solution)/shard_map/all_gather | solution.py:456
  217.7 461.1 %all-gather.16.cloned.1.call-start = ((), (), s32[]{:S(2)}) async-start(), calls=%async_computation.13 | async-start | bytes 7864320 | tf_op jit(solution)/shard_map/all_gather | solution.py:456
  218.3 460.9 %all-gather.24.cloned.1.call-start = ((), (), s32[]{:S(2)}) async-start(), calls=%async_computation.24 | async-start | bytes 7864320 | tf_op jit(solution)/shard_map/all_gather | solution.py:456
  218.4 84.8 %collective-permute-start.11 = (bf16[1536,2048]{1,0:T(8,128)(2,1)}, bf16[1536,2048]{1,0:T(8,128)(2,1)}, u32[]{:S(2)}, u32[]{:S(2)}) collective-permute-start(bf16[1536,2048]{1,0:T(8,128)(2,1)} %bitcast.114), channel_id=1, source_target_pairs={{0,1},{1,0},{2,3},{3,2},{4,5},{5,4},{6,7},{7,6}} | collective-permute-start | bytes 18874376 | tf_op jit(solution)/shard_map/ppermute | solution.py:463
  280.8 81.9 %collective-permute-start.12 = (bf16[1536,2048]{1,0:T(8,128)(2,1)}, bf16[1536,2048]{1,0:T(8,128)(2,1)}, u32[]{:S(2)}, u32[]{:S(2)}) collective-permute-start(bf16[1536,2048]{1,0:T(8,128)(2,1)} %all-gather.20.cloned.1.call-done.refs_0_), channel_id=1, source_target_pairs={{0,1},{1,0},{2,3},{3,2},{4,5},{5,4},{6,7},{7,6}} | collective-permute-start | bytes 18874376 | tf_op jit(solution)/shard_map/ppermute | solution.py:463
  280.9 677.6 %reduce-scatter.16.cloned.1.call-start = ((), (), s32[]{:S(2)}) async-start(), calls=%async_computation.15 | async-start | bytes 7864320 | tf_op jit(solution)/shard_map/reduce_scatter | solution.py:460
  460.5 111.1 %collective-permute-start.16 = (bf16[1536,2048]{1,0:T(8,128)(2,1)}, bf16[1536,2048]{1,0:T(8,128)(2,1)}, u32[]{:S(2)}, u32[]{:S(2)}) collective-permute-start(bf16[1536,2048]{1,0:T(8,128)(2,1)} %bitcast.117), channel_id=1, source_target_pairs={{0,1},{1,0},{2,3},{3,2},{4,5},{5,4},{6,7},{7,6}} | collective-permute-start | bytes 18874376 | tf_op jit(solution)/shard_map/ppermute | solution.py:463
  461.0 110.6 %collective-permute-start.15 = (bf16[1536,2048]{1,0:T(8,128)(2,1)}, bf16[1536,2048]{1,0:T(8,128)(2,1)}, u32[]{:S(2)}, u32[]{:S(2)}) collective-permute-start(bf16[1536,2048]{1,0:T(8,128)(2,1)} %all-gather.22.cloned.1.call-done.refs_0_.refs_2_), channel_id=1, source_target_pairs={{0,1},{1,0},{2,3},{3,2},{4,5},{5,4},{6,7},{7,6}} | collective-permute-start | bytes 18874376 | tf_op jit(solution)/shard_map/ppermute | solution.py:463
  498.9 491.3 %reduce-scatter.18.cloned.1.call-start = ((), (), s32[]{:S(2)}) async-start(), calls=%async_computation.16 | async-start | bytes 7864320 | tf_op jit(solution)/shard_map/reduce_scatter | solution.py:460
  678.9 109.9 %collective-permute-start.20 = (bf16[1536,2048]{1,0:T(8,128)(2,1)}, bf16[1536,2048]{1,0:T(8,128)(2,1)}, u32[]{:S(2)}, u32[]{:S(2)}) collective-permute-start(bf16[1536,2048]{1,0:T(8,128)(2,1)} %bitcast.120), channel_id=1, source_target_pairs={{0,1},{1,0},{2,3},{3,2},{4,5},{5,4},{6,7},{7,6}} | collective-permute-start | bytes 18874376 | tf_op jit(solution)/shard_map/ppermute | solution.py:463
  679.2 109.5 %collective-permute-start.19 = (bf16[1536,2048]{1,0:T(8,128)(2,1)}, bf16[1536,2048]{1,0:T(8,128)(2,1)}, u32[]{:S(2)}, u32[]{:S(2)}) collective-permute-start(bf16[1536,2048]{1,0:T(8,128)(2,1)} %all-gather.24.cloned.1.call-done.refs_0_.refs_4_), channel_id=1, source_target_pairs={{0,1},{1,0},{2,3},{3,2},{4,5},{5,4},{6,7},{7,6}} | collective-permute-start | bytes 18874376 | tf_op jit(solution)/shard_map/ppermute | solution.py:463
  715.8 397.1 %reduce-scatter.20.cloned.1.call-start = ((), (), s32[]{:S(2)}) async-start(), calls=%async_computation.17 | async-start | bytes 7864320 | tf_op jit(solution)/shard_map/reduce_scatter | solution.py:460
  934.3 275.4 %reduce-scatter.22.cloned.1.call-start = ((), (), s32[]{:S(2)}) async-start(), calls=%async_computation.18 | async-start | bytes 5898240 | tf_op jit(solution)/shard_map/reduce_scatter | solution.py:460
  989.8 152.6 %collective-permute-start.23 = (bf16[4,4,96,512]{3,2,1,0:T(8,128)(2,1)}, bf16[4,4,96,512]{3,2,1,0:T(8,128)(2,1)}, u32[]{:S(2)}, u32[]{:S(2)}) collective-permute-start(bf16[4,4,96,512]{3,2,1,0:T(8,128)(2,1)} %get-tuple-element.105), channel_id=1, source_target_pairs={{0,1},{1,0},{2,3},{3,2},{4,5},{5,4},{6,7},{7,6}} | collective-permute-start | bytes 4718600 | tf_op jit(solution)/shard_map/ppermute | solution.py:463
  1021.2 123.3 %collective-permute-start.24 = (bf16[4,4,96,512]{3,2,1,0:T(8,128)(2,1)}, bf16[4,4,96,512]{3,2,1,0:T(8,128)(2,1)}, u32[]{:S(2)}, u32[]{:S(2)}) collective-permute-start(bf16[4,4,96,512]{3,2,1,0:T(8,128)(2,1)} %get-tuple-element.107), channel_id=1, source_target_pairs={{0,1},{1,0},{2,3},{3,2},{4,5},{5,4},{6,7},{7,6}} | collective-permute-start | bytes 4718600 | tf_op jit(solution)/shard_map/ppermute | solution.py:463
  1149.4 119.9 %reduce-scatter.10.cloned.1.call-start = ((), (), s32[]{:S(2)}) async-start(), calls=%async_computation.10 | async-start | bytes 7864320 | tf_op jit(solution)/shard_map/reduce_scatter | solution.py:460
  1150.0 186.8 %reduce-scatter.12.cloned.1.call-start = ((), (), s32[]{:S(2)}) async-start(), calls=%async_computation.12 | async-start | bytes 7864320 | tf_op jit(solution)/shard_map/reduce_scatter | solution.py:460
  1150.8 253.3 %reduce-scatter.14.cloned.1.call-start = ((), (), s32[]{:S(2)}) async-start(), calls=%async_computation.14 | async-start | bytes 7864320 | tf_op jit(solution)/shard_map/reduce_scatter | solution.py:460
  1151.3 491.9 %reduce-scatter.24.cloned.1.call-start = ((), (), s32[]{:S(2)}) async-start(), calls=%async_computation.19 | async-start | bytes 10485760 | tf_op jit(solution)/shard_map/reduce_scatter | solution.py:460
  1209.7 436.5 %all-reduce.6.cloned.1.call-start = ((), (), s32[]{:S(2)}) async-start(), calls=%async_computation.25 | async-start | bytes 8388608 | tf_op jit(solution)/shard_map/psum | solution.py:574
  1220.9 425.8 %reduce-scatter.26.cloned.1.call-start = ((), (), s32[]{:S(2)}) async-start(), calls=%async_computation.20 | async-start | bytes 10485760 | tf_op jit(solution)/shard_map/reduce_scatter | solution.py:460
  (67 other events, 998.5 us)
Sparse Core Ops, SparseCore 0:
  18.2 92.2 all-gather.17
  112.9 77.2 all-gather.11
  216.7 64.1 all-gather.19
  282.5 64.4 all-gather.13
  349.2 64.4 all-gather.21
  415.3 64.4 all-gather.15
  482.1 64.4 all-gather.23
  550.1 64.4 reduce-scatter.15
  715.9 65.6 reduce-scatter.17
  934.4 65.8 reduce-scatter.19
  1149.5 52.4 reduce-scatter.21
  1204.8 64.4 reduce-scatter.9
  1272.3 64.4 reduce-scatter.11
  1339.6 64.4 reduce-scatter.13
  1406.9 80.7 reduce-scatter.23
  1491.4 70.8 all-reduce.5
  1565.8 80.8 reduce-scatter.25

commit v3 on v2

v3 whole, which is shorter than its diff:
```python
import functools
import math
import jax
import jax.numpy as jnp
from jax import lax
from jax.experimental import pallas as pl
from jax.experimental.pallas import tpu as pltpu
from jax.sharding import PartitionSpec as P

NORM_EPS = 1e-6
CHUNKS = 3
F32 = jnp.float32
BF16 = jnp.bfloat16
MASKED = -1e30


def rms_norm(x_in, gain):
    x_f = x_in.astype(F32)
    inv_rms = lax.rsqrt(jnp.mean(x_f * x_f, axis=-1, keepdims=True) + NORM_EPS)
    return (x_f * inv_rms * (1.0 + gain)).astype(BF16)


def rope_tables(positions, head_dim):
    half_dim = head_dim // 2
    exponent = jnp.arange(half_dim, dtype=F32) * (2.0 / head_dim)
    inv_freq = jnp.exp(exponent * (-math.log(10000.0)))
    angles = positions.astype(F32)[:, None] * inv_freq[None, :]
    return jnp.cos(angles), jnp.sin(angles)


def apply_rope(x_f, cos_t, sin_t):
    half_dim = x_f.shape[-1] // 2
    first = x_f[..., :half_dim]
    second = x_f[..., half_dim:]
    return jnp.concatenate([first * cos_t - second * sin_t, second * cos_t + first * sin_t], axis=-1)


def dot_f32(lhs, rhs, lhs_dim, rhs_dim):
    return lax.dot_general(lhs, rhs, (((lhs_dim,), (rhs_dim,)), ((), ())), preferred_element_type=F32)


def own_first(kv_ref, core, lo, hi):
    shards = kv_ref.shape[0] // 2
    return jnp.concatenate([kv_ref[2 * c + side, 0, :, lo:hi] for side in (core, 1 - core) for c in range(shards)], axis=0)


def attn_fwd_kernel(prefix_s, valid_s, core_s, q_own_ref, q_oth_ref, kv_ref, cos_ref, sin_ref, qpos_ref, kpos_ref,
                    o_own_ref, o_oth_ref, r_own_ref, r_oth_ref):
    b = pl.program_id(0)
    rows, width = q_own_ref.shape[1:]
    hd = kv_ref.shape[-1] // 2
    half = hd // 2
    heads = width // hd
    scale = hd ** -0.5
    cos_t, sin_t = cos_ref[...], sin_ref[...]
    queries = []
    for src, dst in ((q_own_ref, r_own_ref), (q_oth_ref, r_oth_ref)):
        for n in range(heads):
            first = src[0, :, n * hd:n * hd + half]
            second = src[0, :, n * hd + half:(n + 1) * hd]
            q_1 = ((first * cos_t - second * sin_t).astype(BF16) * scale).astype(BF16)
            q_2 = ((second * cos_t + first * sin_t).astype(BF16) * scale).astype(BF16)
            dst[0, :, n * hd:n * hd + half] = q_1
            dst[0, :, n * hd + half:(n + 1) * hd] = q_2
            queries.append(jnp.concatenate([q_1, q_2], axis=1))
    keys = own_first(kv_ref, core_s[0], 0, hd)
    values = own_first(kv_ref, core_s[0], hd, 2 * hd)
    limit = jnp.minimum(valid_s[b], jnp.maximum(prefix_s[b], qpos_ref[...] + 1))
    visible = kpos_ref[...] < limit
    for side, dst in ((0, o_own_ref), (1, o_oth_ref)):
        query = jnp.concatenate(queries[side * heads:(side + 1) * heads], axis=0)
        scores = dot_f32(query, keys, 1, 1)
        scores = jnp.where(visible, scores, MASKED)
        top = jnp.max(scores, axis=-1, keepdims=True)
        expo = jnp.exp(scores - top)
        inv = 1.0 / jnp.sum(expo, axis=-1, keepdims=True)
        probs = (expo * inv).astype(BF16)
        mixed = dot_f32(probs, values, 1, 0).astype(BF16)
        for n in range(heads):
            dst[0, :, n * hd:(n + 1) * hd] = mixed[n * rows:(n + 1) * rows]


def attn_bwd_kernel(first, prefix_s, valid_s, core_s, q_own_ref, q_oth_ref, g_own_ref, g_oth_ref, kv_ref, cos_ref, sin_ref,
                    qpos_ref, kpos_ref, dq_own_ref, dq_oth_ref, dkv_own_ref, dkv_oth_ref):
    b = pl.program_id(0) + first
    rows, width = q_own_ref.shape[1:]
    hd = kv_ref.shape[-1] // 2
    half = hd // 2
    heads = width // hd
    scale = hd ** -0.5
    cos_t, sin_t = cos_ref[...], sin_ref[...]
    shards = kv_ref.shape[0] // 2
    n_keys = shards * kv_ref.shape[2]
    keys = own_first(kv_ref, core_s[0], 0, hd)
    values = own_first(kv_ref, core_s[0], hd, 2 * hd)
    limit = jnp.minimum(valid_s[b], jnp.maximum(prefix_s[b], qpos_ref[...] + 1))
    visible = kpos_ref[...] < limit
    d_keys, d_values = 0.0, 0.0
    for q_ref, g_ref, dst in ((q_own_ref, g_own_ref, dq_own_ref), (q_oth_ref, g_oth_ref, dq_oth_ref)):
        query = jnp.concatenate([q_ref[0, :, n * hd:(n + 1) * hd] for n in range(heads)], axis=0)
        grad = jnp.concatenate([g_ref[0, :, n * hd:(n + 1) * hd] for n in range(heads)], axis=0)
        scores = dot_f32(keys, query, 1, 1)
        scores = jnp.where(visible, scores, MASKED)
        top = jnp.max(scores, axis=0, keepdims=True)
        expo = jnp.exp(scores - top)
        inv = 1.0 / jnp.sum(expo, axis=0, keepdims=True)
        probs = expo * inv
        d_probs = dot_f32(values, grad, 1, 1)
        delta = jnp.sum(probs * d_probs, axis=0, keepdims=True)
        d_scores = (probs * (d_probs - delta)).astype(BF16)
        d_values = d_values + dot_f32(probs.astype(BF16), grad, 1, 0)
        d_keys = d_keys + dot_f32(d_scores, query, 1, 0)
        d_query = dot_f32(d_scores, keys, 0, 0) * scale
        for n in range(heads):
            g_1 = d_query[n * rows:(n + 1) * rows, :half]
            g_2 = d_query[n * rows:(n + 1) * rows, half:]
            dst[0, :, n * hd:n * hd + half] = (g_1 * cos_t + g_2 * sin_t).astype(BF16)
            dst[0, :, n * hd + half:(n + 1) * hd] = (g_2 * cos_t - g_1 * sin_t).astype(BF16)
    d_keys = d_keys.astype(BF16)
    d_values = d_values.astype(BF16)
    span = n_keys // shards
    for side, dst in ((0, dkv_own_ref), (1, dkv_oth_ref)):
        for c in range(shards):
            at = side * n_keys + c * span
            dst[c, 0, :, :hd] = d_keys[at:at + span]
            dst[c, 0, :, hd:] = d_values[at:at + span]


def attn_specs(rows, width, shards, two_hd, half):
    q_spec = pl.BlockSpec((1, rows, width), lambda b, *_: (b, 0, 0))
    kv_spec = pl.BlockSpec((shards, 1, rows, two_hd), lambda b, *_: (0, b, 0, 0))
    tab_spec = pl.BlockSpec((rows, half), lambda b, *_: (0, 0))
    return q_spec, kv_spec, tab_spec


def whole(shape):
    return pl.BlockSpec(shape, lambda b, *_: tuple(0 for _ in shape))


def attn_fwd(q_own, q_oth, kv_all, cos_t, sin_t, qpos, kpos, scalars):
    batch, rows, width = q_own.shape
    shards, two_hd = kv_all.shape[0], kv_all.shape[3]
    q_spec, kv_spec, tab_spec = attn_specs(rows, width, shards, two_hd, two_hd // 4)
    heads = width * 2 // two_hd
    out = jax.ShapeDtypeStruct((batch, rows, width), BF16)
    qpos_col = jnp.tile(qpos, heads)[:, None]
    n_keys = kpos.shape[0]
    flops = 2 * 2 * batch * rows * 2 * width * n_keys
    return pl.pallas_call(
        attn_fwd_kernel,
        out_shape=(out, out, out, out),
        grid_spec=pltpu.PrefetchScalarGridSpec(
            num_scalar_prefetch=3, grid=(batch,),
            in_specs=[q_spec, q_spec, kv_spec, tab_spec, tab_spec, whole((heads * rows, 1)), whole((1, n_keys))],
            out_specs=[q_spec] * 4),
        compiler_params=pltpu.CompilerParams(dimension_semantics=("arbitrary",), vmem_limit_bytes=40 << 20),
        cost_estimate=pl.CostEstimate(flops=flops, bytes_accessed=batch * rows * width * 16 + kv_all.size * 2, transcendentals=batch * rows * heads * 2 * n_keys),
        name="attn_fwd",
    )(*scalars, q_own, q_oth, kv_all, cos_t, sin_t, qpos_col, kpos[None, :])


def attn_bwd(order, q_own, q_oth, g_own, g_oth, kv_all, cos_t, sin_t, qpos, kpos, scalars, first, count, earlier):
    batch, rows, width = q_own.shape
    shards, two_hd = kv_all.shape[0], kv_all.shape[3]
    tab_spec = pl.BlockSpec((rows, two_hd // 4), lambda b, *_: (0, 0))
    q_spec = pl.BlockSpec((1, rows, width), lambda b, *_: (b + first, 0, 0))
    kv_spec = pl.BlockSpec((shards, 1, rows, two_hd), lambda b, *_: (0, b + first, 0, 0))
    dkv_spec = pl.BlockSpec((shards // 2, 1, rows, two_hd), lambda b, *_: (0, b + first, 0, 0))
    heads = width * 2 // two_hd
    out = jax.ShapeDtypeStruct((batch, rows, width), BF16)
    kv_out = jax.ShapeDtypeStruct((shards // 2, batch, rows, two_hd), BF16)
    qpos_row = jnp.tile(qpos, heads)[None, :]
    n_keys = kpos.shape[0]
    flops = 2 * 5 * count * rows * 2 * width * n_keys
    return order.call(
        functools.partial(attn_bwd_kernel, first), 9, len(earlier), prefetch=3,
        out_shape=(out, out, kv_out, kv_out), grid=(count,),
        in_specs=[q_spec, q_spec, q_spec, q_spec, kv_spec, tab_spec, tab_spec, whole((1, heads * rows)), whole((n_keys, 1))],
        out_specs=[q_spec, q_spec, dkv_spec, dkv_spec],
        compiler_params=pltpu.CompilerParams(dimension_semantics=("arbitrary",), vmem_limit_bytes=40 << 20),
        cost_estimate=pl.CostEstimate(flops=flops, bytes_accessed=count * rows * width * 12 + kv_all.size * 4, transcendentals=count * rows * heads * 2 * n_keys),
        name="attn_bwd",
    )(*scalars, q_own, q_oth, g_own, g_oth, kv_all, cos_t, sin_t, qpos_row, kpos[:, None], *earlier)


class Order:
    def __init__(self):
        self.last = None

    def call(self, kernel, n_in, n_kept=0, *, in_specs, out_specs, grid, prefetch=0, scratch_shapes=(), **options):
        def run(*args):
            deps = () if self.last is None or any(self.last is a for a in args) else (self.last,)
            n_args = prefetch + n_in

            def body(*refs):
                kernel(*refs[:n_args], *refs[n_args + n_kept + len(deps):])

            n_out = len(out_specs) if isinstance(out_specs, (list, tuple)) else 1
            out = pl.pallas_call(
                body,
                grid_spec=pltpu.PrefetchScalarGridSpec(
                    num_scalar_prefetch=prefetch, grid=grid, scratch_shapes=scratch_shapes, out_specs=out_specs,
                    in_specs=in_specs + [pl.BlockSpec(memory_space=pl.ANY)] * (n_kept + len(deps))),
                input_output_aliases={n_args + k: n_out - n_kept + k for k in range(n_kept)},
                **options)(*args, *deps)
            self.last = out[0] if isinstance(out, (tuple, list)) else out
            return out

        return run


def params(steps, limit=56):
    return pltpu.CompilerParams(dimension_semantics=("arbitrary",) * steps, vmem_limit_bytes=limit << 20)


def cost(flops, *arrays):
    return pl.CostEstimate(flops=flops, bytes_accessed=sum(a.size * a.dtype.itemsize for a in arrays), transcendentals=0)


def rows_of(ref):
    return ref[...].reshape(-1, ref.shape[-1])


def raw_spec(shape):
    return pl.BlockSpec((2, 1) + shape[2:], lambda j, i, core: (lax.rem(i, 2), lax.bitwise_xor(core[0], lax.div(i, 2)), 0, 0))


def d_act_kernel(core_s, g_ref, wd_ref, out_ref):
    out_ref[...] = dot_f32(rows_of(g_ref), wd_ref[...], 1, 1).astype(BF16)


def d_act_call(order, core, g_all, w_down, tn=1024):
    chips, _, rows, dim = g_all.shape
    width = w_down.shape[0]
    out = jax.ShapeDtypeStruct((chips * 2 * rows, width), BF16)
    return order.call(
        d_act_kernel, 2, prefetch=1, out_shape=out, grid=(width // tn, chips),
        in_specs=[raw_spec(g_all.shape), pl.BlockSpec((tn, dim), lambda j, i, core: (j, 0))],
        out_specs=pl.BlockSpec((2 * rows, tn), lambda j, i, core: (i, j)), compiler_params=params(2),
        cost_estimate=cost(2 * g_all.size * width, g_all, w_down, out), name="d_act",
    )(core, g_all, w_down)


def act_kernel(core_s, z_ref, g_ref, wg_ref, wu_ref, *refs, sub):
    c_1 = math.sqrt(2.0 / math.pi)
    c_3 = 0.044715 * c_1
    act_ref, dg_ref, du_ref = refs[-3:]
    z_in = rows_of(z_ref)
    for j in range(0, wg_ref.shape[1], sub):
        gate = dot_f32(z_in, wg_ref[:, j:j + sub], 1, 0)
        upper = dot_f32(z_in, wu_ref[:, j:j + sub], 1, 0)
        if len(refs) == 4:
            d_act = dot_f32(rows_of(g_ref), refs[0][j:j + sub, :], 1, 1).astype(BF16).astype(F32)
        else:
            d_act = g_ref[:, j:j + sub].astype(F32)
        square = gate * gate
        half = 0.5 * jnp.tanh(gate * (c_3 * square + c_1)) + 0.5
        gelu = gate * half
        act_ref[:, j:j + sub] = (gelu * upper).astype(BF16)
        du_ref[:, j:j + sub] = (d_act * gelu).astype(BF16)
        slope = half + gelu * (1.0 - half) * (6.0 * c_3 * square + 2.0 * c_1)
        dg_ref[:, j:j + sub] = (d_act * upper * slope).astype(BF16)


def act_call(order, core, z_all, g_all, w_gate, w_up, w_down, tn=512, sub=256):
    chips, _, rows, dim = z_all.shape
    width = w_gate.shape[1]
    out = jax.ShapeDtypeStruct((chips * 2 * rows, width), BF16)
    raw = raw_spec(z_all.shape)
    col = pl.BlockSpec((dim, tn), lambda j, i, core: (0, j))
    tile = pl.BlockSpec((2 * rows, tn), lambda j, i, core: (i, j))
    args = (z_all, g_all, w_gate, w_up) + (() if w_down is None else (w_down,))
    specs = [raw, tile if w_down is None else raw, col, col] + ([] if w_down is None else [pl.BlockSpec((tn, dim), lambda j, i, core: (j, 0))])
    return order.call(
        functools.partial(act_kernel, sub=sub), len(args), prefetch=1, out_shape=(out, out, out), grid=(width // tn, chips),
        in_specs=specs, out_specs=[tile] * 3, compiler_params=params(2),
        cost_estimate=cost(2 * (len(args) - 2) * z_all.size * width, *args, out, out, out), name="mlp_act",
    )(core, *args)


def back_kernel(dg_ref, du_ref, act_ref, wg_ref, wu_ref, wd_ref, *refs, joined):
    far, out = (refs[:len(refs) // 2], refs[len(refs) // 2:]) if len(refs) == 2 * (1 if joined else 2) else ((), refs)
    d_z = dot_f32(dg_ref[...], wg_ref[...], 1, 1) + dot_f32(du_ref[...], wu_ref[...], 1, 1)
    mlp = dot_f32(act_ref[...], wd_ref[...], 1, 0)
    for kind, total in enumerate((d_z, mlp)):
        at = (slice(None), kind) if joined else (slice(None),)
        dst = out[0 if joined else kind]
        total = total.reshape(dst[at].shape)
        if far:
            total += far[0 if joined else kind][at].astype(F32)
        dst[at] = total.astype(BF16)


def back_call(order, side, d_gate, d_upper, act, w_gate, w_up, w_down, far, joined, chips, tn=512):
    width, dim = w_down.shape
    rows = act.shape[0] // (2 * chips)
    half = chips // 2
    lhs = pl.BlockSpec((2 * rows, width), lambda j, i: (i + side * half, 0))
    row_w = pl.BlockSpec((tn, width), lambda j, i: (j, 0))
    if joined:
        outs = (jax.ShapeDtypeStruct((chips, 2, rows, dim), BF16),)
        tiles = [pl.BlockSpec((2, 2, rows, tn), lambda j, i: (i, 0, 0, j))]
    else:
        outs = (jax.ShapeDtypeStruct((chips, rows, dim), BF16),) * 2
        tiles = [pl.BlockSpec((2, rows, tn), lambda j, i: (i, 0, j))] * 2
    return order.call(
        functools.partial(back_kernel, joined=joined), 6 + len(far), out_shape=outs, grid=(dim // tn, half),
        in_specs=[lhs, lhs, lhs, row_w, row_w, pl.BlockSpec((width, tn), lambda j, i: (0, j))] + tiles[:len(far)],
        out_specs=tiles, compiler_params=params(2),
        cost_estimate=cost(3 * act.size * dim, act, act, w_gate, w_up, w_down, *outs, *outs), name="mlp_back",
    )(d_gate, d_upper, act, w_gate, w_up, w_down, *far)


def wgrad_kernel(core_s, *refs, n, tf, tn, cols):
    lhs, rhs, out, l_buf, r_buf, sems = refs[:n], refs[n:2 * n], *refs[2 * n:]
    i, j, k = pl.program_id(0), pl.program_id(1), pl.program_id(2)
    step = (i * cols + j) * n + k
    slot = lax.rem(step, 2)
    chips = l_buf.shape[1] // 2

    def copies(s, at, p):
        row = pl.multiple_of(lax.div(s, cols * n) * tf, tf)
        col = pl.multiple_of(lax.rem(lax.div(s, n), cols) * tn, tn)
        out = []
        for q, (ref, buf, lanes) in enumerate(((lhs[p], l_buf, pl.ds(row, tf)), (rhs[p], r_buf, pl.ds(col, tn)))):
            if ref.ndim == 4:
                for side in range(2):
                    src = ref.at[:, lax.bitwise_xor(core_s[0], side), :, lanes]
                    out.append(pltpu.make_async_copy(src, buf.at[at, pl.ds(side * chips, chips)], sems.at[q, side, at]))
            else:
                out.append(pltpu.make_async_copy(ref.at[:, :, lanes], buf.at[at], sems.at[q, 0, at]))
        return out

    def fetch(s, at):
        for p in range(n):
            @pl.when(lax.rem(s, n) == p)
            def _(p=p):
                for copy in copies(s, at, p):
                    copy.start()

    @pl.when(step == 0)
    def _():
        fetch(step, slot)

    @pl.when(step + 1 < pl.num_programs(0) * cols * n)
    def _():
        fetch(step + 1, 1 - slot)

    for copy in copies(step, slot, 0):
        copy.wait()
    part = dot_f32(rows_of(l_buf.at[slot]), rows_of(r_buf.at[slot]), 0, 0)
    out[...] = jnp.where(k == 0, part, out[...] + part)


def wgrad_call(order, core, lhs, rhs, tf=1024, tn=1024):
    n = len(lhs)
    rows = lhs[0].shape[-2]
    shards = lhs[0].size // (rows * lhs[0].shape[-1])
    width = rhs[0].shape[-1]
    height = lhs[0].shape[-1]
    cols = width // tn
    out = jax.ShapeDtypeStruct((height, width), F32)
    return order.call(
        functools.partial(wgrad_kernel, n=n, tf=tf, tn=tn, cols=cols), 2 * n, prefetch=1, out_shape=out, grid=(height // tf, cols, n),
        in_specs=[pl.BlockSpec(memory_space=pl.ANY)] * (2 * n), out_specs=pl.BlockSpec((tf, tn), lambda i, j, k, core: (i, j)),
        scratch_shapes=[pltpu.VMEM((2, shards, rows, tf), BF16), pltpu.VMEM((2, shards, rows, tn), BF16), pltpu.SemaphoreType.DMA((2, 2, 2))],
        compiler_params=params(3), cost_estimate=cost(2 * n * shards * rows * height * width, *lhs, *rhs, out), name="wgrad",
    )(core, *lhs, *rhs)


def small_wgrad_kernel(l_ref, r_ref, *refs):
    total = dot_f32(l_ref[...], r_ref[...], 0, 0)
    for extra in refs[:-1]:
        total += extra[...]
    refs[-1][...] = total


def small_wgrad(order, lhs, rhs, extra=(), tf=512, tn=1024):
    tokens, rows = lhs.shape
    width = rhs.shape[1]
    out = jax.ShapeDtypeStruct((rows, width), F32)
    tile = pl.BlockSpec((tf, tn), lambda j, i: (i, j))
    return order.call(
        small_wgrad_kernel, 2 + len(extra), out_shape=out, grid=(width // tn, rows // tf),
        in_specs=[pl.BlockSpec((tokens, tf), lambda j, i: (0, i)), pl.BlockSpec((tokens, tn), lambda j, i: (0, j))] + [tile] * len(extra),
        out_specs=tile, compiler_params=params(2), cost_estimate=cost(2 * tokens * rows * width, lhs, rhs, *extra, out), name="small_wgrad",
    )(lhs, rhs, *extra)


def resid_kernel(h_ref, a_own_ref, a_oth_ref, w_own_ref, w_oth_ref, gain_ref, resid_ref, *z_refs, sub):
    for c, z_ref in enumerate(z_refs):
        @pl.when(pl.program_id(0) == c)
        def _(z_ref=z_ref):
            for r in range(0, z_ref.shape[0], sub):
                at = slice(r, r + sub)
                total = dot_f32(a_own_ref[at], w_own_ref[...], 1, 0) + dot_f32(a_oth_ref[at], w_oth_ref[...], 1, 0)
                resid = (h_ref[at].astype(F32) + total).astype(BF16)
                resid_ref[at] = resid
                x_f = resid.astype(F32)
                inv = lax.rsqrt(jnp.mean(x_f * x_f, axis=-1, keepdims=True) + NORM_EPS)
                z_ref[at] = (x_f * inv * (1.0 + gain_ref[...])).astype(BF16)


def resid_call(order, hidden, mix_own, mix_oth, wo_own, wo_oth, gain, size, sub):
    tokens, dim = hidden.shape
    width = mix_own.shape[1]
    chunks = tokens // size
    row = pl.BlockSpec((size, dim), lambda i: (i, 0))
    mix = pl.BlockSpec((size, width), lambda i: (i, 0))
    whole_w = pl.BlockSpec((width, dim), lambda i: (0, 0))
    outs = (jax.ShapeDtypeStruct((tokens, dim), BF16),) + (jax.ShapeDtypeStruct((size, dim), BF16),) * chunks
    return order.call(
        functools.partial(resid_kernel, sub=sub), 6, out_shape=outs, grid=(chunks,),
        in_specs=[row, mix, mix, whole_w, whole_w, pl.BlockSpec((1, dim), lambda i: (0, 0))],
        out_specs=[row] + [pl.BlockSpec((size, dim), lambda i: (0, 0))] * chunks,
        compiler_params=params(1), cost_estimate=cost(4 * tokens * dim * width, hidden, mix_own, mix_oth, wo_own, wo_oth, *outs), name="resid",
    )(hidden, mix_own, mix_oth, wo_own, wo_oth, gain)


def norm_back(x_f, gain_1, d_out):
    inv = lax.rsqrt(jnp.mean(x_f * x_f, axis=-1, keepdims=True) + NORM_EPS)
    unit = x_f * inv
    scaled = d_out * gain_1
    d_x = inv * (scaled - unit * jnp.mean(scaled * unit, axis=-1, keepdims=True))
    return d_x, d_out * unit


def fold_rows(terms):
    rows, dim = terms.shape
    return jnp.sum(terms.reshape(rows // 8, 8, dim), axis=0)


def d_resid_kernel(*refs, n):
    dz_refs = refs[:n]
    x_ref, g_ref, gain_ref, w_own_ref, w_oth_ref, norm_ref, d_ref, own_ref, oth_ref = refs[n:]
    i = pl.program_id(0)

    @pl.when(i == 0)
    def _():
        norm_ref[...] = jnp.zeros_like(norm_ref)

    for c, dz_ref in enumerate(dz_refs):
        @pl.when(i == c)
        def _(dz_ref=dz_ref):
            d_x, terms = norm_back(x_ref[...].astype(F32), 1.0 + gain_ref[...], rows_of(dz_ref).astype(F32))
            norm_ref[...] += fold_rows(terms)
            d_ref[...] = (g_ref[...].astype(F32) + d_x).astype(BF16)
    own_ref[...] = dot_f32(d_ref[...], w_own_ref[...], 1, 1).astype(BF16)
    oth_ref[...] = dot_f32(d_ref[...], w_oth_ref[...], 1, 1).astype(BF16)


def d_resid_call(order, dz, resid, grad_out, gain, wo_own, wo_oth, first, size, earlier):
    tokens, dim = resid.shape
    n = len(dz)
    width = wo_own.shape[0]
    one = [pl.BlockSpec((1, size, dim) if a.ndim == 3 else (size, dim), lambda i, nd=a.ndim: (0,) * nd) for a in dz]
    far = pl.BlockSpec((size, dim), lambda i: (i + first, 0))
    mix = pl.BlockSpec((size, width), lambda i: (i + first, 0))
    whole_w = pl.BlockSpec((width, dim), lambda i: (0, 0))
    outs = (jax.ShapeDtypeStruct((8, dim), F32), jax.ShapeDtypeStruct((tokens, dim), BF16),
            jax.ShapeDtypeStruct((tokens, width), BF16), jax.ShapeDtypeStruct((tokens, width), BF16))
    return order.call(
        functools.partial(d_resid_kernel, n=n), n + 5, len(earlier), out_shape=outs, grid=(n,),
        in_specs=one + [far, far, pl.BlockSpec((1, dim), lambda i: (0, 0)), whole_w, whole_w],
        out_specs=[pl.BlockSpec((8, dim), lambda i: (0, 0)), far, mix, mix],
        compiler_params=params(1, 48), cost_estimate=cost(4 * n * size * dim * width, *dz, wo_own, wo_oth, outs[1]), name="d_resid",
    )(*dz, resid, grad_out, gain, wo_own, wo_oth, *earlier)


def d_hidden_kernel(q_own_ref, q_oth_ref, dkv_ref, x_ref, d_ref, gain_ref, wq_own_ref, wq_oth_ref, wkv_ref, out_ref, norm_ref, *, sub):
    @pl.when(pl.program_id(0) == 0)
    def _():
        norm_ref[...] = jnp.zeros_like(norm_ref)

    folded = 0.0
    for r in range(0, x_ref.shape[0], sub):
        at = slice(r, r + sub)
        d_normed = (dot_f32(q_own_ref[at], wq_own_ref[...], 1, 0) + dot_f32(q_oth_ref[at], wq_oth_ref[...], 1, 0)
                    + dot_f32(dkv_ref[at], wkv_ref[...], 1, 1)).astype(BF16).astype(F32)
        d_x, terms = norm_back(x_ref[at].astype(F32), 1.0 + gain_ref[...], d_normed)
        folded += fold_rows(terms)
        out_ref[at] = (d_ref[at].astype(F32) + d_x).astype(BF16)
    norm_ref[...] += folded


def d_hidden_call(order, dq_own, dq_oth, dkv, hidden, d_resid, gain, wq_own, wq_oth, w_kv, tm, sub):
    tokens, dim = hidden.shape
    width, two_hd = dq_own.shape[1], dkv.shape[1]
    row = pl.BlockSpec((tm, dim), lambda i: (i, 0))
    mix = pl.BlockSpec((tm, width), lambda i: (i, 0))
    whole_w = pl.BlockSpec((width, dim), lambda i: (0, 0))
    outs = (jax.ShapeDtypeStruct((tokens, dim), BF16), jax.ShapeDtypeStruct((8, dim), F32))
    return order.call(
        functools.partial(d_hidden_kernel, sub=sub), 9, out_shape=outs, grid=(tokens // tm,),
        in_specs=[mix, mix, pl.BlockSpec((tm, two_hd), lambda i: (i, 0)), row, row, pl.BlockSpec((1, dim), lambda i: (0, 0)), whole_w, whole_w,
                  pl.BlockSpec((dim, two_hd), lambda i: (0, 0))],
        out_specs=[row, pl.BlockSpec((8, dim), lambda i: (0, 0))],
        compiler_params=params(1), cost_estimate=cost(4 * tokens * dim * (width + two_hd), dq_own, dq_oth, hidden, d_resid, wq_own, wq_oth, *outs), name="d_hidden",
    )(dq_own, dq_oth, dkv, hidden, d_resid, gain, wq_own, wq_oth, w_kv)


def solution(mesh):
    tp_size = mesh.shape["tp"]
    chips = tp_size // 2
    act_spec = P("dp", "tp", None)
    in_specs = (act_spec, act_spec, P("dp"), P("dp"), P(None), P(None, "tp"), P(None, None), P(None, None), P("tp", None), P(None), P(None, "tp"), P(None, "tp"), P("tp", None))
    out_specs = (act_spec, act_spec, P("dp"), P("dp", "tp"), P("dp", None), P("dp", None), P(("dp", "tp"), None), P("dp"), P("dp", "tp"), P("dp", "tp"), P(("dp", "tp"), None))
    same_core = [[2 * c + k for c in range(chips)] for k in range(2)]
    partner = [(i, i ^ 1) for i in range(tp_size)]

    def scatter4(x_part):
        flat = x_part.reshape((-1,) + x_part.shape[2:])
        return lax.psum_scatter(flat, "tp", scatter_dimension=0, tiled=True, axis_index_groups=same_core)

    def gather8(x_loc):
        return lax.all_gather(x_loc, "tp", axis=0, tiled=False)

    def swap(x_loc):
        return lax.ppermute(x_loc, "tp", partner)

    def flip(x_loc, bits):
        return lax.ppermute(x_loc, "tp", [(i, i ^ bits) for i in range(tp_size)])

    def gather4_direct(x_loc):
        chip = lax.axis_index("tp") // 2
        half = x_loc.shape[0] // 2
        near, far = flip(x_loc, 2), flip(x_loc, 4)
        low, high = flip(near[:half], 4), flip(far[half:], 2)
        out = jnp.zeros((chips,) + x_loc.shape, x_loc.dtype)
        for k, block in ((0, x_loc), (1, near), (2, far)):
            out = lax.dynamic_update_slice(out, block[None], (chip ^ k, 0, 0))
        out = lax.dynamic_update_slice(out, low[None], (chip ^ 3, 0, 0))
        return lax.dynamic_update_slice(out, high[None], (chip ^ 3, half, 0))

    def local_layer(hidden, grad_out, prefix_len, valid_len, attn_norm, w_query, w_key, w_value, w_out, mlp_norm, w_gate, w_up, w_down):
        batch, rows, dim = hidden.shape
        hd = w_key.shape[1]
        tokens = batch * rows
        assert batch % CHUNKS == 0
        me = lax.axis_index("tp")
        core = lax.rem(me, 2)
        qpos = me * rows + jnp.arange(rows, dtype=jnp.int32)
        shard_pos = jnp.arange(rows, dtype=jnp.int32)[None, :] + (jnp.arange(chips, dtype=jnp.int32) * 2 * rows)[:, None]
        kpos = jnp.concatenate([(shard_pos + core * rows).reshape(-1), (shard_pos + (1 - core) * rows).reshape(-1)])
        cos_t, sin_t = rope_tables(qpos, hd)

        def rope_single(raw_proj):
            return apply_rope(raw_proj, cos_t, sin_t)

        order = Order()
        scalars = (prefix_len, valid_len, core[None])
        attn_gain = attn_norm.astype(F32)
        mlp_gain = mlp_norm.astype(F32)
        wq_own = gather4_direct(w_query.T).reshape(chips * hd, dim)
        normed_flat = rms_norm(hidden, attn_gain).reshape(tokens, dim)
        w_kv = jnp.concatenate([w_key, w_value], axis=1)
        kv_raw = dot_f32(normed_flat, w_kv, 1, 0).reshape(batch, rows, 2 * hd)
        keys, key_pull = jax.vjp(rope_single, kv_raw[..., :hd])
        kv_all = gather8(jnp.concatenate([keys, kv_raw[..., hd:]], axis=-1).astype(BF16))
        wo_own = gather4_direct(w_out).reshape(chips * hd, dim)
        wq_oth = swap(wq_own)
        wo_oth = swap(wo_own)
        q_own = dot_f32(normed_flat, wq_own, 1, 1).reshape(batch, rows, chips * hd)
        q_oth = dot_f32(normed_flat, wq_oth, 1, 1).reshape(batch, rows, chips * hd)
        mix_own, mix_oth, q_own, q_oth = attn_fwd(q_own, q_oth, kv_all, cos_t, sin_t, qpos, kpos, scalars)
        mix_own = mix_own.reshape(tokens, chips * hd)
        mix_oth = mix_oth.reshape(tokens, chips * hd)
        hidden_flat = hidden.reshape(tokens, dim)
        grad_flat = grad_out.reshape(tokens, dim)
        size = tokens // CHUNKS
        resid, *z_parts = resid_call(order, hidden_flat, mix_own, mix_oth, wo_own, wo_oth, mlp_gain[None, :], size, 2 * rows)

        g_all, z_all, acts, far = [], [], [], []
        for c in range(CHUNKS):
            g_all.append(gather8(grad_flat[c * size:(c + 1) * size]).reshape(chips, 2, size, dim))
            z_all.append(gather8(z_parts[c]).reshape(chips, 2, size, dim))
        mlp_sums, d_gated = [None] * CHUNKS, [None] * CHUNKS
        weights = (w_gate, w_up, w_down)
        core_1 = core[None]
        grads = None

        def attn_back(first, count, earlier):
            terms, d_res, d_own, d_oth = d_resid_call(
                order, d_gated[first:first + count], resid, grad_flat, mlp_gain[None, :], wo_own, wo_oth, first, size, () if earlier is None else earlier[1])
            per = batch // CHUNKS
            parts = attn_bwd(order, q_own, q_oth, d_own.reshape(batch, rows, -1), d_oth.reshape(batch, rows, -1), kv_all, cos_t, sin_t, qpos, kpos,
                             scalars, first * per, count * per, () if earlier is None else earlier[2])
            return (terms if earlier is None else earlier[0] + terms), (d_res, d_own, d_oth), parts

        def finish(c):
            joined = c < CHUNKS - 1
            parts = back_call(order, 0, acts[c][1], acts[c][2], acts[c][0], *weights, far[c], joined, chips)
            sums = [scatter4(parts[0])]
            if not joined:
                sums.append(scatter4(parts[1]))
            if joined:
                both = sums[0].reshape(2, size, dim)
                d_gated[c], mlp_sums[c] = both, both[1]
            else:
                d_gated[c], mlp_sums[c] = (a.reshape(size, dim) for a in sums)

        for c in range(CHUNKS):
            if c == 0:
                d_act = d_act_call(order, core_1, g_all[c], w_down)
                acts.append(act_call(order, core_1, z_all[c], d_act, w_gate, w_up, None))
            else:
                acts.append(act_call(order, core_1, z_all[c], g_all[c], *weights))
                finish(c - 1)
            joined = c < CHUNKS - 1
            parts = back_call(order, 1, acts[c][1], acts[c][2], acts[c][0], *weights, (), joined, chips)
            far.append(tuple(swap(a) for a in parts))
        grads = attn_back(0, 1, None)
        finish(CHUNKS - 1)
        hidden_out = (resid.astype(F32) + jnp.concatenate(mlp_sums, axis=0).astype(F32)).astype(BF16).reshape(batch, rows, dim)
        shards = [[a.reshape(2 * chips, size, -1) for a in acts[c]] for c in range(CHUNKS)]
        g_gate = wgrad_call(order, core_1, z_all, [a[1] for a in shards])

        norm_terms, (d_resid, _, _), (dq_own, dq_oth, dkv_own, dkv_oth) = attn_back(1, CHUNKS - 1, grads)
        dq_own = dq_own.reshape(tokens, chips * hd)
        dq_oth = dq_oth.reshape(tokens, chips * hd)
        dkv = scatter4((dkv_own.astype(F32) + swap(dkv_oth).astype(F32)).astype(BF16))
        g_out_far = swap(small_wgrad(order, mix_oth, d_resid))
        g_query_far = swap(small_wgrad(order, dq_oth, normed_flat))
        g_out_part = small_wgrad(order, mix_own, d_resid, (g_out_far,))
        g_query_part = small_wgrad(order, dq_own, normed_flat, (g_query_far,))
        g_out = scatter4(g_out_part.reshape(chips, hd, dim))
        g_query = scatter4(g_query_part.reshape(chips, hd, dim)).reshape(hd, dim).T
        d_k_raw = key_pull(dkv[..., :hd].astype(F32))[0]
        dkv = jnp.concatenate([d_k_raw.astype(BF16), dkv[..., hd:]], axis=-1).reshape(tokens, 2 * hd)
        grad_hidden, attn_terms = d_hidden_call(
            order, dq_own, dq_oth, dkv, hidden_flat, d_resid, attn_gain[None, :], wq_own, wq_oth, w_kv, 4 * rows, 2 * rows)
        g_kv = small_wgrad(order, normed_flat, dkv, tf=1024, tn=2 * hd)
        norms = jnp.stack([jnp.sum(attn_terms, axis=0), jnp.sum(norm_terms, axis=0)]).reshape(-1, 2 * hd)
        sums = lax.psum(jnp.concatenate([g_kv, norms], axis=0), "tp")
        g_attn_norm, g_mlp_norm = sums[dim:].reshape(2, dim)
        g_up = wgrad_call(order, core_1, z_all, [a[2] for a in shards])
        g_down = wgrad_call(order, core_1, [a[0] for a in shards], g_all)
        return (hidden_out, grad_hidden.reshape(batch, rows, dim), g_attn_norm, g_query, sums[:dim, :hd], sums[:dim, hd:], g_out.reshape(hd, dim), g_mlp_norm, g_gate, g_up, g_down)

    return jax.shard_map(local_layer, mesh=mesh, in_specs=in_specs, out_specs=out_specs, check_vma=False)
```

time: 1660 us -> 1440 us (0.87)
  waiting for transfers between devices: 334 us -> 213 us
  Pallas kernels: 1140 us -> 1070 us
  blocking collectives: 23.7 us -> 0 us
    reduce_scatter x9 -> x7, waiting for transfers between devices: 182 us -> 69.6 us  [scatter4(): lax.psum_scatter(flat, 'tp', scatter_dimension=0, tiled=True, axis_index_...]
    pallas_call x35 -> x24, Pallas kernels: 1120 us -> 1050 us  [run(): pl.pallas_call(body, grid_spec=pltpu.PrefetchScalarGridSpec(num_scalar_pr...]
    psum x1 -> x0, blocking collectives: 23.7 us -> none  [local_layer(): g_attn_norm = lax.psum(jnp.sum(attn_terms, axis=0), 'tp')]
  transfers between devices with their start and end apart: 45 -> 32, of which waited for: 9 -> 11; matrix products, arithmetic and copies ran while one was open for 5% -> 6% of each run, Pallas kernels for 69% -> 72%
where the time goes in v3:
time: 1440 us; the launch traced here: 1430 us
  Pallas kernels  1070 us (74%)
  waiting for transfers between devices  213 us (15%)
  local copies, waits for them, and re-layouts  69.4 us (5%)
  other arithmetic  30 us (2%)
  matrix products  22.2 us (2%)
  between operations  14.8 us (1%)
    pallas_call x24, Pallas kernels, run(): pl.pallas_call(body, grid_spec=pltpu.PrefetchScalarGridSpec(num_scalar_pr...  1050 us
    ppermute x8, waiting for transfers between devices, flip(): return lax.ppermute(x_loc, 'tp', [(i, i ^ bits) for i in range(tp_size)])  84.3 us
    reduce_scatter x7, waiting for transfers between devices, scatter4(): lax.psum_scatter(flat, 'tp', scatter_dimension=0, tiled=True, axis_index_...  69.6 us
    all_gather x7, waiting for transfers between devices, gather8(): return lax.all_gather(x_loc, 'tp', axis=0, tiled=False)  46.6 us
  transfers between devices with their start and end apart: 32, of which 11 were waited for; matrix products, arithmetic and copies ran while one was open for 6% of the time, Pallas kernels for 72%

profile of v3, /device:TPU:0, one launch (start us, length us, event | category | flops | bytes accessed | tf_op | source)
XLA Modules:
  0.0 1429.9 jit_solution(12938644485438849809)
XLA Ops:
  34.9 32.3 %collective-permute-done = bf16[256,2048]{0,1:T(8,128)(2,1)S(1)} collective-permute-done((bf16[256,2048]{0,1:T(8,128)(2,1)}, bf16[256,2048]{0,1:T(8,128)(2,1)S(1)}, u32[]{:S(2)}, u32[]{:S(2)}) %collective-permute-start) | collective-permute-done | bytes 1048608 | tf_op jit(solution)/shard_map/ppermute | solution.py:522
  79.2 33.1 %collective-permute-done.6 = bf16[256,2048]{1,0:T(8,128)(2,1)S(1)} collective-permute-done((bf16[256,2048]{1,0:T(8,128)(2,1)}, bf16[256,2048]{1,0:T(8,128)(2,1)S(1)}, u32[]{:S(2)}, u32[]{:S(2)}) %collective-permute-start.6) | collective-permute-done | bytes 1048608 | tf_op jit(solution)/shard_map/ppermute | solution.py:522
  131.5 14.2 collective-permute-done.7
  151.0 9.8 fusion.15.q_own_ref
  172.9 20.7 %attn_fwd.1 = (bf16[12,96,1024]{2,1,0:T(8,128)(2,1)S(1)}, bf16[12,96,1024]{2,1,0:T(8,128)(2,1)S(1)}, bf16[12,96,1024]{2,1,0:T(8,128)(2,1)S(1)}, bf16[12,96,1024]{2,1,0:T(8,128)(2,1)S(1)}) custom-call(s32[12]{0:T(128)S(1)} %copy-done.18, s32[12]{0:T(128)S(1)} %copy-done.20, s32[1]{0:T(128)} %bitcast.1.core_s.refs_0_.refs_2_, f32[12,96,1024]{2,1,0:T(8,128)S(1)} %copy-done.29, ...), custom_call_target="tpu_custom_call" | custom-call | flops 7247757312 | bytes 28311552 | tf_op jit(solution)/shard_map/attn_fwd/pallas_call | solution.py:149
  199.3 19.3 %resid.1 = (bf16[1152,2048]{1,0:T(8,128)(2,1)}, bf16[384,2048]{1,0:T(8,128)(2,1)}, bf16[384,2048]{1,0:T(8,128)(2,1)}, bf16[384,2048]{1,0:T(8,128)(2,1)}) custom-call(bf16[1152,2048]{1,0:T(8,128)(2,1)} %bitcast.111, bf16[1152,1024]{1,0:T(8,128)(2,1)} %bitcast.96, bf16[1152,1024]{1,0:T(8,128)(2,1)} %bitcast.103, ...), custom_call_target="tpu_custom_call" | custom-call | flops 9663676416 | bytes 27262976 | tf_op jit(solution)/shard_map/resid/pallas_call | solution.py:199
  221.3 33.6 %d_act.1.refs_2_ = bf16[3072,2048]{1,0:T(8,128)(2,1)} custom-call(s32[1]{0:T(128)} %bitcast.1.core_s.refs_0_.refs_2_, bf16[4,2,384,2048]{3,2,1,0:T(8,128)(2,1)} %bitcast.133, bf16[2048,2048]{1,0:T(8,128)(2,1)} %refs_5_.15, bf16[1152,2048]{1,0:T(8,128)(2,1)} %get-tuple-element.52.refs_3_.refs_1_.refs_2_), custom_call_target="tpu_custom_call" | custom-call | flops 25769803776 | bytes 33554432 | tf_op jit(solution)/shard_map/d_act/pallas_call | solution.py:199
  254.9 30.4 %all-gather.19.cloned.1.call-done = bf16[3072,2048]{1,0:T(8,128)(2,1)} async-done(((bf16[384,2048]{1,0:T(8,128)(2,1)}), bf16[3072,2048]{1,0:T(8,128)(2,1)}) %all-gather.19.cloned.1.call-update) | async-done | bytes 12582928 | tf_op jit(solution)/shard_map/all_gather | solution.py:516
  285.3 70.6 %mlp_act.3 = (bf16[3072,2048]{1,0:T(8,128)(2,1)}, bf16[3072,2048]{1,0:T(8,128)(2,1)}, bf16[3072,2048]{1,0:T(8,128)(2,1)}) custom-call(s32[1]{0:T(128)} %bitcast.1.core_s.refs_0_.refs_2_, bf16[4,2,384,2048]{3,2,1,0:T(8,128)(2,1)} %bitcast.135, bf16[3072,2048]{1,0:T(8,128)(2,1)} %d_act.1.refs_2_, bf16[2048,2048]{1,0:T(8,128)(2,1)} %refs_3_.17, ...), custom_call_target="tpu_custom_call" | custom-call | flops 51539607552 | bytes 79691776 | tf_op jit(solution)/shard_map/mlp_act/pallas_call | solution.py:199
  355.9 51.4 %mlp_back.6.refs_6_ = bf16[4,2,384,2048]{3,2,1,0:T(8,128)(2,1)} custom-call(bf16[3072,2048]{1,0:T(8,128)(2,1)} %get-tuple-element.54.refs_0_, bf16[3072,2048]{1,0:T(8,128)(2,1)} %get-tuple-element.55.refs_1_, bf16[3072,2048]{1,0:T(8,128)(2,1)} %get-tuple-element.56.refs_2_, bf16[2048,2048]{1,0:T(8,128)(2,1)} %refs_3_.17, bf16[2048,2048]{1,0:T(8,128)(2,1)} %refs_4_.17, ...), custom_call_target="tpu_custom_call" | custom-call | flops 38654705664 | bytes 75497472 | tf_op jit(solution)/shard_map/mlp_back/pallas_call | solution.py:199
  407.4 16.2 %all-gather.21.cloned.1.call-done = bf16[3072,2048]{1,0:T(8,128)(2,1)} async-done(((bf16[384,2048]{1,0:T(8,128)(2,1)}), bf16[3072,2048]{1,0:T(8,128)(2,1)}) %all-gather.21.cloned.1.call-update) | async-done | bytes 12582928 | tf_op jit(solution)/shard_map/all_gather | solution.py:516
  423.6 91.7 %mlp_act.4 = (bf16[3072,2048]{1,0:T(8,128)(2,1)}, bf16[3072,2048]{1,0:T(8,128)(2,1)}, bf16[3072,2048]{1,0:T(8,128)(2,1)}) custom-call(s32[1]{0:T(128)} %bitcast.1.core_s.refs_0_.refs_2_, bf16[4,2,384,2048]{3,2,1,0:T(8,128)(2,1)} %bitcast.140, bf16[4,2,384,2048]{3,2,1,0:T(8,128)(2,1)} %bitcast.138, bf16[2048,2048]{1,0:T(8,128)(2,1)} %refs_3_.17, ...), custom_call_target="tpu_custom_call" | custom-call | flops 77309411328 | bytes 88080384 | tf_op jit(solution)/shard_map/mlp_act/pallas_call | solution.py:199
  515.3 54.2 %mlp_back.7.refs_6_ = bf16[4,2,384,2048]{3,2,1,0:T(8,128)(2,1)} custom-call(bf16[3072,2048]{1,0:T(8,128)(2,1)} %get-tuple-element.54.refs_0_, bf16[3072,2048]{1,0:T(8,128)(2,1)} %get-tuple-element.55.refs_1_, bf16[3072,2048]{1,0:T(8,128)(2,1)} %get-tuple-element.56.refs_2_, bf16[2048,2048]{1,0:T(8,128)(2,1)} %refs_3_.17, bf16[2048,2048]{1,0:T(8,128)(2,1)} %refs_4_.17, ...), custom_call_target="tpu_custom_call" | custom-call | flops 38654705664 | bytes 75497472 | tf_op jit(solution)/shard_map/mlp_back/pallas_call | solution.py:199
  569.6 54.8 %mlp_back.8.refs_6_ = bf16[4,2,384,2048]{3,2,1,0:T(8,128)(2,1)} custom-call(bf16[3072,2048]{1,0:T(8,128)(2,1)} %get-tuple-element.59.refs_0_, bf16[3072,2048]{1,0:T(8,128)(2,1)} %get-tuple-element.60.refs_1_, bf16[3072,2048]{1,0:T(8,128)(2,1)} %get-tuple-element.58.refs_7_.refs_2_, bf16[2048,2048]{1,0:T(8,128)(2,1)} %refs_3_.17, ...), custom_call_target="tpu_custom_call" | custom-call | flops 38654705664 | bytes 75497472 | tf_op jit(solution)/shard_map/mlp_back/pallas_call | solution.py:199
  624.5 92.7 %mlp_act.5 = (bf16[3072,2048]{1,0:T(8,128)(2,1)}, bf16[3072,2048]{1,0:T(8,128)(2,1)}, bf16[3072,2048]{1,0:T(8,128)(2,1)}) custom-call(s32[1]{0:T(128)} %bitcast.1.core_s.refs_0_.refs_2_, bf16[4,2,384,2048]{3,2,1,0:T(8,128)(2,1)} %bitcast.145, bf16[4,2,384,2048]{3,2,1,0:T(8,128)(2,1)} %bitcast.143, bf16[2048,2048]{1,0:T(8,128)(2,1)} %refs_3_.17, ...), custom_call_target="tpu_custom_call" | custom-call | flops 77309411328 | bytes 88080384 | tf_op jit(solution)/shard_map/mlp_act/pallas_call | solution.py:199
  717.2 54.0 %mlp_back.9.refs_6_ = bf16[4,2,384,2048]{3,2,1,0:T(8,128)(2,1)} custom-call(bf16[3072,2048]{1,0:T(8,128)(2,1)} %get-tuple-element.59.refs_0_, bf16[3072,2048]{1,0:T(8,128)(2,1)} %get-tuple-element.60.refs_1_, bf16[3072,2048]{1,0:T(8,128)(2,1)} %get-tuple-element.58.refs_7_.refs_2_, bf16[2048,2048]{1,0:T(8,128)(2,1)} %refs_3_.17, ...), custom_call_target="tpu_custom_call" | custom-call | flops 38654705664 | bytes 75497472 | tf_op jit(solution)/shard_map/mlp_back/pallas_call | solution.py:199
  771.2 54.5 %mlp_back.10 = (bf16[4,384,2048]{2,1,0:T(8,128)(2,1)}, bf16[4,384,2048]{2,1,0:T(8,128)(2,1)}) custom-call(bf16[3072,2048]{1,0:T(8,128)(2,1)} %get-tuple-element.63.refs_0_, bf16[3072,2048]{1,0:T(8,128)(2,1)} %get-tuple-element.64.refs_1_, bf16[3072,2048]{1,0:T(8,128)(2,1)} %get-tuple-element.62.refs_7_.refs_2_, bf16[2048,2048]{1,0:T(8,128)(2,1)} %refs_3_.17, ...), custom_call_target="tpu_custom_call" | custom-call | flops 38654705664 | bytes 75497472 | tf_op jit(solution)/shard_map/mlp_back/pallas_call | solution.py:199
  826.6 10.2 d_resid.2
  838.4 14.5 %attn_bwd.2 = (bf16[12,96,1024]{2,1,0:T(8,128)(2,1)S(1)}, bf16[12,96,1024]{2,1,0:T(8,128)(2,1)S(1)}, bf16[4,12,96,512]{3,2,1,0:T(8,128)(2,1)}, bf16[4,12,96,512]{3,2,1,0:T(8,128)(2,1)}) custom-call(s32[12]{0:T(128)S(1)} %copy-done.19, s32[12]{0:T(128)S(1)} %copy-done.21, s32[1]{0:T(128)} %bitcast.1.core_s.refs_0_.refs_2_, ...), custom_call_target="tpu_custom_call" | custom-call | flops 6039797760 | bytes 23592960 | tf_op jit(solution)/shard_map/attn_bwd/pallas_call | solution.py:199
  854.3 54.6 %mlp_back.11 = (bf16[4,384,2048]{2,1,0:T(8,128)(2,1)}, bf16[4,384,2048]{2,1,0:T(8,128)(2,1)}) custom-call(bf16[3072,2048]{1,0:T(8,128)(2,1)} %get-tuple-element.63.refs_0_, bf16[3072,2048]{1,0:T(8,128)(2,1)} %get-tuple-element.64.refs_1_, bf16[3072,2048]{1,0:T(8,128)(2,1)} %get-tuple-element.62.refs_7_.refs_2_, bf16[2048,2048]{1,0:T(8,128)(2,1)} %refs_3_.17, ...), custom_call_target="tpu_custom_call" | custom-call | flops 38654705664 | bytes 75497472 | tf_op jit(solution)/shard_map/mlp_back/pallas_call | solution.py:199
  909.0 88.4 %wgrad.3.refs_10_ = f32[2048,2048]{1,0:T(8,128)} custom-call(s32[1]{0:T(128)} %bitcast.1.core_s.refs_0_.refs_2_, bf16[4,2,384,2048]{3,2,1,0:T(8,128)(2,1)} %bitcast.136, bf16[4,2,384,2048]{3,2,1,0:T(8,128)(2,1)} %bitcast.141, bf16[4,2,384,2048]{3,2,1,0:T(8,128)(2,1)} %bitcast.146, bf16[8,384,2048]{2,1,0:T(8,128)(2,1)} %bitcast.154, ...), custom_call_target="tpu_custom_call" | custom-call | flops 77309411328 | bytes 92274688 | tf_op jit(solution)/shard_map/wgrad/pallas_call | solution.py:199
  1000.5 18.0 %d_resid.3 = (f32[8,2048]{1,0:T(8,128)S(1)}, bf16[1152,2048]{1,0:T(8,128)(2,1)}, bf16[1152,1024]{1,0:T(8,128)(2,1)S(1)}, bf16[1152,1024]{1,0:T(8,128)(2,1)}) custom-call(bf16[2,384,2048]{2,1,0:T(8,128)(2,1)} %reduce-scatter.10.cloned.1.call-done.refs_0_, ...), custom_call_target="tpu_custom_call", output_to_operand_aliasing={{1}: (7, {}), {2}: (8, {}), {3}: (9, {})} | custom-call | flops 6442450944 | bytes 17825792 | tf_op jit(solution)/shard_map/d_resid/pallas_call | solution.py:199
  1021.6 25.8 %attn_bwd.3 = (bf16[12,96,1024]{2,1,0:T(8,128)(2,1)S(1)}, bf16[12,96,1024]{2,1,0:T(8,128)(2,1)S(1)}, bf16[4,12,96,512]{3,2,1,0:T(8,128)(2,1)}, bf16[4,12,96,512]{3,2,1,0:T(8,128)(2,1)}) custom-call(s32[12]{0:T(128)S(1)} %copy-done.19, s32[12]{0:T(128)S(1)} %copy-done.21, ...), custom_call_target="tpu_custom_call", output_to_operand_aliasing={{0}: (12, {}), {1}: (13, {}), {2}: (14, {}), {3}: (15, {})} | custom-call | flops 12079595520 | bytes 28311552 | tf_op jit(solution)/shard_map/attn_bwd/pallas_call | solution.py:199
  1062.8 11.7 small_wgrad.5.refs_2_
  1074.7 11.8 small_wgrad.6.refs_3_
  1088.0 13.1 small_wgrad.7.refs_3_
  1101.1 13.0 small_wgrad.8.refs_9_
  1116.9 25.9 %d_hidden.1 = (bf16[1152,2048]{1,0:T(8,128)(2,1)}, f32[8,2048]{1,0:T(8,128)}) custom-call(bf16[1152,1024]{1,0:T(8,128)(2,1)} %bitcast.99, bf16[1152,1024]{1,0:T(8,128)(2,1)} %bitcast.91, bf16[1152,512]{1,0:T(8,128)(2,1)} %bitcast.122, bf16[1152,2048]{1,0:T(8,128)(2,1)} %bitcast.112, bf16[1152,2048]{1,0:T(8,128)(2,1)} %get-tuple-element.86.refs_1_.refs_4_, ...), custom_call_target="tpu_custom_call" | custom-call | flops 14495514624 | bytes 27328512 | tf_op jit(solution)/shard_map/d_hidden/pallas_call | solution.py:199
  1161.1 20.4 %reduce-scatter.12.cloned.1.call-done = bf16[384,2048]{1,0:T(8,128)(2,1)} async-done(((bf16[1536,2048]{1,0:T(8,128)(2,1)}), bf16[384,2048]{1,0:T(8,128)(2,1)}) %reduce-scatter.12.cloned.1.call-update) | async-done | bytes 1572880 | tf_op jit(solution)/shard_map/reduce_scatter | solution.py:513
  1188.2 87.9 %wgrad.4.refs_7_ = f32[2048,2048]{1,0:T(8,128)} custom-call(s32[1]{0:T(128)} %bitcast.1.core_s.refs_0_.refs_2_, bf16[4,2,384,2048]{3,2,1,0:T(8,128)(2,1)} %bitcast.137, bf16[4,2,384,2048]{3,2,1,0:T(8,128)(2,1)} %bitcast.142, bf16[4,2,384,2048]{3,2,1,0:T(8,128)(2,1)} %bitcast.147, bf16[8,384,2048]{2,1,0:T(8,128)(2,1)} %bitcast.149, ...), custom_call_target="tpu_custom_call" | custom-call | flops 77309411328 | bytes 92274688 | tf_op jit(solution)/shard_map/wgrad/pallas_call | solution.py:199
  1276.1 88.4 %wgrad.5 = f32[2048,2048]{1,0:T(8,128)} custom-call(s32[1]{0:T(128)} %bitcast.1.core_s.refs_0_.refs_2_, bf16[8,384,2048]{2,1,0:T(8,128)(2,1)} %bitcast.148, bf16[8,384,2048]{2,1,0:T(8,128)(2,1)} %bitcast.150, bf16[8,384,2048]{2,1,0:T(8,128)(2,1)} %bitcast.152, bf16[4,2,384,2048]{3,2,1,0:T(8,128)(2,1)} %bitcast.134, bf16[4,2,384,2048]{3,2,1,0:T(8,128)(2,1)} %bitcast.139, ...), custom_call_target="tpu_custom_call" | custom-call | flops 77309411328 | bytes 92274688 | tf_op jit(solution)/shard_map/wgrad/pallas_call | solution.py:199
  1374.1 49.1 %reduce-scatter.20.cloned.1.call-done = f32[256,2048]{1,0:T(8,128)} async-done(((f32[1024,2048]{1,0:T(8,128)}), f32[256,2048]{1,0:T(8,128)}) %reduce-scatter.20.cloned.1.call-update) | async-done | bytes 2097168 | tf_op jit(solution)/shard_map/reduce_scatter | solution.py:513
  (230 shorter events, 148.5 us)
Async XLA Ops:
  7.2 163.3 %all-gather.11.cloned.1.call-start = ((), (), s32[]{:S(2)}) async-start(), calls=%async_computation.7 | async-start | bytes 10616832 | tf_op jit(solution)/shard_map/all_gather | solution.py:516
  17.8 203.5 %all-gather.13.cloned.1.call-start = ((), (), s32[]{:S(2)}) async-start(), calls=%async_computation.8 | async-start | bytes 14155776 | tf_op jit(solution)/shard_map/all_gather | solution.py:516
  22.6 262.7 %all-gather.19.cloned.1.call-start = ((), (), s32[]{:S(2)}) async-start(), calls=%async_computation.19 | async-start | bytes 14155776 | tf_op jit(solution)/shard_map/all_gather | solution.py:516
  23.1 44.1 %collective-permute-start = (bf16[256,2048]{0,1:T(8,128)(2,1)}, bf16[256,2048]{0,1:T(8,128)(2,1)S(1)}, u32[]{:S(2)}, u32[]{:S(2)}) collective-permute-start(bf16[256,2048]{0,1:T(8,128)(2,1)} %bitcast.2), channel_id=1, source_target_pairs={{0,2},{1,3},{2,0},{3,1},{4,6},{5,7},{6,4},{7,5}} | collective-permute-start | bytes 3145736 | tf_op jit(solution)/shard_map/ppermute | solution.py:522
  26.4 43.9 %collective-permute-start.1 = (bf16[256,2048]{0,1:T(8,128)(2,1)}, bf16[256,2048]{0,1:T(8,128)(2,1)}, u32[]{:S(2)}, u32[]{:S(2)}) collective-permute-start(bf16[256,2048]{0,1:T(8,128)(2,1)} %bitcast.2), channel_id=1, source_target_pairs={{0,4},{1,5},{2,6},{3,7},{4,0},{5,1},{6,2},{7,3}} | collective-permute-start | bytes 3145736 | tf_op jit(solution)/shard_map/ppermute | solution.py:522
  27.9 84.4 %collective-permute-start.6 = (bf16[256,2048]{1,0:T(8,128)(2,1)}, bf16[256,2048]{1,0:T(8,128)(2,1)S(1)}, u32[]{:S(2)}, u32[]{:S(2)}) collective-permute-start(bf16[256,2048]{1,0:T(8,128)(2,1)} %param.21), channel_id=1, source_target_pairs={{0,4},{1,5},{2,6},{3,7},{4,0},{5,1},{6,2},{7,3}} | collective-permute-start | bytes 3145736 | tf_op jit(solution)/shard_map/ppermute | solution.py:522
  28.4 85.5 %collective-permute-start.5 = (bf16[256,2048]{1,0:T(8,128)(2,1)}, bf16[256,2048]{1,0:T(8,128)(2,1)}, u32[]{:S(2)}, u32[]{:S(2)}) collective-permute-start(bf16[256,2048]{1,0:T(8,128)(2,1)} %param.21), channel_id=1, source_target_pairs={{0,2},{1,3},{2,0},{3,1},{4,6},{5,7},{6,4},{7,5}} | collective-permute-start | bytes 3145736 | tf_op jit(solution)/shard_map/ppermute | solution.py:522
  68.0 55.9 %collective-permute-start.2 = (bf16[128,2048]{0,1:T(8,128)(2,1)}, bf16[128,2048]{0,1:T(8,128)(2,1)}, u32[]{:S(2)}, u32[]{:S(2)}) collective-permute-start(bf16[128,2048]{0,1:T(8,128)(2,1)} %slice.76), channel_id=1, source_target_pairs={{0,4},{1,5},{2,6},{3,7},{4,0},{5,1},{6,2},{7,3}} | collective-permute-start | bytes 1572872 | tf_op jit(solution)/shard_map/ppermute | solution.py:522
  72.2 53.0 %collective-permute-start.3 = (bf16[128,2048]{0,1:T(8,128)(2,1)}, bf16[128,2048]{0,1:T(8,128)(2,1)}, u32[]{:S(2)}, u32[]{:S(2)}) collective-permute-start(bf16[128,2048]{0,1:T(8,128)(2,1)} %slice.77), channel_id=1, source_target_pairs={{0,2},{1,3},{2,0},{3,1},{4,6},{5,7},{6,4},{7,5}} | collective-permute-start | bytes 1572872 | tf_op jit(solution)/shard_map/ppermute | solution.py:522
  113.2 34.4 %collective-permute-start.8 = (bf16[128,2048]{1,0:T(8,128)(2,1)}, bf16[128,2048]{1,0:T(8,128)(2,1)}, u32[]{:S(2)}, u32[]{:S(2)}) collective-permute-start(bf16[128,2048]{1,0:T(8,128)(2,1)} %slice.82), channel_id=1, source_target_pairs={{0,2},{1,3},{2,0},{3,1},{4,6},{5,7},{6,4},{7,5}} | collective-permute-start | bytes 1572872 | tf_op jit(solution)/shard_map/ppermute | solution.py:522
  115.8 29.9 %collective-permute-start.7 = (bf16[128,2048]{1,0:T(8,128)(2,1)}, bf16[128,2048]{1,0:T(8,128)(2,1)}, u32[]{:S(2)}, u32[]{:S(2)}) collective-permute-start(bf16[128,2048]{1,0:T(8,128)(2,1)} %slice.81), channel_id=1, source_target_pairs={{0,4},{1,5},{2,6},{3,7},{4,0},{5,1},{6,2},{7,3}} | collective-permute-start | bytes 1572872 | tf_op jit(solution)/shard_map/ppermute | solution.py:522
  128.1 32.6 %collective-permute-start.4 = (bf16[1024,2048]{1,0:T(8,128)(2,1)}, bf16[1024,2048]{1,0:T(8,128)(2,1)}, u32[]{:S(2)}, u32[]{:S(2)}) collective-permute-start(bf16[1024,2048]{1,0:T(8,128)(2,1)} %bitcast.8.refs_6_), channel_id=1, source_target_pairs={{0,1},{1,0},{2,3},{3,2},{4,5},{5,4},{6,7},{7,6}} | collective-permute-start | bytes 12582920 | tf_op jit(solution)/shard_map/ppermute | solution.py:519
  149.5 49.9 %collective-permute-start.9 = (bf16[1024,2048]{1,0:T(8,128)(2,1)}, bf16[1024,2048]{1,0:T(8,128)(2,1)}, u32[]{:S(2)}, u32[]{:S(2)}) collective-permute-start(bf16[1024,2048]{1,0:T(8,128)(2,1)} %bitcast.22.refs_3_.refs_4_.refs_5_), channel_id=1, source_target_pairs={{0,1},{1,0},{2,3},{3,2},{4,5},{5,4},{6,7},{7,6}} | collective-permute-start | bytes 12582920 | tf_op jit(solution)/shard_map/ppermute | solution.py:519
  218.7 188.7 %all-gather.15.cloned.1.call-start = ((), (), s32[]{:S(2)}) async-start(), calls=%async_computation.9 | async-start | bytes 14155776 | tf_op jit(solution)/shard_map/all_gather | solution.py:516
  219.3 204.3 %all-gather.21.cloned.1.call-start = ((), (), s32[]{:S(2)}) async-start(), calls=%async_computation.20 | async-start | bytes 14155776 | tf_op jit(solution)/shard_map/all_gather | solution.py:516
  219.9 404.6 %all-gather.17.cloned.1.call-start = ((), (), s32[]{:S(2)}) async-start(), calls=%async_computation.11 | async-start | bytes 14155776 | tf_op jit(solution)/shard_map/all_gather | solution.py:516
  220.4 404.0 %all-gather.23.cloned.1.call-start = ((), (), s32[]{:S(2)}) async-start(), calls=%async_computation.21 | async-start | bytes 14155776 | tf_op jit(solution)/shard_map/all_gather | solution.py:516
  221.2 605.4 %reduce-scatter.8.cloned.1.call-start = ((), (), s32[]{:S(2)}) async-start(), calls=%async_computation.10 | async-start | bytes 15728640 | tf_op jit(solution)/shard_map/reduce_scatter | solution.py:513
  407.4 107.9 %collective-permute-start.10 = (bf16[4,2,384,2048]{3,2,1,0:T(8,128)(2,1)}, bf16[4,2,384,2048]{3,2,1,0:T(8,128)(2,1)}, u32[]{:S(2)}, u32[]{:S(2)}) collective-permute-start(bf16[4,2,384,2048]{3,2,1,0:T(8,128)(2,1)} %mlp_back.6.refs_6_), channel_id=1, source_target_pairs={{0,1},{1,0},{2,3},{3,2},{4,5},{5,4},{6,7},{7,6}} | collective-permute-start | bytes 37748744 | tf_op jit(solution)/shard_map/ppermute | solution.py:519
  569.5 427.9 %reduce-scatter.10.cloned.1.call-start = ((), (), s32[]{:S(2)}) async-start(), calls=%async_computation.12 | async-start | bytes 15728640 | tf_op jit(solution)/shard_map/reduce_scatter | solution.py:513
  624.4 92.8 %collective-permute-start.11 = (bf16[4,2,384,2048]{3,2,1,0:T(8,128)(2,1)}, bf16[4,2,384,2048]{3,2,1,0:T(8,128)(2,1)}, u32[]{:S(2)}, u32[]{:S(2)}) collective-permute-start(bf16[4,2,384,2048]{3,2,1,0:T(8,128)(2,1)} %mlp_back.8.refs_6_), channel_id=1, source_target_pairs={{0,1},{1,0},{2,3},{3,2},{4,5},{5,4},{6,7},{7,6}} | collective-permute-start | bytes 37748744 | tf_op jit(solution)/shard_map/ppermute | solution.py:519
  771.2 226.3 %reduce-scatter.14.cloned.1.call-start = ((), (), s32[]{:S(2)}) async-start(), calls=%async_computation.14 | async-start | bytes 7864320 | tf_op jit(solution)/shard_map/reduce_scatter | solution.py:513
  825.8 28.5 %collective-permute-start.13 = (bf16[4,384,2048]{2,1,0:T(8,128)(2,1)}, bf16[4,384,2048]{2,1,0:T(8,128)(2,1)}, u32[]{:S(2)}, u32[]{:S(2)}) collective-permute-start(bf16[4,384,2048]{2,1,0:T(8,128)(2,1)} %get-tuple-element.66), channel_id=1, source_target_pairs={{0,1},{1,0},{2,3},{3,2},{4,5},{5,4},{6,7},{7,6}} | collective-permute-start | bytes 18874376 | tf_op jit(solution)/shard_map/ppermute | solution.py:519
  825.9 28.4 %collective-permute-start.12 = (bf16[4,384,2048]{2,1,0:T(8,128)(2,1)}, bf16[4,384,2048]{2,1,0:T(8,128)(2,1)}, u32[]{:S(2)}, u32[]{:S(2)}) collective-permute-start(bf16[4,384,2048]{2,1,0:T(8,128)(2,1)} %get-tuple-element.65.refs_6_), channel_id=1, source_target_pairs={{0,1},{1,0},{2,3},{3,2},{4,5},{5,4},{6,7},{7,6}} | collective-permute-start | bytes 18874376 | tf_op jit(solution)/shard_map/ppermute | solution.py:519
  908.9 205.3 %reduce-scatter.16.cloned.1.call-start = ((), (), s32[]{:S(2)}) async-start(), calls=%async_computation.15 | async-start | bytes 5898240 | tf_op jit(solution)/shard_map/reduce_scatter | solution.py:513
  1047.5 8.1 collective-permute-start.14
  1062.2 119.3 %reduce-scatter.12.cloned.1.call-start = ((), (), s32[]{:S(2)}) async-start(), calls=%async_computation.13 | async-start | bytes 7864320 | tf_op jit(solution)/shard_map/reduce_scatter | solution.py:513
  1062.8 301.8 %all-reduce.4.cloned.1.call-start = ((), (), s32[]{:S(2)}) async-start(), calls=%async_computation.16 | async-start | bytes 8421376 | tf_op jit(solution)/shard_map/psum | solution.py:634
  1074.5 13.5 collective-permute-start.16
  1086.5 14.6 %collective-permute-start.15 = (f32[1024,2048]{1,0:T(8,128)}, f32[1024,2048]{1,0:T(8,128)}, u32[]{:S(2)}, u32[]{:S(2)}) collective-permute-start(f32[1024,2048]{1,0:T(8,128)} %small_wgrad.6.refs_3_), channel_id=1, source_target_pairs={{0,1},{1,0},{2,3},{3,2},{4,5},{5,4},{6,7},{7,6}} | collective-permute-start | bytes 25165832 | tf_op jit(solution)/shard_map/ppermute | solution.py:519
  1154.9 216.3 %reduce-scatter.18.cloned.1.call-start = ((), (), s32[]{:S(2)}) async-start(), calls=%async_computation.17 | async-start | bytes 10485760 | tf_op jit(solution)/shard_map/reduce_scatter | solution.py:513
  1155.5 267.7 %reduce-scatter.20.cloned.1.call-start = ((), (), s32[]{:S(2)}) async-start(), calls=%async_computation.18 | async-start | bytes 10485760 | tf_op jit(solution)/shard_map/reduce_scatter | solution.py:513
  (44 other events, 773.2 us)
Sparse Core Ops, SparseCore 0:
  17.9 94.0 all-gather.10
  114.4 77.3 all-gather.12
  218.8 66.4 all-gather.18
  287.5 66.4 all-gather.14
  356.2 67.3 all-gather.20
  425.3 66.4 all-gather.16
  494.1 66.4 all-gather.22
  569.6 115.0 reduce-scatter.7
  771.3 115.5 reduce-scatter.9
  909.0 64.8 reduce-scatter.13
  1062.3 51.8 reduce-scatter.15
  1117.0 64.4 reduce-scatter.11
  1184.8 70.4 all-reduce.3
  1258.2 80.7 reduce-scatter.17
  1342.4 80.7 reduce-scatter.19

commit v4 on v3

--- a/solution.py
+++ b/solution.py
@@ -278,10 +278,29 @@
     )(core, *args)
 
 
-def back_kernel(dg_ref, du_ref, act_ref, wg_ref, wu_ref, wd_ref, *refs, joined):
+def back_kernel(dg_hbm, du_hbm, act_hbm, wg_ref, wu_ref, wd_ref, *refs, joined, base):
+    *refs, dg_buf, du_buf, act_buf, sems = refs
     far, out = (refs[:len(refs) // 2], refs[len(refs) // 2:]) if len(refs) == 2 * (1 if joined else 2) else ((), refs)
-    d_z = dot_f32(dg_ref[...], wg_ref[...], 1, 1) + dot_f32(du_ref[...], wu_ref[...], 1, 1)
-    mlp = dot_f32(act_ref[...], wd_ref[...], 1, 0)
+    j, i = pl.program_id(0), pl.program_id(1)
+    rows = dg_buf.shape[1]
+
+    def copies(at):
+        return [pltpu.make_async_copy(src.at[pl.ds((base + at) * rows, rows)], buf.at[at], sems.at[k, at])
+                for k, (src, buf) in enumerate(((dg_hbm, dg_buf), (du_hbm, du_buf), (act_hbm, act_buf)))]
+
+    @pl.when((j == 0) & (i == 0))
+    def _():
+        for at in range(dg_buf.shape[0]):
+            for copy in copies(at):
+                copy.start()
+
+    @pl.when(j == 0)
+    def _():
+        for copy in copies(i):
+            copy.wait()
+
+    d_z = dot_f32(dg_buf[i], wg_ref[...], 1, 1) + dot_f32(du_buf[i], wu_ref[...], 1, 1)
+    mlp = dot_f32(act_buf[i], wd_ref[...], 1, 0)
     for kind, total in enumerate((d_z, mlp)):
         at = (slice(None), kind) if joined else (slice(None),)
         dst = out[0 if joined else kind]
@@ -295,7 +314,7 @@
     width, dim = w_down.shape
     rows = act.shape[0] // (2 * chips)
     half = chips // 2
-    lhs = pl.BlockSpec((2 * rows, width), lambda j, i: (i + side * half, 0))
+    hbm = pl.BlockSpec(memory_space=pl.ANY)
     row_w = pl.BlockSpec((tn, width), lambda j, i: (j, 0))
     if joined:
         outs = (jax.ShapeDtypeStruct((chips, 2, rows, dim), BF16),)
@@ -304,9 +323,10 @@
         outs = (jax.ShapeDtypeStruct((chips, rows, dim), BF16),) * 2
         tiles = [pl.BlockSpec((2, rows, tn), lambda j, i: (i, 0, j))] * 2
     return order.call(
-        functools.partial(back_kernel, joined=joined), 6 + len(far), out_shape=outs, grid=(dim // tn, half),
-        in_specs=[lhs, lhs, lhs, row_w, row_w, pl.BlockSpec((width, tn), lambda j, i: (0, j))] + tiles[:len(far)],
-        out_specs=tiles, compiler_params=params(2),
+        functools.partial(back_kernel, joined=joined, base=side * half), 6 + len(far), out_shape=outs, grid=(dim // tn, half),
+        in_specs=[hbm, hbm, hbm, row_w, row_w, pl.BlockSpec((width, tn), lambda j, i: (0, j))] + tiles[:len(far)],
+        out_specs=tiles, scratch_shapes=[pltpu.VMEM((half, 2 * rows, width), BF16)] * 3 + [pltpu.SemaphoreType.DMA((3, half))],
+        compiler_params=params(2, 50),
         cost_estimate=cost(3 * act.size * dim, act, act, w_gate, w_up, w_down, *outs, *outs), name="mlp_back",
     )(d_gate, d_upper, act, w_gate, w_up, w_down, *far)
 
@@ -369,22 +389,41 @@
 
 
 def small_wgrad_kernel(l_ref, r_ref, *refs):
-    total = dot_f32(l_ref[...], r_ref[...], 0, 0)
+    total = dot_f32(l_ref[...], r_ref[...], 0, 0).reshape(refs[-1].shape)
     for extra in refs[:-1]:
         total += extra[...]
     refs[-1][...] = total
 
 
-def small_wgrad(order, lhs, rhs, extra=(), tf=512, tn=1024):
+def small_wgrad(order, lhs, rhs, tf=1024, tn=512):
     tokens, rows = lhs.shape
     width = rhs.shape[1]
     out = jax.ShapeDtypeStruct((rows, width), F32)
-    tile = pl.BlockSpec((tf, tn), lambda j, i: (i, j))
-    return order.call(
-        small_wgrad_kernel, 2 + len(extra), out_shape=out, grid=(width // tn, rows // tf),
-        in_specs=[pl.BlockSpec((tokens, tf), lambda j, i: (0, i)), pl.BlockSpec((tokens, tn), lambda j, i: (0, j))] + [tile] * len(extra),
-        out_specs=tile, compiler_params=params(2), cost_estimate=cost(2 * tokens * rows * width, lhs, rhs, *extra, out), name="small_wgrad",
-    )(lhs, rhs, *extra)
+    return order.call(
+        small_wgrad_kernel, 2, out_shape=out, grid=(width // tn, rows // tf),
+        in_specs=[pl.BlockSpec((tokens, tf), lambda j, i: (0, i)), pl.BlockSpec((tokens, tn), lambda j, i: (0, j))],
+        out_specs=pl.BlockSpec((tf, tn), lambda j, i: (i, j)), compiler_params=params(2, 28),
+        cost_estimate=cost(2 * tokens * rows * width, lhs, rhs, out), name="small_wgrad",
+    )(lhs, rhs)
+
+
+def head_wgrad(order, lhs, rhs, hd, far=(), kind=0, earlier=None, tn=1024):
+    tokens, width = lhs.shape
+    dim = rhs.shape[1]
+    heads = width // hd
+    per = 2
+    plain = pl.BlockSpec((per, hd, tn), lambda j, i: (i, 0, j))
+    if far:
+        out = jax.ShapeDtypeStruct((heads, 2, hd, dim), F32)
+        spec = pl.BlockSpec((per, None, hd, tn), lambda j, i: (i, kind, 0, j))
+    else:
+        out, spec = jax.ShapeDtypeStruct((heads, hd, dim), F32), plain
+    kept = () if earlier is None else (earlier,)
+    return order.call(
+        small_wgrad_kernel, 2 + len(far), len(kept), out_shape=out, grid=(dim // tn, heads // per),
+        in_specs=[pl.BlockSpec((tokens, per * hd), lambda j, i: (0, i)), pl.BlockSpec((tokens, tn), lambda j, i: (0, j))] + [plain] * len(far),
+        out_specs=spec, compiler_params=params(2, 28), cost_estimate=cost(2 * tokens * width * dim, lhs, rhs, *far, out), name="head_wgrad",
+    )(lhs, rhs, *far, *kept)
 
 
 def resid_kernel(h_ref, a_own_ref, a_oth_ref, w_own_ref, w_oth_ref, gain_ref, resid_ref, *z_refs, sub):
@@ -521,10 +560,12 @@
     def flip(x_loc, bits):
         return lax.ppermute(x_loc, "tp", [(i, i ^ bits) for i in range(tp_size)])
 
-    def gather4_direct(x_loc):
+    def gather4_direct(x_loc, before=None):
         chip = lax.axis_index("tp") // 2
         half = x_loc.shape[0] // 2
         near, far = flip(x_loc, 2), flip(x_loc, 4)
+        if before is not None:
+            near, far, _ = lax.optimization_barrier((near, far, before))
         low, high = flip(near[:half], 4), flip(far[half:], 2)
         out = jnp.zeros((chips,) + x_loc.shape, x_loc.dtype)
         for k, block in ((0, x_loc), (1, near), (2, far)):
@@ -557,11 +598,13 @@
         kv_raw = dot_f32(normed_flat, w_kv, 1, 0).reshape(batch, rows, 2 * hd)
         keys, key_pull = jax.vjp(rope_single, kv_raw[..., :hd])
         kv_all = gather8(jnp.concatenate([keys, kv_raw[..., hd:]], axis=-1).astype(BF16))
-        wo_own = gather4_direct(w_out).reshape(chips * hd, dim)
         wq_oth = swap(wq_own)
+        q_own = dot_f32(normed_flat, wq_own, 1, 1)
+        q_oth = dot_f32(normed_flat, wq_oth, 1, 1)
+        wo_own = gather4_direct(lax.optimization_barrier((w_out, q_own))[0], q_oth).reshape(chips * hd, dim)
         wo_oth = swap(wo_own)
-        q_own = dot_f32(normed_flat, wq_own, 1, 1).reshape(batch, rows, chips * hd)
-        q_oth = dot_f32(normed_flat, wq_oth, 1, 1).reshape(batch, rows, chips * hd)
+        q_own = q_own.reshape(batch, rows, chips * hd)
+        q_oth = q_oth.reshape(batch, rows, chips * hd)
         mix_own, mix_oth, q_own, q_oth = attn_fwd(q_own, q_oth, kv_all, cos_t, sin_t, qpos, kpos, scalars)
         mix_own = mix_own.reshape(tokens, chips * hd)
         mix_oth = mix_oth.reshape(tokens, chips * hd)
@@ -579,13 +622,14 @@
         core_1 = core[None]
         grads = None
 
-        def attn_back(first, count, earlier):
-            terms, d_res, d_own, d_oth = d_resid_call(
-                order, d_gated[first:first + count], resid, grad_flat, mlp_gain[None, :], wo_own, wo_oth, first, size, () if earlier is None else earlier[1])
+        def d_resid_of(first, count, earlier):
+            return d_resid_call(order, d_gated[first:first + count], resid, grad_flat, mlp_gain[None, :], wo_own, wo_oth, first, size,
+                                () if earlier is None else earlier[1])
+
+        def attn_bwd_of(first, count, d_own, d_oth, earlier):
             per = batch // CHUNKS
-            parts = attn_bwd(order, q_own, q_oth, d_own.reshape(batch, rows, -1), d_oth.reshape(batch, rows, -1), kv_all, cos_t, sin_t, qpos, kpos,
-                             scalars, first * per, count * per, () if earlier is None else earlier[2])
-            return (terms if earlier is None else earlier[0] + terms), (d_res, d_own, d_oth), parts
+            return attn_bwd(order, q_own, q_oth, d_own.reshape(batch, rows, -1), d_oth.reshape(batch, rows, -1), kv_all, cos_t, sin_t, qpos, kpos,
+                            scalars, first * per, count * per, () if earlier is None else earlier[2])
 
         def finish(c):
             joined = c < CHUNKS - 1
@@ -600,31 +644,34 @@
                 d_gated[c], mlp_sums[c] = (a.reshape(size, dim) for a in sums)
 
         for c in range(CHUNKS):
-            if c == 0:
+            if c < CHUNKS - 1:
                 d_act = d_act_call(order, core_1, g_all[c], w_down)
                 acts.append(act_call(order, core_1, z_all[c], d_act, w_gate, w_up, None))
             else:
                 acts.append(act_call(order, core_1, z_all[c], g_all[c], *weights))
+            if c > 0:
                 finish(c - 1)
             joined = c < CHUNKS - 1
             parts = back_call(order, 1, acts[c][1], acts[c][2], acts[c][0], *weights, (), joined, chips)
             far.append(tuple(swap(a) for a in parts))
-        grads = attn_back(0, 1, None)
+        terms, *d_parts = d_resid_of(0, 1, None)
+        grads = terms, d_parts, attn_bwd_of(0, 1, d_parts[1], d_parts[2], None)
         finish(CHUNKS - 1)
         hidden_out = (resid.astype(F32) + jnp.concatenate(mlp_sums, axis=0).astype(F32)).astype(BF16).reshape(batch, rows, dim)
         shards = [[a.reshape(2 * chips, size, -1) for a in acts[c]] for c in range(CHUNKS)]
         g_gate = wgrad_call(order, core_1, z_all, [a[1] for a in shards])
 
-        norm_terms, (d_resid, _, _), (dq_own, dq_oth, dkv_own, dkv_oth) = attn_back(1, CHUNKS - 1, grads)
+        terms, d_resid, d_own, d_oth = d_resid_of(1, CHUNKS - 1, grads)
+        g_out_far = swap(head_wgrad(order, mix_oth, d_resid, hd))
+        norm_terms, (dq_own, dq_oth, dkv_own, dkv_oth) = grads[0] + terms, attn_bwd_of(1, CHUNKS - 1, d_own, d_oth, grads)
         dq_own = dq_own.reshape(tokens, chips * hd)
         dq_oth = dq_oth.reshape(tokens, chips * hd)
         dkv = scatter4((dkv_own.astype(F32) + swap(dkv_oth).astype(F32)).astype(BF16))
-        g_out_far = swap(small_wgrad(order, mix_oth, d_resid))
-        g_query_far = swap(small_wgrad(order, dq_oth, normed_flat))
-        g_out_part = small_wgrad(order, mix_own, d_resid, (g_out_far,))
-        g_query_part = small_wgrad(order, dq_own, normed_flat, (g_query_far,))
-        g_out = scatter4(g_out_part.reshape(chips, hd, dim))
-        g_query = scatter4(g_query_part.reshape(chips, hd, dim)).reshape(hd, dim).T
+        g_query_far = swap(head_wgrad(order, dq_oth, normed_flat, hd))
+        g_heads = head_wgrad(order, mix_own, d_resid, hd, (g_out_far,), 0)
+        g_heads = head_wgrad(order, dq_own, normed_flat, hd, (g_query_far,), 1, g_heads)
+        g_heads = scatter4(g_heads)
+        g_out, g_query = g_heads[0], g_heads[1].T
         d_k_raw = key_pull(dkv[..., :hd].astype(F32))[0]
         dkv = jnp.concatenate([d_k_raw.astype(BF16), dkv[..., hd:]], axis=-1).reshape(tokens, 2 * hd)
         grad_hidden, attn_terms = d_hidden_call(
@@ -635,6 +682,6 @@
         g_attn_norm, g_mlp_norm = sums[dim:].reshape(2, dim)
         g_up = wgrad_call(order, core_1, z_all, [a[2] for a in shards])
         g_down = wgrad_call(order, core_1, [a[0] for a in shards], g_all)
-        return (hidden_out, grad_hidden.reshape(batch, rows, dim), g_attn_norm, g_query, sums[:dim, :hd], sums[:dim, hd:], g_out.reshape(hd, dim), g_mlp_norm, g_gate, g_up, g_down)
+        return (hidden_out, grad_hidden.reshape(batch, rows, dim), g_attn_norm, g_query, sums[:dim, :hd], sums[:dim, hd:], g_out, g_mlp_norm, g_gate, g_up, g_down)
 
     return jax.shard_map(local_layer, mesh=mesh, in_specs=in_specs, out_specs=out_specs, check_vma=False)

time: 1440 us -> 1420 us (0.986)
  Pallas kernels: 1070 us -> 1040 us
    pallas_call x24 -> x25, Pallas kernels: 1050 us -> 1020 us  [run(): pl.pallas_call(body, grid_spec=pltpu.PrefetchScalarGridSpec(num_scalar_pr...]
    ppermute x8, waiting for transfers between devices: 84.3 us -> 104 us  [flip(): return lax.ppermute(x_loc, 'tp', [(i, i ^ bits) for i in range(tp_size)])]
    all_gather x7, waiting for transfers between devices: 46.6 us -> 30.9 us  [gather8(): return lax.all_gather(x_loc, 'tp', axis=0, tiled=False)]
    unnamed x94 -> x132, local copies, waits for them, and re-layouts: 25.8 us -> 41.4 us
    reduce_scatter x7 -> x6, waiting for transfers between devices: 69.6 us -> 71.6 us  [scatter4(): lax.psum_scatter(flat, 'tp', scatter_dimension=0, tiled=True, axis_index_...]
  transfers between devices with their start and end apart: 32 -> 31, of which waited for: 11 -> 14; matrix products, arithmetic and copies ran while one was open for 6% -> 5% of each run, Pallas kernels for 72% -> 70%
where the time goes in v4:
time: 1420 us; the launch traced here: 1410 us
  Pallas kernels  1040 us (73%)
  waiting for transfers between devices  219 us (15%)
  local copies, waits for them, and re-layouts  79 us (6%)
  other arithmetic  27 us (2%)
  matrix products  19.4 us (1%)
  starting transfers between devices  17.6 us (1%)
  between operations  15 us (1%)
    pallas_call x25, Pallas kernels, run(): pl.pallas_call(body, grid_spec=pltpu.PrefetchScalarGridSpec(num_scalar_pr...  1020 us
    ppermute x8, waiting for transfers between devices, flip(): return lax.ppermute(x_loc, 'tp', [(i, i ^ bits) for i in range(tp_size)])  104 us
    reduce_scatter x6, waiting for transfers between devices, scatter4(): lax.psum_scatter(flat, 'tp', scatter_dimension=0, tiled=True, axis_index_...  71.6 us
    unnamed x132, local copies, waits for them, and re-layouts  41.4 us
    all_gather x7, waiting for transfers between devices, gather8(): return lax.all_gather(x_loc, 'tp', axis=0, tiled=False)  30.9 us
  transfers between devices with their start and end apart: 31, of which 14 were waited for; matrix products, arithmetic and copies ran while one was open for 5% of the time, Pallas kernels for 70%

profile of v4, /device:TPU:0, one launch (start us, length us, event | category | flops | bytes accessed | tf_op | source)
XLA Modules:
  0.0 1413.3 jit_solution(16061589685938602769)
XLA Ops:
  29.5 37.0 %collective-permute-done = bf16[256,2048]{0,1:T(8,128)(2,1)S(1)} collective-permute-done((bf16[256,2048]{0,1:T(8,128)(2,1)}, bf16[256,2048]{0,1:T(8,128)(2,1)S(1)}, u32[]{:S(2)}, u32[]{:S(2)}) %collective-permute-start) | collective-permute-done | bytes 1048608 | tf_op jit(solution)/shard_map/ppermute | solution.py:561
  79.1 13.9 collective-permute-done.2
  98.9 10.0 fusion.13
  121.7 29.6 %collective-permute-done.6 = bf16[256,2048]{1,0:T(8,128)(2,1)S(1)} collective-permute-done((bf16[256,2048]{1,0:T(8,128)(2,1)S(1)}, bf16[256,2048]{1,0:T(8,128)(2,1)S(1)}, u32[]{:S(2)}, u32[]{:S(2)}) %collective-permute-start.6) | collective-permute-done | bytes 1048608 | tf_op jit(solution)/shard_map/ppermute | solution.py:561
  157.1 20.0 %collective-permute-done.7 = bf16[128,2048]{1,0:T(8,128)(2,1)S(1)} collective-permute-done((bf16[128,2048]{1,0:T(8,128)(2,1)S(1)}, bf16[128,2048]{1,0:T(8,128)(2,1)S(1)}, u32[]{:S(2)}, u32[]{:S(2)}) %collective-permute-start.7) | collective-permute-done | bytes 524320 | tf_op jit(solution)/shard_map/ppermute | solution.py:561
  184.3 20.5 %attn_fwd.1 = (bf16[12,96,1024]{2,1,0:T(8,128)(2,1)S(1)}, bf16[12,96,1024]{2,1,0:T(8,128)(2,1)S(1)}, bf16[12,96,1024]{2,1,0:T(8,128)(2,1)S(1)}, bf16[12,96,1024]{2,1,0:T(8,128)(2,1)S(1)}) custom-call(s32[12]{0:T(128)S(1)} %copy-done.24, s32[12]{0:T(128)S(1)} %copy-done.26, s32[1]{0:T(128)} %bitcast.1.core_s.refs_0_.refs_2_, f32[12,96,1024]{2,1,0:T(8,128)S(1)} %bitcast.119, ...), custom_call_target="tpu_custom_call" | custom-call | flops 7247757312 | bytes 28311552 | tf_op jit(solution)/shard_map/attn_fwd/pallas_call | solution.py:149
  210.5 19.3 %resid.1 = (bf16[1152,2048]{1,0:T(8,128)(2,1)}, bf16[384,2048]{1,0:T(8,128)(2,1)}, bf16[384,2048]{1,0:T(8,128)(2,1)}, bf16[384,2048]{1,0:T(8,128)(2,1)}) custom-call(bf16[1152,2048]{1,0:T(8,128)(2,1)} %bitcast.128, bf16[1152,1024]{1,0:T(8,128)(2,1)} %bitcast.108, bf16[1152,1024]{1,0:T(8,128)(2,1)} %bitcast.120, ...), custom_call_target="tpu_custom_call" | custom-call | flops 9663676416 | bytes 27262976 | tf_op jit(solution)/shard_map/resid/pallas_call | solution.py:199
  232.4 33.5 %d_act.2.refs_2_ = bf16[3072,2048]{1,0:T(8,128)(2,1)} custom-call(s32[1]{0:T(128)} %bitcast.1.core_s.refs_0_.refs_2_, bf16[4,2,384,2048]{3,2,1,0:T(8,128)(2,1)} %bitcast.147, bf16[2048,2048]{1,0:T(8,128)(2,1)} %refs_5_.13, bf16[1152,2048]{1,0:T(8,128)(2,1)} %get-tuple-element.58.refs_3_.refs_1_.refs_2_), custom_call_target="tpu_custom_call" | custom-call | flops 25769803776 | bytes 33554432 | tf_op jit(solution)/shard_map/d_act/pallas_call | solution.py:199
  265.9 30.9 %all-gather.19.cloned.1.call-done = bf16[3072,2048]{1,0:T(8,128)(2,1)} async-done(((bf16[384,2048]{1,0:T(8,128)(2,1)}), bf16[3072,2048]{1,0:T(8,128)(2,1)}) %all-gather.19.cloned.1.call-update) | async-done | bytes 12582928 | tf_op jit(solution)/shard_map/all_gather | solution.py:555
  296.8 70.6 %mlp_act.3 = (bf16[3072,2048]{1,0:T(8,128)(2,1)}, bf16[3072,2048]{1,0:T(8,128)(2,1)}, bf16[3072,2048]{1,0:T(8,128)(2,1)}) custom-call(s32[1]{0:T(128)} %bitcast.1.core_s.refs_0_.refs_2_, bf16[4,2,384,2048]{3,2,1,0:T(8,128)(2,1)} %bitcast.149, bf16[3072,2048]{1,0:T(8,128)(2,1)} %d_act.2.refs_2_, bf16[2048,2048]{1,0:T(8,128)(2,1)} %refs_3_.17, ...), custom_call_target="tpu_custom_call" | custom-call | flops 51539607552 | bytes 79691776 | tf_op jit(solution)/shard_map/mlp_act/pallas_call | solution.py:199
  367.4 49.7 %mlp_back.6.refs_3_ = bf16[4,2,384,2048]{3,2,1,0:T(8,128)(2,1)} custom-call(bf16[3072,2048]{1,0:T(8,128)(2,1)} %get-tuple-element.60.refs_0_, bf16[3072,2048]{1,0:T(8,128)(2,1)} %get-tuple-element.61.refs_1_, bf16[3072,2048]{1,0:T(8,128)(2,1)} %get-tuple-element.62.refs_2_, bf16[2048,2048]{1,0:T(8,128)(2,1)} %refs_3_.17, bf16[2048,2048]{1,0:T(8,128)(2,1)} %refs_4_.17, ...), custom_call_target="tpu_custom_call" | custom-call | flops 38654705664 | bytes 75497472 | tf_op jit(solution)/shard_map/mlp_back/pallas_call | solution.py:199
  417.3 32.9 %d_act.3.refs_2_ = bf16[3072,2048]{1,0:T(8,128)(2,1)} custom-call(s32[1]{0:T(128)} %bitcast.1.core_s.refs_0_.refs_2_, bf16[4,2,384,2048]{3,2,1,0:T(8,128)(2,1)} %bitcast.152, bf16[2048,2048]{1,0:T(8,128)(2,1)} %refs_5_.13, bf16[4,2,384,2048]{3,2,1,0:T(8,128)(2,1)} %mlp_back.6.refs_3_), custom_call_target="tpu_custom_call" | custom-call | flops 25769803776 | bytes 33554432 | tf_op jit(solution)/shard_map/d_act/pallas_call | solution.py:199
  450.3 71.0 %mlp_act.4 = (bf16[3072,2048]{1,0:T(8,128)(2,1)}, bf16[3072,2048]{1,0:T(8,128)(2,1)}, bf16[3072,2048]{1,0:T(8,128)(2,1)}) custom-call(s32[1]{0:T(128)} %bitcast.1.core_s.refs_0_.refs_2_, bf16[4,2,384,2048]{3,2,1,0:T(8,128)(2,1)} %bitcast.154, bf16[3072,2048]{1,0:T(8,128)(2,1)} %d_act.3.refs_2_, bf16[2048,2048]{1,0:T(8,128)(2,1)} %refs_3_.17, ...), custom_call_target="tpu_custom_call" | custom-call | flops 51539607552 | bytes 79691776 | tf_op jit(solution)/shard_map/mlp_act/pallas_call | solution.py:199
  521.2 49.3 %mlp_back.7.refs_6_ = bf16[4,2,384,2048]{3,2,1,0:T(8,128)(2,1)} custom-call(bf16[3072,2048]{1,0:T(8,128)(2,1)} %get-tuple-element.60.refs_0_, bf16[3072,2048]{1,0:T(8,128)(2,1)} %get-tuple-element.61.refs_1_, bf16[3072,2048]{1,0:T(8,128)(2,1)} %get-tuple-element.62.refs_2_, bf16[2048,2048]{1,0:T(8,128)(2,1)} %refs_3_.17, bf16[2048,2048]{1,0:T(8,128)(2,1)} %refs_4_.17, ...), custom_call_target="tpu_custom_call" | custom-call | flops 38654705664 | bytes 75497472 | tf_op jit(solution)/shard_map/mlp_back/pallas_call | solution.py:199
  570.6 48.8 %mlp_back.8.refs_6_ = bf16[4,2,384,2048]{3,2,1,0:T(8,128)(2,1)} custom-call(bf16[3072,2048]{1,0:T(8,128)(2,1)} %get-tuple-element.65.refs_0_, bf16[3072,2048]{1,0:T(8,128)(2,1)} %get-tuple-element.66.refs_1_, bf16[3072,2048]{1,0:T(8,128)(2,1)} %get-tuple-element.64.refs_7_.refs_2_, bf16[2048,2048]{1,0:T(8,128)(2,1)} %refs_3_.17, ...), custom_call_target="tpu_custom_call" | custom-call | flops 38654705664 | bytes 75497472 | tf_op jit(solution)/shard_map/mlp_back/pallas_call | solution.py:199
  619.8 92.1 %mlp_act.5 = (bf16[3072,2048]{1,0:T(8,128)(2,1)}, bf16[3072,2048]{1,0:T(8,128)(2,1)}, bf16[3072,2048]{1,0:T(8,128)(2,1)}) custom-call(s32[1]{0:T(128)} %bitcast.1.core_s.refs_0_.refs_2_, bf16[4,2,384,2048]{3,2,1,0:T(8,128)(2,1)} %bitcast.159, bf16[4,2,384,2048]{3,2,1,0:T(8,128)(2,1)} %bitcast.157, bf16[2048,2048]{1,0:T(8,128)(2,1)} %refs_3_.17, ...), custom_call_target="tpu_custom_call" | custom-call | flops 77309411328 | bytes 88080384 | tf_op jit(solution)/shard_map/mlp_act/pallas_call | solution.py:199
  711.9 49.2 %mlp_back.9.refs_6_ = bf16[4,2,384,2048]{3,2,1,0:T(8,128)(2,1)} custom-call(bf16[3072,2048]{1,0:T(8,128)(2,1)} %get-tuple-element.65.refs_0_, bf16[3072,2048]{1,0:T(8,128)(2,1)} %get-tuple-element.66.refs_1_, bf16[3072,2048]{1,0:T(8,128)(2,1)} %get-tuple-element.64.refs_7_.refs_2_, bf16[2048,2048]{1,0:T(8,128)(2,1)} %refs_3_.17, ...), custom_call_target="tpu_custom_call" | custom-call | flops 38654705664 | bytes 75497472 | tf_op jit(solution)/shard_map/mlp_back/pallas_call | solution.py:199
  761.3 49.7 %mlp_back.10 = (bf16[4,384,2048]{2,1,0:T(8,128)(2,1)}, bf16[4,384,2048]{2,1,0:T(8,128)(2,1)}) custom-call(bf16[3072,2048]{1,0:T(8,128)(2,1)} %get-tuple-element.69.refs_0_, bf16[3072,2048]{1,0:T(8,128)(2,1)} %get-tuple-element.70.refs_1_, bf16[3072,2048]{1,0:T(8,128)(2,1)} %get-tuple-element.68.refs_7_.refs_2_, bf16[2048,2048]{1,0:T(8,128)(2,1)} %refs_3_.17, ...), custom_call_target="tpu_custom_call" | custom-call | flops 38654705664 | bytes 75497472 | tf_op jit(solution)/shard_map/mlp_back/pallas_call | solution.py:199
  811.8 10.2 d_resid.2
  826.0 14.2 %attn_bwd.2 = (bf16[12,96,1024]{2,1,0:T(8,128)(2,1)S(1)}, bf16[12,96,1024]{2,1,0:T(8,128)(2,1)S(1)}, bf16[4,12,96,512]{3,2,1,0:T(8,128)(2,1)}, bf16[4,12,96,512]{3,2,1,0:T(8,128)(2,1)}) custom-call(s32[12]{0:T(128)S(1)} %copy-done.25, s32[12]{0:T(128)S(1)} %copy-done.27, s32[1]{0:T(128)} %bitcast.1.core_s.refs_0_.refs_2_, ...), custom_call_target="tpu_custom_call" | custom-call | flops 6039797760 | bytes 23592960 | tf_op jit(solution)/shard_map/attn_bwd/pallas_call | solution.py:199
  840.3 49.9 %mlp_back.11 = (bf16[4,384,2048]{2,1,0:T(8,128)(2,1)}, bf16[4,384,2048]{2,1,0:T(8,128)(2,1)}) custom-call(bf16[3072,2048]{1,0:T(8,128)(2,1)} %get-tuple-element.69.refs_0_, bf16[3072,2048]{1,0:T(8,128)(2,1)} %get-tuple-element.70.refs_1_, bf16[3072,2048]{1,0:T(8,128)(2,1)} %get-tuple-element.68.refs_7_.refs_2_, bf16[2048,2048]{1,0:T(8,128)(2,1)} %refs_3_.17, ...), custom_call_target="tpu_custom_call" | custom-call | flops 38654705664 | bytes 75497472 | tf_op jit(solution)/shard_map/mlp_back/pallas_call | solution.py:199
  890.3 87.9 %wgrad.3.refs_10_ = f32[2048,2048]{1,0:T(8,128)} custom-call(s32[1]{0:T(128)} %bitcast.1.core_s.refs_0_.refs_2_, bf16[4,2,384,2048]{3,2,1,0:T(8,128)(2,1)} %bitcast.150, bf16[4,2,384,2048]{3,2,1,0:T(8,128)(2,1)} %bitcast.155, bf16[4,2,384,2048]{3,2,1,0:T(8,128)(2,1)} %bitcast.160, bf16[8,384,2048]{2,1,0:T(8,128)(2,1)} %bitcast.168, ...), custom_call_target="tpu_custom_call" | custom-call | flops 77309411328 | bytes 92274688 | tf_op jit(solution)/shard_map/wgrad/pallas_call | solution.py:199
  981.3 18.0 %d_resid.3 = (f32[8,2048]{1,0:T(8,128)S(1)}, bf16[1152,2048]{1,0:T(8,128)(2,1)}, bf16[1152,1024]{1,0:T(8,128)(2,1)S(1)}, bf16[1152,1024]{1,0:T(8,128)(2,1)}) custom-call(bf16[2,384,2048]{2,1,0:T(8,128)(2,1)} %reduce-scatter.9.cloned.1.call-done.refs_0_, bf16[384,2048]{1,0:T(8,128)(2,1)S(1)} %copy-done.15, ...), custom_call_target="tpu_custom_call", output_to_operand_aliasing={{1}: (7, {}), {2}: (8, {}), {3}: (9, {})} | custom-call | flops 6442450944 | bytes 17825792 | tf_op jit(solution)/shard_map/d_resid/pallas_call | solution.py:199
  1015.0 25.8 %attn_bwd.3 = (bf16[12,96,1024]{2,1,0:T(8,128)(2,1)S(1)}, bf16[12,96,1024]{2,1,0:T(8,128)(2,1)S(1)}, bf16[4,12,96,512]{3,2,1,0:T(8,128)(2,1)}, bf16[4,12,96,512]{3,2,1,0:T(8,128)(2,1)}) custom-call(s32[12]{0:T(128)S(1)} %copy-done.25, s32[12]{0:T(128)S(1)} %copy-done.27, ...), custom_call_target="tpu_custom_call", output_to_operand_aliasing={{0}: (12, {}), {1}: (13, {}), {2}: (14, {}), {3}: (15, {})} | custom-call | flops 12079595520 | bytes 28311552 | tf_op jit(solution)/shard_map/attn_bwd/pallas_call | solution.py:199
  1070.0 11.6 head_wgrad.6.refs_3_
  1082.0 10.6 head_wgrad.7.refs_9_
  1092.7 16.0 %reduce-scatter.15.cloned.1.call-done = bf16[12,96,512]{2,1,0:T(8,128)(2,1)} async-done(((bf16[48,96,512]{2,1,0:T(8,128)(2,1)}), bf16[12,96,512]{2,1,0:T(8,128)(2,1)}) %reduce-scatter.15.cloned.1.call-update) | async-done | bytes 1179664 | tf_op jit(solution)/shard_map/reduce_scatter | solution.py:552
  1111.4 26.0 %d_hidden.1 = (bf16[1152,2048]{1,0:T(8,128)(2,1)}, f32[8,2048]{1,0:T(8,128)}) custom-call(bf16[1152,1024]{1,0:T(8,128)(2,1)} %bitcast.111, bf16[1152,1024]{1,0:T(8,128)(2,1)} %bitcast.122, bf16[1152,512]{1,0:T(8,128)(2,1)} %bitcast.105, bf16[1152,2048]{1,0:T(8,128)(2,1)} %bitcast.129, bf16[1152,2048]{1,0:T(8,128)(2,1)} %get-tuple-element.87.refs_1_.refs_4_, ...), custom_call_target="tpu_custom_call" | custom-call | flops 14495514624 | bytes 27328512 | tf_op jit(solution)/shard_map/d_hidden/pallas_call | solution.py:199
  1156.0 19.9 %reduce-scatter.11.cloned.1.call-done = bf16[384,2048]{1,0:T(8,128)(2,1)} async-done(((bf16[1536,2048]{1,0:T(8,128)(2,1)}), bf16[384,2048]{1,0:T(8,128)(2,1)}) %reduce-scatter.11.cloned.1.call-update) | async-done | bytes 1572880 | tf_op jit(solution)/shard_map/reduce_scatter | solution.py:552
  1181.7 88.3 %wgrad.4.refs_7_ = f32[2048,2048]{1,0:T(8,128)} custom-call(s32[1]{0:T(128)} %bitcast.1.core_s.refs_0_.refs_2_, bf16[4,2,384,2048]{3,2,1,0:T(8,128)(2,1)} %bitcast.151, bf16[4,2,384,2048]{3,2,1,0:T(8,128)(2,1)} %bitcast.156, bf16[4,2,384,2048]{3,2,1,0:T(8,128)(2,1)} %bitcast.161, bf16[8,384,2048]{2,1,0:T(8,128)(2,1)} %bitcast.163, ...), custom_call_target="tpu_custom_call" | custom-call | flops 77309411328 | bytes 92274688 | tf_op jit(solution)/shard_map/wgrad/pallas_call | solution.py:199
  1270.0 88.4 %wgrad.5 = f32[2048,2048]{1,0:T(8,128)} custom-call(s32[1]{0:T(128)} %bitcast.1.core_s.refs_0_.refs_2_, bf16[8,384,2048]{2,1,0:T(8,128)(2,1)} %bitcast.162, bf16[8,384,2048]{2,1,0:T(8,128)(2,1)} %bitcast.164, bf16[8,384,2048]{2,1,0:T(8,128)(2,1)} %bitcast.166, bf16[4,2,384,2048]{3,2,1,0:T(8,128)(2,1)} %bitcast.148, bf16[4,2,384,2048]{3,2,1,0:T(8,128)(2,1)} %bitcast.153, ...), custom_call_target="tpu_custom_call" | custom-call | flops 77309411328 | bytes 92274688 | tf_op jit(solution)/shard_map/wgrad/pallas_call | solution.py:199
  1365.2 35.6 %reduce-scatter.17.cloned.1.call-done = f32[2,256,2048]{2,1,0:T(8,128)} async-done(((f32[8,256,2048]{2,1,0:T(8,128)}), f32[2,256,2048]{2,1,0:T(8,128)}) %reduce-scatter.17.cloned.1.call-update) | async-done | bytes 4194320 | tf_op jit(solution)/shard_map/reduce_scatter | solution.py:552
  (270 shorter events, 167.6 us)
Async XLA Ops:
  7.2 174.5 %all-gather.11.cloned.1.call-start = ((), (), s32[]{:S(2)}) async-start(), calls=%async_computation.6 | async-start | bytes 10616832 | tf_op jit(solution)/shard_map/all_gather | solution.py:555
  16.4 996.9 %copy-start.16 = (f32[96,128]{1,0:T(8,128)}, f32[96,128]{1,0:T(8,128)S(1)}, u32[]{:S(2)}) copy-start(f32[96,128]{1,0:T(8,128)S(1)} %get-tuple-element.143.cos_ref.refs_8_) | copy-start | bytes 147460
  17.8 214.6 %all-gather.13.cloned.1.call-start = ((), (), s32[]{:S(2)}) async-start(), calls=%async_computation.7 | async-start | bytes 14155776 | tf_op jit(solution)/shard_map/all_gather | solution.py:555
  22.6 274.2 %all-gather.19.cloned.1.call-start = ((), (), s32[]{:S(2)}) async-start(), calls=%async_computation.17 | async-start | bytes 14155776 | tf_op jit(solution)/shard_map/all_gather | solution.py:555
  23.1 43.4 %collective-permute-start = (bf16[256,2048]{0,1:T(8,128)(2,1)}, bf16[256,2048]{0,1:T(8,128)(2,1)S(1)}, u32[]{:S(2)}, u32[]{:S(2)}) collective-permute-start(bf16[256,2048]{0,1:T(8,128)(2,1)} %bitcast.3), channel_id=1, source_target_pairs={{0,2},{1,3},{2,0},{3,1},{4,6},{5,7},{6,4},{7,5}} | collective-permute-start | bytes 3145736 | tf_op jit(solution)/shard_map/ppermute | solution.py:561
  26.4 42.9 %collective-permute-start.1 = (bf16[256,2048]{0,1:T(8,128)(2,1)}, bf16[256,2048]{0,1:T(8,128)(2,1)S(1)}, u32[]{:S(2)}, u32[]{:S(2)}) collective-permute-start(bf16[256,2048]{0,1:T(8,128)(2,1)} %bitcast.3), channel_id=1, source_target_pairs={{0,4},{1,5},{2,6},{3,7},{4,0},{5,1},{6,2},{7,3}} | collective-permute-start | bytes 3145736 | tf_op jit(solution)/shard_map/ppermute | solution.py:561
  67.3 25.7 %collective-permute-start.2 = (bf16[128,2048]{0,1:T(8,128)(2,1)}, bf16[128,2048]{0,1:T(8,128)(2,1)}, u32[]{:S(2)}, u32[]{:S(2)}) collective-permute-start(bf16[128,2048]{0,1:T(8,128)(2,1)} %slice.84), channel_id=1, source_target_pairs={{0,4},{1,5},{2,6},{3,7},{4,0},{5,1},{6,2},{7,3}} | collective-permute-start | bytes 1572872 | tf_op jit(solution)/shard_map/ppermute | solution.py:561
  70.2 25.7 %collective-permute-start.3 = (bf16[128,2048]{0,1:T(8,128)(2,1)}, bf16[128,2048]{0,1:T(8,128)(2,1)}, u32[]{:S(2)}, u32[]{:S(2)}) collective-permute-start(bf16[128,2048]{0,1:T(8,128)(2,1)} %slice.85), channel_id=1, source_target_pairs={{0,2},{1,3},{2,0},{3,1},{4,6},{5,7},{6,4},{7,5}} | collective-permute-start | bytes 1572872 | tf_op jit(solution)/shard_map/ppermute | solution.py:561
  98.9 16.0 %collective-permute-start.4 = (bf16[1024,2048]{1,0:T(8,128)(2,1)}, bf16[1024,2048]{1,0:T(8,128)(2,1)S(1)}, u32[]{:S(2)}, u32[]{:S(2)}) collective-permute-start(bf16[1024,2048]{1,0:T(8,128)(2,1)} %bitcast.9.refs_6_), channel_id=1, source_target_pairs={{0,1},{1,0},{2,3},{3,2},{4,5},{5,4},{6,7},{7,6}} | collective-permute-start | bytes 12582920 | tf_op jit(solution)/shard_map/ppermute | solution.py:558
  108.9 42.4 %collective-permute-start.6 = (bf16[256,2048]{1,0:T(8,128)(2,1)S(1)}, bf16[256,2048]{1,0:T(8,128)(2,1)S(1)}, u32[]{:S(2)}, u32[]{:S(2)}) collective-permute-start(bf16[256,2048]{1,0:T(8,128)(2,1)S(1)} %copy-done.44), channel_id=1, source_target_pairs={{0,4},{1,5},{2,6},{3,7},{4,0},{5,1},{6,2},{7,3}} | collective-permute-start | bytes 3145736 | tf_op jit(solution)/shard_map/ppermute | solution.py:561
  109.5 42.2 %collective-permute-start.5 = (bf16[256,2048]{1,0:T(8,128)(2,1)S(1)}, bf16[256,2048]{1,0:T(8,128)(2,1)S(1)}, u32[]{:S(2)}, u32[]{:S(2)}) collective-permute-start(bf16[256,2048]{1,0:T(8,128)(2,1)S(1)} %copy-done.44), channel_id=1, source_target_pairs={{0,2},{1,3},{2,0},{3,1},{4,6},{5,7},{6,4},{7,5}} | collective-permute-start | bytes 3145736 | tf_op jit(solution)/shard_map/ppermute | solution.py:561
  151.7 25.4 %collective-permute-start.7 = (bf16[128,2048]{1,0:T(8,128)(2,1)S(1)}, bf16[128,2048]{1,0:T(8,128)(2,1)S(1)}, u32[]{:S(2)}, u32[]{:S(2)}) collective-permute-start(bf16[128,2048]{1,0:T(8,128)(2,1)S(1)} %slice.71), channel_id=1, source_target_pairs={{0,4},{1,5},{2,6},{3,7},{4,0},{5,1},{6,2},{7,3}} | collective-permute-start | bytes 1572872 | tf_op jit(solution)/shard_map/ppermute | solution.py:561
  154.3 25.5 %collective-permute-start.8 = (bf16[128,2048]{1,0:T(8,128)(2,1)S(1)}, bf16[128,2048]{1,0:T(8,128)(2,1)S(1)}, u32[]{:S(2)}, u32[]{:S(2)}) collective-permute-start(bf16[128,2048]{1,0:T(8,128)(2,1)S(1)} %slice.72), channel_id=1, source_target_pairs={{0,2},{1,3},{2,0},{3,1},{4,6},{5,7},{6,4},{7,5}} | collective-permute-start | bytes 1572872 | tf_op jit(solution)/shard_map/ppermute | solution.py:561
  180.6 29.8 %collective-permute-start.9 = (bf16[1024,2048]{1,0:T(8,128)(2,1)}, bf16[1024,2048]{1,0:T(8,128)(2,1)}, u32[]{:S(2)}, u32[]{:S(2)}) collective-permute-start(bf16[1024,2048]{1,0:T(8,128)(2,1)} %bitcast.23.refs_3_.refs_4_.refs_5_), channel_id=1, source_target_pairs={{0,1},{1,0},{2,3},{3,2},{4,5},{5,4},{6,7},{7,6}} | collective-permute-start | bytes 12582920 | tf_op jit(solution)/shard_map/ppermute | solution.py:558
  229.8 187.5 %all-gather.15.cloned.1.call-start = ((), (), s32[]{:S(2)}) async-start(), calls=%async_computation.8 | async-start | bytes 14155776 | tf_op jit(solution)/shard_map/all_gather | solution.py:555
  230.4 219.8 %all-gather.21.cloned.1.call-start = ((), (), s32[]{:S(2)}) async-start(), calls=%async_computation.18 | async-start | bytes 14155776 | tf_op jit(solution)/shard_map/all_gather | solution.py:555
  231.0 388.8 %all-gather.17.cloned.1.call-start = ((), (), s32[]{:S(2)}) async-start(), calls=%async_computation.10 | async-start | bytes 14155776 | tf_op jit(solution)/shard_map/all_gather | solution.py:555
  231.6 388.2 %all-gather.23.cloned.1.call-start = ((), (), s32[]{:S(2)}) async-start(), calls=%async_computation.19 | async-start | bytes 14155776 | tf_op jit(solution)/shard_map/all_gather | solution.py:555
  232.3 579.4 %reduce-scatter.7.cloned.1.call-start = ((), (), s32[]{:S(2)}) async-start(), calls=%async_computation.9 | async-start | bytes 15728640 | tf_op jit(solution)/shard_map/reduce_scatter | solution.py:552
  417.2 104.0 %collective-permute-start.10 = (bf16[4,2,384,2048]{3,2,1,0:T(8,128)(2,1)}, bf16[4,2,384,2048]{3,2,1,0:T(8,128)(2,1)}, u32[]{:S(2)}, u32[]{:S(2)}) collective-permute-start(bf16[4,2,384,2048]{3,2,1,0:T(8,128)(2,1)} %mlp_back.6.refs_3_), channel_id=1, source_target_pairs={{0,1},{1,0},{2,3},{3,2},{4,5},{5,4},{6,7},{7,6}} | collective-permute-start | bytes 37748744 | tf_op jit(solution)/shard_map/ppermute | solution.py:558
  570.6 407.6 %reduce-scatter.9.cloned.1.call-start = ((), (), s32[]{:S(2)}) async-start(), calls=%async_computation.11 | async-start | bytes 15728640 | tf_op jit(solution)/shard_map/reduce_scatter | solution.py:552
  619.4 92.5 %collective-permute-start.11 = (bf16[4,2,384,2048]{3,2,1,0:T(8,128)(2,1)}, bf16[4,2,384,2048]{3,2,1,0:T(8,128)(2,1)}, u32[]{:S(2)}, u32[]{:S(2)}) collective-permute-start(bf16[4,2,384,2048]{3,2,1,0:T(8,128)(2,1)} %mlp_back.8.refs_6_), channel_id=1, source_target_pairs={{0,1},{1,0},{2,3},{3,2},{4,5},{5,4},{6,7},{7,6}} | collective-permute-start | bytes 37748744 | tf_op jit(solution)/shard_map/ppermute | solution.py:558
  761.2 217.0 %reduce-scatter.13.cloned.1.call-start = ((), (), s32[]{:S(2)}) async-start(), calls=%async_computation.13 | async-start | bytes 7864320 | tf_op jit(solution)/shard_map/reduce_scatter | solution.py:552
  811.0 29.3 %collective-permute-start.13 = (bf16[4,384,2048]{2,1,0:T(8,128)(2,1)}, bf16[4,384,2048]{2,1,0:T(8,128)(2,1)}, u32[]{:S(2)}, u32[]{:S(2)}) collective-permute-start(bf16[4,384,2048]{2,1,0:T(8,128)(2,1)} %get-tuple-element.72), channel_id=1, source_target_pairs={{0,1},{1,0},{2,3},{3,2},{4,5},{5,4},{6,7},{7,6}} | collective-permute-start | bytes 18874376 | tf_op jit(solution)/shard_map/ppermute | solution.py:558
  811.0 29.3 %collective-permute-start.12 = (bf16[4,384,2048]{2,1,0:T(8,128)(2,1)}, bf16[4,384,2048]{2,1,0:T(8,128)(2,1)}, u32[]{:S(2)}, u32[]{:S(2)}) collective-permute-start(bf16[4,384,2048]{2,1,0:T(8,128)(2,1)} %get-tuple-element.71.refs_6_), channel_id=1, source_target_pairs={{0,1},{1,0},{2,3},{3,2},{4,5},{5,4},{6,7},{7,6}} | collective-permute-start | bytes 18874376 | tf_op jit(solution)/shard_map/ppermute | solution.py:558
  890.2 218.4 %reduce-scatter.15.cloned.1.call-start = ((), (), s32[]{:S(2)}) async-start(), calls=%async_computation.14 | async-start | bytes 5898240 | tf_op jit(solution)/shard_map/reduce_scatter | solution.py:552
  1040.8 8.4 collective-permute-start.14
  1055.8 120.1 %reduce-scatter.11.cloned.1.call-start = ((), (), s32[]{:S(2)}) async-start(), calls=%async_computation.12 | async-start | bytes 7864320 | tf_op jit(solution)/shard_map/reduce_scatter | solution.py:552
  1056.4 302.1 %all-reduce.4.cloned.1.call-start = ((), (), s32[]{:S(2)}) async-start(), calls=%async_computation.15 | async-start | bytes 8421376 | tf_op jit(solution)/shard_map/psum | solution.py:681
  1056.4 13.5 collective-permute-start.16
  1068.7 13.3 collective-permute-start.15
  1151.0 249.8 %reduce-scatter.17.cloned.1.call-start = ((), (), s32[]{:S(2)}) async-start(), calls=%async_computation.16 | async-start | bytes 20971520 | tf_op jit(solution)/shard_map/reduce_scatter | solution.py:552
  (62 other events, 1874.4 us)
Sparse Core Ops, SparseCore 0:
  17.9 85.1 all-gather.10
  105.5 94.6 all-gather.12
  230.0 66.7 all-gather.18
  299.0 66.4 all-gather.14
  367.7 67.2 all-gather.20
  436.7 66.4 all-gather.16
  505.6 66.4 all-gather.22
  575.7 115.0 reduce-scatter.6
  761.3 115.9 reduce-scatter.8
  890.3 65.9 reduce-scatter.12
  1055.9 52.6 reduce-scatter.14
  1111.4 64.4 reduce-scatter.10
  1179.2 70.4 all-reduce.3
  1252.6 148.1 reduce-scatter.16

commit v5 on v4

--- a/solution.py
+++ b/solution.py
@@ -12,6 +12,7 @@
 F32 = jnp.float32
 BF16 = jnp.bfloat16
 MASKED = -1e30
+LARGE = 1 << 17
 
 
 def rms_norm(x_in, gain):
@@ -81,7 +82,7 @@
 
 
 def attn_bwd_kernel(first, prefix_s, valid_s, core_s, q_own_ref, q_oth_ref, g_own_ref, g_oth_ref, kv_ref, cos_ref, sin_ref,
-                    qpos_ref, kpos_ref, dq_own_ref, dq_oth_ref, dkv_own_ref, dkv_oth_ref):
+                    qpos_ref, kpos_ref, dq_own_ref, dq_oth_ref, dkv_ref):
     b = pl.program_id(0) + first
     rows, width = q_own_ref.shape[1:]
     hd = kv_ref.shape[-1] // 2
@@ -90,7 +91,6 @@
     scale = hd ** -0.5
     cos_t, sin_t = cos_ref[...], sin_ref[...]
     shards = kv_ref.shape[0] // 2
-    n_keys = shards * kv_ref.shape[2]
     keys = own_first(kv_ref, core_s[0], 0, hd)
     values = own_first(kv_ref, core_s[0], hd, 2 * hd)
     limit = jnp.minimum(valid_s[b], jnp.maximum(prefix_s[b], qpos_ref[...] + 1))
@@ -118,12 +118,12 @@
             dst[0, :, n * hd + half:(n + 1) * hd] = (g_2 * cos_t - g_1 * sin_t).astype(BF16)
     d_keys = d_keys.astype(BF16)
     d_values = d_values.astype(BF16)
-    span = n_keys // shards
-    for side, dst in ((0, dkv_own_ref), (1, dkv_oth_ref)):
+    span = kv_ref.shape[2]
+    for k, side in enumerate((core_s[0], 1 - core_s[0])):
         for c in range(shards):
-            at = side * n_keys + c * span
-            dst[c, 0, :, :hd] = d_keys[at:at + span]
-            dst[c, 0, :, hd:] = d_values[at:at + span]
+            at = (k * shards + c) * span
+            dkv_ref[2 * c + side, 0, :, :hd] = d_keys[at:at + span]
+            dkv_ref[2 * c + side, 0, :, hd:] = d_values[at:at + span]
 
 
 def attn_specs(rows, width, shards, two_hd, half):
@@ -153,7 +153,7 @@
             num_scalar_prefetch=3, grid=(batch,),
             in_specs=[q_spec, q_spec, kv_spec, tab_spec, tab_spec, whole((heads * rows, 1)), whole((1, n_keys))],
             out_specs=[q_spec] * 4),
-        compiler_params=pltpu.CompilerParams(dimension_semantics=("arbitrary",), vmem_limit_bytes=40 << 20),
+        compiler_params=pltpu.CompilerParams(dimension_semantics=("arbitrary",), vmem_limit_bytes=30 << 20),
         cost_estimate=pl.CostEstimate(flops=flops, bytes_accessed=batch * rows * width * 16 + kv_all.size * 2, transcendentals=batch * rows * heads * 2 * n_keys),
         name="attn_fwd",
     )(*scalars, q_own, q_oth, kv_all, cos_t, sin_t, qpos_col, kpos[None, :])
@@ -165,19 +165,18 @@
     tab_spec = pl.BlockSpec((rows, two_hd // 4), lambda b, *_: (0, 0))
     q_spec = pl.BlockSpec((1, rows, width), lambda b, *_: (b + first, 0, 0))
     kv_spec = pl.BlockSpec((shards, 1, rows, two_hd), lambda b, *_: (0, b + first, 0, 0))
-    dkv_spec = pl.BlockSpec((shards // 2, 1, rows, two_hd), lambda b, *_: (0, b + first, 0, 0))
     heads = width * 2 // two_hd
     out = jax.ShapeDtypeStruct((batch, rows, width), BF16)
-    kv_out = jax.ShapeDtypeStruct((shards // 2, batch, rows, two_hd), BF16)
+    kv_out = jax.ShapeDtypeStruct(kv_all.shape, BF16)
     qpos_row = jnp.tile(qpos, heads)[None, :]
     n_keys = kpos.shape[0]
     flops = 2 * 5 * count * rows * 2 * width * n_keys
     return order.call(
         functools.partial(attn_bwd_kernel, first), 9, len(earlier), prefetch=3,
-        out_shape=(out, out, kv_out, kv_out), grid=(count,),
+        out_shape=(out, out, kv_out), grid=(count,),
         in_specs=[q_spec, q_spec, q_spec, q_spec, kv_spec, tab_spec, tab_spec, whole((1, heads * rows)), whole((n_keys, 1))],
-        out_specs=[q_spec, q_spec, dkv_spec, dkv_spec],
-        compiler_params=pltpu.CompilerParams(dimension_semantics=("arbitrary",), vmem_limit_bytes=40 << 20),
+        out_specs=[q_spec, q_spec, kv_spec],
+        compiler_params=pltpu.CompilerParams(dimension_semantics=("arbitrary",), vmem_limit_bytes=30 << 20),
         cost_estimate=pl.CostEstimate(flops=flops, bytes_accessed=count * rows * width * 12 + kv_all.size * 4, transcendentals=count * rows * heads * 2 * n_keys),
         name="attn_bwd",
     )(*scalars, q_own, q_oth, g_own, g_oth, kv_all, cos_t, sin_t, qpos_row, kpos[:, None], *earlier)
@@ -187,17 +186,20 @@
     def __init__(self):
         self.last = None
 
-    def call(self, kernel, n_in, n_kept=0, *, in_specs, out_specs, grid, prefetch=0, scratch_shapes=(), **options):
+    def call(self, kernel, n_in, n_kept=0, *, in_specs, out_specs, out_shape, grid, prefetch=0, scratch_shapes=(), **options):
         def run(*args):
             deps = () if self.last is None or any(self.last is a for a in args) else (self.last,)
+            args = args[:prefetch] + tuple(pltpu.with_memory_space_constraint(a, pltpu.HBM) if a.size >= LARGE else a for a in args[prefetch:])
             n_args = prefetch + n_in
 
             def body(*refs):
                 kernel(*refs[:n_args], *refs[n_args + n_kept + len(deps):])
 
-            n_out = len(out_specs) if isinstance(out_specs, (list, tuple)) else 1
+            single = not isinstance(out_specs, (list, tuple))
+            n_out = 1 if single else len(out_specs)
+            shapes = [pltpu.HBM(o.shape, o.dtype) if o.size >= LARGE else o for o in ([out_shape] if single else out_shape)]
             out = pl.pallas_call(
-                body,
+                body, out_shape=shapes[0] if single else shapes,
                 grid_spec=pltpu.PrefetchScalarGridSpec(
                     num_scalar_prefetch=prefetch, grid=grid, scratch_shapes=scratch_shapes, out_specs=out_specs,
                     in_specs=in_specs + [pl.BlockSpec(memory_space=pl.ANY)] * (n_kept + len(deps))),
@@ -278,60 +280,93 @@
     )(core, *args)
 
 
-def back_kernel(dg_hbm, du_hbm, act_hbm, wg_ref, wu_ref, wd_ref, *refs, joined, base):
-    *refs, dg_buf, du_buf, act_buf, sems = refs
-    far, out = (refs[:len(refs) // 2], refs[len(refs) // 2:]) if len(refs) == 2 * (1 if joined else 2) else ((), refs)
+def back_kernel(*refs, terms, joined, n_far, base, tn):
+    n = len(terms)
+    lhs, rhs, far, out = refs[:n], refs[n:2 * n], refs[2 * n:2 * n + n_far], refs[2 * n + n_far]
+    l_bufs, r_bufs, (l_sems, r_sems) = refs[2 * n + n_far + 1:][:n], refs[3 * n + n_far + 1:][:n], refs[4 * n + n_far + 1:]
     j, i = pl.program_id(0), pl.program_id(1)
-    rows = dg_buf.shape[1]
-
-    def copies(at):
-        return [pltpu.make_async_copy(src.at[pl.ds((base + at) * rows, rows)], buf.at[at], sems.at[k, at])
-                for k, (src, buf) in enumerate(((dg_hbm, dg_buf), (du_hbm, du_buf), (act_hbm, act_buf)))]
+    blocks, rows = l_bufs[0].shape[:2]
+
+    def left(p, at):
+        return pltpu.make_async_copy(lhs[p].at[pl.ds((base + at) * rows, rows)], l_bufs[p].at[at], l_sems.at[p, at])
+
+    def right(p, tile):
+        cols = pl.ds(pl.multiple_of(tile * tn, tn), tn)
+        src = rhs[p].at[:, cols] if terms[p][0] == 0 else rhs[p].at[cols]
+        return pltpu.make_async_copy(src, r_bufs[p].at[lax.rem(tile, 2)], r_sems.at[p, lax.rem(tile, 2)])
 
     @pl.when((j == 0) & (i == 0))
     def _():
-        for at in range(dg_buf.shape[0]):
-            for copy in copies(at):
-                copy.start()
+        for p in range(n):
+            right(p, 0).start()
+            left(p, 0).start()
+        for at in range(1, blocks):
+            for p in range(n):
+                left(p, at).start()
+
+    @pl.when((i == blocks - 1) & (j + 1 < pl.num_programs(0)))
+    def _():
+        for p in range(n):
+            right(p, j + 1).start()
+
+    def compute(ready):
+        totals = {}
+        for p, (dim, kind) in enumerate(terms):
+            ready(p)
+            part = dot_f32(l_bufs[p][i], r_bufs[p][lax.rem(j, 2)], 1, dim)
+            totals[kind] = totals[kind] + part if kind in totals else part
+        for kind, total in totals.items():
+            at = (slice(None), kind) if joined else (slice(None),)
+            total = total.reshape(out[at].shape)
+            if far:
+                total += far[0][at].astype(F32)
+            out[at] = total.astype(BF16)
 
     @pl.when(j == 0)
     def _():
-        for copy in copies(i):
-            copy.wait()
-
-    d_z = dot_f32(dg_buf[i], wg_ref[...], 1, 1) + dot_f32(du_buf[i], wu_ref[...], 1, 1)
-    mlp = dot_f32(act_buf[i], wd_ref[...], 1, 0)
-    for kind, total in enumerate((d_z, mlp)):
-        at = (slice(None), kind) if joined else (slice(None),)
-        dst = out[0 if joined else kind]
-        total = total.reshape(dst[at].shape)
-        if far:
-            total += far[0 if joined else kind][at].astype(F32)
-        dst[at] = total.astype(BF16)
-
-
-def back_call(order, side, d_gate, d_upper, act, w_gate, w_up, w_down, far, joined, chips, tn=512):
-    width, dim = w_down.shape
-    rows = act.shape[0] // (2 * chips)
-    half = chips // 2
+        def ready(p):
+            @pl.when(i == 0)
+            def _():
+                right(p, 0).wait()
+
+            left(p, i).wait()
+
+        compute(ready)
+
+    @pl.when(j > 0)
+    def _():
+        @pl.when(i == 0)
+        def _():
+            for p in range(n):
+                right(p, j).wait()
+
+        compute(lambda p: None)
+
+
+def back_call(order, side, lhs, rhs, terms, far, chips, tn=512):
+    dim = rhs[0].shape[0 if terms[0][0] else 1]
+    rows = lhs[0].shape[0] // (2 * chips)
+    half, n = chips // 2, len(terms)
+    kinds = sorted({kind for _, kind in terms})
+    joined = len(kinds) == 2
     hbm = pl.BlockSpec(memory_space=pl.ANY)
-    row_w = pl.BlockSpec((tn, width), lambda j, i: (j, 0))
-    if joined:
-        outs = (jax.ShapeDtypeStruct((chips, 2, rows, dim), BF16),)
-        tiles = [pl.BlockSpec((2, 2, rows, tn), lambda j, i: (i, 0, 0, j))]
-    else:
-        outs = (jax.ShapeDtypeStruct((chips, rows, dim), BF16),) * 2
-        tiles = [pl.BlockSpec((2, rows, tn), lambda j, i: (i, 0, j))] * 2
-    return order.call(
-        functools.partial(back_kernel, joined=joined, base=side * half), 6 + len(far), out_shape=outs, grid=(dim // tn, half),
-        in_specs=[hbm, hbm, hbm, row_w, row_w, pl.BlockSpec((width, tn), lambda j, i: (0, j))] + tiles[:len(far)],
-        out_specs=tiles, scratch_shapes=[pltpu.VMEM((half, 2 * rows, width), BF16)] * 3 + [pltpu.SemaphoreType.DMA((3, half))],
-        compiler_params=params(2, 50),
-        cost_estimate=cost(3 * act.size * dim, act, act, w_gate, w_up, w_down, *outs, *outs), name="mlp_back",
-    )(d_gate, d_upper, act, w_gate, w_up, w_down, *far)
-
-
-def wgrad_kernel(core_s, *refs, n, tf, tn, cols):
+    both = pl.BlockSpec((2, 2, rows, tn), lambda j, i: (i, 0, 0, j))
+    out = jax.ShapeDtypeStruct((chips, 2, rows, dim) if joined else (chips, rows, dim), BF16)
+    far_spec = both if joined else pl.BlockSpec((2, None, rows, tn), lambda j, i: (i, kinds[0], 0, j))
+    depth = lhs[0].shape[1]
+    return order.call(
+        functools.partial(back_kernel, terms=terms, joined=joined, n_far=len(far), base=side * half, tn=tn), 2 * n + len(far), out_shape=out,
+        grid=(dim // tn, half), in_specs=[hbm] * (2 * n) + [far_spec] * len(far),
+        out_specs=both if joined else pl.BlockSpec((2, rows, tn), lambda j, i: (i, 0, j)),
+        scratch_shapes=[pltpu.VMEM((half, 2 * rows, depth), BF16)] * n
+        + [pltpu.VMEM((2, depth, tn) if d == 0 else (2, tn, depth), BF16) for d, _ in terms]
+        + [pltpu.SemaphoreType.DMA((n, half)), pltpu.SemaphoreType.DMA((n, 2))],
+        compiler_params=params(2, 54),
+        cost_estimate=cost(n * lhs[0].size * dim, *lhs, *rhs, out), name="mlp_back",
+    )(*lhs, *rhs, *far)
+
+
+def wgrad_kernel(core_s, *refs, n, tf, tn, cols, first):
     lhs, rhs, out, l_buf, r_buf, sems = refs[:n], refs[n:2 * n], *refs[2 * n:]
     i, j, k = pl.program_id(0), pl.program_id(1), pl.program_id(2)
     step = (i * cols + j) * n + k
@@ -339,7 +374,7 @@
     chips = l_buf.shape[1] // 2
 
     def copies(s, at, p):
-        row = pl.multiple_of(lax.div(s, cols * n) * tf, tf)
+        row = pl.multiple_of((lax.div(s, cols * n) + first) * tf, tf)
         col = pl.multiple_of(lax.rem(lax.div(s, n), cols) * tn, tn)
         out = []
         for q, (ref, buf, lanes) in enumerate(((lhs[p], l_buf, pl.ds(row, tf)), (rhs[p], r_buf, pl.ds(col, tn)))):
@@ -372,20 +407,22 @@
     out[...] = jnp.where(k == 0, part, out[...] + part)
 
 
-def wgrad_call(order, core, lhs, rhs, tf=1024, tn=1024):
+def wgrad_call(order, core, lhs, rhs, tf=1024, tn=1024, tiles=None, earlier=None):
     n = len(lhs)
     rows = lhs[0].shape[-2]
     shards = lhs[0].size // (rows * lhs[0].shape[-1])
     width = rhs[0].shape[-1]
     height = lhs[0].shape[-1]
     cols = width // tn
+    first, last = tiles or (0, height // tf)
+    kept = () if earlier is None else (earlier,)
     out = jax.ShapeDtypeStruct((height, width), F32)
     return order.call(
-        functools.partial(wgrad_kernel, n=n, tf=tf, tn=tn, cols=cols), 2 * n, prefetch=1, out_shape=out, grid=(height // tf, cols, n),
-        in_specs=[pl.BlockSpec(memory_space=pl.ANY)] * (2 * n), out_specs=pl.BlockSpec((tf, tn), lambda i, j, k, core: (i, j)),
+        functools.partial(wgrad_kernel, n=n, tf=tf, tn=tn, cols=cols, first=first), 2 * n, len(kept), prefetch=1, out_shape=out, grid=(last - first, cols, n),
+        in_specs=[pl.BlockSpec(memory_space=pl.ANY)] * (2 * n), out_specs=pl.BlockSpec((tf, tn), lambda i, j, k, core: (i + first, j)),
         scratch_shapes=[pltpu.VMEM((2, shards, rows, tf), BF16), pltpu.VMEM((2, shards, rows, tn), BF16), pltpu.SemaphoreType.DMA((2, 2, 2))],
         compiler_params=params(3), cost_estimate=cost(2 * n * shards * rows * height * width, *lhs, *rhs, out), name="wgrad",
-    )(core, *lhs, *rhs)
+    )(core, *lhs, *rhs, *kept)
 
 
 def small_wgrad_kernel(l_ref, r_ref, *refs):
@@ -601,7 +638,7 @@
         wq_oth = swap(wq_own)
         q_own = dot_f32(normed_flat, wq_own, 1, 1)
         q_oth = dot_f32(normed_flat, wq_oth, 1, 1)
-        wo_own = gather4_direct(lax.optimization_barrier((w_out, q_own))[0], q_oth).reshape(chips * hd, dim)
+        wo_own = gather4_direct(w_out, (q_own, q_oth)).reshape(chips * hd, dim)
         wo_oth = swap(wo_own)
         q_own = q_own.reshape(batch, rows, chips * hd)
         q_oth = q_oth.reshape(batch, rows, chips * hd)
@@ -631,17 +668,21 @@
             return attn_bwd(order, q_own, q_oth, d_own.reshape(batch, rows, -1), d_oth.reshape(batch, rows, -1), kv_all, cos_t, sin_t, qpos, kpos,
                             scalars, first * per, count * per, () if earlier is None else earlier[2])
 
+        d_z_terms, mlp_terms = ((1, 0), (1, 0)), ((0, 1),)
+
+        def back_both(c, side, far):
+            return back_call(order, side, (acts[c][1], acts[c][2], acts[c][0]), weights, d_z_terms + mlp_terms, far, chips)
+
         def finish(c):
-            joined = c < CHUNKS - 1
-            parts = back_call(order, 0, acts[c][1], acts[c][2], acts[c][0], *weights, far[c], joined, chips)
-            sums = [scatter4(parts[0])]
-            if not joined:
-                sums.append(scatter4(parts[1]))
-            if joined:
-                both = sums[0].reshape(2, size, dim)
-                d_gated[c], mlp_sums[c] = both, both[1]
-            else:
-                d_gated[c], mlp_sums[c] = (a.reshape(size, dim) for a in sums)
+            both = back_both(c, 0, (far[c],))
+            both = scatter4(both).reshape(2, size, dim)
+            d_gated[c], mlp_sums[c] = both, both[1]
+
+        def finish_last(c):
+            part = back_call(order, 0, acts[c][1:], weights[:2], d_z_terms, (far[c],), chips)
+            d_gated[c] = scatter4(part).reshape(size, dim)
+            part = back_call(order, 0, acts[c][:1], weights[2:], mlp_terms, (far[c],), chips)
+            mlp_sums[c] = scatter4(part).reshape(size, dim)
 
         for c in range(CHUNKS):
             if c < CHUNKS - 1:
@@ -651,22 +692,20 @@
                 acts.append(act_call(order, core_1, z_all[c], g_all[c], *weights))
             if c > 0:
                 finish(c - 1)
-            joined = c < CHUNKS - 1
-            parts = back_call(order, 1, acts[c][1], acts[c][2], acts[c][0], *weights, (), joined, chips)
-            far.append(tuple(swap(a) for a in parts))
+            far.append(swap(back_both(c, 1, ())))
         terms, *d_parts = d_resid_of(0, 1, None)
         grads = terms, d_parts, attn_bwd_of(0, 1, d_parts[1], d_parts[2], None)
-        finish(CHUNKS - 1)
+        finish_last(CHUNKS - 1)
         hidden_out = (resid.astype(F32) + jnp.concatenate(mlp_sums, axis=0).astype(F32)).astype(BF16).reshape(batch, rows, dim)
         shards = [[a.reshape(2 * chips, size, -1) for a in acts[c]] for c in range(CHUNKS)]
-        g_gate = wgrad_call(order, core_1, z_all, [a[1] for a in shards])
+        g_gate = wgrad_call(order, core_1, z_all, [a[1] for a in shards], tiles=(0, 1))
 
         terms, d_resid, d_own, d_oth = d_resid_of(1, CHUNKS - 1, grads)
         g_out_far = swap(head_wgrad(order, mix_oth, d_resid, hd))
-        norm_terms, (dq_own, dq_oth, dkv_own, dkv_oth) = grads[0] + terms, attn_bwd_of(1, CHUNKS - 1, d_own, d_oth, grads)
+        norm_terms, (dq_own, dq_oth, dkv) = grads[0] + terms, attn_bwd_of(1, CHUNKS - 1, d_own, d_oth, grads)
         dq_own = dq_own.reshape(tokens, chips * hd)
         dq_oth = dq_oth.reshape(tokens, chips * hd)
-        dkv = scatter4((dkv_own.astype(F32) + swap(dkv_oth).astype(F32)).astype(BF16))
+        dkv = lax.psum_scatter(dkv.reshape(tp_size * batch, rows, 2 * hd), "tp", scatter_dimension=0, tiled=True)
         g_query_far = swap(head_wgrad(order, dq_oth, normed_flat, hd))
         g_heads = head_wgrad(order, mix_own, d_resid, hd, (g_out_far,), 0)
         g_heads = head_wgrad(order, dq_own, normed_flat, hd, (g_query_far,), 1, g_heads)
@@ -680,6 +719,7 @@
         norms = jnp.stack([jnp.sum(attn_terms, axis=0), jnp.sum(norm_terms, axis=0)]).reshape(-1, 2 * hd)
         sums = lax.psum(jnp.concatenate([g_kv, norms], axis=0), "tp")
         g_attn_norm, g_mlp_norm = sums[dim:].reshape(2, dim)
+        g_gate = wgrad_call(order, core_1, z_all, [a[1] for a in shards], tiles=(1, 2), earlier=g_gate)
         g_up = wgrad_call(order, core_1, z_all, [a[2] for a in shards])
         g_down = wgrad_call(order, core_1, [a[0] for a in shards], g_all)
         return (hidden_out, grad_hidden.reshape(batch, rows, dim), g_attn_norm, g_query, sums[:dim, :hd], sums[:dim, hd:], g_out, g_mlp_norm, g_gate, g_up, g_down)

time: 1420 us -> 1380 us (0.972)
  waiting for transfers between devices: 219 us -> 163 us
  Pallas kernels: 1040 us -> 1070 us
    reduce_scatter x6 -> x5, waiting for transfers between devices: 71.6 us -> 21.6 us  [scatter4(): lax.psum_scatter(flat, 'tp', scatter_dimension=0, tiled=True, axis_index_...]
    pallas_call x25 -> x27, Pallas kernels: 1020 us -> 1040 us  [run(): pl.pallas_call(body, out_shape=shapes[0] if single else shapes, grid_spec...]
    ppermute x8, waiting for transfers between devices: 104 us -> 87.4 us  [flip(): return lax.ppermute(x_loc, 'tp', [(i, i ^ bits) for i in range(tp_size)])]
    unnamed x132 -> x90, local copies, waits for them, and re-layouts: 41.4 us -> 34.8 us
  transfers between devices with their start and end apart: 31 -> 29, of which waited for: 14 -> 12; matrix products, arithmetic and copies ran while one was open for 5% -> 5% of each run, Pallas kernels for 70% -> 73%
where the time goes in v5:
time: 1380 us; the launch traced here: 1370 us
  Pallas kernels  1070 us (78%)
  waiting for transfers between devices  163 us (12%)
  local copies, waits for them, and re-layouts  72.7 us (5%)
  other arithmetic  23.1 us (2%)
  matrix products  18.2 us (1%)
  starting transfers between devices  16.3 us (1%)
  between operations  14.8 us (1%)
    pallas_call x27, Pallas kernels, run(): pl.pallas_call(body, out_shape=shapes[0] if single else shapes, grid_spec...  1040 us
    ppermute x8, waiting for transfers between devices, flip(): return lax.ppermute(x_loc, 'tp', [(i, i ^ bits) for i in range(tp_size)])  87.4 us
    unnamed x90, local copies, waits for them, and re-layouts  34.8 us
    all_gather x7, waiting for transfers between devices, gather8(): return lax.all_gather(x_loc, 'tp', axis=0, tiled=False)  32.1 us
  transfers between devices with their start and end apart: 29, of which 12 were waited for; matrix products, arithmetic and copies ran while one was open for 5% of the time, Pallas kernels for 73%

profile of v5, /device:TPU:0, one launch (start us, length us, event | category | flops | bytes accessed | tf_op | source)
XLA Modules:
  0.0 1373.5 jit_solution(13170587547316096285)
XLA Ops:
  29.2 37.0 %collective-permute-done = bf16[256,2048]{0,1:T(8,128)(2,1)S(1)} collective-permute-done((bf16[256,2048]{0,1:T(8,128)(2,1)}, bf16[256,2048]{0,1:T(8,128)(2,1)S(1)}, u32[]{:S(2)}, u32[]{:S(2)}) %collective-permute-start) | collective-permute-done | bytes 1048608 | tf_op jit(solution)/shard_map/ppermute | solution.py:598
  80.6 12.0 collective-permute-done.2
  121.0 15.0 %collective-permute-done.6 = bf16[256,2048]{1,0:T(8,128)(2,1)S(1)} collective-permute-done((bf16[256,2048]{1,0:T(8,128)(2,1)S(1)}, bf16[256,2048]{1,0:T(8,128)(2,1)S(1)}, u32[]{:S(2)}, u32[]{:S(2)}) %collective-permute-start.6) | collective-permute-done | bytes 1048608 | tf_op jit(solution)/shard_map/ppermute | solution.py:598
  144.4 14.0 %collective-permute-done.7 = bf16[128,2048]{1,0:T(8,128)(2,1)S(1)} collective-permute-done((bf16[128,2048]{1,0:T(8,128)(2,1)S(1)}, bf16[128,2048]{1,0:T(8,128)(2,1)S(1)}, u32[]{:S(2)}, u32[]{:S(2)}) %collective-permute-start.7) | collective-permute-done | bytes 524320 | tf_op jit(solution)/shard_map/ppermute | solution.py:598
  168.8 20.4 %attn_fwd.1 = (bf16[12,96,1024]{2,1,0:T(8,128)(2,1)S(1)}, bf16[12,96,1024]{2,1,0:T(8,128)(2,1)S(1)}, bf16[12,96,1024]{2,1,0:T(8,128)(2,1)S(1)}, bf16[12,96,1024]{2,1,0:T(8,128)(2,1)S(1)}) custom-call(s32[12]{0:T(128)S(1)} %copy-done.12, s32[12]{0:T(128)S(1)} %copy-done.14, s32[1]{0:T(128)} %bitcast.1.core_s.refs_0_.refs_2_, f32[12,96,1024]{2,1,0:T(8,128)S(1)} %bitcast.102, ...), custom_call_target="tpu_custom_call" | custom-call | flops 7247757312 | bytes 28311552 | tf_op jit(solution)/shard_map/attn_fwd/pallas_call | solution.py:149
  194.8 19.4 %resid.1 = (bf16[1152,2048]{1,0:T(8,128)(2,1)}, bf16[384,2048]{1,0:T(8,128)(2,1)}, bf16[384,2048]{1,0:T(8,128)(2,1)}, bf16[384,2048]{1,0:T(8,128)(2,1)}) custom-call(bf16[1152,2048]{1,0:T(8,128)(2,1)} %bitcast.116, bf16[1152,1024]{1,0:T(8,128)(2,1)} %bitcast.95, bf16[1152,1024]{1,0:T(8,128)(2,1)} %bitcast.104, ...), custom_call_target="tpu_custom_call" | custom-call | flops 9663676416 | bytes 27262976 | tf_op jit(solution)/shard_map/resid/pallas_call | solution.py:201
  216.8 33.3 %d_act.2.refs_2_ = bf16[3072,2048]{1,0:T(8,128)(2,1)} custom-call(s32[1]{0:T(128)} %bitcast.1.core_s.refs_0_.refs_2_, bf16[4,2,384,2048]{3,2,1,0:T(8,128)(2,1)} %bitcast.142, bf16[2048,2048]{1,0:T(8,128)(2,1)} %refs_1_.4, bf16[1152,2048]{1,0:T(8,128)(2,1)} %get-tuple-element.50.refs_3_.refs_1_.refs_2_), custom_call_target="tpu_custom_call" | custom-call | flops 25769803776 | bytes 33554432 | tf_op jit(solution)/shard_map/d_act/pallas_call | solution.py:201
  250.2 32.1 %all-gather.19.cloned.1.call-done = bf16[3072,2048]{1,0:T(8,128)(2,1)} async-done(((bf16[384,2048]{1,0:T(8,128)(2,1)}), bf16[3072,2048]{1,0:T(8,128)(2,1)}) %all-gather.19.cloned.1.call-update) | async-done | bytes 12582928 | tf_op jit(solution)/shard_map/all_gather | solution.py:592
  282.2 70.6 %mlp_act.3 = (bf16[3072,2048]{1,0:T(8,128)(2,1)}, bf16[3072,2048]{1,0:T(8,128)(2,1)}, bf16[3072,2048]{1,0:T(8,128)(2,1)}) custom-call(s32[1]{0:T(128)} %bitcast.1.core_s.refs_0_.refs_2_, bf16[4,2,384,2048]{3,2,1,0:T(8,128)(2,1)} %bitcast.144, bf16[3072,2048]{1,0:T(8,128)(2,1)} %d_act.2.refs_2_, bf16[2048,2048]{1,0:T(8,128)(2,1)} %refs_2_.5, ...), custom_call_target="tpu_custom_call" | custom-call | flops 51539607552 | bytes 79691776 | tf_op jit(solution)/shard_map/mlp_act/pallas_call | solution.py:201
  352.8 47.1 %mlp_back.7.refs_3_ = bf16[4,2,384,2048]{3,2,1,0:T(8,128)(2,1)} custom-call(bf16[3072,2048]{1,0:T(8,128)(2,1)} %get-tuple-element.52.refs_0_, bf16[3072,2048]{1,0:T(8,128)(2,1)} %get-tuple-element.53.refs_1_, bf16[3072,2048]{1,0:T(8,128)(2,1)} %get-tuple-element.54.refs_2_, bf16[2048,2048]{1,0:T(8,128)(2,1)} %refs_2_.5, bf16[2048,2048]{1,0:T(8,128)(2,1)} %refs_3_.17, ...), custom_call_target="tpu_custom_call" | custom-call | flops 38654705664 | bytes 75497472 | tf_op jit(solution)/shard_map/mlp_back/pallas_call | solution.py:201
  400.0 32.5 %d_act.3.refs_2_ = bf16[3072,2048]{1,0:T(8,128)(2,1)} custom-call(s32[1]{0:T(128)} %bitcast.1.core_s.refs_0_.refs_2_, bf16[4,2,384,2048]{3,2,1,0:T(8,128)(2,1)} %bitcast.148, bf16[2048,2048]{1,0:T(8,128)(2,1)} %refs_1_.4, bf16[4,2,384,2048]{3,2,1,0:T(8,128)(2,1)} %mlp_back.7.refs_3_), custom_call_target="tpu_custom_call" | custom-call | flops 25769803776 | bytes 33554432 | tf_op jit(solution)/shard_map/d_act/pallas_call | solution.py:201
  432.6 73.3 %mlp_act.4 = (bf16[3072,2048]{1,0:T(8,128)(2,1)}, bf16[3072,2048]{1,0:T(8,128)(2,1)}, bf16[3072,2048]{1,0:T(8,128)(2,1)}) custom-call(s32[1]{0:T(128)} %bitcast.1.core_s.refs_0_.refs_2_, bf16[4,2,384,2048]{3,2,1,0:T(8,128)(2,1)} %bitcast.150, bf16[3072,2048]{1,0:T(8,128)(2,1)} %d_act.3.refs_2_, bf16[2048,2048]{1,0:T(8,128)(2,1)} %refs_2_.5, ...), custom_call_target="tpu_custom_call" | custom-call | flops 51539607552 | bytes 79691776 | tf_op jit(solution)/shard_map/mlp_act/pallas_call | solution.py:201
  505.9 49.2 %mlp_back.8.refs_6_ = bf16[4,2,384,2048]{3,2,1,0:T(8,128)(2,1)} custom-call(bf16[3072,2048]{1,0:T(8,128)(2,1)} %get-tuple-element.52.refs_0_, bf16[3072,2048]{1,0:T(8,128)(2,1)} %get-tuple-element.53.refs_1_, bf16[3072,2048]{1,0:T(8,128)(2,1)} %get-tuple-element.54.refs_2_, bf16[2048,2048]{1,0:T(8,128)(2,1)} %refs_2_.5, bf16[2048,2048]{1,0:T(8,128)(2,1)} %refs_3_.17, ...), custom_call_target="tpu_custom_call" | custom-call | flops 38654705664 | bytes 75497472 | tf_op jit(solution)/shard_map/mlp_back/pallas_call | solution.py:201
  555.2 47.4 %mlp_back.9.refs_6_ = bf16[4,2,384,2048]{3,2,1,0:T(8,128)(2,1)} custom-call(bf16[3072,2048]{1,0:T(8,128)(2,1)} %get-tuple-element.57.refs_0_, bf16[3072,2048]{1,0:T(8,128)(2,1)} %get-tuple-element.58.refs_1_, bf16[3072,2048]{1,0:T(8,128)(2,1)} %get-tuple-element.56.refs_7_.refs_2_, bf16[2048,2048]{1,0:T(8,128)(2,1)} %refs_2_.5, bf16[2048,2048]{1,0:T(8,128)(2,1)} %refs_3_.17, ...), custom_call_target="tpu_custom_call" | custom-call | flops 38654705664 | bytes 75497472 | tf_op jit(solution)/shard_map/mlp_back/pallas_call | solution.py:201
  602.9 91.8 %mlp_act.5 = (bf16[3072,2048]{1,0:T(8,128)(2,1)}, bf16[3072,2048]{1,0:T(8,128)(2,1)}, bf16[3072,2048]{1,0:T(8,128)(2,1)}) custom-call(s32[1]{0:T(128)} %bitcast.1.core_s.refs_0_.refs_2_, bf16[4,2,384,2048]{3,2,1,0:T(8,128)(2,1)} %bitcast.156, bf16[4,2,384,2048]{3,2,1,0:T(8,128)(2,1)} %bitcast.154, bf16[2048,2048]{1,0:T(8,128)(2,1)} %refs_2_.5, ...), custom_call_target="tpu_custom_call" | custom-call | flops 77309411328 | bytes 88080384 | tf_op jit(solution)/shard_map/mlp_act/pallas_call | solution.py:201
  694.7 49.6 %mlp_back.10.refs_6_ = bf16[4,2,384,2048]{3,2,1,0:T(8,128)(2,1)} custom-call(bf16[3072,2048]{1,0:T(8,128)(2,1)} %get-tuple-element.57.refs_0_, bf16[3072,2048]{1,0:T(8,128)(2,1)} %get-tuple-element.58.refs_1_, bf16[3072,2048]{1,0:T(8,128)(2,1)} %get-tuple-element.56.refs_7_.refs_2_, bf16[2048,2048]{1,0:T(8,128)(2,1)} %refs_2_.5, ...), custom_call_target="tpu_custom_call" | custom-call | flops 38654705664 | bytes 75497472 | tf_op jit(solution)/shard_map/mlp_back/pallas_call | solution.py:201
  744.5 47.8 %mlp_back.11.refs_6_ = bf16[4,2,384,2048]{3,2,1,0:T(8,128)(2,1)} custom-call(bf16[3072,2048]{1,0:T(8,128)(2,1)} %get-tuple-element.61.refs_0_, bf16[3072,2048]{1,0:T(8,128)(2,1)} %get-tuple-element.62.refs_1_, bf16[3072,2048]{1,0:T(8,128)(2,1)} %get-tuple-element.60.refs_7_.refs_2_.refs_0_, bf16[2048,2048]{1,0:T(8,128)(2,1)} %refs_2_.5, ...), custom_call_target="tpu_custom_call" | custom-call | flops 38654705664 | bytes 75497472 | tf_op jit(solution)/shard_map/mlp_back/pallas_call | solution.py:201
  804.4 15.0 %attn_bwd.2 = (bf16[12,96,1024]{2,1,0:T(8,128)(2,1)}, bf16[12,96,1024]{2,1,0:T(8,128)(2,1)}, bf16[8,12,96,512]{3,2,1,0:T(8,128)(2,1)}) custom-call(s32[12]{0:T(128)S(1)} %copy-done.13, s32[12]{0:T(128)S(1)} %copy-done.15, s32[1]{0:T(128)} %bitcast.1.core_s.refs_0_.refs_2_, bf16[12,96,1024]{2,1,0:T(8,128)(2,1)} %copy-done.19, ...), custom_call_target="tpu_custom_call" | custom-call | flops 6039797760 | bytes 23592960 | tf_op jit(solution)/shard_map/attn_bwd/pallas_call | solution.py:201
  819.3 35.6 %mlp_back.12.refs_3_ = bf16[4,384,2048]{2,1,0:T(8,128)(2,1)} custom-call(bf16[3072,2048]{1,0:T(8,128)(2,1)} %get-tuple-element.61.refs_0_, bf16[3072,2048]{1,0:T(8,128)(2,1)} %get-tuple-element.62.refs_1_, bf16[2048,2048]{1,0:T(8,128)(2,1)} %refs_2_.5, bf16[2048,2048]{1,0:T(8,128)(2,1)} %refs_3_.17, ...), custom_call_target="tpu_custom_call" | custom-call | flops 25769803776 | bytes 48234496 | tf_op jit(solution)/shard_map/mlp_back/pallas_call | solution.py:201
  855.0 20.8 %mlp_back.13.refs_7_ = bf16[4,384,2048]{2,1,0:T(8,128)(2,1)} custom-call(bf16[3072,2048]{1,0:T(8,128)(2,1)} %get-tuple-element.60.refs_7_.refs_2_.refs_0_, bf16[2048,2048]{1,0:T(8,128)(2,1)} %refs_1_.4, bf16[4,2,384,2048]{3,2,1,0:T(8,128)(2,1)} %collective-permute-done.12.refs_4_.refs_2_, bf16[4,384,2048]{2,1,0:T(8,128)(2,1)} %mlp_back.12.refs_3_), custom_call_target="tpu_custom_call" | custom-call | flops 12884901888 | bytes 27262976 | tf_op jit(solution)/shard_map/mlp_back/pallas_call | solution.py:201
  875.8 48.1 %wgrad.4.refs_10_.refs_7_ = f32[2048,2048]{1,0:T(8,128)} custom-call(s32[1]{0:T(128)} %bitcast.1.core_s.refs_0_.refs_2_, bf16[4,2,384,2048]{3,2,1,0:T(8,128)(2,1)} %bitcast.145, bf16[4,2,384,2048]{3,2,1,0:T(8,128)(2,1)} %bitcast.151, bf16[4,2,384,2048]{3,2,1,0:T(8,128)(2,1)} %bitcast.157, bf16[8,384,2048]{2,1,0:T(8,128)(2,1)} %bitcast.162, ...), custom_call_target="tpu_custom_call" | custom-call | flops 77309411328 | bytes 92274688 | tf_op jit(solution)/shard_map/wgrad/pallas_call | solution.py:201
  926.8 18.4 %d_resid.3 = (f32[8,2048]{1,0:T(8,128)S(1)}, bf16[1152,2048]{1,0:T(8,128)(2,1)}, bf16[1152,1024]{1,0:T(8,128)(2,1)}, bf16[1152,1024]{1,0:T(8,128)(2,1)}) custom-call(bf16[2,384,2048]{2,1,0:T(8,128)(2,1)} %reduce-scatter.9.cloned.1.call-done.refs_0_, ...), custom_call_target="tpu_custom_call", output_to_operand_aliasing={{1}: (7, {}), {2}: (8, {}), {3}: (9, {})} | custom-call | flops 6442450944 | bytes 17825792 | tf_op jit(solution)/shard_map/d_resid/pallas_call | solution.py:201
  960.0 26.1 %attn_bwd.3 = (bf16[12,96,1024]{2,1,0:T(8,128)(2,1)}, bf16[12,96,1024]{2,1,0:T(8,128)(2,1)}, bf16[8,12,96,512]{3,2,1,0:T(8,128)(2,1)}) custom-call(s32[12]{0:T(128)S(1)} %copy-done.13, s32[12]{0:T(128)S(1)} %copy-done.15, s32[1]{0:T(128)} %bitcast.1.core_s.refs_0_.refs_2_, ...), custom_call_target="tpu_custom_call", output_to_operand_aliasing={{0}: (12, {}), {1}: (13, {}), {2}: (14, {})} | custom-call | flops 12079595520 | bytes 28311552 | tf_op jit(solution)/shard_map/attn_bwd/pallas_call | solution.py:201
  987.8 12.9 head_wgrad.5.refs_3_
  1013.9 13.3 head_wgrad.6.refs_3_
  1030.5 13.0 head_wgrad.7.refs_9_
  1043.5 13.0 reduce-scatter.15.cloned.1.call-done
  1059.2 25.9 %d_hidden.1 = (bf16[1152,2048]{1,0:T(8,128)(2,1)}, f32[8,2048]{1,0:T(8,128)}) custom-call(bf16[1152,1024]{1,0:T(8,128)(2,1)} %bitcast.98, bf16[1152,1024]{1,0:T(8,128)(2,1)} %bitcast.173, bf16[1152,512]{1,0:T(8,128)(2,1)} %bitcast.128, bf16[1152,2048]{1,0:T(8,128)(2,1)} %bitcast.117, bf16[1152,2048]{1,0:T(8,128)(2,1)} %get-tuple-element.74.refs_1_.refs_4_, ...), custom_call_target="tpu_custom_call" | custom-call | flops 14495514624 | bytes 27328512 | tf_op jit(solution)/shard_map/d_hidden/pallas_call | solution.py:201
  1105.1 18.7 %reduce-scatter.11.cloned.1.call-done = bf16[384,2048]{1,0:T(8,128)(2,1)} async-done(((bf16[1536,2048]{1,0:T(8,128)(2,1)}), bf16[384,2048]{1,0:T(8,128)(2,1)}) %reduce-scatter.11.cloned.1.call-update) | async-done | bytes 1572880 | tf_op jit(solution)/shard_map/reduce_scatter | solution.py:589
  1129.8 47.4 %wgrad.5.refs_7_ = f32[2048,2048]{1,0:T(8,128)} custom-call(s32[1]{0:T(128)} %bitcast.1.core_s.refs_0_.refs_2_, bf16[4,2,384,2048]{3,2,1,0:T(8,128)(2,1)} %bitcast.146, bf16[4,2,384,2048]{3,2,1,0:T(8,128)(2,1)} %bitcast.152, bf16[4,2,384,2048]{3,2,1,0:T(8,128)(2,1)} %bitcast.158, bf16[8,384,2048]{2,1,0:T(8,128)(2,1)} %bitcast.163, ...), custom_call_target="tpu_custom_call", output_to_operand_aliasing={{}: (7, {})} | custom-call | flops 77309411328 | bytes 92274688 | tf_op jit(solution)/shard_map/wgrad/pallas_call | solution.py:201
  1177.2 88.7 %wgrad.6.refs_7_ = f32[2048,2048]{1,0:T(8,128)} custom-call(s32[1]{0:T(128)} %bitcast.1.core_s.refs_0_.refs_2_, bf16[4,2,384,2048]{3,2,1,0:T(8,128)(2,1)} %bitcast.147, bf16[4,2,384,2048]{3,2,1,0:T(8,128)(2,1)} %bitcast.153, bf16[4,2,384,2048]{3,2,1,0:T(8,128)(2,1)} %bitcast.159, bf16[8,384,2048]{2,1,0:T(8,128)(2,1)} %bitcast.161, ...), custom_call_target="tpu_custom_call" | custom-call | flops 77309411328 | bytes 92274688 | tf_op jit(solution)/shard_map/wgrad/pallas_call | solution.py:201
  1265.9 88.6 %wgrad.7 = f32[2048,2048]{1,0:T(8,128)} custom-call(s32[1]{0:T(128)} %bitcast.1.core_s.refs_0_.refs_2_, bf16[8,384,2048]{2,1,0:T(8,128)(2,1)} %bitcast.160, bf16[8,384,2048]{2,1,0:T(8,128)(2,1)} %bitcast.164, bf16[8,384,2048]{2,1,0:T(8,128)(2,1)} %bitcast.168, bf16[4,2,384,2048]{3,2,1,0:T(8,128)(2,1)} %bitcast.143, bf16[4,2,384,2048]{3,2,1,0:T(8,128)(2,1)} %bitcast.149, ...), custom_call_target="tpu_custom_call" | custom-call | flops 77309411328 | bytes 92274688 | tf_op jit(solution)/shard_map/wgrad/pallas_call | solution.py:201
  (223 shorter events, 180.6 us)
Async XLA Ops:
  7.2 156.9 %all-gather.11.cloned.1.call-start = ((), (), s32[]{:S(2)}) async-start(), calls=%async_computation.6 | async-start | bytes 10616832 | tf_op jit(solution)/shard_map/all_gather | solution.py:592
  16.5 940.2 %copy-start.4 = (f32[96,128]{1,0:T(8,128)}, f32[96,128]{1,0:T(8,128)S(1)}, u32[]{:S(2)}) copy-start(f32[96,128]{1,0:T(8,128)S(1)} %get-tuple-element.129.cos_ref.refs_8_) | copy-start | bytes 147460
  16.5 940.1 %copy-start.6 = (f32[96,128]{1,0:T(8,128)}, f32[96,128]{1,0:T(8,128)S(1)}, u32[]{:S(2)}) copy-start(f32[96,128]{1,0:T(8,128)S(1)} %get-tuple-element.130.sin_ref.refs_9_) | copy-start | bytes 147460
  17.8 199.0 %all-gather.13.cloned.1.call-start = ((), (), s32[]{:S(2)}) async-start(), calls=%async_computation.7 | async-start | bytes 14155776 | tf_op jit(solution)/shard_map/all_gather | solution.py:592
  22.6 259.7 %all-gather.19.cloned.1.call-start = ((), (), s32[]{:S(2)}) async-start(), calls=%async_computation.17 | async-start | bytes 14155776 | tf_op jit(solution)/shard_map/all_gather | solution.py:592
  22.8 43.4 %collective-permute-start = (bf16[256,2048]{0,1:T(8,128)(2,1)}, bf16[256,2048]{0,1:T(8,128)(2,1)S(1)}, u32[]{:S(2)}, u32[]{:S(2)}) collective-permute-start(bf16[256,2048]{0,1:T(8,128)(2,1)} %bitcast.3), channel_id=1, source_target_pairs={{0,2},{1,3},{2,0},{3,1},{4,6},{5,7},{6,4},{7,5}} | collective-permute-start | bytes 3145736 | tf_op jit(solution)/shard_map/ppermute | solution.py:598
  26.1 42.8 %collective-permute-start.1 = (bf16[256,2048]{0,1:T(8,128)(2,1)}, bf16[256,2048]{0,1:T(8,128)(2,1)}, u32[]{:S(2)}, u32[]{:S(2)}) collective-permute-start(bf16[256,2048]{0,1:T(8,128)(2,1)} %bitcast.3), channel_id=1, source_target_pairs={{0,4},{1,5},{2,6},{3,7},{4,0},{5,1},{6,2},{7,3}} | collective-permute-start | bytes 3145736 | tf_op jit(solution)/shard_map/ppermute | solution.py:598
  67.0 25.5 %collective-permute-start.2 = (bf16[128,2048]{0,1:T(8,128)(2,1)}, bf16[128,2048]{0,1:T(8,128)(2,1)S(1)}, u32[]{:S(2)}, u32[]{:S(2)}) collective-permute-start(bf16[128,2048]{0,1:T(8,128)(2,1)} %slice.84), channel_id=1, source_target_pairs={{0,4},{1,5},{2,6},{3,7},{4,0},{5,1},{6,2},{7,3}} | collective-permute-start | bytes 1572872 | tf_op jit(solution)/shard_map/ppermute | solution.py:598
  70.8 25.5 %collective-permute-start.3 = (bf16[128,2048]{0,1:T(8,128)(2,1)}, bf16[128,2048]{0,1:T(8,128)(2,1)}, u32[]{:S(2)}, u32[]{:S(2)}) collective-permute-start(bf16[128,2048]{0,1:T(8,128)(2,1)} %slice.85), channel_id=1, source_target_pairs={{0,2},{1,3},{2,0},{3,1},{4,6},{5,7},{6,4},{7,5}} | collective-permute-start | bytes 1572872 | tf_op jit(solution)/shard_map/ppermute | solution.py:598
  99.3 15.0 %collective-permute-start.4 = (bf16[1024,2048]{1,0:T(8,128)(2,1)}, bf16[1024,2048]{1,0:T(8,128)(2,1)S(1)}, u32[]{:S(2)}, u32[]{:S(2)}) collective-permute-start(bf16[1024,2048]{1,0:T(8,128)(2,1)} %bitcast.9.refs_6_), channel_id=1, source_target_pairs={{0,1},{1,0},{2,3},{3,2},{4,5},{5,4},{6,7},{7,6}} | collective-permute-start | bytes 12582920 | tf_op jit(solution)/shard_map/ppermute | solution.py:595
  99.3 36.8 %collective-permute-start.6 = (bf16[256,2048]{1,0:T(8,128)(2,1)S(1)}, bf16[256,2048]{1,0:T(8,128)(2,1)S(1)}, u32[]{:S(2)}, u32[]{:S(2)}) collective-permute-start(bf16[256,2048]{1,0:T(8,128)(2,1)S(1)} %copy-done.27), channel_id=1, source_target_pairs={{0,4},{1,5},{2,6},{3,7},{4,0},{5,1},{6,2},{7,3}} | collective-permute-start | bytes 3145736 | tf_op jit(solution)/shard_map/ppermute | solution.py:598
  100.6 38.4 %collective-permute-start.5 = (bf16[256,2048]{1,0:T(8,128)(2,1)S(1)}, bf16[256,2048]{1,0:T(8,128)(2,1)S(1)}, u32[]{:S(2)}, u32[]{:S(2)}) collective-permute-start(bf16[256,2048]{1,0:T(8,128)(2,1)S(1)} %copy-done.27), channel_id=1, source_target_pairs={{0,2},{1,3},{2,0},{3,1},{4,6},{5,7},{6,4},{7,5}} | collective-permute-start | bytes 3145736 | tf_op jit(solution)/shard_map/ppermute | solution.py:598
  139.0 19.4 %collective-permute-start.7 = (bf16[128,2048]{1,0:T(8,128)(2,1)S(1)}, bf16[128,2048]{1,0:T(8,128)(2,1)S(1)}, u32[]{:S(2)}, u32[]{:S(2)}) collective-permute-start(bf16[128,2048]{1,0:T(8,128)(2,1)S(1)} %slice.71), channel_id=1, source_target_pairs={{0,4},{1,5},{2,6},{3,7},{4,0},{5,1},{6,2},{7,3}} | collective-permute-start | bytes 1572872 | tf_op jit(solution)/shard_map/ppermute | solution.py:598
  140.8 21.3 %collective-permute-start.8 = (bf16[128,2048]{1,0:T(8,128)(2,1)S(1)}, bf16[128,2048]{1,0:T(8,128)(2,1)S(1)}, u32[]{:S(2)}, u32[]{:S(2)}) collective-permute-start(bf16[128,2048]{1,0:T(8,128)(2,1)S(1)} %slice.72), channel_id=1, source_target_pairs={{0,2},{1,3},{2,0},{3,1},{4,6},{5,7},{6,4},{7,5}} | collective-permute-start | bytes 1572872 | tf_op jit(solution)/shard_map/ppermute | solution.py:598
  163.0 31.9 %collective-permute-start.9 = (bf16[1024,2048]{1,0:T(8,128)(2,1)}, bf16[1024,2048]{1,0:T(8,128)(2,1)}, u32[]{:S(2)}, u32[]{:S(2)}) collective-permute-start(bf16[1024,2048]{1,0:T(8,128)(2,1)} %bitcast.23.refs_3_.refs_4_.refs_5_), channel_id=1, source_target_pairs={{0,1},{1,0},{2,3},{3,2},{4,5},{5,4},{6,7},{7,6}} | collective-permute-start | bytes 12582920 | tf_op jit(solution)/shard_map/ppermute | solution.py:595
  214.2 185.8 %all-gather.15.cloned.1.call-start = ((), (), s32[]{:S(2)}) async-start(), calls=%async_computation.8 | async-start | bytes 14155776 | tf_op jit(solution)/shard_map/all_gather | solution.py:592
  214.8 217.8 %all-gather.21.cloned.1.call-start = ((), (), s32[]{:S(2)}) async-start(), calls=%async_computation.18 | async-start | bytes 14155776 | tf_op jit(solution)/shard_map/all_gather | solution.py:592
  215.4 387.5 %all-gather.17.cloned.1.call-start = ((), (), s32[]{:S(2)}) async-start(), calls=%async_computation.10 | async-start | bytes 14155776 | tf_op jit(solution)/shard_map/all_gather | solution.py:592
  216.0 386.9 %all-gather.23.cloned.1.call-start = ((), (), s32[]{:S(2)}) async-start(), calls=%async_computation.19 | async-start | bytes 14155776 | tf_op jit(solution)/shard_map/all_gather | solution.py:592
  216.7 576.5 %reduce-scatter.7.cloned.1.call-start = ((), (), s32[]{:S(2)}) async-start(), calls=%async_computation.9 | async-start | bytes 15728640 | tf_op jit(solution)/shard_map/reduce_scatter | solution.py:589
  400.0 106.0 %collective-permute-start.10 = (bf16[4,2,384,2048]{3,2,1,0:T(8,128)(2,1)}, bf16[4,2,384,2048]{3,2,1,0:T(8,128)(2,1)}, u32[]{:S(2)}, u32[]{:S(2)}) collective-permute-start(bf16[4,2,384,2048]{3,2,1,0:T(8,128)(2,1)} %mlp_back.7.refs_3_), channel_id=1, source_target_pairs={{0,1},{1,0},{2,3},{3,2},{4,5},{5,4},{6,7},{7,6}} | collective-permute-start | bytes 37748744 | tf_op jit(solution)/shard_map/ppermute | solution.py:595
  555.1 368.8 %reduce-scatter.9.cloned.1.call-start = ((), (), s32[]{:S(2)}) async-start(), calls=%async_computation.11 | async-start | bytes 15728640 | tf_op jit(solution)/shard_map/reduce_scatter | solution.py:589
  602.6 92.1 %collective-permute-start.11 = (bf16[4,2,384,2048]{3,2,1,0:T(8,128)(2,1)}, bf16[4,2,384,2048]{3,2,1,0:T(8,128)(2,1)}, u32[]{:S(2)}, u32[]{:S(2)}) collective-permute-start(bf16[4,2,384,2048]{3,2,1,0:T(8,128)(2,1)} %mlp_back.9.refs_6_), channel_id=1, source_target_pairs={{0,1},{1,0},{2,3},{3,2},{4,5},{5,4},{6,7},{7,6}} | collective-permute-start | bytes 37748744 | tf_op jit(solution)/shard_map/ppermute | solution.py:595
  744.4 182.4 %reduce-scatter.13.cloned.1.call-start = ((), (), s32[]{:S(2)}) async-start(), calls=%async_computation.13 | async-start | bytes 7864320 | tf_op jit(solution)/shard_map/reduce_scatter | solution.py:589
  744.5 48.8 %copy-start.8 = (f32[2048]{0:T(1024)S(1)}, f32[2048]{0:T(1024)}, u32[]{:S(2)}) copy-start(f32[2048]{0:T(1024)} %broadcast_in_dim.77) | copy-start | bytes 24580
  792.3 27.0 %collective-permute-start.12 = (bf16[4,2,384,2048]{3,2,1,0:T(8,128)(2,1)}, bf16[4,2,384,2048]{3,2,1,0:T(8,128)(2,1)}, u32[]{:S(2)}, u32[]{:S(2)}) collective-permute-start(bf16[4,2,384,2048]{3,2,1,0:T(8,128)(2,1)} %mlp_back.11.refs_6_), channel_id=1, source_target_pairs={{0,1},{1,0},{2,3},{3,2},{4,5},{5,4},{6,7},{7,6}} | collective-permute-start | bytes 37748744 | tf_op jit(solution)/shard_map/ppermute | solution.py:595
  854.9 201.5 %reduce-scatter.15.cloned.1.call-start = ((), (), s32[]{:S(2)}) async-start(), calls=%async_computation.14 | async-start | bytes 10616832 | tf_op jit(solution)/shard_map/reduce_scatter | solution.py:708
  986.2 137.6 %reduce-scatter.11.cloned.1.call-start = ((), (), s32[]{:S(2)}) async-start(), calls=%async_computation.12 | async-start | bytes 7864320 | tf_op jit(solution)/shard_map/reduce_scatter | solution.py:589
  986.7 367.7 %all-reduce.4.cloned.1.call-start = ((), (), s32[]{:S(2)}) async-start(), calls=%async_computation.15 | async-start | bytes 8421376 | tf_op jit(solution)/shard_map/psum | solution.py:720
  986.8 20.1 %collective-permute-start.14 = (f32[4,256,2048]{2,1,0:T(8,128)}, f32[4,256,2048]{2,1,0:T(8,128)S(1)}, u32[]{:S(2)}, u32[]{:S(2)}) collective-permute-start(f32[4,256,2048]{2,1,0:T(8,128)} %head_wgrad.4.refs_15_), channel_id=1, source_target_pairs={{0,1},{1,0},{2,3},{3,2},{4,5},{5,4},{6,7},{7,6}} | collective-permute-start | bytes 25165832 | tf_op jit(solution)/shard_map/ppermute | solution.py:595
  1000.8 26.5 %collective-permute-start.13 = (f32[4,256,2048]{2,1,0:T(8,128)}, f32[4,256,2048]{2,1,0:T(8,128)S(1)}, u32[]{:S(2)}, u32[]{:S(2)}) collective-permute-start(f32[4,256,2048]{2,1,0:T(8,128)} %head_wgrad.5.refs_3_), channel_id=1, source_target_pairs={{0,1},{1,0},{2,3},{3,2},{4,5},{5,4},{6,7},{7,6}} | collective-permute-start | bytes 25165832 | tf_op jit(solution)/shard_map/ppermute | solution.py:595
  1099.8 261.2 %reduce-scatter.17.cloned.1.call-start = ((), (), s32[]{:S(2)}) async-start(), calls=%async_computation.16 | async-start | bytes 20971520 | tf_op jit(solution)/shard_map/reduce_scatter | solution.py:589
  (39 other events, 505.9 us)
Sparse Core Ops, SparseCore 0:
  17.9 84.8 all-gather.10
  105.2 84.1 all-gather.12
  214.4 67.8 all-gather.18
  284.5 66.4 all-gather.14
  353.2 67.2 all-gather.20
  422.2 66.4 all-gather.16
  491.0 66.4 all-gather.22
  561.1 115.0 reduce-scatter.6
  744.5 114.9 reduce-scatter.8
  862.3 64.4 reduce-scatter.12
  986.3 70.1 reduce-scatter.14
  1059.2 64.4 reduce-scatter.10
  1127.0 70.4 all-reduce.3
  1200.4 148.1 reduce-scatter.16

commit v6 on v5

--- a/solution.py
+++ b/solution.py
@@ -12,7 +12,6 @@
 F32 = jnp.float32
 BF16 = jnp.bfloat16
 MASKED = -1e30
-LARGE = 1 << 17
 
 
 def rms_norm(x_in, gain):
@@ -189,7 +188,6 @@
     def call(self, kernel, n_in, n_kept=0, *, in_specs, out_specs, out_shape, grid, prefetch=0, scratch_shapes=(), **options):
         def run(*args):
             deps = () if self.last is None or any(self.last is a for a in args) else (self.last,)
-            args = args[:prefetch] + tuple(pltpu.with_memory_space_constraint(a, pltpu.HBM) if a.size >= LARGE else a for a in args[prefetch:])
             n_args = prefetch + n_in
 
             def body(*refs):
@@ -197,9 +195,8 @@
 
             single = not isinstance(out_specs, (list, tuple))
             n_out = 1 if single else len(out_specs)
-            shapes = [pltpu.HBM(o.shape, o.dtype) if o.size >= LARGE else o for o in ([out_shape] if single else out_shape)]
             out = pl.pallas_call(
-                body, out_shape=shapes[0] if single else shapes,
+                body, out_shape=out_shape,
                 grid_spec=pltpu.PrefetchScalarGridSpec(
                     num_scalar_prefetch=prefetch, grid=grid, scratch_shapes=scratch_shapes, out_specs=out_specs,
                     in_specs=in_specs + [pl.BlockSpec(memory_space=pl.ANY)] * (n_kept + len(deps))),
@@ -264,10 +261,11 @@
         dg_ref[:, j:j + sub] = (d_act * upper * slope).astype(BF16)
 
 
-def act_call(order, core, z_all, g_all, w_gate, w_up, w_down, tn=512, sub=256):
+def act_call(order, core, z_all, g_all, w_gate, w_up, w_down, sub=256):
     chips, _, rows, dim = z_all.shape
     width = w_gate.shape[1]
     out = jax.ShapeDtypeStruct((chips * 2 * rows, width), BF16)
+    tn = 1024 if w_down is None else 512
     raw = raw_spec(z_all.shape)
     col = pl.BlockSpec((dim, tn), lambda j, i, core: (0, j))
     tile = pl.BlockSpec((2 * rows, tn), lambda j, i, core: (i, j))
@@ -425,42 +423,78 @@
     )(core, *lhs, *rhs, *kept)
 
 
-def small_wgrad_kernel(l_ref, r_ref, *refs):
-    total = dot_f32(l_ref[...], r_ref[...], 0, 0).reshape(refs[-1].shape)
-    for extra in refs[:-1]:
-        total += extra[...]
-    refs[-1][...] = total
-
-
-def small_wgrad(order, lhs, rhs, tf=1024, tn=512):
+def kv_wgrad_kernel(l_ref, r_ref, *refs):
+    out, steps = refs[-1], pl.num_programs(0)
+    width = out.shape[1]
+
+    @pl.when(pl.program_id(0) < steps - 1)
+    def _():
+        out[...] = dot_f32(l_ref[...], r_ref[...], 0, 0)
+
+    @pl.when(pl.program_id(0) == steps - 1)
+    def _():
+        row = 0
+        for terms in refs[:-1]:
+            total = jnp.sum(terms[...], axis=0, keepdims=True)
+            for k in range(0, total.shape[1], width):
+                out[row:row + 1] = total[:, k:k + width]
+                row += 1
+
+
+def kv_wgrad(order, lhs, rhs, terms, tf=512):
     tokens, rows = lhs.shape
     width = rhs.shape[1]
-    out = jax.ShapeDtypeStruct((rows, width), F32)
-    return order.call(
-        small_wgrad_kernel, 2, out_shape=out, grid=(width // tn, rows // tf),
-        in_specs=[pl.BlockSpec((tokens, tf), lambda j, i: (0, i)), pl.BlockSpec((tokens, tn), lambda j, i: (0, j))],
-        out_specs=pl.BlockSpec((tf, tn), lambda j, i: (i, j)), compiler_params=params(2, 28),
-        cost_estimate=cost(2 * tokens * rows * width, lhs, rhs, out), name="small_wgrad",
-    )(lhs, rhs)
-
-
-def head_wgrad(order, lhs, rhs, hd, far=(), kind=0, earlier=None, tn=1024):
-    tokens, width = lhs.shape
-    dim = rhs.shape[1]
+    extra = sum(t.shape[1] for t in terms) // width
+    steps = rows // tf
+    out = jax.ShapeDtypeStruct((rows + extra, width), F32)
+    return order.call(
+        kv_wgrad_kernel, 2 + len(terms), out_shape=out, grid=(steps + 1,),
+        in_specs=[pl.BlockSpec((tokens, tf), lambda i: (0, jnp.minimum(i, steps - 1))), pl.BlockSpec((tokens, width), lambda i: (0, 0))]
+        + [pl.BlockSpec(t.shape, lambda i: (0, 0)) for t in terms],
+        out_specs=pl.BlockSpec((tf, width), lambda i: (i, 0)), compiler_params=params(1, 40),
+        cost_estimate=cost(2 * tokens * rows * width, lhs, rhs, out), name="kv_wgrad",
+    )(lhs, rhs, *terms)
+
+
+def head_wgrad_kernel(*refs):
+    lhs, rhs, out = refs[:2], refs[2:4], refs[-1]
+    for kind in range(2):
+        total = dot_f32(lhs[kind][...], rhs[kind][...], 0, 0).reshape(out.shape[0], *out.shape[2:])
+        for far in refs[4:-1]:
+            total += far[:, kind]
+        out[:, kind] = total
+
+
+def head_wgrad(order, lhs, rhs, hd, far=(), tn=512):
+    tokens, width = lhs[0].shape
+    dim = rhs[0].shape[1]
     heads = width // hd
-    per = 2
-    plain = pl.BlockSpec((per, hd, tn), lambda j, i: (i, 0, j))
-    if far:
-        out = jax.ShapeDtypeStruct((heads, 2, hd, dim), F32)
-        spec = pl.BlockSpec((per, None, hd, tn), lambda j, i: (i, kind, 0, j))
-    else:
-        out, spec = jax.ShapeDtypeStruct((heads, hd, dim), F32), plain
-    kept = () if earlier is None else (earlier,)
-    return order.call(
-        small_wgrad_kernel, 2 + len(far), len(kept), out_shape=out, grid=(dim // tn, heads // per),
-        in_specs=[pl.BlockSpec((tokens, per * hd), lambda j, i: (0, i)), pl.BlockSpec((tokens, tn), lambda j, i: (0, j))] + [plain] * len(far),
-        out_specs=spec, compiler_params=params(2, 28), cost_estimate=cost(2 * tokens * width * dim, lhs, rhs, *far, out), name="head_wgrad",
-    )(lhs, rhs, *far, *kept)
+    out = jax.ShapeDtypeStruct((heads, 2, hd, dim), F32)
+    tile = pl.BlockSpec((heads, 2, hd, tn), lambda j: (0, 0, 0, j))
+    return order.call(
+        head_wgrad_kernel, 4 + len(far), out_shape=out, grid=(dim // tn,),
+        in_specs=[pl.BlockSpec((tokens, width), lambda j: (0, 0), pipeline_mode=pl.Buffered(1))] * 2
+        + [pl.BlockSpec((tokens, tn), lambda j: (0, j))] * 2 + [tile] * len(far),
+        out_specs=tile, compiler_params=params(1, 48), cost_estimate=cost(4 * tokens * width * dim, *lhs, *rhs, *far, out), name="head_wgrad",
+    )(*lhs, *rhs, *far)
+
+
+def add_kernel(base_ref, *refs):
+    for c, part in enumerate(refs[:-1]):
+        @pl.when(pl.program_id(0) == c)
+        def _(part=part):
+            refs[-1][...] = (base_ref[...].astype(F32) + rows_of(part).astype(F32)).astype(BF16)
+
+
+def add_call(order, base, parts):
+    tokens, dim = base.shape
+    size = tokens // len(parts)
+    row = pl.BlockSpec((size, dim), lambda i: (i, 0))
+    specs = [pl.BlockSpec((1, size, dim), lambda i, at=a.shape[0] - 1: (at, 0, 0)) if a.ndim == 3 else pl.BlockSpec((size, dim), lambda i: (0, 0)) for a in parts]
+    return order.call(
+        add_kernel, 1 + len(parts), out_shape=jax.ShapeDtypeStruct(base.shape, BF16), grid=(len(parts),), in_specs=[row] + specs, out_specs=row,
+        compiler_params=params(1, 40), cost_estimate=cost(base.size, base, base, base), name="add",
+    )(base, *parts)
 
 
 def resid_kernel(h_ref, a_own_ref, a_oth_ref, w_own_ref, w_oth_ref, gain_ref, resid_ref, *z_refs, sub):
@@ -676,7 +710,7 @@
         def finish(c):
             both = back_both(c, 0, (far[c],))
             both = scatter4(both).reshape(2, size, dim)
-            d_gated[c], mlp_sums[c] = both, both[1]
+            d_gated[c] = mlp_sums[c] = both
 
         def finish_last(c):
             part = back_call(order, 0, acts[c][1:], weights[:2], d_z_terms, (far[c],), chips)
@@ -696,30 +730,28 @@
         terms, *d_parts = d_resid_of(0, 1, None)
         grads = terms, d_parts, attn_bwd_of(0, 1, d_parts[1], d_parts[2], None)
         finish_last(CHUNKS - 1)
-        hidden_out = (resid.astype(F32) + jnp.concatenate(mlp_sums, axis=0).astype(F32)).astype(BF16).reshape(batch, rows, dim)
         shards = [[a.reshape(2 * chips, size, -1) for a in acts[c]] for c in range(CHUNKS)]
         g_gate = wgrad_call(order, core_1, z_all, [a[1] for a in shards], tiles=(0, 1))
 
         terms, d_resid, d_own, d_oth = d_resid_of(1, CHUNKS - 1, grads)
-        g_out_far = swap(head_wgrad(order, mix_oth, d_resid, hd))
         norm_terms, (dq_own, dq_oth, dkv) = grads[0] + terms, attn_bwd_of(1, CHUNKS - 1, d_own, d_oth, grads)
         dq_own = dq_own.reshape(tokens, chips * hd)
         dq_oth = dq_oth.reshape(tokens, chips * hd)
         dkv = lax.psum_scatter(dkv.reshape(tp_size * batch, rows, 2 * hd), "tp", scatter_dimension=0, tiled=True)
-        g_query_far = swap(head_wgrad(order, dq_oth, normed_flat, hd))
-        g_heads = head_wgrad(order, mix_own, d_resid, hd, (g_out_far,), 0)
-        g_heads = head_wgrad(order, dq_own, normed_flat, hd, (g_query_far,), 1, g_heads)
+        heads_far = head_wgrad(order, (mix_oth, dq_oth), (d_resid, normed_flat), hd)
+        heads_far = swap(heads_far)
+        g_gate = wgrad_call(order, core_1, z_all, [a[1] for a in shards], tiles=(1, 2), earlier=g_gate)
+        g_heads = head_wgrad(order, (mix_own, dq_own), (d_resid, normed_flat), hd, (heads_far,))
         g_heads = scatter4(g_heads)
         g_out, g_query = g_heads[0], g_heads[1].T
         d_k_raw = key_pull(dkv[..., :hd].astype(F32))[0]
         dkv = jnp.concatenate([d_k_raw.astype(BF16), dkv[..., hd:]], axis=-1).reshape(tokens, 2 * hd)
         grad_hidden, attn_terms = d_hidden_call(
             order, dq_own, dq_oth, dkv, hidden_flat, d_resid, attn_gain[None, :], wq_own, wq_oth, w_kv, 4 * rows, 2 * rows)
-        g_kv = small_wgrad(order, normed_flat, dkv, tf=1024, tn=2 * hd)
-        norms = jnp.stack([jnp.sum(attn_terms, axis=0), jnp.sum(norm_terms, axis=0)]).reshape(-1, 2 * hd)
-        sums = lax.psum(jnp.concatenate([g_kv, norms], axis=0), "tp")
+        sums = kv_wgrad(order, normed_flat, dkv, (attn_terms, norm_terms))
+        sums = lax.psum(sums, "tp")
         g_attn_norm, g_mlp_norm = sums[dim:].reshape(2, dim)
-        g_gate = wgrad_call(order, core_1, z_all, [a[1] for a in shards], tiles=(1, 2), earlier=g_gate)
+        hidden_out = add_call(order, resid, mlp_sums).reshape(batch, rows, dim)
         g_up = wgrad_call(order, core_1, z_all, [a[2] for a in shards])
         g_down = wgrad_call(order, core_1, [a[0] for a in shards], g_all)
         return (hidden_out, grad_hidden.reshape(batch, rows, dim), g_attn_norm, g_query, sums[:dim, :hd], sums[:dim, hd:], g_out, g_mlp_norm, g_gate, g_up, g_down)

time: 1380 us -> 1380 us (level)
  Pallas kernels: 1070 us -> 1050 us
  local copies, waits for them, and re-layouts: 72.7 us -> 90.5 us
    reduce_scatter x5, waiting for transfers between devices: 21.6 us -> 48 us  [scatter4(): lax.psum_scatter(flat, 'tp', scatter_dimension=0, tiled=True, axis_index_...]
    unnamed x90 -> x134, local copies, waits for them, and re-layouts: 34.8 us -> 53.9 us
    pallas_call x27 -> x26, Pallas kernels: 1040 us -> 1030 us  [run(): pl.pallas_call(body, out_shape=out_shape, grid_spec=pltpu.PrefetchScalarG...]
  transfers between devices with their start and end apart: 29 -> 28, of which waited for: 12 -> 10; matrix products, arithmetic and copies ran while one was open for 5% -> 4% of each run, Pallas kernels for 73% -> 73%
where the time goes in v6:
time: 1380 us; the launch traced here: 1370 us
  Pallas kernels  1050 us (76%)
  waiting for transfers between devices  171 us (12%)
  local copies, waits for them, and re-layouts  90.5 us (7%)
  matrix products  18.2 us (1%)
  starting transfers between devices  16.3 us (1%)
  between operations  15.1 us (1%)
    pallas_call x26, Pallas kernels, run(): pl.pallas_call(body, out_shape=out_shape, grid_spec=pltpu.PrefetchScalarG...  1030 us
    ppermute x8, waiting for transfers between devices, flip(): return lax.ppermute(x_loc, 'tp', [(i, i ^ bits) for i in range(tp_size)])  87.1 us
    unnamed x134, local copies, waits for them, and re-layouts  53.9 us
    reduce_scatter x5, waiting for transfers between devices, scatter4(): lax.psum_scatter(flat, 'tp', scatter_dimension=0, tiled=True, axis_index_...  48 us
    all_gather x7, waiting for transfers between devices, gather8(): return lax.all_gather(x_loc, 'tp', axis=0, tiled=False)  32.5 us
  transfers between devices with their start and end apart: 28, of which 10 were waited for; matrix products, arithmetic and copies ran while one was open for 4% of the time, Pallas kernels for 73%

profile of v6, /device:TPU:0, one launch (start us, length us, event | category | flops | bytes accessed | tf_op | source)
XLA Modules:
  0.0 1371.5 jit_solution(12926936244904221413)
XLA Ops:
  29.3 37.0 %collective-permute-done = bf16[256,2048]{0,1:T(8,128)(2,1)S(1)} collective-permute-done((bf16[256,2048]{0,1:T(8,128)(2,1)}, bf16[256,2048]{0,1:T(8,128)(2,1)S(1)}, u32[]{:S(2)}, u32[]{:S(2)}) %collective-permute-start) | collective-permute-done | bytes 1048608 | tf_op jit(solution)/shard_map/ppermute | solution.py:632
  80.8 12.0 collective-permute-done.2
  105.6 8.9 fusion.13
  121.3 15.3 %collective-permute-done.6 = bf16[256,2048]{1,0:T(8,128)(2,1)S(1)} collective-permute-done((bf16[256,2048]{1,0:T(8,128)(2,1)S(1)}, bf16[256,2048]{1,0:T(8,128)(2,1)S(1)}, u32[]{:S(2)}, u32[]{:S(2)}) %collective-permute-start.6) | collective-permute-done | bytes 1048608 | tf_op jit(solution)/shard_map/ppermute | solution.py:632
  144.7 14.1 %collective-permute-done.7 = bf16[128,2048]{1,0:T(8,128)(2,1)S(1)} collective-permute-done((bf16[128,2048]{1,0:T(8,128)(2,1)S(1)}, bf16[128,2048]{1,0:T(8,128)(2,1)S(1)}, u32[]{:S(2)}, u32[]{:S(2)}) %collective-permute-start.7) | collective-permute-done | bytes 524320 | tf_op jit(solution)/shard_map/ppermute | solution.py:632
  169.0 20.4 %attn_fwd.1 = (bf16[12,96,1024]{2,1,0:T(8,128)(2,1)S(1)}, bf16[12,96,1024]{2,1,0:T(8,128)(2,1)S(1)}, bf16[12,96,1024]{2,1,0:T(8,128)(2,1)S(1)}, bf16[12,96,1024]{2,1,0:T(8,128)(2,1)S(1)}) custom-call(s32[12]{0:T(128)S(1)} %copy-done.29, s32[12]{0:T(128)S(1)} %copy-done.31, s32[1]{0:T(128)} %bitcast.1.core_s.refs_0_.refs_2_, f32[12,96,1024]{2,1,0:T(8,128)S(1)} %bitcast.111, ...), custom_call_target="tpu_custom_call" | custom-call | flops 7247757312 | bytes 28311552 | tf_op jit(solution)/shard_map/attn_fwd/pallas_call | solution.py:148
  195.1 19.7 %resid.1 = (bf16[1152,2048]{1,0:T(8,128)(2,1)}, bf16[384,2048]{1,0:T(8,128)(2,1)}, bf16[384,2048]{1,0:T(8,128)(2,1)}, bf16[384,2048]{1,0:T(8,128)(2,1)}) custom-call(bf16[1152,2048]{1,0:T(8,128)(2,1)} %bitcast.120, bf16[1152,1024]{1,0:T(8,128)(2,1)} %bitcast.100, bf16[1152,1024]{1,0:T(8,128)(2,1)} %bitcast.113, ...), custom_call_target="tpu_custom_call" | custom-call | flops 9663676416 | bytes 27262976 | tf_op jit(solution)/shard_map/resid/pallas_call | solution.py:198
  217.4 32.9 %d_act.2.refs_2_ = bf16[3072,2048]{1,0:T(8,128)(2,1)} custom-call(s32[1]{0:T(128)} %bitcast.1.core_s.refs_0_.refs_2_, bf16[4,2,384,2048]{3,2,1,0:T(8,128)(2,1)} %bitcast.138, bf16[2048,2048]{1,0:T(8,128)(2,1)} %refs_1_.4, bf16[1152,2048]{1,0:T(8,128)(2,1)} %get-tuple-element.50.refs_3_.refs_1_.refs_2_.refs_0_), custom_call_target="tpu_custom_call" | custom-call | flops 25769803776 | bytes 33554432 | tf_op jit(solution)/shard_map/d_act/pallas_call | solution.py:198
  250.3 32.5 %all-gather.19.cloned.1.call-done = bf16[3072,2048]{1,0:T(8,128)(2,1)} async-done(((bf16[384,2048]{1,0:T(8,128)(2,1)}), bf16[3072,2048]{1,0:T(8,128)(2,1)}) %all-gather.19.cloned.1.call-update) | async-done | bytes 12582928 | tf_op jit(solution)/shard_map/all_gather | solution.py:626
  282.8 70.7 %mlp_act.3 = (bf16[3072,2048]{1,0:T(8,128)(2,1)}, bf16[3072,2048]{1,0:T(8,128)(2,1)}, bf16[3072,2048]{1,0:T(8,128)(2,1)}) custom-call(s32[1]{0:T(128)} %bitcast.1.core_s.refs_0_.refs_2_, bf16[4,2,384,2048]{3,2,1,0:T(8,128)(2,1)} %bitcast.140, bf16[3072,2048]{1,0:T(8,128)(2,1)} %d_act.2.refs_2_, bf16[2048,2048]{1,0:T(8,128)(2,1)} %refs_2_.5, ...), custom_call_target="tpu_custom_call" | custom-call | flops 51539607552 | bytes 79691776 | tf_op jit(solution)/shard_map/mlp_act/pallas_call | solution.py:198
  353.5 47.4 %mlp_back.7.refs_3_ = bf16[4,2,384,2048]{3,2,1,0:T(8,128)(2,1)} custom-call(bf16[3072,2048]{1,0:T(8,128)(2,1)} %get-tuple-element.52.refs_0_, bf16[3072,2048]{1,0:T(8,128)(2,1)} %get-tuple-element.53.refs_1_, bf16[3072,2048]{1,0:T(8,128)(2,1)} %get-tuple-element.54.refs_2_, bf16[2048,2048]{1,0:T(8,128)(2,1)} %refs_2_.5, bf16[2048,2048]{1,0:T(8,128)(2,1)} %refs_3_.17, ...), custom_call_target="tpu_custom_call" | custom-call | flops 38654705664 | bytes 75497472 | tf_op jit(solution)/shard_map/mlp_back/pallas_call | solution.py:198
  401.2 32.5 %d_act.3.refs_2_ = bf16[3072,2048]{1,0:T(8,128)(2,1)} custom-call(s32[1]{0:T(128)} %bitcast.1.core_s.refs_0_.refs_2_, bf16[4,2,384,2048]{3,2,1,0:T(8,128)(2,1)} %bitcast.144, bf16[2048,2048]{1,0:T(8,128)(2,1)} %refs_1_.4, bf16[4,2,384,2048]{3,2,1,0:T(8,128)(2,1)} %mlp_back.7.refs_3_), custom_call_target="tpu_custom_call" | custom-call | flops 25769803776 | bytes 33554432 | tf_op jit(solution)/shard_map/d_act/pallas_call | solution.py:198
  433.7 70.9 %mlp_act.4 = (bf16[3072,2048]{1,0:T(8,128)(2,1)}, bf16[3072,2048]{1,0:T(8,128)(2,1)}, bf16[3072,2048]{1,0:T(8,128)(2,1)}) custom-call(s32[1]{0:T(128)} %bitcast.1.core_s.refs_0_.refs_2_, bf16[4,2,384,2048]{3,2,1,0:T(8,128)(2,1)} %bitcast.146, bf16[3072,2048]{1,0:T(8,128)(2,1)} %d_act.3.refs_2_, bf16[2048,2048]{1,0:T(8,128)(2,1)} %refs_2_.5, ...), custom_call_target="tpu_custom_call" | custom-call | flops 51539607552 | bytes 79691776 | tf_op jit(solution)/shard_map/mlp_act/pallas_call | solution.py:198
  504.7 49.6 %mlp_back.8.refs_6_ = bf16[4,2,384,2048]{3,2,1,0:T(8,128)(2,1)} custom-call(bf16[3072,2048]{1,0:T(8,128)(2,1)} %get-tuple-element.52.refs_0_, bf16[3072,2048]{1,0:T(8,128)(2,1)} %get-tuple-element.53.refs_1_, bf16[3072,2048]{1,0:T(8,128)(2,1)} %get-tuple-element.54.refs_2_, bf16[2048,2048]{1,0:T(8,128)(2,1)} %refs_2_.5, bf16[2048,2048]{1,0:T(8,128)(2,1)} %refs_3_.17, ...), custom_call_target="tpu_custom_call" | custom-call | flops 38654705664 | bytes 75497472 | tf_op jit(solution)/shard_map/mlp_back/pallas_call | solution.py:198
  554.4 47.4 %mlp_back.9.refs_6_ = bf16[4,2,384,2048]{3,2,1,0:T(8,128)(2,1)} custom-call(bf16[3072,2048]{1,0:T(8,128)(2,1)} %get-tuple-element.57.refs_0_, bf16[3072,2048]{1,0:T(8,128)(2,1)} %get-tuple-element.58.refs_1_, bf16[3072,2048]{1,0:T(8,128)(2,1)} %get-tuple-element.56.refs_7_.refs_2_, bf16[2048,2048]{1,0:T(8,128)(2,1)} %refs_2_.5, bf16[2048,2048]{1,0:T(8,128)(2,1)} %refs_3_.17, ...), custom_call_target="tpu_custom_call" | custom-call | flops 38654705664 | bytes 75497472 | tf_op jit(solution)/shard_map/mlp_back/pallas_call | solution.py:198
  601.9 92.0 %mlp_act.5 = (bf16[3072,2048]{1,0:T(8,128)(2,1)}, bf16[3072,2048]{1,0:T(8,128)(2,1)}, bf16[3072,2048]{1,0:T(8,128)(2,1)}) custom-call(s32[1]{0:T(128)} %bitcast.1.core_s.refs_0_.refs_2_, bf16[4,2,384,2048]{3,2,1,0:T(8,128)(2,1)} %bitcast.152, bf16[4,2,384,2048]{3,2,1,0:T(8,128)(2,1)} %bitcast.150, bf16[2048,2048]{1,0:T(8,128)(2,1)} %refs_2_.5, ...), custom_call_target="tpu_custom_call" | custom-call | flops 77309411328 | bytes 88080384 | tf_op jit(solution)/shard_map/mlp_act/pallas_call | solution.py:198
  693.9 49.5 %mlp_back.10.refs_6_ = bf16[4,2,384,2048]{3,2,1,0:T(8,128)(2,1)} custom-call(bf16[3072,2048]{1,0:T(8,128)(2,1)} %get-tuple-element.57.refs_0_, bf16[3072,2048]{1,0:T(8,128)(2,1)} %get-tuple-element.58.refs_1_, bf16[3072,2048]{1,0:T(8,128)(2,1)} %get-tuple-element.56.refs_7_.refs_2_, bf16[2048,2048]{1,0:T(8,128)(2,1)} %refs_2_.5, ...), custom_call_target="tpu_custom_call" | custom-call | flops 38654705664 | bytes 75497472 | tf_op jit(solution)/shard_map/mlp_back/pallas_call | solution.py:198
  743.5 47.8 %mlp_back.11.refs_6_ = bf16[4,2,384,2048]{3,2,1,0:T(8,128)(2,1)} custom-call(bf16[3072,2048]{1,0:T(8,128)(2,1)} %get-tuple-element.61.refs_0_, bf16[3072,2048]{1,0:T(8,128)(2,1)} %get-tuple-element.62.refs_1_, bf16[3072,2048]{1,0:T(8,128)(2,1)} %get-tuple-element.60.refs_7_.refs_2_.refs_0_, bf16[2048,2048]{1,0:T(8,128)(2,1)} %refs_2_.5, ...), custom_call_target="tpu_custom_call" | custom-call | flops 38654705664 | bytes 75497472 | tf_op jit(solution)/shard_map/mlp_back/pallas_call | solution.py:198
  792.0 10.3 d_resid.2
  805.7 13.5 attn_bwd.2
  826.2 34.9 %mlp_back.12.refs_3_ = bf16[4,384,2048]{2,1,0:T(8,128)(2,1)} custom-call(bf16[3072,2048]{1,0:T(8,128)(2,1)} %get-tuple-element.61.refs_0_, bf16[3072,2048]{1,0:T(8,128)(2,1)} %get-tuple-element.62.refs_1_, bf16[2048,2048]{1,0:T(8,128)(2,1)} %refs_2_.5, bf16[2048,2048]{1,0:T(8,128)(2,1)} %refs_3_.17, ...), custom_call_target="tpu_custom_call" | custom-call | flops 25769803776 | bytes 48234496 | tf_op jit(solution)/shard_map/mlp_back/pallas_call | solution.py:198
  861.3 20.1 %mlp_back.13.refs_7_ = bf16[4,384,2048]{2,1,0:T(8,128)(2,1)} custom-call(bf16[3072,2048]{1,0:T(8,128)(2,1)} %get-tuple-element.60.refs_7_.refs_2_.refs_0_, bf16[2048,2048]{1,0:T(8,128)(2,1)} %refs_1_.4, bf16[4,2,384,2048]{3,2,1,0:T(8,128)(2,1)} %collective-permute-done.12.refs_4_.refs_2_, bf16[4,384,2048]{2,1,0:T(8,128)(2,1)} %mlp_back.12.refs_3_), custom_call_target="tpu_custom_call" | custom-call | flops 12884901888 | bytes 27262976 | tf_op jit(solution)/shard_map/mlp_back/pallas_call | solution.py:198
  881.4 47.6 %wgrad.4.refs_10_.refs_7_ = f32[2048,2048]{1,0:T(8,128)} custom-call(s32[1]{0:T(128)} %bitcast.1.core_s.refs_0_.refs_2_, bf16[4,2,384,2048]{3,2,1,0:T(8,128)(2,1)} %bitcast.141, bf16[4,2,384,2048]{3,2,1,0:T(8,128)(2,1)} %bitcast.147, bf16[4,2,384,2048]{3,2,1,0:T(8,128)(2,1)} %bitcast.153, bf16[8,384,2048]{2,1,0:T(8,128)(2,1)} %bitcast.162, ...), custom_call_target="tpu_custom_call" | custom-call | flops 77309411328 | bytes 92274688 | tf_op jit(solution)/shard_map/wgrad/pallas_call | solution.py:198
  932.2 18.1 %d_resid.3 = (f32[8,2048]{1,0:T(8,128)S(1)}, bf16[1152,2048]{1,0:T(8,128)(2,1)}, bf16[1152,1024]{1,0:T(8,128)(2,1)S(1)}, bf16[1152,1024]{1,0:T(8,128)(2,1)}) custom-call(bf16[2,384,2048]{2,1,0:T(8,128)(2,1)} %reduce-scatter.9.cloned.1.call-done.refs_0_.refs_2_, ...), custom_call_target="tpu_custom_call", output_to_operand_aliasing={{1}: (7, {}), {2}: (8, {}), {3}: (9, {})} | custom-call | flops 6442450944 | bytes 17825792 | tf_op jit(solution)/shard_map/d_resid/pallas_call | solution.py:198
  955.7 25.1 %attn_bwd.3 = (bf16[12,96,1024]{2,1,0:T(8,128)(2,1)S(1)}, bf16[12,96,1024]{2,1,0:T(8,128)(2,1)S(1)}, bf16[8,12,96,512]{3,2,1,0:T(8,128)(2,1)S(1)}) custom-call(s32[12]{0:T(128)S(1)} %copy-done.30, s32[12]{0:T(128)S(1)} %copy-done.32, s32[1]{0:T(128)} %bitcast.1.core_s.refs_0_.refs_2_, ...), custom_call_target="tpu_custom_call", output_to_operand_aliasing={{0}: (12, {}), {1}: (13, {}), {2}: (14, {})} | custom-call | flops 12079595520 | bytes 28311552 | tf_op jit(solution)/shard_map/attn_bwd/pallas_call | solution.py:198
  991.1 17.0 %head_wgrad.2.refs_8_ = f32[4,2,256,2048]{3,2,1,0:T(8,128)} custom-call(bf16[1152,1024]{1,0:T(8,128)(2,1)S(1)} %bitcast.114, bf16[1152,1024]{1,0:T(8,128)(2,1)S(1)} %bitcast.116, bf16[1152,2048]{1,0:T(8,128)(2,1)} %get-tuple-element.78.refs_2_.refs_4_, bf16[1152,2048]{1,0:T(8,128)(2,1)} %bitcast.88, bf16[12,96,1024]{2,1,0:T(8,128)(2,1)} %copy-done.13), custom_call_target="tpu_custom_call" | custom-call | flops 9663676416 | bytes 30932992 | tf_op jit(solution)/shard_map/head_wgrad/pallas_call | solution.py:198
  1009.3 47.4 %wgrad.5.refs_5_ = f32[2048,2048]{1,0:T(8,128)} custom-call(s32[1]{0:T(128)} %bitcast.1.core_s.refs_0_.refs_2_, bf16[4,2,384,2048]{3,2,1,0:T(8,128)(2,1)} %bitcast.142, bf16[4,2,384,2048]{3,2,1,0:T(8,128)(2,1)} %bitcast.148, bf16[4,2,384,2048]{3,2,1,0:T(8,128)(2,1)} %bitcast.154, bf16[8,384,2048]{2,1,0:T(8,128)(2,1)} %bitcast.163, ...), custom_call_target="tpu_custom_call", output_to_operand_aliasing={{}: (7, {})} | custom-call | flops 77309411328 | bytes 92274688 | tf_op jit(solution)/shard_map/wgrad/pallas_call | solution.py:198
  1059.7 21.5 %head_wgrad.3.refs_9_ = f32[4,2,256,2048]{3,2,1,0:T(8,128)} custom-call(bf16[1152,1024]{1,0:T(8,128)(2,1)S(1)} %bitcast.101, bf16[1152,1024]{1,0:T(8,128)(2,1)S(1)} %bitcast.103, bf16[1152,2048]{1,0:T(8,128)(2,1)} %get-tuple-element.78.refs_2_.refs_4_, bf16[1152,2048]{1,0:T(8,128)(2,1)} %bitcast.89, f32[4,2,256,2048]{3,2,1,0:T(8,128)} %collective-permute-done.13.refs_4_, ...), custom_call_target="tpu_custom_call" | custom-call | flops 9663676416 | bytes 47710208 | tf_op jit(solution)/shard_map/head_wgrad/pallas_call | solution.py:198
  1081.2 25.5 %d_hidden.1 = (bf16[1152,2048]{1,0:T(8,128)(2,1)}, f32[8,2048]{1,0:T(8,128)}) custom-call(bf16[1152,1024]{1,0:T(8,128)(2,1)} %bitcast.102, bf16[1152,1024]{1,0:T(8,128)(2,1)} %bitcast.115, bf16[1152,512]{1,0:T(8,128)(2,1)} %bitcast.98, bf16[1152,2048]{1,0:T(8,128)(2,1)} %bitcast.121, bf16[1152,2048]{1,0:T(8,128)(2,1)} %get-tuple-element.78.refs_2_.refs_4_, ...), custom_call_target="tpu_custom_call" | custom-call | flops 14495514624 | bytes 27328512 | tf_op jit(solution)/shard_map/d_hidden/pallas_call | solution.py:198
  1134.6 88.1 %wgrad.6.refs_7_ = f32[2048,2048]{1,0:T(8,128)} custom-call(s32[1]{0:T(128)} %bitcast.1.core_s.refs_0_.refs_2_, bf16[4,2,384,2048]{3,2,1,0:T(8,128)(2,1)} %bitcast.143, bf16[4,2,384,2048]{3,2,1,0:T(8,128)(2,1)} %bitcast.149, bf16[4,2,384,2048]{3,2,1,0:T(8,128)(2,1)} %bitcast.155, bf16[8,384,2048]{2,1,0:T(8,128)(2,1)} %bitcast.157, ...), custom_call_target="tpu_custom_call" | custom-call | flops 77309411328 | bytes 92274688 | tf_op jit(solution)/shard_map/wgrad/pallas_call | solution.py:198
  1222.7 88.5 %wgrad.7 = f32[2048,2048]{1,0:T(8,128)} custom-call(s32[1]{0:T(128)} %bitcast.1.core_s.refs_0_.refs_2_, bf16[8,384,2048]{2,1,0:T(8,128)(2,1)} %bitcast.156, bf16[8,384,2048]{2,1,0:T(8,128)(2,1)} %bitcast.158, bf16[8,384,2048]{2,1,0:T(8,128)(2,1)} %bitcast.160, bf16[4,2,384,2048]{3,2,1,0:T(8,128)(2,1)} %bitcast.139, bf16[4,2,384,2048]{3,2,1,0:T(8,128)(2,1)} %bitcast.145, ...), custom_call_target="tpu_custom_call" | custom-call | flops 77309411328 | bytes 92274688 | tf_op jit(solution)/shard_map/wgrad/pallas_call | solution.py:198
  1317.7 41.2 %reduce-scatter.17.cloned.1.call-done = f32[2,256,2048]{2,1,0:T(8,128)} async-done(((f32[8,256,2048]{2,1,0:T(8,128)}), f32[2,256,2048]{2,1,0:T(8,128)}) %reduce-scatter.17.cloned.1.call-update) | async-done | bytes 4194320 | tf_op jit(solution)/shard_map/reduce_scatter | solution.py:623
  (258 shorter events, 157.1 us)
Async XLA Ops:
  7.2 157.1 %all-gather.11.cloned.1.call-start = ((), (), s32[]{:S(2)}) async-start(), calls=%async_computation.6 | async-start | bytes 10616832 | tf_op jit(solution)/shard_map/all_gather | solution.py:626
  16.5 785.8 %copy-start.21 = (f32[96,128]{1,0:T(8,128)}, f32[96,128]{1,0:T(8,128)S(1)}, u32[]{:S(2)}) copy-start(f32[96,128]{1,0:T(8,128)S(1)} %get-tuple-element.129.cos_ref.refs_8_) | copy-start | bytes 147460
  16.5 785.8 %copy-start.23 = (f32[96,128]{1,0:T(8,128)}, f32[96,128]{1,0:T(8,128)S(1)}, u32[]{:S(2)}) copy-start(f32[96,128]{1,0:T(8,128)S(1)} %get-tuple-element.130.sin_ref.refs_9_) | copy-start | bytes 147460
  17.8 199.6 %all-gather.13.cloned.1.call-start = ((), (), s32[]{:S(2)}) async-start(), calls=%async_computation.7 | async-start | bytes 14155776 | tf_op jit(solution)/shard_map/all_gather | solution.py:626
  22.6 260.2 %all-gather.19.cloned.1.call-start = ((), (), s32[]{:S(2)}) async-start(), calls=%async_computation.17 | async-start | bytes 14155776 | tf_op jit(solution)/shard_map/all_gather | solution.py:626
  22.9 43.4 %collective-permute-start = (bf16[256,2048]{0,1:T(8,128)(2,1)}, bf16[256,2048]{0,1:T(8,128)(2,1)S(1)}, u32[]{:S(2)}, u32[]{:S(2)}) collective-permute-start(bf16[256,2048]{0,1:T(8,128)(2,1)} %bitcast.3), channel_id=1, source_target_pairs={{0,2},{1,3},{2,0},{3,1},{4,6},{5,7},{6,4},{7,5}} | collective-permute-start | bytes 3145736 | tf_op jit(solution)/shard_map/ppermute | solution.py:632
  26.3 42.9 %collective-permute-start.1 = (bf16[256,2048]{0,1:T(8,128)(2,1)}, bf16[256,2048]{0,1:T(8,128)(2,1)}, u32[]{:S(2)}, u32[]{:S(2)}) collective-permute-start(bf16[256,2048]{0,1:T(8,128)(2,1)} %bitcast.3), channel_id=1, source_target_pairs={{0,4},{1,5},{2,6},{3,7},{4,0},{5,1},{6,2},{7,3}} | collective-permute-start | bytes 3145736 | tf_op jit(solution)/shard_map/ppermute | solution.py:632
  67.2 25.6 %collective-permute-start.2 = (bf16[128,2048]{0,1:T(8,128)(2,1)}, bf16[128,2048]{0,1:T(8,128)(2,1)S(1)}, u32[]{:S(2)}, u32[]{:S(2)}) collective-permute-start(bf16[128,2048]{0,1:T(8,128)(2,1)} %slice.76), channel_id=1, source_target_pairs={{0,4},{1,5},{2,6},{3,7},{4,0},{5,1},{6,2},{7,3}} | collective-permute-start | bytes 1572872 | tf_op jit(solution)/shard_map/ppermute | solution.py:632
  71.0 25.6 %collective-permute-start.3 = (bf16[128,2048]{0,1:T(8,128)(2,1)}, bf16[128,2048]{0,1:T(8,128)(2,1)}, u32[]{:S(2)}, u32[]{:S(2)}) collective-permute-start(bf16[128,2048]{0,1:T(8,128)(2,1)} %slice.77), channel_id=1, source_target_pairs={{0,2},{1,3},{2,0},{3,1},{4,6},{5,7},{6,4},{7,5}} | collective-permute-start | bytes 1572872 | tf_op jit(solution)/shard_map/ppermute | solution.py:632
  99.6 14.9 %collective-permute-start.4 = (bf16[1024,2048]{1,0:T(8,128)(2,1)}, bf16[1024,2048]{1,0:T(8,128)(2,1)S(1)}, u32[]{:S(2)}, u32[]{:S(2)}) collective-permute-start(bf16[1024,2048]{1,0:T(8,128)(2,1)} %bitcast.9.refs_6_), channel_id=1, source_target_pairs={{0,1},{1,0},{2,3},{3,2},{4,5},{5,4},{6,7},{7,6}} | collective-permute-start | bytes 12582920 | tf_op jit(solution)/shard_map/ppermute | solution.py:629
  99.6 36.9 %collective-permute-start.6 = (bf16[256,2048]{1,0:T(8,128)(2,1)S(1)}, bf16[256,2048]{1,0:T(8,128)(2,1)S(1)}, u32[]{:S(2)}, u32[]{:S(2)}) collective-permute-start(bf16[256,2048]{1,0:T(8,128)(2,1)S(1)} %copy-done.47), channel_id=1, source_target_pairs={{0,4},{1,5},{2,6},{3,7},{4,0},{5,1},{6,2},{7,3}} | collective-permute-start | bytes 3145736 | tf_op jit(solution)/shard_map/ppermute | solution.py:632
  100.6 38.3 %collective-permute-start.5 = (bf16[256,2048]{1,0:T(8,128)(2,1)S(1)}, bf16[256,2048]{1,0:T(8,128)(2,1)S(1)}, u32[]{:S(2)}, u32[]{:S(2)}) collective-permute-start(bf16[256,2048]{1,0:T(8,128)(2,1)S(1)} %copy-done.47), channel_id=1, source_target_pairs={{0,2},{1,3},{2,0},{3,1},{4,6},{5,7},{6,4},{7,5}} | collective-permute-start | bytes 3145736 | tf_op jit(solution)/shard_map/ppermute | solution.py:632
  138.9 19.9 %collective-permute-start.7 = (bf16[128,2048]{1,0:T(8,128)(2,1)S(1)}, bf16[128,2048]{1,0:T(8,128)(2,1)S(1)}, u32[]{:S(2)}, u32[]{:S(2)}) collective-permute-start(bf16[128,2048]{1,0:T(8,128)(2,1)S(1)} %slice.65), channel_id=1, source_target_pairs={{0,4},{1,5},{2,6},{3,7},{4,0},{5,1},{6,2},{7,3}} | collective-permute-start | bytes 1572872 | tf_op jit(solution)/shard_map/ppermute | solution.py:632
  141.1 21.3 %collective-permute-start.8 = (bf16[128,2048]{1,0:T(8,128)(2,1)S(1)}, bf16[128,2048]{1,0:T(8,128)(2,1)S(1)}, u32[]{:S(2)}, u32[]{:S(2)}) collective-permute-start(bf16[128,2048]{1,0:T(8,128)(2,1)S(1)} %slice.66), channel_id=1, source_target_pairs={{0,2},{1,3},{2,0},{3,1},{4,6},{5,7},{6,4},{7,5}} | collective-permute-start | bytes 1572872 | tf_op jit(solution)/shard_map/ppermute | solution.py:632
  163.2 31.9 %collective-permute-start.9 = (bf16[1024,2048]{1,0:T(8,128)(2,1)}, bf16[1024,2048]{1,0:T(8,128)(2,1)}, u32[]{:S(2)}, u32[]{:S(2)}) collective-permute-start(bf16[1024,2048]{1,0:T(8,128)(2,1)} %bitcast.23.refs_3_.refs_4_.refs_5_), channel_id=1, source_target_pairs={{0,1},{1,0},{2,3},{3,2},{4,5},{5,4},{6,7},{7,6}} | collective-permute-start | bytes 12582920 | tf_op jit(solution)/shard_map/ppermute | solution.py:629
  214.8 186.4 %all-gather.15.cloned.1.call-start = ((), (), s32[]{:S(2)}) async-start(), calls=%async_computation.8 | async-start | bytes 14155776 | tf_op jit(solution)/shard_map/all_gather | solution.py:626
  215.4 218.3 %all-gather.21.cloned.1.call-start = ((), (), s32[]{:S(2)}) async-start(), calls=%async_computation.18 | async-start | bytes 14155776 | tf_op jit(solution)/shard_map/all_gather | solution.py:626
  216.0 385.9 %all-gather.17.cloned.1.call-start = ((), (), s32[]{:S(2)}) async-start(), calls=%async_computation.10 | async-start | bytes 14155776 | tf_op jit(solution)/shard_map/all_gather | solution.py:626
  216.6 385.3 %all-gather.23.cloned.1.call-start = ((), (), s32[]{:S(2)}) async-start(), calls=%async_computation.19 | async-start | bytes 14155776 | tf_op jit(solution)/shard_map/all_gather | solution.py:626
  217.3 574.6 %reduce-scatter.7.cloned.1.call-start = ((), (), s32[]{:S(2)}) async-start(), calls=%async_computation.9 | async-start | bytes 15728640 | tf_op jit(solution)/shard_map/reduce_scatter | solution.py:623
  400.9 103.8 %collective-permute-start.10 = (bf16[4,2,384,2048]{3,2,1,0:T(8,128)(2,1)}, bf16[4,2,384,2048]{3,2,1,0:T(8,128)(2,1)}, u32[]{:S(2)}, u32[]{:S(2)}) collective-permute-start(bf16[4,2,384,2048]{3,2,1,0:T(8,128)(2,1)} %mlp_back.7.refs_3_), channel_id=1, source_target_pairs={{0,1},{1,0},{2,3},{3,2},{4,5},{5,4},{6,7},{7,6}} | collective-permute-start | bytes 37748744 | tf_op jit(solution)/shard_map/ppermute | solution.py:629
  554.3 374.7 %reduce-scatter.9.cloned.1.call-start = ((), (), s32[]{:S(2)}) async-start(), calls=%async_computation.11 | async-start | bytes 15728640 | tf_op jit(solution)/shard_map/reduce_scatter | solution.py:623
  601.8 92.1 %collective-permute-start.11 = (bf16[4,2,384,2048]{3,2,1,0:T(8,128)(2,1)}, bf16[4,2,384,2048]{3,2,1,0:T(8,128)(2,1)}, u32[]{:S(2)}, u32[]{:S(2)}) collective-permute-start(bf16[4,2,384,2048]{3,2,1,0:T(8,128)(2,1)} %mlp_back.9.refs_6_), channel_id=1, source_target_pairs={{0,1},{1,0},{2,3},{3,2},{4,5},{5,4},{6,7},{7,6}} | collective-permute-start | bytes 37748744 | tf_op jit(solution)/shard_map/ppermute | solution.py:629
  743.4 185.6 %reduce-scatter.13.cloned.1.call-start = ((), (), s32[]{:S(2)}) async-start(), calls=%async_computation.13 | async-start | bytes 7864320 | tf_op jit(solution)/shard_map/reduce_scatter | solution.py:623
  743.5 48.5 %copy-start.25 = (f32[2048]{0:T(1024)S(1)}, f32[2048]{0:T(1024)}, u32[]{:S(2)}) copy-start(f32[2048]{0:T(1024)} %broadcast_in_dim.77) | copy-start | bytes 24580
  791.3 35.0 %collective-permute-start.12 = (bf16[4,2,384,2048]{3,2,1,0:T(8,128)(2,1)}, bf16[4,2,384,2048]{3,2,1,0:T(8,128)(2,1)}, u32[]{:S(2)}, u32[]{:S(2)}) collective-permute-start(bf16[4,2,384,2048]{3,2,1,0:T(8,128)(2,1)} %mlp_back.11.refs_6_), channel_id=1, source_target_pairs={{0,1},{1,0},{2,3},{3,2},{4,5},{5,4},{6,7},{7,6}} | collective-permute-start | bytes 37748744 | tf_op jit(solution)/shard_map/ppermute | solution.py:629
  861.2 195.6 %reduce-scatter.15.cloned.1.call-start = ((), (), s32[]{:S(2)}) async-start(), calls=%async_computation.14 | async-start | bytes 10616832 | tf_op jit(solution)/shard_map/reduce_scatter | solution.py:740
  987.4 134.6 %reduce-scatter.11.cloned.1.call-start = ((), (), s32[]{:S(2)}) async-start(), calls=%async_computation.12 | async-start | bytes 7864320 | tf_op jit(solution)/shard_map/reduce_scatter | solution.py:623
  1008.0 51.7 %collective-permute-start.13 = (f32[4,2,256,2048]{3,2,1,0:T(8,128)}, f32[4,2,256,2048]{3,2,1,0:T(8,128)}, u32[]{:S(2)}, u32[]{:S(2)}) collective-permute-start(f32[4,2,256,2048]{3,2,1,0:T(8,128)} %head_wgrad.2.refs_8_), channel_id=1, source_target_pairs={{0,1},{1,0},{2,3},{3,2},{4,5},{5,4},{6,7},{7,6}} | collective-permute-start | bytes 50331656 | tf_op jit(solution)/shard_map/ppermute | solution.py:629
  1058.3 48.4 %slice-start.2 = ((s8[4718592]{0:T(1024)(128)(4,1)}), s8[4194304]{0:T(1024)(128)(4,1)S(1)}, s32[]{:S(2)}) async-start(s8[4718592]{0:T(1024)(128)(4,1)} %bitcast.94), calls=%async_computation.22 | async-start | bytes 8388608
  1133.3 177.9 %all-reduce.4.cloned.1.call-start = ((), (), s32[]{:S(2)}) async-start(), calls=%async_computation.15 | async-start | bytes 8421376 | tf_op jit(solution)/shard_map/psum | solution.py:752
  1134.0 225.0 %reduce-scatter.17.cloned.1.call-start = ((), (), s32[]{:S(2)}) async-start(), calls=%async_computation.16 | async-start | bytes 20971520 | tf_op jit(solution)/shard_map/reduce_scatter | solution.py:623
  (60 other events, 658.9 us)
Sparse Core Ops, SparseCore 0:
  17.9 84.9 all-gather.10
  105.3 83.9 all-gather.12
  214.9 67.7 all-gather.18
  285.0 66.4 all-gather.14
  353.7 67.2 all-gather.20
  422.7 66.4 all-gather.16
  491.6 66.4 all-gather.22
  561.6 115.0 reduce-scatter.6
  743.5 115.4 reduce-scatter.8
  861.8 64.4 reduce-scatter.12
  986.1 68.5 reduce-scatter.14
  1057.4 64.4 reduce-scatter.10
  1137.4 70.4 all-reduce.3
  1210.8 148.1 reduce-scatter.16

commit v7 on v6

--- a/solution.py
+++ b/solution.py
@@ -81,7 +81,7 @@
 
 
 def attn_bwd_kernel(first, prefix_s, valid_s, core_s, q_own_ref, q_oth_ref, g_own_ref, g_oth_ref, kv_ref, cos_ref, sin_ref,
-                    qpos_ref, kpos_ref, dq_own_ref, dq_oth_ref, dkv_ref):
+                    qpos_ref, kpos_ref, dq_own_ref, dq_oth_ref, dkv_own_ref, dkv_oth_ref):
     b = pl.program_id(0) + first
     rows, width = q_own_ref.shape[1:]
     hd = kv_ref.shape[-1] // 2
@@ -118,11 +118,11 @@
     d_keys = d_keys.astype(BF16)
     d_values = d_values.astype(BF16)
     span = kv_ref.shape[2]
-    for k, side in enumerate((core_s[0], 1 - core_s[0])):
+    for k, dst in enumerate((dkv_own_ref, dkv_oth_ref)):
         for c in range(shards):
             at = (k * shards + c) * span
-            dkv_ref[2 * c + side, 0, :, :hd] = d_keys[at:at + span]
-            dkv_ref[2 * c + side, 0, :, hd:] = d_values[at:at + span]
+            dst[c, 0, :, :hd] = d_keys[at:at + span]
+            dst[c, 0, :, hd:] = d_values[at:at + span]
 
 
 def attn_specs(rows, width, shards, two_hd, half):
@@ -166,15 +166,16 @@
     kv_spec = pl.BlockSpec((shards, 1, rows, two_hd), lambda b, *_: (0, b + first, 0, 0))
     heads = width * 2 // two_hd
     out = jax.ShapeDtypeStruct((batch, rows, width), BF16)
-    kv_out = jax.ShapeDtypeStruct(kv_all.shape, BF16)
+    dkv_spec = pl.BlockSpec((shards // 2, 1, rows, two_hd), lambda b, *_: (0, b + first, 0, 0))
+    kv_out = jax.ShapeDtypeStruct((shards // 2, batch, rows, two_hd), BF16)
     qpos_row = jnp.tile(qpos, heads)[None, :]
     n_keys = kpos.shape[0]
     flops = 2 * 5 * count * rows * 2 * width * n_keys
     return order.call(
-        functools.partial(attn_bwd_kernel, first), 9, len(earlier), prefetch=3,
-        out_shape=(out, out, kv_out), grid=(count,),
+        functools.partial(attn_bwd_kernel, first), 9, len(earlier), prefetch=3, in_parts=True,
+        out_shape=(out, out, kv_out, kv_out), grid=(count,),
         in_specs=[q_spec, q_spec, q_spec, q_spec, kv_spec, tab_spec, tab_spec, whole((1, heads * rows)), whole((n_keys, 1))],
-        out_specs=[q_spec, q_spec, kv_spec],
+        out_specs=[q_spec, q_spec, dkv_spec, dkv_spec],
         compiler_params=pltpu.CompilerParams(dimension_semantics=("arbitrary",), vmem_limit_bytes=30 << 20),
         cost_estimate=pl.CostEstimate(flops=flops, bytes_accessed=count * rows * width * 12 + kv_all.size * 4, transcendentals=count * rows * heads * 2 * n_keys),
         name="attn_bwd",
@@ -185,18 +186,20 @@
     def __init__(self):
         self.last = None
 
-    def call(self, kernel, n_in, n_kept=0, *, in_specs, out_specs, out_shape, grid, prefetch=0, scratch_shapes=(), **options):
+    def call(self, kernel, n_in, n_kept=0, *, in_specs, out_specs, out_shape, grid, in_parts=False, after=(), prefetch=0, scratch_shapes=(), **options):
         def run(*args):
-            deps = () if self.last is None or any(self.last is a for a in args) else (self.last,)
+            deps = (() if self.last is None or any(self.last is a for a in args) else (self.last,)) + tuple(after)
             n_args = prefetch + n_in
 
             def body(*refs):
                 kernel(*refs[:n_args], *refs[n_args + n_kept + len(deps):])
 
-            single = not isinstance(out_specs, (list, tuple))
-            n_out = 1 if single else len(out_specs)
+            n_out = len(out_specs) if isinstance(out_specs, (list, tuple)) else 1
+            shapes = [pltpu.HBM(o.shape, o.dtype) if in_parts and o.size > 1 << 17 else o for o in out_shape] if in_parts else out_shape
+            first = n_args
+            args = args[:first] + tuple(pltpu.with_memory_space_constraint(a, pltpu.HBM) for a in args[first:])
             out = pl.pallas_call(
-                body, out_shape=out_shape,
+                body, out_shape=shapes,
                 grid_spec=pltpu.PrefetchScalarGridSpec(
                     num_scalar_prefetch=prefetch, grid=grid, scratch_shapes=scratch_shapes, out_specs=out_specs,
                     in_specs=in_specs + [pl.BlockSpec(memory_space=pl.ANY)] * (n_kept + len(deps))),
@@ -364,7 +367,7 @@
     )(*lhs, *rhs, *far)
 
 
-def wgrad_kernel(core_s, *refs, n, tf, tn, cols, first):
+def wgrad_kernel(core_s, *refs, n, tf, tn, cols, first, first_col):
     lhs, rhs, out, l_buf, r_buf, sems = refs[:n], refs[n:2 * n], *refs[2 * n:]
     i, j, k = pl.program_id(0), pl.program_id(1), pl.program_id(2)
     step = (i * cols + j) * n + k
@@ -373,7 +376,7 @@
 
     def copies(s, at, p):
         row = pl.multiple_of((lax.div(s, cols * n) + first) * tf, tf)
-        col = pl.multiple_of(lax.rem(lax.div(s, n), cols) * tn, tn)
+        col = pl.multiple_of((lax.rem(lax.div(s, n), cols) + first_col) * tn, tn)
         out = []
         for q, (ref, buf, lanes) in enumerate(((lhs[p], l_buf, pl.ds(row, tf)), (rhs[p], r_buf, pl.ds(col, tn)))):
             if ref.ndim == 4:
@@ -405,19 +408,20 @@
     out[...] = jnp.where(k == 0, part, out[...] + part)
 
 
-def wgrad_call(order, core, lhs, rhs, tf=1024, tn=1024, tiles=None, earlier=None):
+def wgrad_call(order, core, lhs, rhs, tf=1024, tn=1024, tiles=None, col_tiles=None, earlier=None, after=()):
     n = len(lhs)
     rows = lhs[0].shape[-2]
     shards = lhs[0].size // (rows * lhs[0].shape[-1])
     width = rhs[0].shape[-1]
     height = lhs[0].shape[-1]
-    cols = width // tn
+    first_col, last_col = col_tiles or (0, width // tn)
+    cols = last_col - first_col
     first, last = tiles or (0, height // tf)
     kept = () if earlier is None else (earlier,)
     out = jax.ShapeDtypeStruct((height, width), F32)
     return order.call(
-        functools.partial(wgrad_kernel, n=n, tf=tf, tn=tn, cols=cols, first=first), 2 * n, len(kept), prefetch=1, out_shape=out, grid=(last - first, cols, n),
-        in_specs=[pl.BlockSpec(memory_space=pl.ANY)] * (2 * n), out_specs=pl.BlockSpec((tf, tn), lambda i, j, k, core: (i + first, j)),
+        functools.partial(wgrad_kernel, n=n, tf=tf, tn=tn, cols=cols, first=first, first_col=first_col), 2 * n, len(kept), prefetch=1, after=after, out_shape=out, grid=(last - first, cols, n),
+        in_specs=[pl.BlockSpec(memory_space=pl.ANY)] * (2 * n), out_specs=pl.BlockSpec((tf, tn), lambda i, j, k, core: (i + first, j + first_col)),
         scratch_shapes=[pltpu.VMEM((2, shards, rows, tf), BF16), pltpu.VMEM((2, shards, rows, tn), BF16), pltpu.SemaphoreType.DMA((2, 2, 2))],
         compiler_params=params(3), cost_estimate=cost(2 * n * shards * rows * height * width, *lhs, *rhs, out), name="wgrad",
     )(core, *lhs, *rhs, *kept)
@@ -570,7 +574,7 @@
     outs = (jax.ShapeDtypeStruct((8, dim), F32), jax.ShapeDtypeStruct((tokens, dim), BF16),
             jax.ShapeDtypeStruct((tokens, width), BF16), jax.ShapeDtypeStruct((tokens, width), BF16))
     return order.call(
-        functools.partial(d_resid_kernel, n=n), n + 5, len(earlier), out_shape=outs, grid=(n,),
+        functools.partial(d_resid_kernel, n=n), n + 5, len(earlier), in_parts=True, out_shape=outs, grid=(n,),
         in_specs=one + [far, far, pl.BlockSpec((1, dim), lambda i: (0, 0)), whole_w, whole_w],
         out_specs=[pl.BlockSpec((8, dim), lambda i: (0, 0)), far, mix, mix],
         compiler_params=params(1, 48), cost_estimate=cost(4 * n * size * dim * width, *dz, wo_own, wo_oth, outs[1]), name="d_resid",
@@ -631,18 +635,22 @@
     def flip(x_loc, bits):
         return lax.ppermute(x_loc, "tp", [(i, i ^ bits) for i in range(tp_size)])
 
-    def gather4_direct(x_loc, before=None):
+    def gather4_direct(x_loc, before=None, after=None):
         chip = lax.axis_index("tp") // 2
         half = x_loc.shape[0] // 2
         near, far = flip(x_loc, 2), flip(x_loc, 4)
         if before is not None:
             near, far, _ = lax.optimization_barrier((near, far, before))
         low, high = flip(near[:half], 4), flip(far[half:], 2)
+        if after is not None:
+            result = after()
+            x_loc, near, far, low, high, _ = lax.optimization_barrier((x_loc, near, far, low, high, result[0]))
         out = jnp.zeros((chips,) + x_loc.shape, x_loc.dtype)
         for k, block in ((0, x_loc), (1, near), (2, far)):
             out = lax.dynamic_update_slice(out, block[None], (chip ^ k, 0, 0))
         out = lax.dynamic_update_slice(out, low[None], (chip ^ 3, 0, 0))
-        return lax.dynamic_update_slice(out, high[None], (chip ^ 3, half, 0))
+        out = lax.dynamic_update_slice(out, high[None], (chip ^ 3, half, 0))
+        return out if after is None else (out, result)
 
     def local_layer(hidden, grad_out, prefix_len, valid_len, attn_norm, w_query, w_key, w_value, w_out, mlp_norm, w_gate, w_up, w_down):
         batch, rows, dim = hidden.shape
@@ -672,11 +680,14 @@
         wq_oth = swap(wq_own)
         q_own = dot_f32(normed_flat, wq_own, 1, 1)
         q_oth = dot_f32(normed_flat, wq_oth, 1, 1)
-        wo_own = gather4_direct(w_out, (q_own, q_oth)).reshape(chips * hd, dim)
+
+        def attend():
+            shape = batch, rows, chips * hd
+            return attn_fwd(q_own.reshape(shape), q_oth.reshape(shape), kv_all, cos_t, sin_t, qpos, kpos, scalars)
+
+        wo_own, (mix_own, mix_oth, q_own, q_oth) = gather4_direct(w_out, (q_own, q_oth), attend)
+        wo_own = wo_own.reshape(chips * hd, dim)
         wo_oth = swap(wo_own)
-        q_own = q_own.reshape(batch, rows, chips * hd)
-        q_oth = q_oth.reshape(batch, rows, chips * hd)
-        mix_own, mix_oth, q_own, q_oth = attn_fwd(q_own, q_oth, kv_all, cos_t, sin_t, qpos, kpos, scalars)
         mix_own = mix_own.reshape(tokens, chips * hd)
         mix_oth = mix_oth.reshape(tokens, chips * hd)
         hidden_flat = hidden.reshape(tokens, dim)
@@ -724,9 +735,11 @@
                 acts.append(act_call(order, core_1, z_all[c], d_act, w_gate, w_up, None))
             else:
                 acts.append(act_call(order, core_1, z_all[c], g_all[c], *weights))
-            if c > 0:
-                finish(c - 1)
-            far.append(swap(back_both(c, 1, ())))
+            part = back_both(c, 1, ())
+            far.append(swap(part))
+            if c == CHUNKS - 2:
+                for earlier in range(c + 1):
+                    finish(earlier)
         terms, *d_parts = d_resid_of(0, 1, None)
         grads = terms, d_parts, attn_bwd_of(0, 1, d_parts[1], d_parts[2], None)
         finish_last(CHUNKS - 1)
@@ -734,15 +747,23 @@
         g_gate = wgrad_call(order, core_1, z_all, [a[1] for a in shards], tiles=(0, 1))
 
         terms, d_resid, d_own, d_oth = d_resid_of(1, CHUNKS - 1, grads)
-        norm_terms, (dq_own, dq_oth, dkv) = grads[0] + terms, attn_bwd_of(1, CHUNKS - 1, d_own, d_oth, grads)
+        norm_terms, (dq_own, dq_oth, dkv_own, dkv_oth) = grads[0] + terms, attn_bwd_of(1, CHUNKS - 1, d_own, d_oth, grads)
         dq_own = dq_own.reshape(tokens, chips * hd)
         dq_oth = dq_oth.reshape(tokens, chips * hd)
-        dkv = lax.psum_scatter(dkv.reshape(tp_size * batch, rows, 2 * hd), "tp", scatter_dimension=0, tiled=True)
+        dkv_far = swap(dkv_oth)
         heads_far = head_wgrad(order, (mix_oth, dq_oth), (d_resid, normed_flat), hd)
+        dkv_far, dkv_own, _ = lax.optimization_barrier((dkv_far, dkv_own, heads_far))
+        dkv = scatter4((dkv_own.astype(F32) + dkv_far.astype(F32)).astype(BF16))
         heads_far = swap(heads_far)
-        g_gate = wgrad_call(order, core_1, z_all, [a[1] for a in shards], tiles=(1, 2), earlier=g_gate)
+
+        def gate_quarter(k, earlier):
+            return wgrad_call(order, core_1, z_all, [a[1] for a in shards], tiles=(1, 2), col_tiles=(k, k + 1), earlier=earlier)
+
+        g_gate = gate_quarter(0, g_gate)
         g_heads = head_wgrad(order, (mix_own, dq_own), (d_resid, normed_flat), hd, (heads_far,))
         g_heads = scatter4(g_heads)
+        g_gate = gate_quarter(1, g_gate)
+        dkv, g_gate = lax.optimization_barrier((dkv, g_gate))
         g_out, g_query = g_heads[0], g_heads[1].T
         d_k_raw = key_pull(dkv[..., :hd].astype(F32))[0]
         dkv = jnp.concatenate([d_k_raw.astype(BF16), dkv[..., hd:]], axis=-1).reshape(tokens, 2 * hd)
@@ -753,7 +774,8 @@
         g_attn_norm, g_mlp_norm = sums[dim:].reshape(2, dim)
         hidden_out = add_call(order, resid, mlp_sums).reshape(batch, rows, dim)
         g_up = wgrad_call(order, core_1, z_all, [a[2] for a in shards])
-        g_down = wgrad_call(order, core_1, [a[0] for a in shards], g_all)
+        g_down = wgrad_call(order, core_1, [a[0] for a in shards], g_all, tiles=(0, 1))
+        g_down = wgrad_call(order, core_1, [a[0] for a in shards], g_all, tiles=(1, 2), earlier=g_down, after=(g_heads,))
         return (hidden_out, grad_hidden.reshape(batch, rows, dim), g_attn_norm, g_query, sums[:dim, :hd], sums[:dim, hd:], g_out, g_mlp_norm, g_gate, g_up, g_down)
 
     return jax.shard_map(local_layer, mesh=mesh, in_specs=in_specs, out_specs=out_specs, check_vma=False)

time: 1380 us -> 1440 us (1.043)
  waiting for transfers between devices: 171 us -> 219 us
    reduce_scatter x5 -> x6, waiting for transfers between devices: 48 us -> 88.8 us  [scatter4(): lax.psum_scatter(flat, 'tp', scatter_dimension=0, tiled=True, axis_index_...]
    ppermute x6 -> x7, waiting for transfers between devices: 0.02 us -> 27 us  [swap(): return lax.ppermute(x_loc, 'tp', partner)]
    ppermute x8, waiting for transfers between devices: 87.1 us -> 70.9 us  [flip(): return lax.ppermute(x_loc, 'tp', [(i, i ^ bits) for i in range(tp_size)])]
    pallas_call x26 -> x28, Pallas kernels: 1030 us -> 1040 us  [run(): pl.pallas_call(body, out_shape=shapes, grid_spec=pltpu.PrefetchScalarGrid...]
    unnamed x134 -> x130, local copies, waits for them, and re-layouts: 53.9 us -> 49.7 us
  transfers between devices with their start and end apart: 28 -> 29, of which waited for: 10 -> 11; matrix products, arithmetic and copies ran while one was open for 4% -> 4% of each run, Pallas kernels for 73% -> 67%
where the time goes in v7:
time: 1440 us; the launch traced here: 1430 us
  Pallas kernels  1060 us (74%)
  waiting for transfers between devices  219 us (15%)
  local copies, waits for them, and re-layouts  82.8 us (6%)
  matrix products  21.7 us (2%)
  other arithmetic  19.3 us (1%)
  between operations  15.1 us (1%)
  starting transfers between devices  15 us (1%)
    pallas_call x28, Pallas kernels, run(): pl.pallas_call(body, out_shape=shapes, grid_spec=pltpu.PrefetchScalarGrid...  1040 us
    reduce_scatter x6, waiting for transfers between devices, scatter4(): lax.psum_scatter(flat, 'tp', scatter_dimension=0, tiled=True, axis_index_...  88.8 us
    ppermute x8, waiting for transfers between devices, flip(): return lax.ppermute(x_loc, 'tp', [(i, i ^ bits) for i in range(tp_size)])  70.9 us
    unnamed x130, local copies, waits for them, and re-layouts  49.7 us
    all_gather x7, waiting for transfers between devices, gather8(): return lax.all_gather(x_loc, 'tp', axis=0, tiled=False)  29 us
  transfers between devices with their start and end apart: 29, of which 11 were waited for; matrix products, arithmetic and copies ran while one was open for 4% of the time, Pallas kernels for 67%

profile of v7, /device:TPU:0, one launch (start us, length us, event | category | flops | bytes accessed | tf_op | source)
XLA Modules:
  0.0 1434.4 jit_solution(8098157084148622592)
XLA Ops:
  31.9 37.0 %collective-permute-done = bf16[256,2048]{0,1:T(8,128)(2,1)S(1)} collective-permute-done((bf16[256,2048]{0,1:T(8,128)(2,1)}, bf16[256,2048]{0,1:T(8,128)(2,1)S(1)}, u32[]{:S(2)}, u32[]{:S(2)}) %collective-permute-start) | collective-permute-done | bytes 1048608 | tf_op jit(solution)/shard_map/ppermute | solution.py:636
  82.5 11.9 collective-permute-done.2
  124.2 15.3 %collective-permute-done.5 = bf16[256,2048]{1,0:T(8,128)(2,1)S(1)} collective-permute-done((bf16[256,2048]{1,0:T(8,128)(2,1)}, bf16[256,2048]{1,0:T(8,128)(2,1)S(1)}, u32[]{:S(2)}, u32[]{:S(2)}) %collective-permute-start.5) | collective-permute-done | bytes 1048608 | tf_op jit(solution)/shard_map/ppermute | solution.py:636
  151.2 20.3 %attn_fwd.1 = (bf16[12,96,1024]{2,1,0:T(8,128)(2,1)S(1)}, bf16[12,96,1024]{2,1,0:T(8,128)(2,1)S(1)}, bf16[12,96,1024]{2,1,0:T(8,128)(2,1)S(1)}, bf16[12,96,1024]{2,1,0:T(8,128)(2,1)S(1)}) custom-call(s32[12]{0:T(128)S(1)} %copy-done.27, s32[12]{0:T(128)S(1)} %copy-done.28, s32[1]{0:T(128)} %bitcast.1.core_s.refs_0_.refs_2_, f32[12,96,1024]{2,1,0:T(8,128)S(1)} %bitcast.110, ...), custom_call_target="tpu_custom_call" | custom-call | flops 7247757312 | bytes 28311552 | tf_op jit(solution)/shard_map/attn_fwd/pallas_call | solution.py:148
  189.7 19.6 %resid.1 = (bf16[1152,2048]{1,0:T(8,128)(2,1)}, bf16[384,2048]{1,0:T(8,128)(2,1)}, bf16[384,2048]{1,0:T(8,128)(2,1)}, bf16[384,2048]{1,0:T(8,128)(2,1)}) custom-call(bf16[1152,2048]{1,0:T(8,128)(2,1)} %bitcast.124, bf16[1152,1024]{1,0:T(8,128)(2,1)} %bitcast.99, bf16[1152,1024]{1,0:T(8,128)(2,1)} %bitcast.112, bf16[1024,2048]{1,0:T(8,128)(2,1)} %bitcast.120, ...), custom_call_target="tpu_custom_call" | custom-call | flops 9663676416 | bytes 27262976 | tf_op jit(solution)/shard_map/resid/pallas_call | solution.py:201
  211.8 33.7 %d_act.2.refs_2_ = bf16[3072,2048]{1,0:T(8,128)(2,1)} custom-call(s32[1]{0:T(128)} %bitcast.1.core_s.refs_0_.refs_2_, bf16[4,2,384,2048]{3,2,1,0:T(8,128)(2,1)} %bitcast.140, bf16[2048,2048]{1,0:T(8,128)(2,1)} %refs_1_.4, bf16[1152,2048]{1,0:T(8,128)(2,1)} %get-tuple-element.66.refs_3_.refs_1_.refs_2_.refs_0_), custom_call_target="tpu_custom_call" | custom-call | flops 25769803776 | bytes 33554432 | tf_op jit(solution)/shard_map/d_act/pallas_call | solution.py:201
  245.6 28.9 %all-gather.19.cloned.1.call-done = bf16[3072,2048]{1,0:T(8,128)(2,1)} async-done(((bf16[384,2048]{1,0:T(8,128)(2,1)}), bf16[3072,2048]{1,0:T(8,128)(2,1)}) %all-gather.19.cloned.1.call-update) | async-done | bytes 12582928 | tf_op jit(solution)/shard_map/all_gather | solution.py:630
  274.5 70.8 %mlp_act.3 = (bf16[3072,2048]{1,0:T(8,128)(2,1)}, bf16[3072,2048]{1,0:T(8,128)(2,1)}, bf16[3072,2048]{1,0:T(8,128)(2,1)}) custom-call(s32[1]{0:T(128)} %bitcast.1.core_s.refs_0_.refs_2_, bf16[4,2,384,2048]{3,2,1,0:T(8,128)(2,1)} %bitcast.149, bf16[3072,2048]{1,0:T(8,128)(2,1)} %d_act.2.refs_2_, bf16[2048,2048]{1,0:T(8,128)(2,1)} %refs_2_.5, ...), custom_call_target="tpu_custom_call" | custom-call | flops 51539607552 | bytes 79691776 | tf_op jit(solution)/shard_map/mlp_act/pallas_call | solution.py:201
  345.3 47.4 %mlp_back.7.refs_3_ = bf16[4,2,384,2048]{3,2,1,0:T(8,128)(2,1)} custom-call(bf16[3072,2048]{1,0:T(8,128)(2,1)} %get-tuple-element.68.refs_0_, bf16[3072,2048]{1,0:T(8,128)(2,1)} %get-tuple-element.69.refs_1_, bf16[3072,2048]{1,0:T(8,128)(2,1)} %get-tuple-element.70.refs_2_, bf16[2048,2048]{1,0:T(8,128)(2,1)} %refs_2_.5, bf16[2048,2048]{1,0:T(8,128)(2,1)} %refs_3_.17, ...), custom_call_target="tpu_custom_call" | custom-call | flops 38654705664 | bytes 75497472 | tf_op jit(solution)/shard_map/mlp_back/pallas_call | solution.py:201
  393.0 32.5 %d_act.3.refs_2_ = bf16[3072,2048]{1,0:T(8,128)(2,1)} custom-call(s32[1]{0:T(128)} %bitcast.1.core_s.refs_0_.refs_2_, bf16[4,2,384,2048]{3,2,1,0:T(8,128)(2,1)} %bitcast.143, bf16[2048,2048]{1,0:T(8,128)(2,1)} %refs_1_.4, bf16[4,2,384,2048]{3,2,1,0:T(8,128)(2,1)} %mlp_back.7.refs_3_), custom_call_target="tpu_custom_call" | custom-call | flops 25769803776 | bytes 33554432 | tf_op jit(solution)/shard_map/d_act/pallas_call | solution.py:201
  425.5 70.9 %mlp_act.4 = (bf16[3072,2048]{1,0:T(8,128)(2,1)}, bf16[3072,2048]{1,0:T(8,128)(2,1)}, bf16[3072,2048]{1,0:T(8,128)(2,1)}) custom-call(s32[1]{0:T(128)} %bitcast.1.core_s.refs_0_.refs_2_, bf16[4,2,384,2048]{3,2,1,0:T(8,128)(2,1)} %bitcast.154, bf16[3072,2048]{1,0:T(8,128)(2,1)} %d_act.3.refs_2_, bf16[2048,2048]{1,0:T(8,128)(2,1)} %refs_2_.5, ...), custom_call_target="tpu_custom_call" | custom-call | flops 51539607552 | bytes 79691776 | tf_op jit(solution)/shard_map/mlp_act/pallas_call | solution.py:201
  496.5 47.3 %mlp_back.8.refs_7_ = bf16[4,2,384,2048]{3,2,1,0:T(8,128)(2,1)} custom-call(bf16[3072,2048]{1,0:T(8,128)(2,1)} %get-tuple-element.72.refs_0_, bf16[3072,2048]{1,0:T(8,128)(2,1)} %get-tuple-element.73.refs_1_, bf16[3072,2048]{1,0:T(8,128)(2,1)} %get-tuple-element.74.refs_2_, bf16[2048,2048]{1,0:T(8,128)(2,1)} %refs_2_.5, bf16[2048,2048]{1,0:T(8,128)(2,1)} %refs_3_.17, ...), custom_call_target="tpu_custom_call" | custom-call | flops 38654705664 | bytes 75497472 | tf_op jit(solution)/shard_map/mlp_back/pallas_call | solution.py:201
  543.8 49.8 %mlp_back.9.refs_7_ = bf16[4,2,384,2048]{3,2,1,0:T(8,128)(2,1)} custom-call(bf16[3072,2048]{1,0:T(8,128)(2,1)} %get-tuple-element.68.refs_0_, bf16[3072,2048]{1,0:T(8,128)(2,1)} %get-tuple-element.69.refs_1_, bf16[3072,2048]{1,0:T(8,128)(2,1)} %get-tuple-element.70.refs_2_, bf16[2048,2048]{1,0:T(8,128)(2,1)} %refs_2_.5, bf16[2048,2048]{1,0:T(8,128)(2,1)} %refs_3_.17, ...), custom_call_target="tpu_custom_call" | custom-call | flops 38654705664 | bytes 75497472 | tf_op jit(solution)/shard_map/mlp_back/pallas_call | solution.py:201
  593.8 19.5 %collective-permute-done.11.refs_6_ = bf16[4,2,384,2048]{3,2,1,0:T(8,128)(2,1)} collective-permute-done((bf16[4,2,384,2048]{3,2,1,0:T(8,128)(2,1)}, bf16[4,2,384,2048]{3,2,1,0:T(8,128)(2,1)}, u32[]{:S(2)}, u32[]{:S(2)}) %collective-permute-start.11) | collective-permute-done | bytes 12582944 | tf_op jit(solution)/shard_map/ppermute | solution.py:633
  613.2 49.6 %mlp_back.10.refs_6_ = bf16[4,2,384,2048]{3,2,1,0:T(8,128)(2,1)} custom-call(bf16[3072,2048]{1,0:T(8,128)(2,1)} %get-tuple-element.72.refs_0_, bf16[3072,2048]{1,0:T(8,128)(2,1)} %get-tuple-element.73.refs_1_, bf16[3072,2048]{1,0:T(8,128)(2,1)} %get-tuple-element.74.refs_2_, bf16[2048,2048]{1,0:T(8,128)(2,1)} %refs_2_.5, bf16[2048,2048]{1,0:T(8,128)(2,1)} %refs_3_.17, ...), custom_call_target="tpu_custom_call" | custom-call | flops 38654705664 | bytes 75497472 | tf_op jit(solution)/shard_map/mlp_back/pallas_call | solution.py:201
  663.0 92.3 %mlp_act.5 = (bf16[3072,2048]{1,0:T(8,128)(2,1)}, bf16[3072,2048]{1,0:T(8,128)(2,1)}, bf16[3072,2048]{1,0:T(8,128)(2,1)}) custom-call(s32[1]{0:T(128)} %bitcast.1.core_s.refs_0_.refs_2_, bf16[4,2,384,2048]{3,2,1,0:T(8,128)(2,1)} %bitcast.159, bf16[4,2,384,2048]{3,2,1,0:T(8,128)(2,1)} %bitcast.146, bf16[2048,2048]{1,0:T(8,128)(2,1)} %refs_2_.5, ...), custom_call_target="tpu_custom_call" | custom-call | flops 77309411328 | bytes 88080384 | tf_op jit(solution)/shard_map/mlp_act/pallas_call | solution.py:201
  755.3 47.9 %mlp_back.11.refs_6_ = bf16[4,2,384,2048]{3,2,1,0:T(8,128)(2,1)} custom-call(bf16[3072,2048]{1,0:T(8,128)(2,1)} %get-tuple-element.77.refs_0_, bf16[3072,2048]{1,0:T(8,128)(2,1)} %get-tuple-element.78.refs_1_, bf16[3072,2048]{1,0:T(8,128)(2,1)} %get-tuple-element.76.refs_2_.refs_0_, bf16[2048,2048]{1,0:T(8,128)(2,1)} %refs_2_.5, ...), custom_call_target="tpu_custom_call" | custom-call | flops 38654705664 | bytes 75497472 | tf_op jit(solution)/shard_map/mlp_back/pallas_call | solution.py:201
  823.7 13.2 attn_bwd.2
  836.9 34.5 %mlp_back.12.refs_3_ = bf16[4,384,2048]{2,1,0:T(8,128)(2,1)} custom-call(bf16[3072,2048]{1,0:T(8,128)(2,1)} %get-tuple-element.77.refs_0_, bf16[3072,2048]{1,0:T(8,128)(2,1)} %get-tuple-element.78.refs_1_, bf16[2048,2048]{1,0:T(8,128)(2,1)} %refs_2_.5, bf16[2048,2048]{1,0:T(8,128)(2,1)} %refs_3_.17, ...), custom_call_target="tpu_custom_call" | custom-call | flops 25769803776 | bytes 48234496 | tf_op jit(solution)/shard_map/mlp_back/pallas_call | solution.py:201
  871.4 20.3 %mlp_back.13.refs_7_ = bf16[4,384,2048]{2,1,0:T(8,128)(2,1)} custom-call(bf16[3072,2048]{1,0:T(8,128)(2,1)} %get-tuple-element.76.refs_2_.refs_0_, bf16[2048,2048]{1,0:T(8,128)(2,1)} %refs_1_.4, bf16[4,2,384,2048]{3,2,1,0:T(8,128)(2,1)} %collective-permute-done.12.refs_4_.refs_2_, bf16[4,384,2048]{2,1,0:T(8,128)(2,1)} %mlp_back.12.refs_3_), custom_call_target="tpu_custom_call" | custom-call | flops 12884901888 | bytes 27262976 | tf_op jit(solution)/shard_map/mlp_back/pallas_call | solution.py:201
  891.8 47.7 %wgrad.6.refs_10_.refs_7_ = f32[2048,2048]{1,0:T(8,128)} custom-call(s32[1]{0:T(128)} %bitcast.1.core_s.refs_0_.refs_2_, bf16[4,2,384,2048]{3,2,1,0:T(8,128)(2,1)} %bitcast.150, bf16[4,2,384,2048]{3,2,1,0:T(8,128)(2,1)} %bitcast.155, bf16[4,2,384,2048]{3,2,1,0:T(8,128)(2,1)} %bitcast.160, bf16[8,384,2048]{2,1,0:T(8,128)(2,1)} %bitcast.173, ...), custom_call_target="tpu_custom_call" | custom-call | flops 77309411328 | bytes 92274688 | tf_op jit(solution)/shard_map/wgrad/pallas_call | solution.py:201
  942.8 17.4 %d_resid.3 = (f32[8,2048]{1,0:T(8,128)S(1)}, bf16[1152,2048]{1,0:T(8,128)(2,1)}, bf16[1152,1024]{1,0:T(8,128)(2,1)}, bf16[1152,1024]{1,0:T(8,128)(2,1)}) custom-call(bf16[2,384,2048]{2,1,0:T(8,128)(2,1)S(1)} %copy-done.5, bf16[384,2048]{1,0:T(8,128)(2,1)S(1)} %copy-done.15, ...), custom_call_target="tpu_custom_call", output_to_operand_aliasing={{1}: (7, {}), {2}: (8, {}), {3}: (9, {})} | custom-call | flops 6442450944 | bytes 17825792 | tf_op jit(solution)/shard_map/d_resid/pallas_call | solution.py:201
  967.3 24.9 %attn_bwd.3 = (bf16[12,96,1024]{2,1,0:T(8,128)(2,1)}, bf16[12,96,1024]{2,1,0:T(8,128)(2,1)}, bf16[4,12,96,512]{3,2,1,0:T(8,128)(2,1)}, bf16[4,12,96,512]{3,2,1,0:T(8,128)(2,1)}) custom-call(s32[12]{0:T(128)S(1)} %copy-done.27, s32[12]{0:T(128)S(1)} %copy-done.28, ...), custom_call_target="tpu_custom_call", output_to_operand_aliasing={{0}: (12, {}), {1}: (13, {}), {2}: (14, {}), {3}: (15, {})} | custom-call | flops 12079595520 | bytes 28311552 | tf_op jit(solution)/shard_map/attn_bwd/pallas_call | solution.py:201
  994.1 15.7 %head_wgrad.2.refs_8_ = f32[4,2,256,2048]{3,2,1,0:T(8,128)} custom-call(bf16[1152,1024]{1,0:T(8,128)(2,1)S(1)} %bitcast.113, bf16[1152,1024]{1,0:T(8,128)(2,1)S(1)} %bitcast.115, bf16[1152,2048]{1,0:T(8,128)(2,1)} %get-tuple-element.95.refs_2_.refs_4_, bf16[1152,2048]{1,0:T(8,128)(2,1)} %bitcast.89, bf16[12,96,1024]{2,1,0:T(8,128)(2,1)} %get-tuple-element.96.refs_4_), custom_call_target="tpu_custom_call" | custom-call | flops 9663676416 | bytes 30932992 | tf_op jit(solution)/shard_map/head_wgrad/pallas_call | solution.py:201
  1018.0 28.3 %wgrad.7.refs_5_.refs_7_ = f32[2048,2048]{1,0:T(8,128)} custom-call(s32[1]{0:T(128)} %bitcast.1.core_s.refs_0_.refs_2_, bf16[4,2,384,2048]{3,2,1,0:T(8,128)(2,1)} %bitcast.151, bf16[4,2,384,2048]{3,2,1,0:T(8,128)(2,1)} %bitcast.156, bf16[4,2,384,2048]{3,2,1,0:T(8,128)(2,1)} %bitcast.161, ...), custom_call_target="tpu_custom_call", output_to_operand_aliasing={{}: (7, {})} | custom-call | flops 77309411328 | bytes 92274688 | tf_op jit(solution)/shard_map/wgrad/pallas_call | solution.py:201
  1046.4 19.9 %head_wgrad.3.refs_8_ = f32[4,2,256,2048]{3,2,1,0:T(8,128)} custom-call(bf16[1152,1024]{1,0:T(8,128)(2,1)S(1)} %bitcast.100, bf16[1152,1024]{1,0:T(8,128)(2,1)S(1)} %bitcast.102, bf16[1152,2048]{1,0:T(8,128)(2,1)} %get-tuple-element.95.refs_2_.refs_4_, bf16[1152,2048]{1,0:T(8,128)(2,1)} %bitcast.90, f32[4,2,256,2048]{3,2,1,0:T(8,128)} %collective-permute-done.14.refs_4_, ...), custom_call_target="tpu_custom_call" | custom-call | flops 9663676416 | bytes 47710208 | tf_op jit(solution)/shard_map/head_wgrad/pallas_call | solution.py:201
  1066.3 27.1 %wgrad.8.refs_9_ = f32[2048,2048]{1,0:T(8,128)} custom-call(s32[1]{0:T(128)} %bitcast.1.core_s.refs_0_.refs_2_, bf16[4,2,384,2048]{3,2,1,0:T(8,128)(2,1)} %bitcast.152, bf16[4,2,384,2048]{3,2,1,0:T(8,128)(2,1)} %bitcast.157, bf16[4,2,384,2048]{3,2,1,0:T(8,128)(2,1)} %bitcast.162, bf16[8,384,2048]{2,1,0:T(8,128)(2,1)} %bitcast.175, ...), custom_call_target="tpu_custom_call", output_to_operand_aliasing={{}: (7, {})} | custom-call | flops 77309411328 | bytes 92274688 | tf_op jit(solution)/shard_map/wgrad/pallas_call | solution.py:201
  1096.3 25.9 %d_hidden.1 = (bf16[1152,2048]{1,0:T(8,128)(2,1)}, f32[8,2048]{1,0:T(8,128)}) custom-call(bf16[1152,1024]{1,0:T(8,128)(2,1)} %bitcast.101, bf16[1152,1024]{1,0:T(8,128)(2,1)} %bitcast.114, bf16[1152,512]{1,0:T(8,128)(2,1)} %bitcast.97, bf16[1152,2048]{1,0:T(8,128)(2,1)} %bitcast.125, bf16[1152,2048]{1,0:T(8,128)(2,1)} %get-tuple-element.95.refs_2_.refs_4_, ...), custom_call_target="tpu_custom_call" | custom-call | flops 14495514624 | bytes 27328512 | tf_op jit(solution)/shard_map/d_hidden/pallas_call | solution.py:201
  1150.0 88.1 %wgrad.9.refs_7_ = f32[2048,2048]{1,0:T(8,128)} custom-call(s32[1]{0:T(128)} %bitcast.1.core_s.refs_0_.refs_2_, bf16[4,2,384,2048]{3,2,1,0:T(8,128)(2,1)} %bitcast.153, bf16[4,2,384,2048]{3,2,1,0:T(8,128)(2,1)} %bitcast.158, bf16[4,2,384,2048]{3,2,1,0:T(8,128)(2,1)} %bitcast.163, bf16[8,384,2048]{2,1,0:T(8,128)(2,1)} %bitcast.168, ...), custom_call_target="tpu_custom_call" | custom-call | flops 77309411328 | bytes 92274688 | tf_op jit(solution)/shard_map/wgrad/pallas_call | solution.py:201
  1238.1 47.8 %wgrad.10.refs_7_ = f32[2048,2048]{1,0:T(8,128)} custom-call(s32[1]{0:T(128)} %bitcast.1.core_s.refs_0_.refs_2_, bf16[8,384,2048]{2,1,0:T(8,128)(2,1)} %bitcast.164, bf16[8,384,2048]{2,1,0:T(8,128)(2,1)} %bitcast.166, bf16[8,384,2048]{2,1,0:T(8,128)(2,1)} %bitcast.170, bf16[4,2,384,2048]{3,2,1,0:T(8,128)(2,1)} %bitcast.141, ...), custom_call_target="tpu_custom_call" | custom-call | flops 77309411328 | bytes 92274688 | tf_op jit(solution)/shard_map/wgrad/pallas_call | solution.py:201
  1292.5 81.9 %reduce-scatter.17.cloned.1.call-done.refs_8_ = f32[2,256,2048]{2,1,0:T(8,128)} async-done(((f32[8,256,2048]{2,1,0:T(8,128)}), f32[2,256,2048]{2,1,0:T(8,128)}) %reduce-scatter.17.cloned.1.call-update) | async-done | bytes 4194320 | tf_op jit(solution)/shard_map/reduce_scatter | solution.py:627
  1380.1 47.5 %wgrad.11 = f32[2048,2048]{1,0:T(8,128)} custom-call(s32[1]{0:T(128)} %bitcast.1.core_s.refs_0_.refs_2_, bf16[8,384,2048]{2,1,0:T(8,128)(2,1)} %bitcast.165, bf16[8,384,2048]{2,1,0:T(8,128)(2,1)} %bitcast.167, bf16[8,384,2048]{2,1,0:T(8,128)(2,1)} %bitcast.171, bf16[4,2,384,2048]{3,2,1,0:T(8,128)(2,1)} %bitcast.142, ...), custom_call_target="tpu_custom_call", output_to_operand_aliasing={{}: (7, {})} | custom-call | flops 77309411328 | bytes 92274688 | tf_op jit(solution)/shard_map/wgrad/pallas_call | solution.py:201
  (258 shorter events, 184.4 us)
Async XLA Ops:
  7.2 138.6 %all-gather.11.cloned.1.call-start = ((), (), s32[]{:S(2)}) async-start(), calls=%async_computation.6 | async-start | bytes 10616832 | tf_op jit(solution)/shard_map/all_gather | solution.py:630
  17.9 942.3 %copy-start.17 = (f32[96,128]{1,0:T(8,128)}, f32[96,128]{1,0:T(8,128)S(1)}, u32[]{:S(2)}) copy-start(f32[96,128]{1,0:T(8,128)S(1)} %get-tuple-element.151.cos_ref.refs_8_) | copy-start | bytes 147460
  17.9 942.3 %copy-start.19 = (f32[96,128]{1,0:T(8,128)}, f32[96,128]{1,0:T(8,128)S(1)}, u32[]{:S(2)}) copy-start(f32[96,128]{1,0:T(8,128)S(1)} %get-tuple-element.152.sin_ref.refs_9_) | copy-start | bytes 147460
  20.5 191.3 %all-gather.13.cloned.1.call-start = ((), (), s32[]{:S(2)}) async-start(), calls=%async_computation.7 | async-start | bytes 14155776 | tf_op jit(solution)/shard_map/all_gather | solution.py:630
  25.3 249.2 %all-gather.19.cloned.1.call-start = ((), (), s32[]{:S(2)}) async-start(), calls=%async_computation.17 | async-start | bytes 14155776 | tf_op jit(solution)/shard_map/all_gather | solution.py:630
  25.5 43.4 %collective-permute-start = (bf16[256,2048]{0,1:T(8,128)(2,1)}, bf16[256,2048]{0,1:T(8,128)(2,1)S(1)}, u32[]{:S(2)}, u32[]{:S(2)}) collective-permute-start(bf16[256,2048]{0,1:T(8,128)(2,1)} %bitcast.3), channel_id=1, source_target_pairs={{0,2},{1,3},{2,0},{3,1},{4,6},{5,7},{6,4},{7,5}} | collective-permute-start | bytes 3145736 | tf_op jit(solution)/shard_map/ppermute | solution.py:636
  28.8 43.0 %collective-permute-start.1 = (bf16[256,2048]{0,1:T(8,128)(2,1)}, bf16[256,2048]{0,1:T(8,128)(2,1)}, u32[]{:S(2)}, u32[]{:S(2)}) collective-permute-start(bf16[256,2048]{0,1:T(8,128)(2,1)} %bitcast.3), channel_id=1, source_target_pairs={{0,4},{1,5},{2,6},{3,7},{4,0},{5,1},{6,2},{7,3}} | collective-permute-start | bytes 3145736 | tf_op jit(solution)/shard_map/ppermute | solution.py:636
  68.9 25.4 %collective-permute-start.2 = (bf16[128,2048]{0,1:T(8,128)(2,1)S(1)}, bf16[128,2048]{0,1:T(8,128)(2,1)S(1)}, u32[]{:S(2)}, u32[]{:S(2)}) collective-permute-start(bf16[128,2048]{0,1:T(8,128)(2,1)S(1)} %slice.76), channel_id=1, source_target_pairs={{0,4},{1,5},{2,6},{3,7},{4,0},{5,1},{6,2},{7,3}} | collective-permute-start | bytes 1572872 | tf_op jit(solution)/shard_map/ppermute | solution.py:636
  73.8 25.2 %collective-permute-start.3 = (bf16[128,2048]{0,1:T(8,128)(2,1)}, bf16[128,2048]{0,1:T(8,128)(2,1)}, u32[]{:S(2)}, u32[]{:S(2)}) collective-permute-start(bf16[128,2048]{0,1:T(8,128)(2,1)} %slice.77), channel_id=1, source_target_pairs={{0,2},{1,3},{2,0},{3,1},{4,6},{5,7},{6,4},{7,5}} | collective-permute-start | bytes 1572872 | tf_op jit(solution)/shard_map/ppermute | solution.py:636
  101.9 13.4 collective-permute-start.4
  101.9 37.6 %collective-permute-start.5 = (bf16[256,2048]{1,0:T(8,128)(2,1)}, bf16[256,2048]{1,0:T(8,128)(2,1)S(1)}, u32[]{:S(2)}, u32[]{:S(2)}) collective-permute-start(bf16[256,2048]{1,0:T(8,128)(2,1)} %param.21), channel_id=1, source_target_pairs={{0,2},{1,3},{2,0},{3,1},{4,6},{5,7},{6,4},{7,5}} | collective-permute-start | bytes 3145736 | tf_op jit(solution)/shard_map/ppermute | solution.py:636
  103.0 37.9 %collective-permute-start.6 = (bf16[256,2048]{1,0:T(8,128)(2,1)}, bf16[256,2048]{1,0:T(8,128)(2,1)S(1)}, u32[]{:S(2)}, u32[]{:S(2)}) collective-permute-start(bf16[256,2048]{1,0:T(8,128)(2,1)} %param.21), channel_id=1, source_target_pairs={{0,4},{1,5},{2,6},{3,7},{4,0},{5,1},{6,2},{7,3}} | collective-permute-start | bytes 3145736 | tf_op jit(solution)/shard_map/ppermute | solution.py:636
  141.9 31.0 %collective-permute-start.7 = (bf16[128,2048]{1,0:T(8,128)(2,1)}, bf16[128,2048]{1,0:T(8,128)(2,1)}, u32[]{:S(2)}, u32[]{:S(2)}) collective-permute-start(bf16[128,2048]{1,0:T(8,128)(2,1)} %slice.65), channel_id=1, source_target_pairs={{0,4},{1,5},{2,6},{3,7},{4,0},{5,1},{6,2},{7,3}} | collective-permute-start | bytes 1572872 | tf_op jit(solution)/shard_map/ppermute | solution.py:636
  144.2 28.8 %collective-permute-start.8 = (bf16[128,2048]{1,0:T(8,128)(2,1)}, bf16[128,2048]{1,0:T(8,128)(2,1)}, u32[]{:S(2)}, u32[]{:S(2)}) collective-permute-start(bf16[128,2048]{1,0:T(8,128)(2,1)} %slice.66), channel_id=1, source_target_pairs={{0,2},{1,3},{2,0},{3,1},{4,6},{5,7},{6,4},{7,5}} | collective-permute-start | bytes 1572872 | tf_op jit(solution)/shard_map/ppermute | solution.py:636
  172.9 643.5 %copy-start.34 = (bf16[12,96,1024]{2,1,0:T(8,128)(2,1)}, bf16[12,96,1024]{2,1,0:T(8,128)(2,1)S(1)}, u32[]{:S(2)}) copy-start(bf16[12,96,1024]{2,1,0:T(8,128)(2,1)S(1)} %get-tuple-element.79.refs_3_) | copy-start | bytes 7077892
  179.4 8.3 collective-permute-start.9
  209.3 183.7 %all-gather.15.cloned.1.call-start = ((), (), s32[]{:S(2)}) async-start(), calls=%async_computation.8 | async-start | bytes 14155776 | tf_op jit(solution)/shard_map/all_gather | solution.py:630
  209.9 215.7 %all-gather.21.cloned.1.call-start = ((), (), s32[]{:S(2)}) async-start(), calls=%async_computation.18 | async-start | bytes 14155776 | tf_op jit(solution)/shard_map/all_gather | solution.py:630
  210.4 452.5 %all-gather.17.cloned.1.call-start = ((), (), s32[]{:S(2)}) async-start(), calls=%async_computation.11 | async-start | bytes 14155776 | tf_op jit(solution)/shard_map/all_gather | solution.py:630
  211.0 451.9 %all-gather.23.cloned.1.call-start = ((), (), s32[]{:S(2)}) async-start(), calls=%async_computation.19 | async-start | bytes 14155776 | tf_op jit(solution)/shard_map/all_gather | solution.py:630
  211.8 592.3 %reduce-scatter.7.cloned.1.call-start = ((), (), s32[]{:S(2)}) async-start(), calls=%async_computation.9 | async-start | bytes 15728640 | tf_op jit(solution)/shard_map/reduce_scatter | solution.py:627
  392.7 151.0 %collective-permute-start.10 = (bf16[4,2,384,2048]{3,2,1,0:T(8,128)(2,1)}, bf16[4,2,384,2048]{3,2,1,0:T(8,128)(2,1)}, u32[]{:S(2)}, u32[]{:S(2)}) collective-permute-start(bf16[4,2,384,2048]{3,2,1,0:T(8,128)(2,1)} %mlp_back.7.refs_3_), channel_id=1, source_target_pairs={{0,1},{1,0},{2,3},{3,2},{4,5},{5,4},{6,7},{7,6}} | collective-permute-start | bytes 37748744 | tf_op jit(solution)/shard_map/ppermute | solution.py:633
  593.7 345.8 %reduce-scatter.9.cloned.1.call-start = ((), (), s32[]{:S(2)}) async-start(), calls=%async_computation.10 | async-start | bytes 15728640 | tf_op jit(solution)/shard_map/reduce_scatter | solution.py:627
  593.7 19.5 %collective-permute-start.11 = (bf16[4,2,384,2048]{3,2,1,0:T(8,128)(2,1)}, bf16[4,2,384,2048]{3,2,1,0:T(8,128)(2,1)}, u32[]{:S(2)}, u32[]{:S(2)}) collective-permute-start(bf16[4,2,384,2048]{3,2,1,0:T(8,128)(2,1)} %mlp_back.8.refs_7_), channel_id=1, source_target_pairs={{0,1},{1,0},{2,3},{3,2},{4,5},{5,4},{6,7},{7,6}} | collective-permute-start | bytes 37748744 | tf_op jit(solution)/shard_map/ppermute | solution.py:633
  662.9 276.6 %reduce-scatter.13.cloned.1.call-start = ((), (), s32[]{:S(2)}) async-start(), calls=%async_computation.13 | async-start | bytes 7864320 | tf_op jit(solution)/shard_map/reduce_scatter | solution.py:627
  803.2 33.7 %collective-permute-start.12 = (bf16[4,2,384,2048]{3,2,1,0:T(8,128)(2,1)}, bf16[4,2,384,2048]{3,2,1,0:T(8,128)(2,1)}, u32[]{:S(2)}, u32[]{:S(2)}) collective-permute-start(bf16[4,2,384,2048]{3,2,1,0:T(8,128)(2,1)} %mlp_back.11.refs_6_), channel_id=1, source_target_pairs={{0,1},{1,0},{2,3},{3,2},{4,5},{5,4},{6,7},{7,6}} | collective-permute-start | bytes 37748744 | tf_op jit(solution)/shard_map/ppermute | solution.py:633
  871.4 222.0 %reduce-scatter.15.cloned.1.call-start = ((), (), s32[]{:S(2)}) async-start(), calls=%async_computation.14 | async-start | bytes 5898240 | tf_op jit(solution)/shard_map/reduce_scatter | solution.py:627
  992.2 17.9 %collective-permute-start.13 = (bf16[4,12,96,512]{3,2,1,0:T(8,128)(2,1)}, bf16[4,12,96,512]{3,2,1,0:T(8,128)(2,1)}, u32[]{:S(2)}, u32[]{:S(2)}) collective-permute-start(bf16[4,12,96,512]{3,2,1,0:T(8,128)(2,1)} %get-tuple-element.92), channel_id=1, source_target_pairs={{0,1},{1,0},{2,3},{3,2},{4,5},{5,4},{6,7},{7,6}} | collective-permute-start | bytes 14155784 | tf_op jit(solution)/shard_map/ppermute | solution.py:633
  1009.9 36.5 %collective-permute-start.14 = (f32[4,2,256,2048]{3,2,1,0:T(8,128)}, f32[4,2,256,2048]{3,2,1,0:T(8,128)}, u32[]{:S(2)}, u32[]{:S(2)}) collective-permute-start(f32[4,2,256,2048]{3,2,1,0:T(8,128)} %head_wgrad.2.refs_8_), channel_id=1, source_target_pairs={{0,1},{1,0},{2,3},{3,2},{4,5},{5,4},{6,7},{7,6}} | collective-permute-start | bytes 50331656 | tf_op jit(solution)/shard_map/ppermute | solution.py:633
  1016.7 120.7 %reduce-scatter.11.cloned.1.call-start = ((), (), s32[]{:S(2)}) async-start(), calls=%async_computation.12 | async-start | bytes 7864320 | tf_op jit(solution)/shard_map/reduce_scatter | solution.py:627
  1148.7 137.2 %all-reduce.4.cloned.1.call-start = ((), (), s32[]{:S(2)}) async-start(), calls=%async_computation.15 | async-start | bytes 8421376 | tf_op jit(solution)/shard_map/psum | solution.py:773
  1149.5 224.9 %reduce-scatter.17.cloned.1.call-start = ((), (), s32[]{:S(2)}) async-start(), calls=%async_computation.16 | async-start | bytes 20971520 | tf_op jit(solution)/shard_map/reduce_scatter | solution.py:627
  (59 other events, 647.8 us)
Sparse Core Ops, SparseCore 0:
  20.6 84.8 all-gather.10
  107.9 84.6 all-gather.12
  209.4 65.0 all-gather.18
  276.8 66.4 all-gather.14
  345.5 67.2 all-gather.20
  414.5 66.4 all-gather.16
  483.3 66.4 all-gather.22
  593.8 115.3 reduce-scatter.6
  712.2 115.0 reduce-scatter.8
  871.5 65.5 reduce-scatter.12
  1016.8 53.2 reduce-scatter.14
  1072.9 64.4 reduce-scatter.10
  1152.8 70.4 all-reduce.3
  1226.2 148.1 reduce-scatter.16

commit v8 on v7

--- a/solution.py
+++ b/solution.py
@@ -152,7 +152,7 @@
             num_scalar_prefetch=3, grid=(batch,),
             in_specs=[q_spec, q_spec, kv_spec, tab_spec, tab_spec, whole((heads * rows, 1)), whole((1, n_keys))],
             out_specs=[q_spec] * 4),
-        compiler_params=pltpu.CompilerParams(dimension_semantics=("arbitrary",), vmem_limit_bytes=30 << 20),
+        compiler_params=pltpu.CompilerParams(dimension_semantics=("arbitrary",), vmem_limit_bytes=60 << 20),
         cost_estimate=pl.CostEstimate(flops=flops, bytes_accessed=batch * rows * width * 16 + kv_all.size * 2, transcendentals=batch * rows * heads * 2 * n_keys),
         name="attn_fwd",
     )(*scalars, q_own, q_oth, kv_all, cos_t, sin_t, qpos_col, kpos[None, :])
@@ -176,7 +176,7 @@
         out_shape=(out, out, kv_out, kv_out), grid=(count,),
         in_specs=[q_spec, q_spec, q_spec, q_spec, kv_spec, tab_spec, tab_spec, whole((1, heads * rows)), whole((n_keys, 1))],
         out_specs=[q_spec, q_spec, dkv_spec, dkv_spec],
-        compiler_params=pltpu.CompilerParams(dimension_semantics=("arbitrary",), vmem_limit_bytes=30 << 20),
+        compiler_params=pltpu.CompilerParams(dimension_semantics=("arbitrary",), vmem_limit_bytes=60 << 20),
         cost_estimate=pl.CostEstimate(flops=flops, bytes_accessed=count * rows * width * 12 + kv_all.size * 4, transcendentals=count * rows * heads * 2 * n_keys),
         name="attn_bwd",
     )(*scalars, q_own, q_oth, g_own, g_oth, kv_all, cos_t, sin_t, qpos_row, kpos[:, None], *earlier)
@@ -211,7 +211,7 @@
         return run
 
 
-def params(steps, limit=56):
+def params(steps, limit=60):
     return pltpu.CompilerParams(dimension_semantics=("arbitrary",) * steps, vmem_limit_bytes=limit << 20)
 
 
@@ -362,7 +362,7 @@
         scratch_shapes=[pltpu.VMEM((half, 2 * rows, depth), BF16)] * n
         + [pltpu.VMEM((2, depth, tn) if d == 0 else (2, tn, depth), BF16) for d, _ in terms]
         + [pltpu.SemaphoreType.DMA((n, half)), pltpu.SemaphoreType.DMA((n, 2))],
-        compiler_params=params(2, 54),
+        compiler_params=params(2),
         cost_estimate=cost(n * lhs[0].size * dim, *lhs, *rhs, out), name="mlp_back",
     )(*lhs, *rhs, *far)
 
@@ -455,7 +455,7 @@
         kv_wgrad_kernel, 2 + len(terms), out_shape=out, grid=(steps + 1,),
         in_specs=[pl.BlockSpec((tokens, tf), lambda i: (0, jnp.minimum(i, steps - 1))), pl.BlockSpec((tokens, width), lambda i: (0, 0))]
         + [pl.BlockSpec(t.shape, lambda i: (0, 0)) for t in terms],
-        out_specs=pl.BlockSpec((tf, width), lambda i: (i, 0)), compiler_params=params(1, 40),
+        out_specs=pl.BlockSpec((tf, width), lambda i: (i, 0)), compiler_params=params(1),
         cost_estimate=cost(2 * tokens * rows * width, lhs, rhs, out), name="kv_wgrad",
     )(lhs, rhs, *terms)
 
@@ -479,7 +479,7 @@
         head_wgrad_kernel, 4 + len(far), out_shape=out, grid=(dim // tn,),
         in_specs=[pl.BlockSpec((tokens, width), lambda j: (0, 0), pipeline_mode=pl.Buffered(1))] * 2
         + [pl.BlockSpec((tokens, tn), lambda j: (0, j))] * 2 + [tile] * len(far),
-        out_specs=tile, compiler_params=params(1, 48), cost_estimate=cost(4 * tokens * width * dim, *lhs, *rhs, *far, out), name="head_wgrad",
+        out_specs=tile, compiler_params=params(1), cost_estimate=cost(4 * tokens * width * dim, *lhs, *rhs, *far, out), name="head_wgrad",
     )(*lhs, *rhs, *far)
 
 
@@ -497,7 +497,7 @@
     specs = [pl.BlockSpec((1, size, dim), lambda i, at=a.shape[0] - 1: (at, 0, 0)) if a.ndim == 3 else pl.BlockSpec((size, dim), lambda i: (0, 0)) for a in parts]
     return order.call(
         add_kernel, 1 + len(parts), out_shape=jax.ShapeDtypeStruct(base.shape, BF16), grid=(len(parts),), in_specs=[row] + specs, out_specs=row,
-        compiler_params=params(1, 40), cost_estimate=cost(base.size, base, base, base), name="add",
+        compiler_params=params(1), cost_estimate=cost(base.size, base, base, base), name="add",
     )(base, *parts)
 
 
@@ -577,7 +577,7 @@
         functools.partial(d_resid_kernel, n=n), n + 5, len(earlier), in_parts=True, out_shape=outs, grid=(n,),
         in_specs=one + [far, far, pl.BlockSpec((1, dim), lambda i: (0, 0)), whole_w, whole_w],
         out_specs=[pl.BlockSpec((8, dim), lambda i: (0, 0)), far, mix, mix],
-        compiler_params=params(1, 48), cost_estimate=cost(4 * n * size * dim * width, *dz, wo_own, wo_oth, outs[1]), name="d_resid",
+        compiler_params=params(1), cost_estimate=cost(4 * n * size * dim * width, *dz, wo_own, wo_oth, outs[1]), name="d_resid",
     )(*dz, resid, grad_out, gain, wo_own, wo_oth, *earlier)
 
 
@@ -756,14 +756,10 @@
         dkv = scatter4((dkv_own.astype(F32) + dkv_far.astype(F32)).astype(BF16))
         heads_far = swap(heads_far)
 
-        def gate_quarter(k, earlier):
-            return wgrad_call(order, core_1, z_all, [a[1] for a in shards], tiles=(1, 2), col_tiles=(k, k + 1), earlier=earlier)
-
-        g_gate = gate_quarter(0, g_gate)
-        g_heads = head_wgrad(order, (mix_own, dq_own), (d_resid, normed_flat), hd, (heads_far,))
-        g_heads = scatter4(g_heads)
-        g_gate = gate_quarter(1, g_gate)
-        dkv, g_gate = lax.optimization_barrier((dkv, g_gate))
+        g_gate = wgrad_call(order, core_1, z_all, [a[1] for a in shards], tiles=(1, 2), earlier=g_gate)
+        g_heads_part = head_wgrad(order, (mix_own, dq_own), (d_resid, normed_flat), hd, (heads_far,))
+        g_heads = scatter4(g_heads_part)
+        dkv, g_heads_part = lax.optimization_barrier((dkv, g_heads_part))
         g_out, g_query = g_heads[0], g_heads[1].T
         d_k_raw = key_pull(dkv[..., :hd].astype(F32))[0]
         dkv = jnp.concatenate([d_k_raw.astype(BF16), dkv[..., hd:]], axis=-1).reshape(tokens, 2 * hd)
@@ -774,8 +770,7 @@
         g_attn_norm, g_mlp_norm = sums[dim:].reshape(2, dim)
         hidden_out = add_call(order, resid, mlp_sums).reshape(batch, rows, dim)
         g_up = wgrad_call(order, core_1, z_all, [a[2] for a in shards])
-        g_down = wgrad_call(order, core_1, [a[0] for a in shards], g_all, tiles=(0, 1))
-        g_down = wgrad_call(order, core_1, [a[0] for a in shards], g_all, tiles=(1, 2), earlier=g_down, after=(g_heads,))
+        g_down = wgrad_call(order, core_1, [a[0] for a in shards], g_all)
         return (hidden_out, grad_hidden.reshape(batch, rows, dim), g_attn_norm, g_query, sums[:dim, :hd], sums[:dim, hd:], g_out, g_mlp_norm, g_gate, g_up, g_down)
 
     return jax.shard_map(local_layer, mesh=mesh, in_specs=in_specs, out_specs=out_specs, check_vma=False)

time: 1440 us -> 1370 us (0.951)
  local copies, waits for them, and re-layouts: 82.8 us -> 43.2 us
  waiting for transfers between devices: 219 us -> 186 us
    unnamed x130 -> x50, local copies, waits for them, and re-layouts: 49.7 us -> 8.18 us
    reduce_scatter x6, waiting for transfers between devices: 88.8 us -> 53.7 us  [scatter4(): lax.psum_scatter(flat, 'tp', scatter_dimension=0, tiled=True, axis_index_...]
    pallas_call x28 -> x26, Pallas kernels: 1040 us -> 1040 us  [run(): pl.pallas_call(body, out_shape=shapes, grid_spec=pltpu.PrefetchScalarGrid...]
  transfers between devices with their start and end apart: 29 -> 29, of which waited for: 11 -> 10; matrix products, arithmetic and copies ran while one was open for 4% -> 4% of each run, Pallas kernels for 67% -> 74%
where the time goes in v8:
time: 1370 us; the launch traced here: 1360 us
  Pallas kernels  1060 us (77%)
  waiting for transfers between devices  186 us (14%)
  local copies, waits for them, and re-layouts  43.2 us (3%)
  matrix products  21.6 us (2%)
  other arithmetic  20 us (1%)
  between operations  14.8 us (1%)
  starting transfers between devices  14.1 us (1%)
    pallas_call x26, Pallas kernels, run(): pl.pallas_call(body, out_shape=shapes, grid_spec=pltpu.PrefetchScalarGrid...  1040 us
    ppermute x8, waiting for transfers between devices, flip(): return lax.ppermute(x_loc, 'tp', [(i, i ^ bits) for i in range(tp_size)])  69.3 us
    reduce_scatter x6, waiting for transfers between devices, scatter4(): lax.psum_scatter(flat, 'tp', scatter_dimension=0, tiled=True, axis_index_...  53.7 us
    all_gather x7, waiting for transfers between devices, gather8(): return lax.all_gather(x_loc, 'tp', axis=0, tiled=False)  32.5 us
  transfers between devices with their start and end apart: 29, of which 10 were waited for; matrix products, arithmetic and copies ran while one was open for 4% of the time, Pallas kernels for 74%

profile of v8, /device:TPU:0, one launch (start us, length us, event | category | flops | bytes accessed | tf_op | source)
XLA Modules:
  0.0 1361.2 jit_solution(10511080195598487713)
XLA Ops:
  29.5 37.0 %collective-permute-done = bf16[256,2048]{0,1:T(8,128)(2,1)S(1)} collective-permute-done((bf16[256,2048]{0,1:T(8,128)(2,1)}, bf16[256,2048]{0,1:T(8,128)(2,1)S(1)}, u32[]{:S(2)}, u32[]{:S(2)}) %collective-permute-start) | collective-permute-done | bytes 1048608 | tf_op jit(solution)/shard_map/ppermute | solution.py:636
  79.0 14.0 %collective-permute-done.2 = bf16[128,2048]{0,1:T(8,128)(2,1)} collective-permute-done((bf16[128,2048]{0,1:T(8,128)(2,1)}, bf16[128,2048]{0,1:T(8,128)(2,1)}, u32[]{:S(2)}, u32[]{:S(2)}) %collective-permute-start.2) | collective-permute-done | bytes 524320 | tf_op jit(solution)/shard_map/ppermute | solution.py:636
  121.9 14.8 %collective-permute-done.5 = bf16[256,2048]{1,0:T(8,128)(2,1)S(1)} collective-permute-done((bf16[256,2048]{1,0:T(8,128)(2,1)}, bf16[256,2048]{1,0:T(8,128)(2,1)S(1)}, u32[]{:S(2)}, u32[]{:S(2)}) %collective-permute-start.5) | collective-permute-done | bytes 1048608 | tf_op jit(solution)/shard_map/ppermute | solution.py:636
  139.5 22.3 %attn_fwd.1 = (bf16[12,96,1024]{2,1,0:T(8,128)(2,1)}, bf16[12,96,1024]{2,1,0:T(8,128)(2,1)}, bf16[12,96,1024]{2,1,0:T(8,128)(2,1)}, bf16[12,96,1024]{2,1,0:T(8,128)(2,1)}) custom-call(s32[12]{0:T(128)} %refs_0_.3, s32[12]{0:T(128)} %refs_1_.5, s32[1]{0:T(128)} %bitcast.1.core_s.refs_0_.refs_2_, f32[12,96,1024]{2,1,0:T(8,128)} %bitcast.164, ...), custom_call_target="tpu_custom_call" | custom-call | flops 7247757312 | bytes 28311552 | tf_op jit(solution)/shard_map/attn_fwd/pallas_call | solution.py:148
  178.1 19.5 %resid.1 = (bf16[1152,2048]{1,0:T(8,128)(2,1)}, bf16[384,2048]{1,0:T(8,128)(2,1)}, bf16[384,2048]{1,0:T(8,128)(2,1)}, bf16[384,2048]{1,0:T(8,128)(2,1)}) custom-call(bf16[1152,2048]{1,0:T(8,128)(2,1)} %bitcast.103, bf16[1152,1024]{1,0:T(8,128)(2,1)} %bitcast.118, bf16[1152,1024]{1,0:T(8,128)(2,1)} %bitcast.166, bf16[1024,2048]{1,0:T(8,128)(2,1)} %bitcast.99, ...), custom_call_target="tpu_custom_call" | custom-call | flops 9663676416 | bytes 27262976 | tf_op jit(solution)/shard_map/resid/pallas_call | solution.py:201
  200.2 33.0 %d_act.2.refs_2_ = bf16[3072,2048]{1,0:T(8,128)(2,1)} custom-call(s32[1]{0:T(128)} %bitcast.1.core_s.refs_0_.refs_2_, bf16[4,2,384,2048]{3,2,1,0:T(8,128)(2,1)} %bitcast.134, bf16[2048,2048]{1,0:T(8,128)(2,1)} %refs_1_.4, bf16[1152,2048]{1,0:T(8,128)(2,1)} %get-tuple-element.65.refs_3_.refs_1_.refs_2_.refs_0_), custom_call_target="tpu_custom_call" | custom-call | flops 25769803776 | bytes 33554432 | tf_op jit(solution)/shard_map/d_act/pallas_call | solution.py:201
  233.2 32.4 %all-gather.19.cloned.1.call-done = bf16[3072,2048]{1,0:T(8,128)(2,1)} async-done(((bf16[384,2048]{1,0:T(8,128)(2,1)}), bf16[3072,2048]{1,0:T(8,128)(2,1)}) %all-gather.19.cloned.1.call-update) | async-done | bytes 12582928 | tf_op jit(solution)/shard_map/all_gather | solution.py:630
  265.6 70.7 %mlp_act.3 = (bf16[3072,2048]{1,0:T(8,128)(2,1)}, bf16[3072,2048]{1,0:T(8,128)(2,1)}, bf16[3072,2048]{1,0:T(8,128)(2,1)}) custom-call(s32[1]{0:T(128)} %bitcast.1.core_s.refs_0_.refs_2_, bf16[4,2,384,2048]{3,2,1,0:T(8,128)(2,1)} %bitcast.136, bf16[3072,2048]{1,0:T(8,128)(2,1)} %d_act.2.refs_2_, bf16[2048,2048]{1,0:T(8,128)(2,1)} %refs_2_.5, ...), custom_call_target="tpu_custom_call" | custom-call | flops 51539607552 | bytes 79691776 | tf_op jit(solution)/shard_map/mlp_act/pallas_call | solution.py:201
  336.2 47.5 %mlp_back.7.refs_3_ = bf16[4,2,384,2048]{3,2,1,0:T(8,128)(2,1)} custom-call(bf16[3072,2048]{1,0:T(8,128)(2,1)} %get-tuple-element.67.refs_0_, bf16[3072,2048]{1,0:T(8,128)(2,1)} %get-tuple-element.68.refs_1_, bf16[3072,2048]{1,0:T(8,128)(2,1)} %get-tuple-element.69.refs_2_, bf16[2048,2048]{1,0:T(8,128)(2,1)} %refs_2_.5, bf16[2048,2048]{1,0:T(8,128)(2,1)} %refs_3_.17, ...), custom_call_target="tpu_custom_call" | custom-call | flops 38654705664 | bytes 75497472 | tf_op jit(solution)/shard_map/mlp_back/pallas_call | solution.py:201
  384.0 32.5 %d_act.3.refs_2_ = bf16[3072,2048]{1,0:T(8,128)(2,1)} custom-call(s32[1]{0:T(128)} %bitcast.1.core_s.refs_0_.refs_2_, bf16[4,2,384,2048]{3,2,1,0:T(8,128)(2,1)} %bitcast.140, bf16[2048,2048]{1,0:T(8,128)(2,1)} %refs_1_.4, bf16[4,2,384,2048]{3,2,1,0:T(8,128)(2,1)} %mlp_back.7.refs_3_), custom_call_target="tpu_custom_call" | custom-call | flops 25769803776 | bytes 33554432 | tf_op jit(solution)/shard_map/d_act/pallas_call | solution.py:201
  416.5 71.1 %mlp_act.4 = (bf16[3072,2048]{1,0:T(8,128)(2,1)}, bf16[3072,2048]{1,0:T(8,128)(2,1)}, bf16[3072,2048]{1,0:T(8,128)(2,1)}) custom-call(s32[1]{0:T(128)} %bitcast.1.core_s.refs_0_.refs_2_, bf16[4,2,384,2048]{3,2,1,0:T(8,128)(2,1)} %bitcast.142, bf16[3072,2048]{1,0:T(8,128)(2,1)} %d_act.3.refs_2_, bf16[2048,2048]{1,0:T(8,128)(2,1)} %refs_2_.5, ...), custom_call_target="tpu_custom_call" | custom-call | flops 51539607552 | bytes 79691776 | tf_op jit(solution)/shard_map/mlp_act/pallas_call | solution.py:201
  487.7 47.2 %mlp_back.8.refs_7_ = bf16[4,2,384,2048]{3,2,1,0:T(8,128)(2,1)} custom-call(bf16[3072,2048]{1,0:T(8,128)(2,1)} %get-tuple-element.71.refs_0_, bf16[3072,2048]{1,0:T(8,128)(2,1)} %get-tuple-element.72.refs_1_, bf16[3072,2048]{1,0:T(8,128)(2,1)} %get-tuple-element.73.refs_2_, bf16[2048,2048]{1,0:T(8,128)(2,1)} %refs_2_.5, bf16[2048,2048]{1,0:T(8,128)(2,1)} %refs_3_.17, ...), custom_call_target="tpu_custom_call" | custom-call | flops 38654705664 | bytes 75497472 | tf_op jit(solution)/shard_map/mlp_back/pallas_call | solution.py:201
  534.9 49.6 %mlp_back.9.refs_7_ = bf16[4,2,384,2048]{3,2,1,0:T(8,128)(2,1)} custom-call(bf16[3072,2048]{1,0:T(8,128)(2,1)} %get-tuple-element.67.refs_0_, bf16[3072,2048]{1,0:T(8,128)(2,1)} %get-tuple-element.68.refs_1_, bf16[3072,2048]{1,0:T(8,128)(2,1)} %get-tuple-element.69.refs_2_, bf16[2048,2048]{1,0:T(8,128)(2,1)} %refs_2_.5, bf16[2048,2048]{1,0:T(8,128)(2,1)} %refs_3_.17, ...), custom_call_target="tpu_custom_call" | custom-call | flops 38654705664 | bytes 75497472 | tf_op jit(solution)/shard_map/mlp_back/pallas_call | solution.py:201
  584.6 19.5 %collective-permute-done.11.refs_6_ = bf16[4,2,384,2048]{3,2,1,0:T(8,128)(2,1)} collective-permute-done((bf16[4,2,384,2048]{3,2,1,0:T(8,128)(2,1)}, bf16[4,2,384,2048]{3,2,1,0:T(8,128)(2,1)}, u32[]{:S(2)}, u32[]{:S(2)}) %collective-permute-start.11) | collective-permute-done | bytes 12582944 | tf_op jit(solution)/shard_map/ppermute | solution.py:633
  604.1 49.9 %mlp_back.10.refs_6_ = bf16[4,2,384,2048]{3,2,1,0:T(8,128)(2,1)} custom-call(bf16[3072,2048]{1,0:T(8,128)(2,1)} %get-tuple-element.71.refs_0_, bf16[3072,2048]{1,0:T(8,128)(2,1)} %get-tuple-element.72.refs_1_, bf16[3072,2048]{1,0:T(8,128)(2,1)} %get-tuple-element.73.refs_2_, bf16[2048,2048]{1,0:T(8,128)(2,1)} %refs_2_.5, bf16[2048,2048]{1,0:T(8,128)(2,1)} %refs_3_.17, ...), custom_call_target="tpu_custom_call" | custom-call | flops 38654705664 | bytes 75497472 | tf_op jit(solution)/shard_map/mlp_back/pallas_call | solution.py:201
  654.1 92.5 %mlp_act.5 = (bf16[3072,2048]{1,0:T(8,128)(2,1)}, bf16[3072,2048]{1,0:T(8,128)(2,1)}, bf16[3072,2048]{1,0:T(8,128)(2,1)}) custom-call(s32[1]{0:T(128)} %bitcast.1.core_s.refs_0_.refs_2_, bf16[4,2,384,2048]{3,2,1,0:T(8,128)(2,1)} %bitcast.148, bf16[4,2,384,2048]{3,2,1,0:T(8,128)(2,1)} %bitcast.146, bf16[2048,2048]{1,0:T(8,128)(2,1)} %refs_2_.5, ...), custom_call_target="tpu_custom_call" | custom-call | flops 77309411328 | bytes 88080384 | tf_op jit(solution)/shard_map/mlp_act/pallas_call | solution.py:201
  746.7 47.6 %mlp_back.11.refs_6_ = bf16[4,2,384,2048]{3,2,1,0:T(8,128)(2,1)} custom-call(bf16[3072,2048]{1,0:T(8,128)(2,1)} %get-tuple-element.76.refs_0_, bf16[3072,2048]{1,0:T(8,128)(2,1)} %get-tuple-element.77.refs_1_, bf16[3072,2048]{1,0:T(8,128)(2,1)} %get-tuple-element.75.refs_2_.refs_0_, bf16[2048,2048]{1,0:T(8,128)(2,1)} %refs_2_.5, ...), custom_call_target="tpu_custom_call" | custom-call | flops 38654705664 | bytes 75497472 | tf_op jit(solution)/shard_map/mlp_back/pallas_call | solution.py:201
  796.2 11.0 d_resid.2
  807.2 14.8 %attn_bwd.2 = (bf16[12,96,1024]{2,1,0:T(8,128)(2,1)}, bf16[12,96,1024]{2,1,0:T(8,128)(2,1)}, bf16[4,12,96,512]{3,2,1,0:T(8,128)(2,1)}, bf16[4,12,96,512]{3,2,1,0:T(8,128)(2,1)}) custom-call(s32[12]{0:T(128)} %refs_0_.3, s32[12]{0:T(128)} %refs_1_.5, s32[1]{0:T(128)} %bitcast.1.core_s.refs_0_.refs_2_, bf16[12,96,1024]{2,1,0:T(8,128)(2,1)} %get-tuple-element.78.refs_3_, ...), custom_call_target="tpu_custom_call" | custom-call | flops 6039797760 | bytes 23592960 | tf_op jit(solution)/shard_map/attn_bwd/pallas_call | solution.py:201
  822.0 34.5 %mlp_back.12.refs_3_ = bf16[4,384,2048]{2,1,0:T(8,128)(2,1)} custom-call(bf16[3072,2048]{1,0:T(8,128)(2,1)} %get-tuple-element.76.refs_0_, bf16[3072,2048]{1,0:T(8,128)(2,1)} %get-tuple-element.77.refs_1_, bf16[2048,2048]{1,0:T(8,128)(2,1)} %refs_2_.5, bf16[2048,2048]{1,0:T(8,128)(2,1)} %refs_3_.17, ...), custom_call_target="tpu_custom_call" | custom-call | flops 25769803776 | bytes 48234496 | tf_op jit(solution)/shard_map/mlp_back/pallas_call | solution.py:201
  856.6 20.4 %mlp_back.13.refs_7_ = bf16[4,384,2048]{2,1,0:T(8,128)(2,1)} custom-call(bf16[3072,2048]{1,0:T(8,128)(2,1)} %get-tuple-element.75.refs_2_.refs_0_, bf16[2048,2048]{1,0:T(8,128)(2,1)} %refs_1_.4, bf16[4,2,384,2048]{3,2,1,0:T(8,128)(2,1)} %collective-permute-done.12.refs_4_.refs_2_, bf16[4,384,2048]{2,1,0:T(8,128)(2,1)} %mlp_back.12.refs_3_), custom_call_target="tpu_custom_call" | custom-call | flops 12884901888 | bytes 27262976 | tf_op jit(solution)/shard_map/mlp_back/pallas_call | solution.py:201
  877.0 47.6 %wgrad.4.refs_10_.refs_7_ = f32[2048,2048]{1,0:T(8,128)} custom-call(s32[1]{0:T(128)} %bitcast.1.core_s.refs_0_.refs_2_, bf16[4,2,384,2048]{3,2,1,0:T(8,128)(2,1)} %bitcast.137, bf16[4,2,384,2048]{3,2,1,0:T(8,128)(2,1)} %bitcast.143, bf16[4,2,384,2048]{3,2,1,0:T(8,128)(2,1)} %bitcast.149, bf16[8,384,2048]{2,1,0:T(8,128)(2,1)} %bitcast.158, ...), custom_call_target="tpu_custom_call" | custom-call | flops 77309411328 | bytes 92274688 | tf_op jit(solution)/shard_map/wgrad/pallas_call | solution.py:201
  924.6 18.7 %d_resid.3 = (f32[8,2048]{1,0:T(8,128)}, bf16[1152,2048]{1,0:T(8,128)(2,1)}, bf16[1152,1024]{1,0:T(8,128)(2,1)}, bf16[1152,1024]{1,0:T(8,128)(2,1)}) custom-call(bf16[2,384,2048]{2,1,0:T(8,128)(2,1)} %reduce-scatter.9.cloned.1.call-done.refs_0_.refs_2_, ...), custom_call_target="tpu_custom_call", output_to_operand_aliasing={{1}: (7, {}), {2}: (8, {}), {3}: (9, {})} | custom-call | flops 6442450944 | bytes 17825792 | tf_op jit(solution)/shard_map/d_resid/pallas_call | solution.py:201
  943.3 26.6 %attn_bwd.3 = (bf16[12,96,1024]{2,1,0:T(8,128)(2,1)}, bf16[12,96,1024]{2,1,0:T(8,128)(2,1)}, bf16[4,12,96,512]{3,2,1,0:T(8,128)(2,1)}, bf16[4,12,96,512]{3,2,1,0:T(8,128)(2,1)}) custom-call(s32[12]{0:T(128)} %refs_0_.3, s32[12]{0:T(128)} %refs_1_.5, ...), custom_call_target="tpu_custom_call", output_to_operand_aliasing={{0}: (12, {}), {1}: (13, {}), {2}: (14, {}), {3}: (15, {})} | custom-call | flops 12079595520 | bytes 28311552 | tf_op jit(solution)/shard_map/attn_bwd/pallas_call | solution.py:201
  970.3 17.3 %head_wgrad.2.refs_8_ = f32[4,2,256,2048]{3,2,1,0:T(8,128)} custom-call(bf16[1152,1024]{1,0:T(8,128)(2,1)} %bitcast.167, bf16[1152,1024]{1,0:T(8,128)(2,1)} %bitcast.168, bf16[1152,2048]{1,0:T(8,128)(2,1)} %get-tuple-element.94.refs_2_.refs_4_, bf16[1152,2048]{1,0:T(8,128)(2,1)} %bitcast.92, bf16[12,96,1024]{2,1,0:T(8,128)(2,1)} %get-tuple-element.95.refs_4_), custom_call_target="tpu_custom_call" | custom-call | flops 9663676416 | bytes 30932992 | tf_op jit(solution)/shard_map/head_wgrad/pallas_call | solution.py:201
  997.6 48.0 %wgrad.5.refs_5_ = f32[2048,2048]{1,0:T(8,128)} custom-call(s32[1]{0:T(128)} %bitcast.1.core_s.refs_0_.refs_2_, bf16[4,2,384,2048]{3,2,1,0:T(8,128)(2,1)} %bitcast.138, bf16[4,2,384,2048]{3,2,1,0:T(8,128)(2,1)} %bitcast.144, bf16[4,2,384,2048]{3,2,1,0:T(8,128)(2,1)} %bitcast.150, bf16[8,384,2048]{2,1,0:T(8,128)(2,1)} %bitcast.159, ...), custom_call_target="tpu_custom_call", output_to_operand_aliasing={{}: (7, {})} | custom-call | flops 77309411328 | bytes 92274688 | tf_op jit(solution)/shard_map/wgrad/pallas_call | solution.py:201
  1045.6 21.8 %head_wgrad.3.refs_9_ = f32[4,2,256,2048]{3,2,1,0:T(8,128)} custom-call(bf16[1152,1024]{1,0:T(8,128)(2,1)} %bitcast.119, bf16[1152,1024]{1,0:T(8,128)(2,1)} %bitcast.120, bf16[1152,2048]{1,0:T(8,128)(2,1)} %get-tuple-element.94.refs_2_.refs_4_, bf16[1152,2048]{1,0:T(8,128)(2,1)} %bitcast.93, f32[4,2,256,2048]{3,2,1,0:T(8,128)} %collective-permute-done.14.refs_4_, ...), custom_call_target="tpu_custom_call" | custom-call | flops 9663676416 | bytes 47710208 | tf_op jit(solution)/shard_map/head_wgrad/pallas_call | solution.py:201
  1070.3 25.9 %d_hidden.1 = (bf16[1152,2048]{1,0:T(8,128)(2,1)}, f32[8,2048]{1,0:T(8,128)}) custom-call(bf16[1152,1024]{1,0:T(8,128)(2,1)} %bitcast.121, bf16[1152,1024]{1,0:T(8,128)(2,1)} %bitcast.169, bf16[1152,512]{1,0:T(8,128)(2,1)} %bitcast.114, bf16[1152,2048]{1,0:T(8,128)(2,1)} %bitcast.104, bf16[1152,2048]{1,0:T(8,128)(2,1)} %get-tuple-element.94.refs_2_.refs_4_, ...), custom_call_target="tpu_custom_call" | custom-call | flops 14495514624 | bytes 27328512 | tf_op jit(solution)/shard_map/d_hidden/pallas_call | solution.py:201
  1103.3 12.5 reduce-scatter.11.cloned.1.call-done.refs_3_
  1124.3 88.1 %wgrad.6.refs_7_ = f32[2048,2048]{1,0:T(8,128)} custom-call(s32[1]{0:T(128)} %bitcast.1.core_s.refs_0_.refs_2_, bf16[4,2,384,2048]{3,2,1,0:T(8,128)(2,1)} %bitcast.139, bf16[4,2,384,2048]{3,2,1,0:T(8,128)(2,1)} %bitcast.145, bf16[4,2,384,2048]{3,2,1,0:T(8,128)(2,1)} %bitcast.151, bf16[8,384,2048]{2,1,0:T(8,128)(2,1)} %bitcast.153, ...), custom_call_target="tpu_custom_call" | custom-call | flops 77309411328 | bytes 92274688 | tf_op jit(solution)/shard_map/wgrad/pallas_call | solution.py:201
  1212.5 88.5 %wgrad.7 = f32[2048,2048]{1,0:T(8,128)} custom-call(s32[1]{0:T(128)} %bitcast.1.core_s.refs_0_.refs_2_, bf16[8,384,2048]{2,1,0:T(8,128)(2,1)} %bitcast.152, bf16[8,384,2048]{2,1,0:T(8,128)(2,1)} %bitcast.154, bf16[8,384,2048]{2,1,0:T(8,128)(2,1)} %bitcast.156, bf16[4,2,384,2048]{3,2,1,0:T(8,128)(2,1)} %bitcast.135, bf16[4,2,384,2048]{3,2,1,0:T(8,128)(2,1)} %bitcast.141, ...), custom_call_target="tpu_custom_call" | custom-call | flops 77309411328 | bytes 92274688 | tf_op jit(solution)/shard_map/wgrad/pallas_call | solution.py:201
  1307.5 41.2 %reduce-scatter.17.cloned.1.call-done = f32[2,256,2048]{2,1,0:T(8,128)} async-done(((f32[8,256,2048]{2,1,0:T(8,128)}), f32[2,256,2048]{2,1,0:T(8,128)}) %reduce-scatter.17.cloned.1.call-update) | async-done | bytes 4194320 | tf_op jit(solution)/shard_map/reduce_scatter | solution.py:627
  (176 shorter events, 128.6 us)
Async XLA Ops:
  7.2 132.3 %all-gather.11.cloned.1.call-start = ((), (), s32[]{:S(2)}) async-start(), calls=%async_computation.6 | async-start | bytes 10616832 | tf_op jit(solution)/shard_map/all_gather | solution.py:630
  17.8 182.4 %all-gather.13.cloned.1.call-start = ((), (), s32[]{:S(2)}) async-start(), calls=%async_computation.7 | async-start | bytes 14155776 | tf_op jit(solution)/shard_map/all_gather | solution.py:630
  22.6 243.0 %all-gather.19.cloned.1.call-start = ((), (), s32[]{:S(2)}) async-start(), calls=%async_computation.17 | async-start | bytes 14155776 | tf_op jit(solution)/shard_map/all_gather | solution.py:630
  23.1 43.4 %collective-permute-start = (bf16[256,2048]{0,1:T(8,128)(2,1)}, bf16[256,2048]{0,1:T(8,128)(2,1)S(1)}, u32[]{:S(2)}, u32[]{:S(2)}) collective-permute-start(bf16[256,2048]{0,1:T(8,128)(2,1)} %bitcast.3), channel_id=1, source_target_pairs={{0,2},{1,3},{2,0},{3,1},{4,6},{5,7},{6,4},{7,5}} | collective-permute-start | bytes 3145736 | tf_op jit(solution)/shard_map/ppermute | solution.py:636
  26.4 42.9 %collective-permute-start.1 = (bf16[256,2048]{0,1:T(8,128)(2,1)}, bf16[256,2048]{0,1:T(8,128)(2,1)S(1)}, u32[]{:S(2)}, u32[]{:S(2)}) collective-permute-start(bf16[256,2048]{0,1:T(8,128)(2,1)} %bitcast.3), channel_id=1, source_target_pairs={{0,4},{1,5},{2,6},{3,7},{4,0},{5,1},{6,2},{7,3}} | collective-permute-start | bytes 3145736 | tf_op jit(solution)/shard_map/ppermute | solution.py:636
  67.3 25.7 %collective-permute-start.2 = (bf16[128,2048]{0,1:T(8,128)(2,1)}, bf16[128,2048]{0,1:T(8,128)(2,1)}, u32[]{:S(2)}, u32[]{:S(2)}) collective-permute-start(bf16[128,2048]{0,1:T(8,128)(2,1)} %slice.76), channel_id=1, source_target_pairs={{0,4},{1,5},{2,6},{3,7},{4,0},{5,1},{6,2},{7,3}} | collective-permute-start | bytes 1572872 | tf_op jit(solution)/shard_map/ppermute | solution.py:636
  70.2 25.7 %collective-permute-start.3 = (bf16[128,2048]{0,1:T(8,128)(2,1)}, bf16[128,2048]{0,1:T(8,128)(2,1)}, u32[]{:S(2)}, u32[]{:S(2)}) collective-permute-start(bf16[128,2048]{0,1:T(8,128)(2,1)} %slice.77), channel_id=1, source_target_pairs={{0,2},{1,3},{2,0},{3,1},{4,6},{5,7},{6,4},{7,5}} | collective-permute-start | bytes 1572872 | tf_op jit(solution)/shard_map/ppermute | solution.py:636
  98.8 14.2 %collective-permute-start.4 = (bf16[1024,2048]{1,0:T(8,128)(2,1)}, bf16[1024,2048]{1,0:T(8,128)(2,1)}, u32[]{:S(2)}, u32[]{:S(2)}) collective-permute-start(bf16[1024,2048]{1,0:T(8,128)(2,1)} %bitcast.9.refs_6_), channel_id=1, source_target_pairs={{0,1},{1,0},{2,3},{3,2},{4,5},{5,4},{6,7},{7,6}} | collective-permute-start | bytes 12582920 | tf_op jit(solution)/shard_map/ppermute | solution.py:633
  98.8 37.9 %collective-permute-start.5 = (bf16[256,2048]{1,0:T(8,128)(2,1)}, bf16[256,2048]{1,0:T(8,128)(2,1)S(1)}, u32[]{:S(2)}, u32[]{:S(2)}) collective-permute-start(bf16[256,2048]{1,0:T(8,128)(2,1)} %param.21), channel_id=1, source_target_pairs={{0,2},{1,3},{2,0},{3,1},{4,6},{5,7},{6,4},{7,5}} | collective-permute-start | bytes 3145736 | tf_op jit(solution)/shard_map/ppermute | solution.py:636
  100.6 37.9 %collective-permute-start.6 = (bf16[256,2048]{1,0:T(8,128)(2,1)}, bf16[256,2048]{1,0:T(8,128)(2,1)S(1)}, u32[]{:S(2)}, u32[]{:S(2)}) collective-permute-start(bf16[256,2048]{1,0:T(8,128)(2,1)} %param.21), channel_id=1, source_target_pairs={{0,4},{1,5},{2,6},{3,7},{4,0},{5,1},{6,2},{7,3}} | collective-permute-start | bytes 3145736 | tf_op jit(solution)/shard_map/ppermute | solution.py:636
  138.6 23.2 %collective-permute-start.8 = (bf16[128,2048]{1,0:T(8,128)(2,1)S(1)}, bf16[128,2048]{1,0:T(8,128)(2,1)}, u32[]{:S(2)}, u32[]{:S(2)}) collective-permute-start(bf16[128,2048]{1,0:T(8,128)(2,1)S(1)} %slice.66), channel_id=1, source_target_pairs={{0,2},{1,3},{2,0},{3,1},{4,6},{5,7},{6,4},{7,5}} | collective-permute-start | bytes 1572872 | tf_op jit(solution)/shard_map/ppermute | solution.py:636
  139.2 22.6 %collective-permute-start.7 = (bf16[128,2048]{1,0:T(8,128)(2,1)S(1)}, bf16[128,2048]{1,0:T(8,128)(2,1)}, u32[]{:S(2)}, u32[]{:S(2)}) collective-permute-start(bf16[128,2048]{1,0:T(8,128)(2,1)S(1)} %slice.65), channel_id=1, source_target_pairs={{0,4},{1,5},{2,6},{3,7},{4,0},{5,1},{6,2},{7,3}} | collective-permute-start | bytes 1572872 | tf_op jit(solution)/shard_map/ppermute | solution.py:636
  168.1 8.0 collective-permute-start.9
  197.6 186.4 %all-gather.15.cloned.1.call-start = ((), (), s32[]{:S(2)}) async-start(), calls=%async_computation.8 | async-start | bytes 14155776 | tf_op jit(solution)/shard_map/all_gather | solution.py:630
  198.2 218.3 %all-gather.21.cloned.1.call-start = ((), (), s32[]{:S(2)}) async-start(), calls=%async_computation.18 | async-start | bytes 14155776 | tf_op jit(solution)/shard_map/all_gather | solution.py:630
  198.8 455.3 %all-gather.17.cloned.1.call-start = ((), (), s32[]{:S(2)}) async-start(), calls=%async_computation.11 | async-start | bytes 14155776 | tf_op jit(solution)/shard_map/all_gather | solution.py:630
  199.4 454.8 %all-gather.23.cloned.1.call-start = ((), (), s32[]{:S(2)}) async-start(), calls=%async_computation.19 | async-start | bytes 14155776 | tf_op jit(solution)/shard_map/all_gather | solution.py:630
  200.1 596.1 %reduce-scatter.7.cloned.1.call-start = ((), (), s32[]{:S(2)}) async-start(), calls=%async_computation.9 | async-start | bytes 15728640 | tf_op jit(solution)/shard_map/reduce_scatter | solution.py:627
  383.7 151.2 %collective-permute-start.10 = (bf16[4,2,384,2048]{3,2,1,0:T(8,128)(2,1)}, bf16[4,2,384,2048]{3,2,1,0:T(8,128)(2,1)}, u32[]{:S(2)}, u32[]{:S(2)}) collective-permute-start(bf16[4,2,384,2048]{3,2,1,0:T(8,128)(2,1)} %mlp_back.7.refs_3_), channel_id=1, source_target_pairs={{0,1},{1,0},{2,3},{3,2},{4,5},{5,4},{6,7},{7,6}} | collective-permute-start | bytes 37748744 | tf_op jit(solution)/shard_map/ppermute | solution.py:633
  584.6 340.0 %reduce-scatter.9.cloned.1.call-start = ((), (), s32[]{:S(2)}) async-start(), calls=%async_computation.10 | async-start | bytes 15728640 | tf_op jit(solution)/shard_map/reduce_scatter | solution.py:627
  584.6 19.5 %collective-permute-start.11 = (bf16[4,2,384,2048]{3,2,1,0:T(8,128)(2,1)}, bf16[4,2,384,2048]{3,2,1,0:T(8,128)(2,1)}, u32[]{:S(2)}, u32[]{:S(2)}) collective-permute-start(bf16[4,2,384,2048]{3,2,1,0:T(8,128)(2,1)} %mlp_back.8.refs_7_), channel_id=1, source_target_pairs={{0,1},{1,0},{2,3},{3,2},{4,5},{5,4},{6,7},{7,6}} | collective-permute-start | bytes 37748744 | tf_op jit(solution)/shard_map/ppermute | solution.py:633
  654.0 270.6 %reduce-scatter.13.cloned.1.call-start = ((), (), s32[]{:S(2)}) async-start(), calls=%async_computation.13 | async-start | bytes 7864320 | tf_op jit(solution)/shard_map/reduce_scatter | solution.py:627
  746.7 47.9 %copy-start.13 = (s32[4,96]{1,0:T(4,128)S(1)}, s32[4,96]{1,0:T(4,128)}, u32[]{:S(2)}) copy-start(s32[4,96]{1,0:T(4,128)} %copy-done.12) | copy-start | bytes 4612
  746.7 48.6 %copy-start.15 = (s32[768]{0:T(1024)S(1)}, s32[768]{0:T(1024)}, u32[]{:S(2)}) copy-start(s32[768]{0:T(1024)} %copy-done.14) | copy-start | bytes 9220
  794.3 27.7 %collective-permute-start.12 = (bf16[4,2,384,2048]{3,2,1,0:T(8,128)(2,1)}, bf16[4,2,384,2048]{3,2,1,0:T(8,128)(2,1)}, u32[]{:S(2)}, u32[]{:S(2)}) collective-permute-start(bf16[4,2,384,2048]{3,2,1,0:T(8,128)(2,1)} %mlp_back.11.refs_6_), channel_id=1, source_target_pairs={{0,1},{1,0},{2,3},{3,2},{4,5},{5,4},{6,7},{7,6}} | collective-permute-start | bytes 37748744 | tf_op jit(solution)/shard_map/ppermute | solution.py:633
  856.6 210.9 %reduce-scatter.15.cloned.1.call-start = ((), (), s32[]{:S(2)}) async-start(), calls=%async_computation.14 | async-start | bytes 5898240 | tf_op jit(solution)/shard_map/reduce_scatter | solution.py:627
  969.9 17.8 %collective-permute-start.13 = (bf16[4,12,96,512]{3,2,1,0:T(8,128)(2,1)}, bf16[4,12,96,512]{3,2,1,0:T(8,128)(2,1)}, u32[]{:S(2)}, u32[]{:S(2)}) collective-permute-start(bf16[4,12,96,512]{3,2,1,0:T(8,128)(2,1)} %get-tuple-element.91), channel_id=1, source_target_pairs={{0,1},{1,0},{2,3},{3,2},{4,5},{5,4},{6,7},{7,6}} | collective-permute-start | bytes 14155784 | tf_op jit(solution)/shard_map/ppermute | solution.py:633
  995.7 120.1 %reduce-scatter.11.cloned.1.call-start = ((), (), s32[]{:S(2)}) async-start(), calls=%async_computation.12 | async-start | bytes 7864320 | tf_op jit(solution)/shard_map/reduce_scatter | solution.py:627
  995.7 49.9 %collective-permute-start.14 = (f32[4,2,256,2048]{3,2,1,0:T(8,128)}, f32[4,2,256,2048]{3,2,1,0:T(8,128)}, u32[]{:S(2)}, u32[]{:S(2)}) collective-permute-start(f32[4,2,256,2048]{3,2,1,0:T(8,128)} %head_wgrad.2.refs_8_), channel_id=1, source_target_pairs={{0,1},{1,0},{2,3},{3,2},{4,5},{5,4},{6,7},{7,6}} | collective-permute-start | bytes 50331656 | tf_op jit(solution)/shard_map/ppermute | solution.py:633
  1045.6 23.3 %copy-start.7 = (f32[96,128]{1,0:T(8,128)S(1)}, f32[96,128]{1,0:T(8,128)}, u32[]{:S(2)}) copy-start(f32[96,128]{1,0:T(8,128)} %copy-done.6) | copy-start | bytes 147460
  1123.0 178.0 %all-reduce.4.cloned.1.call-start = ((), (), s32[]{:S(2)}) async-start(), calls=%async_computation.15 | async-start | bytes 8421376 | tf_op jit(solution)/shard_map/psum | solution.py:769
  1123.8 224.9 %reduce-scatter.17.cloned.1.call-start = ((), (), s32[]{:S(2)}) async-start(), calls=%async_computation.16 | async-start | bytes 20971520 | tf_op jit(solution)/shard_map/reduce_scatter | solution.py:627
  (19 other events, 107.5 us)
Sparse Core Ops, SparseCore 0:
  17.9 85.1 all-gather.10
  105.5 84.6 all-gather.12
  197.7 67.7 all-gather.18
  267.8 66.4 all-gather.14
  336.5 67.2 all-gather.20
  405.5 66.4 all-gather.16
  474.4 66.4 all-gather.22
  584.7 115.3 reduce-scatter.6
  703.1 115.0 reduce-scatter.8
  856.7 65.0 reduce-scatter.12
  995.8 52.6 reduce-scatter.14
  1051.3 64.4 reduce-scatter.10
  1127.1 70.4 all-reduce.3
  1200.5 148.1 reduce-scatter.16

commit v9 on v8

--- a/solution.py
+++ b/solution.py
@@ -281,10 +281,10 @@
     )(core, *args)
 
 
-def back_kernel(*refs, terms, joined, n_far, base, tn):
+def back_kernel(*refs, terms, joined, n_far, n_out, base, tn):
     n = len(terms)
-    lhs, rhs, far, out = refs[:n], refs[n:2 * n], refs[2 * n:2 * n + n_far], refs[2 * n + n_far]
-    l_bufs, r_bufs, (l_sems, r_sems) = refs[2 * n + n_far + 1:][:n], refs[3 * n + n_far + 1:][:n], refs[4 * n + n_far + 1:]
+    lhs, rhs, far, outs = refs[:n], refs[n:2 * n], refs[2 * n:2 * n + n_far], refs[2 * n + n_far:][:n_out]
+    l_bufs, r_bufs, (l_sems, r_sems) = refs[2 * n + n_far + n_out:][:n], refs[3 * n + n_far + n_out:][:n], refs[4 * n + n_far + n_out:]
     j, i = pl.program_id(0), pl.program_id(1)
     blocks, rows = l_bufs[0].shape[:2]
 
@@ -317,10 +317,10 @@
             part = dot_f32(l_bufs[p][i], r_bufs[p][lax.rem(j, 2)], 1, dim)
             totals[kind] = totals[kind] + part if kind in totals else part
         for kind, total in totals.items():
-            at = (slice(None), kind) if joined else (slice(None),)
+            out, at = (outs[0], (slice(None), kind)) if joined else (outs[kind], (slice(None),))
             total = total.reshape(out[at].shape)
             if far:
-                total += far[0][at].astype(F32)
+                total += far[0][:, kind].astype(F32)
             out[at] = total.astype(BF16)
 
     @pl.when(j == 0)
@@ -344,26 +344,23 @@
         compute(lambda p: None)
 
 
-def back_call(order, side, lhs, rhs, terms, far, chips, tn=512):
+def back_call(order, side, lhs, rhs, terms, far, chips, joined, tn=512):
     dim = rhs[0].shape[0 if terms[0][0] else 1]
     rows = lhs[0].shape[0] // (2 * chips)
     half, n = chips // 2, len(terms)
-    kinds = sorted({kind for _, kind in terms})
-    joined = len(kinds) == 2
     hbm = pl.BlockSpec(memory_space=pl.ANY)
     both = pl.BlockSpec((2, 2, rows, tn), lambda j, i: (i, 0, 0, j))
-    out = jax.ShapeDtypeStruct((chips, 2, rows, dim) if joined else (chips, rows, dim), BF16)
-    far_spec = both if joined else pl.BlockSpec((2, None, rows, tn), lambda j, i: (i, kinds[0], 0, j))
+    outs = [jax.ShapeDtypeStruct((chips, 2, rows, dim), BF16)] if joined else [jax.ShapeDtypeStruct((chips, rows, dim), BF16)] * 2
     depth = lhs[0].shape[1]
     return order.call(
-        functools.partial(back_kernel, terms=terms, joined=joined, n_far=len(far), base=side * half, tn=tn), 2 * n + len(far), out_shape=out,
-        grid=(dim // tn, half), in_specs=[hbm] * (2 * n) + [far_spec] * len(far),
-        out_specs=both if joined else pl.BlockSpec((2, rows, tn), lambda j, i: (i, 0, j)),
+        functools.partial(back_kernel, terms=terms, joined=joined, n_far=len(far), n_out=len(outs), base=side * half, tn=tn), 2 * n + len(far), out_shape=outs,
+        grid=(dim // tn, half), in_specs=[hbm] * (2 * n) + [both] * len(far),
+        out_specs=[both] if joined else [pl.BlockSpec((2, rows, tn), lambda j, i: (i, 0, j))] * 2,
         scratch_shapes=[pltpu.VMEM((half, 2 * rows, depth), BF16)] * n
         + [pltpu.VMEM((2, depth, tn) if d == 0 else (2, tn, depth), BF16) for d, _ in terms]
         + [pltpu.SemaphoreType.DMA((n, half)), pltpu.SemaphoreType.DMA((n, 2))],
         compiler_params=params(2),
-        cost_estimate=cost(n * lhs[0].size * dim, *lhs, *rhs, out), name="mlp_back",
+        cost_estimate=cost(n * lhs[0].size * dim, *lhs, *rhs, *outs), name="mlp_back",
     )(*lhs, *rhs, *far)
 
 
@@ -377,22 +374,21 @@
     def copies(s, at, p):
         row = pl.multiple_of((lax.div(s, cols * n) + first) * tf, tf)
         col = pl.multiple_of((lax.rem(lax.div(s, n), cols) + first_col) * tn, tn)
-        out = []
-        for q, (ref, buf, lanes) in enumerate(((lhs[p], l_buf, pl.ds(row, tf)), (rhs[p], r_buf, pl.ds(col, tn)))):
-            if ref.ndim == 4:
-                for side in range(2):
-                    src = ref.at[:, lax.bitwise_xor(core_s[0], side), :, lanes]
-                    out.append(pltpu.make_async_copy(src, buf.at[at, pl.ds(side * chips, chips)], sems.at[q, side, at]))
-            else:
-                out.append(pltpu.make_async_copy(ref.at[:, :, lanes], buf.at[at], sems.at[q, 0, at]))
-        return out
+        halves = [], []
+        for side in range(2):
+            half = pl.ds(side * chips, chips)
+            for q, (ref, buf, lanes) in enumerate(((lhs[p], l_buf, pl.ds(row, tf)), (rhs[p], r_buf, pl.ds(col, tn)))):
+                src = ref.at[:, lax.bitwise_xor(core_s[0], side), :, lanes] if ref.ndim == 4 else ref.at[half, :, lanes]
+                halves[side].append(pltpu.make_async_copy(src, buf.at[at, half], sems.at[q, side, at]))
+        return halves
 
     def fetch(s, at):
         for p in range(n):
             @pl.when(lax.rem(s, n) == p)
             def _(p=p):
-                for copy in copies(s, at, p):
-                    copy.start()
+                for half in copies(s, at, p):
+                    for copy in half:
+                        copy.start()
 
     @pl.when(step == 0)
     def _():
@@ -402,10 +398,22 @@
     def _():
         fetch(step + 1, 1 - slot)
 
-    for copy in copies(step, slot, 0):
-        copy.wait()
-    part = dot_f32(rows_of(l_buf.at[slot]), rows_of(r_buf.at[slot]), 0, 0)
-    out[...] = jnp.where(k == 0, part, out[...] + part)
+    @pl.when(step == 0)
+    def _():
+        for side, half in enumerate(copies(step, slot, 0)):
+            for copy in half:
+                copy.wait()
+            rows = pl.ds(side * chips, chips)
+            part = dot_f32(rows_of(l_buf.at[0, rows]), rows_of(r_buf.at[0, rows]), 0, 0)
+            out[...] = part if side == 0 else out[...] + part
+
+    @pl.when(step > 0)
+    def _():
+        for half in copies(step, slot, 0):
+            for copy in half:
+                copy.wait()
+        part = dot_f32(rows_of(l_buf.at[slot]), rows_of(r_buf.at[slot]), 0, 0)
+        out[...] = jnp.where(k == 0, part, out[...] + part)
 
 
 def wgrad_call(order, core, lhs, rhs, tf=1024, tn=1024, tiles=None, col_tiles=None, earlier=None, after=()):
@@ -713,21 +721,18 @@
             return attn_bwd(order, q_own, q_oth, d_own.reshape(batch, rows, -1), d_oth.reshape(batch, rows, -1), kv_all, cos_t, sin_t, qpos, kpos,
                             scalars, first * per, count * per, () if earlier is None else earlier[2])
 
-        d_z_terms, mlp_terms = ((1, 0), (1, 0)), ((0, 1),)
-
-        def back_both(c, side, far):
-            return back_call(order, side, (acts[c][1], acts[c][2], acts[c][0]), weights, d_z_terms + mlp_terms, far, chips)
+        def back_both(c, side, far, joined=True):
+            return back_call(order, side, (acts[c][1], acts[c][2], acts[c][0]), weights, ((1, 0), (1, 0), (0, 1)), far, chips, joined)
 
         def finish(c):
-            both = back_both(c, 0, (far[c],))
+            both, = back_both(c, 0, (far[c],))
             both = scatter4(both).reshape(2, size, dim)
             d_gated[c] = mlp_sums[c] = both
 
         def finish_last(c):
-            part = back_call(order, 0, acts[c][1:], weights[:2], d_z_terms, (far[c],), chips)
-            d_gated[c] = scatter4(part).reshape(size, dim)
-            part = back_call(order, 0, acts[c][:1], weights[2:], mlp_terms, (far[c],), chips)
-            mlp_sums[c] = scatter4(part).reshape(size, dim)
+            parts = back_both(c, 0, (far[c],), joined=False)
+            d_gated[c] = scatter4(parts[0]).reshape(size, dim)
+            mlp_sums[c] = scatter4(parts[1]).reshape(size, dim)
 
         for c in range(CHUNKS):
             if c < CHUNKS - 1:
@@ -735,7 +740,7 @@
                 acts.append(act_call(order, core_1, z_all[c], d_act, w_gate, w_up, None))
             else:
                 acts.append(act_call(order, core_1, z_all[c], g_all[c], *weights))
-            part = back_both(c, 1, ())
+            part, = back_both(c, 1, ())
             far.append(swap(part))
             if c == CHUNKS - 2:
                 for earlier in range(c + 1):

time: 1370 us -> 1380 us (level)
  waiting for transfers between devices: 186 us -> 207 us
    reduce_scatter x6, waiting for transfers between devices: 53.7 us -> 75.4 us  [scatter4(): lax.psum_scatter(flat, 'tp', scatter_dimension=0, tiled=True, axis_index_...]
    pallas_call x26 -> x25, Pallas kernels: 1040 us -> 1030 us  [run(): pl.pallas_call(body, out_shape=shapes, grid_spec=pltpu.PrefetchScalarGrid...]
  transfers between devices with their start and end apart: 29 -> 29, of which waited for: 10 -> 11; matrix products, arithmetic and copies ran while one was open for 4% -> 4% of each run, Pallas kernels for 74% -> 73%
where the time goes in v9:
time: 1380 us; the launch traced here: 1370 us
  Pallas kernels  1050 us (76%)
  waiting for transfers between devices  207 us (15%)
  local copies, waits for them, and re-layouts  43.3 us (3%)
  matrix products  21.6 us (2%)
  other arithmetic  20 us (1%)
  between operations  14.7 us (1%)
  starting transfers between devices  14.6 us (1%)
    pallas_call x25, Pallas kernels, run(): pl.pallas_call(body, out_shape=shapes, grid_spec=pltpu.PrefetchScalarGrid...  1030 us
    reduce_scatter x6, waiting for transfers between devices, scatter4(): lax.psum_scatter(flat, 'tp', scatter_dimension=0, tiled=True, axis_index_...  75.4 us
    ppermute x8, waiting for transfers between devices, flip(): return lax.ppermute(x_loc, 'tp', [(i, i ^ bits) for i in range(tp_size)])  68.9 us
    all_gather x7, waiting for transfers between devices, gather8(): return lax.all_gather(x_loc, 'tp', axis=0, tiled=False)  31.6 us
  transfers between devices with their start and end apart: 29, of which 11 were waited for; matrix products, arithmetic and copies ran while one was open for 4% of the time, Pallas kernels for 73%

profile of v9, /device:TPU:0, one launch (start us, length us, event | category | flops | bytes accessed | tf_op | source)
XLA Modules:
  0.0 1371.3 jit_solution(532062620642530617)
XLA Ops:
  29.3 37.0 %collective-permute-done = bf16[256,2048]{0,1:T(8,128)(2,1)S(1)} collective-permute-done((bf16[256,2048]{0,1:T(8,128)(2,1)}, bf16[256,2048]{0,1:T(8,128)(2,1)S(1)}, u32[]{:S(2)}, u32[]{:S(2)}) %collective-permute-start) | collective-permute-done | bytes 1048608 | tf_op jit(solution)/shard_map/ppermute | solution.py:644
  78.7 14.2 %collective-permute-done.2 = bf16[128,2048]{0,1:T(8,128)(2,1)} collective-permute-done((bf16[128,2048]{0,1:T(8,128)(2,1)}, bf16[128,2048]{0,1:T(8,128)(2,1)}, u32[]{:S(2)}, u32[]{:S(2)}) %collective-permute-start.2) | collective-permute-done | bytes 524320 | tf_op jit(solution)/shard_map/ppermute | solution.py:644
  121.8 14.3 %collective-permute-done.5 = bf16[256,2048]{1,0:T(8,128)(2,1)S(1)} collective-permute-done((bf16[256,2048]{1,0:T(8,128)(2,1)}, bf16[256,2048]{1,0:T(8,128)(2,1)S(1)}, u32[]{:S(2)}, u32[]{:S(2)}) %collective-permute-start.5) | collective-permute-done | bytes 1048608 | tf_op jit(solution)/shard_map/ppermute | solution.py:644
  139.4 22.3 %attn_fwd.1 = (bf16[12,96,1024]{2,1,0:T(8,128)(2,1)}, bf16[12,96,1024]{2,1,0:T(8,128)(2,1)}, bf16[12,96,1024]{2,1,0:T(8,128)(2,1)}, bf16[12,96,1024]{2,1,0:T(8,128)(2,1)}) custom-call(s32[12]{0:T(128)} %refs_0_.3, s32[12]{0:T(128)} %refs_1_.3, s32[1]{0:T(128)} %bitcast.1.core_s.refs_0_.refs_2_, f32[12,96,1024]{2,1,0:T(8,128)} %bitcast.164, ...), custom_call_target="tpu_custom_call" | custom-call | flops 7247757312 | bytes 28311552 | tf_op jit(solution)/shard_map/attn_fwd/pallas_call | solution.py:148
  178.0 19.9 %resid.1 = (bf16[1152,2048]{1,0:T(8,128)(2,1)}, bf16[384,2048]{1,0:T(8,128)(2,1)}, bf16[384,2048]{1,0:T(8,128)(2,1)}, bf16[384,2048]{1,0:T(8,128)(2,1)}) custom-call(bf16[1152,2048]{1,0:T(8,128)(2,1)} %bitcast.103, bf16[1152,1024]{1,0:T(8,128)(2,1)} %bitcast.118, bf16[1152,1024]{1,0:T(8,128)(2,1)} %bitcast.166, bf16[1024,2048]{1,0:T(8,128)(2,1)} %bitcast.99, ...), custom_call_target="tpu_custom_call" | custom-call | flops 9663676416 | bytes 27262976 | tf_op jit(solution)/shard_map/resid/pallas_call | solution.py:201
  200.5 33.3 %d_act.2.refs_2_ = bf16[3072,2048]{1,0:T(8,128)(2,1)} custom-call(s32[1]{0:T(128)} %bitcast.1.core_s.refs_0_.refs_2_, bf16[4,2,384,2048]{3,2,1,0:T(8,128)(2,1)} %bitcast.134, bf16[2048,2048]{1,0:T(8,128)(2,1)} %refs_5_.13, bf16[1152,2048]{1,0:T(8,128)(2,1)} %get-tuple-element.67.refs_3_.refs_1_.refs_2_.refs_0_), custom_call_target="tpu_custom_call" | custom-call | flops 25769803776 | bytes 33554432 | tf_op jit(solution)/shard_map/d_act/pallas_call | solution.py:201
  233.7 31.6 %all-gather.19.cloned.1.call-done = bf16[3072,2048]{1,0:T(8,128)(2,1)} async-done(((bf16[384,2048]{1,0:T(8,128)(2,1)}), bf16[3072,2048]{1,0:T(8,128)(2,1)}) %all-gather.19.cloned.1.call-update) | async-done | bytes 12582928 | tf_op jit(solution)/shard_map/all_gather | solution.py:638
  265.3 70.7 %mlp_act.3 = (bf16[3072,2048]{1,0:T(8,128)(2,1)}, bf16[3072,2048]{1,0:T(8,128)(2,1)}, bf16[3072,2048]{1,0:T(8,128)(2,1)}) custom-call(s32[1]{0:T(128)} %bitcast.1.core_s.refs_0_.refs_2_, bf16[4,2,384,2048]{3,2,1,0:T(8,128)(2,1)} %bitcast.136, bf16[3072,2048]{1,0:T(8,128)(2,1)} %d_act.2.refs_2_, bf16[2048,2048]{1,0:T(8,128)(2,1)} %refs_3_.17, ...), custom_call_target="tpu_custom_call" | custom-call | flops 51539607552 | bytes 79691776 | tf_op jit(solution)/shard_map/mlp_act/pallas_call | solution.py:201
  336.0 47.4 %mlp_back.6.refs_3_ = bf16[4,2,384,2048]{3,2,1,0:T(8,128)(2,1)} custom-call(bf16[3072,2048]{1,0:T(8,128)(2,1)} %get-tuple-element.69.refs_0_, bf16[3072,2048]{1,0:T(8,128)(2,1)} %get-tuple-element.70.refs_1_, bf16[3072,2048]{1,0:T(8,128)(2,1)} %get-tuple-element.71.refs_2_, bf16[2048,2048]{1,0:T(8,128)(2,1)} %refs_3_.17, bf16[2048,2048]{1,0:T(8,128)(2,1)} %refs_4_.17, ...), custom_call_target="tpu_custom_call" | custom-call | flops 38654705664 | bytes 75497472 | tf_op jit(solution)/shard_map/mlp_back/pallas_call | solution.py:201
  383.7 32.5 %d_act.3.refs_2_ = bf16[3072,2048]{1,0:T(8,128)(2,1)} custom-call(s32[1]{0:T(128)} %bitcast.1.core_s.refs_0_.refs_2_, bf16[4,2,384,2048]{3,2,1,0:T(8,128)(2,1)} %bitcast.140, bf16[2048,2048]{1,0:T(8,128)(2,1)} %refs_5_.13, bf16[4,2,384,2048]{3,2,1,0:T(8,128)(2,1)} %mlp_back.6.refs_3_), custom_call_target="tpu_custom_call" | custom-call | flops 25769803776 | bytes 33554432 | tf_op jit(solution)/shard_map/d_act/pallas_call | solution.py:201
  416.2 70.9 %mlp_act.4 = (bf16[3072,2048]{1,0:T(8,128)(2,1)}, bf16[3072,2048]{1,0:T(8,128)(2,1)}, bf16[3072,2048]{1,0:T(8,128)(2,1)}) custom-call(s32[1]{0:T(128)} %bitcast.1.core_s.refs_0_.refs_2_, bf16[4,2,384,2048]{3,2,1,0:T(8,128)(2,1)} %bitcast.142, bf16[3072,2048]{1,0:T(8,128)(2,1)} %d_act.3.refs_2_, bf16[2048,2048]{1,0:T(8,128)(2,1)} %refs_3_.17, ...), custom_call_target="tpu_custom_call" | custom-call | flops 51539607552 | bytes 79691776 | tf_op jit(solution)/shard_map/mlp_act/pallas_call | solution.py:201
  487.1 47.5 %mlp_back.7.refs_7_ = bf16[4,2,384,2048]{3,2,1,0:T(8,128)(2,1)} custom-call(bf16[3072,2048]{1,0:T(8,128)(2,1)} %get-tuple-element.73.refs_0_, bf16[3072,2048]{1,0:T(8,128)(2,1)} %get-tuple-element.74.refs_1_, bf16[3072,2048]{1,0:T(8,128)(2,1)} %get-tuple-element.75.refs_2_, bf16[2048,2048]{1,0:T(8,128)(2,1)} %refs_3_.17, bf16[2048,2048]{1,0:T(8,128)(2,1)} %refs_4_.17, ...), custom_call_target="tpu_custom_call" | custom-call | flops 38654705664 | bytes 75497472 | tf_op jit(solution)/shard_map/mlp_back/pallas_call | solution.py:201
  534.6 49.6 %mlp_back.8.refs_7_ = bf16[4,2,384,2048]{3,2,1,0:T(8,128)(2,1)} custom-call(bf16[3072,2048]{1,0:T(8,128)(2,1)} %get-tuple-element.69.refs_0_, bf16[3072,2048]{1,0:T(8,128)(2,1)} %get-tuple-element.70.refs_1_, bf16[3072,2048]{1,0:T(8,128)(2,1)} %get-tuple-element.71.refs_2_, bf16[2048,2048]{1,0:T(8,128)(2,1)} %refs_3_.17, bf16[2048,2048]{1,0:T(8,128)(2,1)} %refs_4_.17, ...), custom_call_target="tpu_custom_call" | custom-call | flops 38654705664 | bytes 75497472 | tf_op jit(solution)/shard_map/mlp_back/pallas_call | solution.py:201
  584.3 19.5 %collective-permute-done.11.refs_6_ = bf16[4,2,384,2048]{3,2,1,0:T(8,128)(2,1)} collective-permute-done((bf16[4,2,384,2048]{3,2,1,0:T(8,128)(2,1)}, bf16[4,2,384,2048]{3,2,1,0:T(8,128)(2,1)}, u32[]{:S(2)}, u32[]{:S(2)}) %collective-permute-start.11) | collective-permute-done | bytes 12582944 | tf_op jit(solution)/shard_map/ppermute | solution.py:641
  603.8 49.8 %mlp_back.9.refs_6_ = bf16[4,2,384,2048]{3,2,1,0:T(8,128)(2,1)} custom-call(bf16[3072,2048]{1,0:T(8,128)(2,1)} %get-tuple-element.73.refs_0_, bf16[3072,2048]{1,0:T(8,128)(2,1)} %get-tuple-element.74.refs_1_, bf16[3072,2048]{1,0:T(8,128)(2,1)} %get-tuple-element.75.refs_2_, bf16[2048,2048]{1,0:T(8,128)(2,1)} %refs_3_.17, bf16[2048,2048]{1,0:T(8,128)(2,1)} %refs_4_.17, ...), custom_call_target="tpu_custom_call" | custom-call | flops 38654705664 | bytes 75497472 | tf_op jit(solution)/shard_map/mlp_back/pallas_call | solution.py:201
  653.7 92.3 %mlp_act.5 = (bf16[3072,2048]{1,0:T(8,128)(2,1)}, bf16[3072,2048]{1,0:T(8,128)(2,1)}, bf16[3072,2048]{1,0:T(8,128)(2,1)}) custom-call(s32[1]{0:T(128)} %bitcast.1.core_s.refs_0_.refs_2_, bf16[4,2,384,2048]{3,2,1,0:T(8,128)(2,1)} %bitcast.148, bf16[4,2,384,2048]{3,2,1,0:T(8,128)(2,1)} %bitcast.146, bf16[2048,2048]{1,0:T(8,128)(2,1)} %refs_3_.17, ...), custom_call_target="tpu_custom_call" | custom-call | flops 77309411328 | bytes 88080384 | tf_op jit(solution)/shard_map/mlp_act/pallas_call | solution.py:201
  746.0 47.9 %mlp_back.10.refs_6_ = bf16[4,2,384,2048]{3,2,1,0:T(8,128)(2,1)} custom-call(bf16[3072,2048]{1,0:T(8,128)(2,1)} %get-tuple-element.77.refs_0_, bf16[3072,2048]{1,0:T(8,128)(2,1)} %get-tuple-element.78.refs_1_, bf16[3072,2048]{1,0:T(8,128)(2,1)} %get-tuple-element.79.refs_2_, bf16[2048,2048]{1,0:T(8,128)(2,1)} %refs_3_.17, bf16[2048,2048]{1,0:T(8,128)(2,1)} %refs_4_.17, ...), custom_call_target="tpu_custom_call" | custom-call | flops 38654705664 | bytes 75497472 | tf_op jit(solution)/shard_map/mlp_back/pallas_call | solution.py:201
  796.0 11.0 d_resid.2
  807.0 14.8 %attn_bwd.2 = (bf16[12,96,1024]{2,1,0:T(8,128)(2,1)}, bf16[12,96,1024]{2,1,0:T(8,128)(2,1)}, bf16[4,12,96,512]{3,2,1,0:T(8,128)(2,1)}, bf16[4,12,96,512]{3,2,1,0:T(8,128)(2,1)}) custom-call(s32[12]{0:T(128)} %refs_0_.3, s32[12]{0:T(128)} %refs_1_.3, s32[1]{0:T(128)} %bitcast.1.core_s.refs_0_.refs_2_, bf16[12,96,1024]{2,1,0:T(8,128)(2,1)} %get-tuple-element.80.refs_3_, ...), custom_call_target="tpu_custom_call" | custom-call | flops 6039797760 | bytes 23592960 | tf_op jit(solution)/shard_map/attn_bwd/pallas_call | solution.py:201
  821.8 49.4 %mlp_back.11 = (bf16[4,384,2048]{2,1,0:T(8,128)(2,1)}, bf16[4,384,2048]{2,1,0:T(8,128)(2,1)}) custom-call(bf16[3072,2048]{1,0:T(8,128)(2,1)} %get-tuple-element.77.refs_0_, bf16[3072,2048]{1,0:T(8,128)(2,1)} %get-tuple-element.78.refs_1_, bf16[3072,2048]{1,0:T(8,128)(2,1)} %get-tuple-element.79.refs_2_, bf16[2048,2048]{1,0:T(8,128)(2,1)} %refs_3_.17, ...), custom_call_target="tpu_custom_call" | custom-call | flops 38654705664 | bytes 75497472 | tf_op jit(solution)/shard_map/mlp_back/pallas_call | solution.py:201
  871.4 46.1 %wgrad.4.refs_10_.refs_7_ = f32[2048,2048]{1,0:T(8,128)} custom-call(s32[1]{0:T(128)} %bitcast.1.core_s.refs_0_.refs_2_, bf16[4,2,384,2048]{3,2,1,0:T(8,128)(2,1)} %bitcast.137, bf16[4,2,384,2048]{3,2,1,0:T(8,128)(2,1)} %bitcast.143, bf16[4,2,384,2048]{3,2,1,0:T(8,128)(2,1)} %bitcast.149, bf16[8,384,2048]{2,1,0:T(8,128)(2,1)} %bitcast.158, ...), custom_call_target="tpu_custom_call" | custom-call | flops 77309411328 | bytes 92274688 | tf_op jit(solution)/shard_map/wgrad/pallas_call | solution.py:201
  917.5 19.0 %reduce-scatter.13.cloned.1.call-done.refs_1_ = bf16[384,2048]{1,0:T(8,128)(2,1)} async-done(((bf16[1536,2048]{1,0:T(8,128)(2,1)}), bf16[384,2048]{1,0:T(8,128)(2,1)}) %reduce-scatter.13.cloned.1.call-update) | async-done | bytes 1572880 | tf_op jit(solution)/shard_map/reduce_scatter | solution.py:635
  936.5 18.7 %d_resid.3 = (f32[8,2048]{1,0:T(8,128)}, bf16[1152,2048]{1,0:T(8,128)(2,1)}, bf16[1152,1024]{1,0:T(8,128)(2,1)}, bf16[1152,1024]{1,0:T(8,128)(2,1)}) custom-call(bf16[2,384,2048]{2,1,0:T(8,128)(2,1)} %reduce-scatter.9.cloned.1.call-done.refs_0_.refs_2_, ...), custom_call_target="tpu_custom_call", output_to_operand_aliasing={{1}: (7, {}), {2}: (8, {}), {3}: (9, {})} | custom-call | flops 6442450944 | bytes 17825792 | tf_op jit(solution)/shard_map/d_resid/pallas_call | solution.py:201
  955.2 26.6 %attn_bwd.3 = (bf16[12,96,1024]{2,1,0:T(8,128)(2,1)}, bf16[12,96,1024]{2,1,0:T(8,128)(2,1)}, bf16[4,12,96,512]{3,2,1,0:T(8,128)(2,1)}, bf16[4,12,96,512]{3,2,1,0:T(8,128)(2,1)}) custom-call(s32[12]{0:T(128)} %refs_0_.3, s32[12]{0:T(128)} %refs_1_.3, ...), custom_call_target="tpu_custom_call", output_to_operand_aliasing={{0}: (12, {}), {1}: (13, {}), {2}: (14, {}), {3}: (15, {})} | custom-call | flops 12079595520 | bytes 28311552 | tf_op jit(solution)/shard_map/attn_bwd/pallas_call | solution.py:201
  981.7 17.1 %head_wgrad.2.refs_8_ = f32[4,2,256,2048]{3,2,1,0:T(8,128)} custom-call(bf16[1152,1024]{1,0:T(8,128)(2,1)} %bitcast.167, bf16[1152,1024]{1,0:T(8,128)(2,1)} %bitcast.168, bf16[1152,2048]{1,0:T(8,128)(2,1)} %get-tuple-element.98.refs_2_.refs_4_, bf16[1152,2048]{1,0:T(8,128)(2,1)} %bitcast.92, bf16[12,96,1024]{2,1,0:T(8,128)(2,1)} %get-tuple-element.99.refs_4_), custom_call_target="tpu_custom_call" | custom-call | flops 9663676416 | bytes 30932992 | tf_op jit(solution)/shard_map/head_wgrad/pallas_call | solution.py:201
  1008.8 46.7 %wgrad.5.refs_5_ = f32[2048,2048]{1,0:T(8,128)} custom-call(s32[1]{0:T(128)} %bitcast.1.core_s.refs_0_.refs_2_, bf16[4,2,384,2048]{3,2,1,0:T(8,128)(2,1)} %bitcast.138, bf16[4,2,384,2048]{3,2,1,0:T(8,128)(2,1)} %bitcast.144, bf16[4,2,384,2048]{3,2,1,0:T(8,128)(2,1)} %bitcast.150, bf16[8,384,2048]{2,1,0:T(8,128)(2,1)} %bitcast.159, ...), custom_call_target="tpu_custom_call", output_to_operand_aliasing={{}: (7, {})} | custom-call | flops 77309411328 | bytes 92274688 | tf_op jit(solution)/shard_map/wgrad/pallas_call | solution.py:201
  1055.6 22.0 %head_wgrad.3.refs_9_ = f32[4,2,256,2048]{3,2,1,0:T(8,128)} custom-call(bf16[1152,1024]{1,0:T(8,128)(2,1)} %bitcast.119, bf16[1152,1024]{1,0:T(8,128)(2,1)} %bitcast.120, bf16[1152,2048]{1,0:T(8,128)(2,1)} %get-tuple-element.98.refs_2_.refs_4_, bf16[1152,2048]{1,0:T(8,128)(2,1)} %bitcast.93, f32[4,2,256,2048]{3,2,1,0:T(8,128)} %collective-permute-done.14.refs_4_, ...), custom_call_target="tpu_custom_call" | custom-call | flops 9663676416 | bytes 47710208 | tf_op jit(solution)/shard_map/head_wgrad/pallas_call | solution.py:201
  1080.5 25.7 %d_hidden.1 = (bf16[1152,2048]{1,0:T(8,128)(2,1)}, f32[8,2048]{1,0:T(8,128)}) custom-call(bf16[1152,1024]{1,0:T(8,128)(2,1)} %bitcast.121, bf16[1152,1024]{1,0:T(8,128)(2,1)} %bitcast.169, bf16[1152,512]{1,0:T(8,128)(2,1)} %bitcast.114, bf16[1152,2048]{1,0:T(8,128)(2,1)} %bitcast.104, bf16[1152,2048]{1,0:T(8,128)(2,1)} %get-tuple-element.98.refs_2_.refs_4_, ...), custom_call_target="tpu_custom_call" | custom-call | flops 14495514624 | bytes 27328512 | tf_op jit(solution)/shard_map/d_hidden/pallas_call | solution.py:201
  1113.3 12.6 reduce-scatter.11.cloned.1.call-done.refs_3_
  1134.5 87.0 %wgrad.6.refs_7_ = f32[2048,2048]{1,0:T(8,128)} custom-call(s32[1]{0:T(128)} %bitcast.1.core_s.refs_0_.refs_2_, bf16[4,2,384,2048]{3,2,1,0:T(8,128)(2,1)} %bitcast.139, bf16[4,2,384,2048]{3,2,1,0:T(8,128)(2,1)} %bitcast.145, bf16[4,2,384,2048]{3,2,1,0:T(8,128)(2,1)} %bitcast.151, bf16[8,384,2048]{2,1,0:T(8,128)(2,1)} %bitcast.153, ...), custom_call_target="tpu_custom_call" | custom-call | flops 77309411328 | bytes 92274688 | tf_op jit(solution)/shard_map/wgrad/pallas_call | solution.py:201
  1221.5 87.0 %wgrad.7 = f32[2048,2048]{1,0:T(8,128)} custom-call(s32[1]{0:T(128)} %bitcast.1.core_s.refs_0_.refs_2_, bf16[8,384,2048]{2,1,0:T(8,128)(2,1)} %bitcast.152, bf16[8,384,2048]{2,1,0:T(8,128)(2,1)} %bitcast.154, bf16[8,384,2048]{2,1,0:T(8,128)(2,1)} %bitcast.156, bf16[4,2,384,2048]{3,2,1,0:T(8,128)(2,1)} %bitcast.135, bf16[4,2,384,2048]{3,2,1,0:T(8,128)(2,1)} %bitcast.141, ...), custom_call_target="tpu_custom_call" | custom-call | flops 77309411328 | bytes 92274688 | tf_op jit(solution)/shard_map/wgrad/pallas_call | solution.py:201
  1315.1 43.8 %reduce-scatter.17.cloned.1.call-done = f32[2,256,2048]{2,1,0:T(8,128)} async-done(((f32[8,256,2048]{2,1,0:T(8,128)}), f32[2,256,2048]{2,1,0:T(8,128)}) %reduce-scatter.17.cloned.1.call-update) | async-done | bytes 4194320 | tf_op jit(solution)/shard_map/reduce_scatter | solution.py:635
  (175 shorter events, 128.4 us)
Async XLA Ops:
  7.2 132.2 %all-gather.11.cloned.1.call-start = ((), (), s32[]{:S(2)}) async-start(), calls=%async_computation.6 | async-start | bytes 10616832 | tf_op jit(solution)/shard_map/all_gather | solution.py:638
  17.8 182.7 %all-gather.13.cloned.1.call-start = ((), (), s32[]{:S(2)}) async-start(), calls=%async_computation.7 | async-start | bytes 14155776 | tf_op jit(solution)/shard_map/all_gather | solution.py:638
  22.6 242.7 %all-gather.19.cloned.1.call-start = ((), (), s32[]{:S(2)}) async-start(), calls=%async_computation.17 | async-start | bytes 14155776 | tf_op jit(solution)/shard_map/all_gather | solution.py:638
  22.9 43.4 %collective-permute-start = (bf16[256,2048]{0,1:T(8,128)(2,1)}, bf16[256,2048]{0,1:T(8,128)(2,1)S(1)}, u32[]{:S(2)}, u32[]{:S(2)}) collective-permute-start(bf16[256,2048]{0,1:T(8,128)(2,1)} %bitcast.3), channel_id=1, source_target_pairs={{0,2},{1,3},{2,0},{3,1},{4,6},{5,7},{6,4},{7,5}} | collective-permute-start | bytes 3145736 | tf_op jit(solution)/shard_map/ppermute | solution.py:644
  26.3 42.9 %collective-permute-start.1 = (bf16[256,2048]{0,1:T(8,128)(2,1)}, bf16[256,2048]{0,1:T(8,128)(2,1)S(1)}, u32[]{:S(2)}, u32[]{:S(2)}) collective-permute-start(bf16[256,2048]{0,1:T(8,128)(2,1)} %bitcast.3), channel_id=1, source_target_pairs={{0,4},{1,5},{2,6},{3,7},{4,0},{5,1},{6,2},{7,3}} | collective-permute-start | bytes 3145736 | tf_op jit(solution)/shard_map/ppermute | solution.py:644
  67.2 25.7 %collective-permute-start.2 = (bf16[128,2048]{0,1:T(8,128)(2,1)}, bf16[128,2048]{0,1:T(8,128)(2,1)}, u32[]{:S(2)}, u32[]{:S(2)}) collective-permute-start(bf16[128,2048]{0,1:T(8,128)(2,1)} %slice.76), channel_id=1, source_target_pairs={{0,4},{1,5},{2,6},{3,7},{4,0},{5,1},{6,2},{7,3}} | collective-permute-start | bytes 1572872 | tf_op jit(solution)/shard_map/ppermute | solution.py:644
  70.0 25.6 %collective-permute-start.3 = (bf16[128,2048]{0,1:T(8,128)(2,1)}, bf16[128,2048]{0,1:T(8,128)(2,1)}, u32[]{:S(2)}, u32[]{:S(2)}) collective-permute-start(bf16[128,2048]{0,1:T(8,128)(2,1)} %slice.77), channel_id=1, source_target_pairs={{0,2},{1,3},{2,0},{3,1},{4,6},{5,7},{6,4},{7,5}} | collective-permute-start | bytes 1572872 | tf_op jit(solution)/shard_map/ppermute | solution.py:644
  98.5 14.3 %collective-permute-start.4 = (bf16[1024,2048]{1,0:T(8,128)(2,1)}, bf16[1024,2048]{1,0:T(8,128)(2,1)}, u32[]{:S(2)}, u32[]{:S(2)}) collective-permute-start(bf16[1024,2048]{1,0:T(8,128)(2,1)} %bitcast.9.refs_6_), channel_id=1, source_target_pairs={{0,1},{1,0},{2,3},{3,2},{4,5},{5,4},{6,7},{7,6}} | collective-permute-start | bytes 12582920 | tf_op jit(solution)/shard_map/ppermute | solution.py:641
  98.5 37.6 %collective-permute-start.5 = (bf16[256,2048]{1,0:T(8,128)(2,1)}, bf16[256,2048]{1,0:T(8,128)(2,1)S(1)}, u32[]{:S(2)}, u32[]{:S(2)}) collective-permute-start(bf16[256,2048]{1,0:T(8,128)(2,1)} %param.21), channel_id=1, source_target_pairs={{0,2},{1,3},{2,0},{3,1},{4,6},{5,7},{6,4},{7,5}} | collective-permute-start | bytes 3145736 | tf_op jit(solution)/shard_map/ppermute | solution.py:644
  100.3 37.7 %collective-permute-start.6 = (bf16[256,2048]{1,0:T(8,128)(2,1)}, bf16[256,2048]{1,0:T(8,128)(2,1)S(1)}, u32[]{:S(2)}, u32[]{:S(2)}) collective-permute-start(bf16[256,2048]{1,0:T(8,128)(2,1)} %param.21), channel_id=1, source_target_pairs={{0,4},{1,5},{2,6},{3,7},{4,0},{5,1},{6,2},{7,3}} | collective-permute-start | bytes 3145736 | tf_op jit(solution)/shard_map/ppermute | solution.py:644
  138.1 23.6 %collective-permute-start.8 = (bf16[128,2048]{1,0:T(8,128)(2,1)S(1)}, bf16[128,2048]{1,0:T(8,128)(2,1)}, u32[]{:S(2)}, u32[]{:S(2)}) collective-permute-start(bf16[128,2048]{1,0:T(8,128)(2,1)S(1)} %slice.66), channel_id=1, source_target_pairs={{0,2},{1,3},{2,0},{3,1},{4,6},{5,7},{6,4},{7,5}} | collective-permute-start | bytes 1572872 | tf_op jit(solution)/shard_map/ppermute | solution.py:644
  138.6 23.1 %collective-permute-start.7 = (bf16[128,2048]{1,0:T(8,128)(2,1)S(1)}, bf16[128,2048]{1,0:T(8,128)(2,1)}, u32[]{:S(2)}, u32[]{:S(2)}) collective-permute-start(bf16[128,2048]{1,0:T(8,128)(2,1)S(1)} %slice.65), channel_id=1, source_target_pairs={{0,4},{1,5},{2,6},{3,7},{4,0},{5,1},{6,2},{7,3}} | collective-permute-start | bytes 1572872 | tf_op jit(solution)/shard_map/ppermute | solution.py:644
  168.0 8.1 collective-permute-start.9
  197.9 185.8 %all-gather.15.cloned.1.call-start = ((), (), s32[]{:S(2)}) async-start(), calls=%async_computation.8 | async-start | bytes 14155776 | tf_op jit(solution)/shard_map/all_gather | solution.py:638
  198.5 217.7 %all-gather.21.cloned.1.call-start = ((), (), s32[]{:S(2)}) async-start(), calls=%async_computation.18 | async-start | bytes 14155776 | tf_op jit(solution)/shard_map/all_gather | solution.py:638
  199.1 454.6 %all-gather.17.cloned.1.call-start = ((), (), s32[]{:S(2)}) async-start(), calls=%async_computation.11 | async-start | bytes 14155776 | tf_op jit(solution)/shard_map/all_gather | solution.py:638
  199.7 454.1 %all-gather.23.cloned.1.call-start = ((), (), s32[]{:S(2)}) async-start(), calls=%async_computation.19 | async-start | bytes 14155776 | tf_op jit(solution)/shard_map/all_gather | solution.py:638
  200.4 595.6 %reduce-scatter.7.cloned.1.call-start = ((), (), s32[]{:S(2)}) async-start(), calls=%async_computation.9 | async-start | bytes 15728640 | tf_op jit(solution)/shard_map/reduce_scatter | solution.py:635
  383.4 151.2 %collective-permute-start.10 = (bf16[4,2,384,2048]{3,2,1,0:T(8,128)(2,1)}, bf16[4,2,384,2048]{3,2,1,0:T(8,128)(2,1)}, u32[]{:S(2)}, u32[]{:S(2)}) collective-permute-start(bf16[4,2,384,2048]{3,2,1,0:T(8,128)(2,1)} %mlp_back.6.refs_3_), channel_id=1, source_target_pairs={{0,1},{1,0},{2,3},{3,2},{4,5},{5,4},{6,7},{7,6}} | collective-permute-start | bytes 37748744 | tf_op jit(solution)/shard_map/ppermute | solution.py:641
  584.2 333.2 %reduce-scatter.9.cloned.1.call-start = ((), (), s32[]{:S(2)}) async-start(), calls=%async_computation.10 | async-start | bytes 15728640 | tf_op jit(solution)/shard_map/reduce_scatter | solution.py:635
  584.3 19.5 %collective-permute-start.11 = (bf16[4,2,384,2048]{3,2,1,0:T(8,128)(2,1)}, bf16[4,2,384,2048]{3,2,1,0:T(8,128)(2,1)}, u32[]{:S(2)}, u32[]{:S(2)}) collective-permute-start(bf16[4,2,384,2048]{3,2,1,0:T(8,128)(2,1)} %mlp_back.7.refs_7_), channel_id=1, source_target_pairs={{0,1},{1,0},{2,3},{3,2},{4,5},{5,4},{6,7},{7,6}} | collective-permute-start | bytes 37748744 | tf_op jit(solution)/shard_map/ppermute | solution.py:641
  653.6 282.8 %reduce-scatter.13.cloned.1.call-start = ((), (), s32[]{:S(2)}) async-start(), calls=%async_computation.13 | async-start | bytes 7864320 | tf_op jit(solution)/shard_map/reduce_scatter | solution.py:635
  746.0 48.4 %copy-start.13 = (s32[4,96]{1,0:T(4,128)S(1)}, s32[4,96]{1,0:T(4,128)}, u32[]{:S(2)}) copy-start(s32[4,96]{1,0:T(4,128)} %copy-done.12) | copy-start | bytes 4612
  746.0 49.1 %copy-start.15 = (s32[768]{0:T(1024)S(1)}, s32[768]{0:T(1024)}, u32[]{:S(2)}) copy-start(s32[768]{0:T(1024)} %copy-done.14) | copy-start | bytes 9220
  793.9 27.9 %collective-permute-start.12 = (bf16[4,2,384,2048]{3,2,1,0:T(8,128)(2,1)}, bf16[4,2,384,2048]{3,2,1,0:T(8,128)(2,1)}, u32[]{:S(2)}, u32[]{:S(2)}) collective-permute-start(bf16[4,2,384,2048]{3,2,1,0:T(8,128)(2,1)} %mlp_back.10.refs_6_), channel_id=1, source_target_pairs={{0,1},{1,0},{2,3},{3,2},{4,5},{5,4},{6,7},{7,6}} | collective-permute-start | bytes 37748744 | tf_op jit(solution)/shard_map/ppermute | solution.py:641
  871.3 206.3 %reduce-scatter.15.cloned.1.call-start = ((), (), s32[]{:S(2)}) async-start(), calls=%async_computation.14 | async-start | bytes 5898240 | tf_op jit(solution)/shard_map/reduce_scatter | solution.py:635
  981.7 17.1 %collective-permute-start.13 = (bf16[4,12,96,512]{3,2,1,0:T(8,128)(2,1)}, bf16[4,12,96,512]{3,2,1,0:T(8,128)(2,1)}, u32[]{:S(2)}, u32[]{:S(2)}) collective-permute-start(bf16[4,12,96,512]{3,2,1,0:T(8,128)(2,1)} %get-tuple-element.95), channel_id=1, source_target_pairs={{0,1},{1,0},{2,3},{3,2},{4,5},{5,4},{6,7},{7,6}} | collective-permute-start | bytes 14155784 | tf_op jit(solution)/shard_map/ppermute | solution.py:641
  1006.9 119.0 %reduce-scatter.11.cloned.1.call-start = ((), (), s32[]{:S(2)}) async-start(), calls=%async_computation.12 | async-start | bytes 7864320 | tf_op jit(solution)/shard_map/reduce_scatter | solution.py:635
  1007.0 48.6 %collective-permute-start.14 = (f32[4,2,256,2048]{3,2,1,0:T(8,128)}, f32[4,2,256,2048]{3,2,1,0:T(8,128)}, u32[]{:S(2)}, u32[]{:S(2)}) collective-permute-start(f32[4,2,256,2048]{3,2,1,0:T(8,128)} %head_wgrad.2.refs_8_), channel_id=1, source_target_pairs={{0,1},{1,0},{2,3},{3,2},{4,5},{5,4},{6,7},{7,6}} | collective-permute-start | bytes 50331656 | tf_op jit(solution)/shard_map/ppermute | solution.py:641
  1055.5 23.5 %copy-start.7 = (f32[96,128]{1,0:T(8,128)S(1)}, f32[96,128]{1,0:T(8,128)}, u32[]{:S(2)}) copy-start(f32[96,128]{1,0:T(8,128)} %copy-done.6) | copy-start | bytes 147460
  1133.1 175.4 %all-reduce.4.cloned.1.call-start = ((), (), s32[]{:S(2)}) async-start(), calls=%async_computation.15 | async-start | bytes 8421376 | tf_op jit(solution)/shard_map/psum | solution.py:774
  1133.9 225.0 %reduce-scatter.17.cloned.1.call-start = ((), (), s32[]{:S(2)}) async-start(), calls=%async_computation.16 | async-start | bytes 20971520 | tf_op jit(solution)/shard_map/reduce_scatter | solution.py:635
  (19 other events, 107.9 us)
Sparse Core Ops, SparseCore 0:
  17.9 84.9 all-gather.10
  105.3 84.4 all-gather.12
  198.0 67.2 all-gather.18
  267.5 66.4 all-gather.14
  336.2 67.2 all-gather.20
  405.2 66.4 all-gather.16
  474.1 66.4 all-gather.22
  584.4 115.3 reduce-scatter.6
  702.8 115.0 reduce-scatter.8
  871.4 64.9 reduce-scatter.12
  1007.0 51.5 reduce-scatter.14
  1061.3 64.4 reduce-scatter.10
  1137.2 70.4 all-reduce.3
  1210.6 148.1 reduce-scatter.16

commit v10 on v8

--- a/solution.py
+++ b/solution.py
@@ -377,22 +377,21 @@
     def copies(s, at, p):
         row = pl.multiple_of((lax.div(s, cols * n) + first) * tf, tf)
         col = pl.multiple_of((lax.rem(lax.div(s, n), cols) + first_col) * tn, tn)
-        out = []
-        for q, (ref, buf, lanes) in enumerate(((lhs[p], l_buf, pl.ds(row, tf)), (rhs[p], r_buf, pl.ds(col, tn)))):
-            if ref.ndim == 4:
-                for side in range(2):
-                    src = ref.at[:, lax.bitwise_xor(core_s[0], side), :, lanes]
-                    out.append(pltpu.make_async_copy(src, buf.at[at, pl.ds(side * chips, chips)], sems.at[q, side, at]))
-            else:
-                out.append(pltpu.make_async_copy(ref.at[:, :, lanes], buf.at[at], sems.at[q, 0, at]))
-        return out
+        halves = [], []
+        for side in range(2):
+            half = pl.ds(side * chips, chips)
+            for q, (ref, buf, lanes) in enumerate(((lhs[p], l_buf, pl.ds(row, tf)), (rhs[p], r_buf, pl.ds(col, tn)))):
+                src = ref.at[:, lax.bitwise_xor(core_s[0], side), :, lanes] if ref.ndim == 4 else ref.at[half, :, lanes]
+                halves[side].append(pltpu.make_async_copy(src, buf.at[at, half], sems.at[q, side, at]))
+        return halves
 
     def fetch(s, at):
         for p in range(n):
             @pl.when(lax.rem(s, n) == p)
             def _(p=p):
-                for copy in copies(s, at, p):
-                    copy.start()
+                for half in copies(s, at, p):
+                    for copy in half:
+                        copy.start()
 
     @pl.when(step == 0)
     def _():
@@ -402,10 +401,22 @@
     def _():
         fetch(step + 1, 1 - slot)
 
-    for copy in copies(step, slot, 0):
-        copy.wait()
-    part = dot_f32(rows_of(l_buf.at[slot]), rows_of(r_buf.at[slot]), 0, 0)
-    out[...] = jnp.where(k == 0, part, out[...] + part)
+    @pl.when(step == 0)
+    def _():
+        for side, half in enumerate(copies(step, slot, 0)):
+            for copy in half:
+                copy.wait()
+            rows = pl.ds(side * chips, chips)
+            part = dot_f32(rows_of(l_buf.at[0, rows]), rows_of(r_buf.at[0, rows]), 0, 0)
+            out[...] = part if side == 0 else out[...] + part
+
+    @pl.when(step > 0)
+    def _():
+        for half in copies(step, slot, 0):
+            for copy in half:
+                copy.wait()
+        part = dot_f32(rows_of(l_buf.at[slot]), rows_of(r_buf.at[slot]), 0, 0)
+        out[...] = jnp.where(k == 0, part, out[...] + part)
 
 
 def wgrad_call(order, core, lhs, rhs, tf=1024, tn=1024, tiles=None, col_tiles=None, earlier=None, after=()):

time: 1370 us -> 1360 us (level)
  no operation moved by 1% of the time
where the time goes in v10:
time: 1360 us
  Pallas kernels  1050 us (77%)
  waiting for transfers between devices  191 us (14%)
  local copies, waits for them, and re-layouts  43.3 us (3%)
  matrix products  21.6 us (2%)
  other arithmetic  20 us (1%)
  between operations  14.8 us (1%)
  starting transfers between devices  14.6 us (1%)
    pallas_call x26, Pallas kernels, run(): pl.pallas_call(body, out_shape=shapes, grid_spec=pltpu.PrefetchScalarGrid...  1030 us
    ppermute x8, waiting for transfers between devices, flip(): return lax.ppermute(x_loc, 'tp', [(i, i ^ bits) for i in range(tp_size)])  68.9 us
    reduce_scatter x6, waiting for transfers between devices, scatter4(): lax.psum_scatter(flat, 'tp', scatter_dimension=0, tiled=True, axis_index_...  59.6 us
    all_gather x7, waiting for transfers between devices, gather8(): return lax.all_gather(x_loc, 'tp', axis=0, tiled=False)  31.7 us
  transfers between devices with their start and end apart: 29, of which 10 were waited for; matrix products, arithmetic and copies ran while one was open for 4% of the time, Pallas kernels for 74%

profile of v10, /device:TPU:0, one launch (start us, length us, event | category | flops | bytes accessed | tf_op | source)
XLA Modules:
  0.0 1359.0 jit_solution(7502051175839364960)
XLA Ops:
  29.3 37.0 %collective-permute-done = bf16[256,2048]{0,1:T(8,128)(2,1)S(1)} collective-permute-done((bf16[256,2048]{0,1:T(8,128)(2,1)}, bf16[256,2048]{0,1:T(8,128)(2,1)S(1)}, u32[]{:S(2)}, u32[]{:S(2)}) %collective-permute-start) | collective-permute-done | bytes 1048608 | tf_op jit(solution)/shard_map/ppermute | solution.py:647
  78.7 14.2 %collective-permute-done.2 = bf16[128,2048]{0,1:T(8,128)(2,1)} collective-permute-done((bf16[128,2048]{0,1:T(8,128)(2,1)}, bf16[128,2048]{0,1:T(8,128)(2,1)}, u32[]{:S(2)}, u32[]{:S(2)}) %collective-permute-start.2) | collective-permute-done | bytes 524320 | tf_op jit(solution)/shard_map/ppermute | solution.py:647
  121.8 14.3 %collective-permute-done.5 = bf16[256,2048]{1,0:T(8,128)(2,1)S(1)} collective-permute-done((bf16[256,2048]{1,0:T(8,128)(2,1)}, bf16[256,2048]{1,0:T(8,128)(2,1)S(1)}, u32[]{:S(2)}, u32[]{:S(2)}) %collective-permute-start.5) | collective-permute-done | bytes 1048608 | tf_op jit(solution)/shard_map/ppermute | solution.py:647
  139.3 22.3 %attn_fwd.1 = (bf16[12,96,1024]{2,1,0:T(8,128)(2,1)}, bf16[12,96,1024]{2,1,0:T(8,128)(2,1)}, bf16[12,96,1024]{2,1,0:T(8,128)(2,1)}, bf16[12,96,1024]{2,1,0:T(8,128)(2,1)}) custom-call(s32[12]{0:T(128)} %refs_0_.3, s32[12]{0:T(128)} %refs_1_.5, s32[1]{0:T(128)} %bitcast.1.core_s.refs_0_.refs_2_, f32[12,96,1024]{2,1,0:T(8,128)} %bitcast.164, ...), custom_call_target="tpu_custom_call" | custom-call | flops 7247757312 | bytes 28311552 | tf_op jit(solution)/shard_map/attn_fwd/pallas_call | solution.py:148
  177.9 19.9 %resid.1 = (bf16[1152,2048]{1,0:T(8,128)(2,1)}, bf16[384,2048]{1,0:T(8,128)(2,1)}, bf16[384,2048]{1,0:T(8,128)(2,1)}, bf16[384,2048]{1,0:T(8,128)(2,1)}) custom-call(bf16[1152,2048]{1,0:T(8,128)(2,1)} %bitcast.103, bf16[1152,1024]{1,0:T(8,128)(2,1)} %bitcast.118, bf16[1152,1024]{1,0:T(8,128)(2,1)} %bitcast.166, bf16[1024,2048]{1,0:T(8,128)(2,1)} %bitcast.99, ...), custom_call_target="tpu_custom_call" | custom-call | flops 9663676416 | bytes 27262976 | tf_op jit(solution)/shard_map/resid/pallas_call | solution.py:201
  200.4 33.2 %d_act.2.refs_2_ = bf16[3072,2048]{1,0:T(8,128)(2,1)} custom-call(s32[1]{0:T(128)} %bitcast.1.core_s.refs_0_.refs_2_, bf16[4,2,384,2048]{3,2,1,0:T(8,128)(2,1)} %bitcast.134, bf16[2048,2048]{1,0:T(8,128)(2,1)} %refs_1_.4, bf16[1152,2048]{1,0:T(8,128)(2,1)} %get-tuple-element.65.refs_3_.refs_1_.refs_2_.refs_0_), custom_call_target="tpu_custom_call" | custom-call | flops 25769803776 | bytes 33554432 | tf_op jit(solution)/shard_map/d_act/pallas_call | solution.py:201
  233.6 31.7 %all-gather.19.cloned.1.call-done = bf16[3072,2048]{1,0:T(8,128)(2,1)} async-done(((bf16[384,2048]{1,0:T(8,128)(2,1)}), bf16[3072,2048]{1,0:T(8,128)(2,1)}) %all-gather.19.cloned.1.call-update) | async-done | bytes 12582928 | tf_op jit(solution)/shard_map/all_gather | solution.py:641
  265.3 70.7 %mlp_act.3 = (bf16[3072,2048]{1,0:T(8,128)(2,1)}, bf16[3072,2048]{1,0:T(8,128)(2,1)}, bf16[3072,2048]{1,0:T(8,128)(2,1)}) custom-call(s32[1]{0:T(128)} %bitcast.1.core_s.refs_0_.refs_2_, bf16[4,2,384,2048]{3,2,1,0:T(8,128)(2,1)} %bitcast.136, bf16[3072,2048]{1,0:T(8,128)(2,1)} %d_act.2.refs_2_, bf16[2048,2048]{1,0:T(8,128)(2,1)} %refs_2_.5, ...), custom_call_target="tpu_custom_call" | custom-call | flops 51539607552 | bytes 79691776 | tf_op jit(solution)/shard_map/mlp_act/pallas_call | solution.py:201
  335.9 47.4 %mlp_back.7.refs_3_ = bf16[4,2,384,2048]{3,2,1,0:T(8,128)(2,1)} custom-call(bf16[3072,2048]{1,0:T(8,128)(2,1)} %get-tuple-element.67.refs_0_, bf16[3072,2048]{1,0:T(8,128)(2,1)} %get-tuple-element.68.refs_1_, bf16[3072,2048]{1,0:T(8,128)(2,1)} %get-tuple-element.69.refs_2_, bf16[2048,2048]{1,0:T(8,128)(2,1)} %refs_2_.5, bf16[2048,2048]{1,0:T(8,128)(2,1)} %refs_3_.17, ...), custom_call_target="tpu_custom_call" | custom-call | flops 38654705664 | bytes 75497472 | tf_op jit(solution)/shard_map/mlp_back/pallas_call | solution.py:201
  383.6 32.5 %d_act.3.refs_2_ = bf16[3072,2048]{1,0:T(8,128)(2,1)} custom-call(s32[1]{0:T(128)} %bitcast.1.core_s.refs_0_.refs_2_, bf16[4,2,384,2048]{3,2,1,0:T(8,128)(2,1)} %bitcast.140, bf16[2048,2048]{1,0:T(8,128)(2,1)} %refs_1_.4, bf16[4,2,384,2048]{3,2,1,0:T(8,128)(2,1)} %mlp_back.7.refs_3_), custom_call_target="tpu_custom_call" | custom-call | flops 25769803776 | bytes 33554432 | tf_op jit(solution)/shard_map/d_act/pallas_call | solution.py:201
  416.2 70.9 %mlp_act.4 = (bf16[3072,2048]{1,0:T(8,128)(2,1)}, bf16[3072,2048]{1,0:T(8,128)(2,1)}, bf16[3072,2048]{1,0:T(8,128)(2,1)}) custom-call(s32[1]{0:T(128)} %bitcast.1.core_s.refs_0_.refs_2_, bf16[4,2,384,2048]{3,2,1,0:T(8,128)(2,1)} %bitcast.142, bf16[3072,2048]{1,0:T(8,128)(2,1)} %d_act.3.refs_2_, bf16[2048,2048]{1,0:T(8,128)(2,1)} %refs_2_.5, ...), custom_call_target="tpu_custom_call" | custom-call | flops 51539607552 | bytes 79691776 | tf_op jit(solution)/shard_map/mlp_act/pallas_call | solution.py:201
  487.1 47.5 %mlp_back.8.refs_7_ = bf16[4,2,384,2048]{3,2,1,0:T(8,128)(2,1)} custom-call(bf16[3072,2048]{1,0:T(8,128)(2,1)} %get-tuple-element.71.refs_0_, bf16[3072,2048]{1,0:T(8,128)(2,1)} %get-tuple-element.72.refs_1_, bf16[3072,2048]{1,0:T(8,128)(2,1)} %get-tuple-element.73.refs_2_, bf16[2048,2048]{1,0:T(8,128)(2,1)} %refs_2_.5, bf16[2048,2048]{1,0:T(8,128)(2,1)} %refs_3_.17, ...), custom_call_target="tpu_custom_call" | custom-call | flops 38654705664 | bytes 75497472 | tf_op jit(solution)/shard_map/mlp_back/pallas_call | solution.py:201
  534.6 49.6 %mlp_back.9.refs_7_ = bf16[4,2,384,2048]{3,2,1,0:T(8,128)(2,1)} custom-call(bf16[3072,2048]{1,0:T(8,128)(2,1)} %get-tuple-element.67.refs_0_, bf16[3072,2048]{1,0:T(8,128)(2,1)} %get-tuple-element.68.refs_1_, bf16[3072,2048]{1,0:T(8,128)(2,1)} %get-tuple-element.69.refs_2_, bf16[2048,2048]{1,0:T(8,128)(2,1)} %refs_2_.5, bf16[2048,2048]{1,0:T(8,128)(2,1)} %refs_3_.17, ...), custom_call_target="tpu_custom_call" | custom-call | flops 38654705664 | bytes 75497472 | tf_op jit(solution)/shard_map/mlp_back/pallas_call | solution.py:201
  584.3 19.5 %collective-permute-done.11.refs_6_ = bf16[4,2,384,2048]{3,2,1,0:T(8,128)(2,1)} collective-permute-done((bf16[4,2,384,2048]{3,2,1,0:T(8,128)(2,1)}, bf16[4,2,384,2048]{3,2,1,0:T(8,128)(2,1)}, u32[]{:S(2)}, u32[]{:S(2)}) %collective-permute-start.11) | collective-permute-done | bytes 12582944 | tf_op jit(solution)/shard_map/ppermute | solution.py:644
  603.8 49.7 %mlp_back.10.refs_6_ = bf16[4,2,384,2048]{3,2,1,0:T(8,128)(2,1)} custom-call(bf16[3072,2048]{1,0:T(8,128)(2,1)} %get-tuple-element.71.refs_0_, bf16[3072,2048]{1,0:T(8,128)(2,1)} %get-tuple-element.72.refs_1_, bf16[3072,2048]{1,0:T(8,128)(2,1)} %get-tuple-element.73.refs_2_, bf16[2048,2048]{1,0:T(8,128)(2,1)} %refs_2_.5, bf16[2048,2048]{1,0:T(8,128)(2,1)} %refs_3_.17, ...), custom_call_target="tpu_custom_call" | custom-call | flops 38654705664 | bytes 75497472 | tf_op jit(solution)/shard_map/mlp_back/pallas_call | solution.py:201
  653.6 92.4 %mlp_act.5 = (bf16[3072,2048]{1,0:T(8,128)(2,1)}, bf16[3072,2048]{1,0:T(8,128)(2,1)}, bf16[3072,2048]{1,0:T(8,128)(2,1)}) custom-call(s32[1]{0:T(128)} %bitcast.1.core_s.refs_0_.refs_2_, bf16[4,2,384,2048]{3,2,1,0:T(8,128)(2,1)} %bitcast.148, bf16[4,2,384,2048]{3,2,1,0:T(8,128)(2,1)} %bitcast.146, bf16[2048,2048]{1,0:T(8,128)(2,1)} %refs_2_.5, ...), custom_call_target="tpu_custom_call" | custom-call | flops 77309411328 | bytes 88080384 | tf_op jit(solution)/shard_map/mlp_act/pallas_call | solution.py:201
  746.0 47.6 %mlp_back.11.refs_6_ = bf16[4,2,384,2048]{3,2,1,0:T(8,128)(2,1)} custom-call(bf16[3072,2048]{1,0:T(8,128)(2,1)} %get-tuple-element.76.refs_0_, bf16[3072,2048]{1,0:T(8,128)(2,1)} %get-tuple-element.77.refs_1_, bf16[3072,2048]{1,0:T(8,128)(2,1)} %get-tuple-element.75.refs_2_.refs_0_, bf16[2048,2048]{1,0:T(8,128)(2,1)} %refs_2_.5, ...), custom_call_target="tpu_custom_call" | custom-call | flops 38654705664 | bytes 75497472 | tf_op jit(solution)/shard_map/mlp_back/pallas_call | solution.py:201
  795.8 11.0 d_resid.2
  806.8 14.8 %attn_bwd.2 = (bf16[12,96,1024]{2,1,0:T(8,128)(2,1)}, bf16[12,96,1024]{2,1,0:T(8,128)(2,1)}, bf16[4,12,96,512]{3,2,1,0:T(8,128)(2,1)}, bf16[4,12,96,512]{3,2,1,0:T(8,128)(2,1)}) custom-call(s32[12]{0:T(128)} %refs_0_.3, s32[12]{0:T(128)} %refs_1_.5, s32[1]{0:T(128)} %bitcast.1.core_s.refs_0_.refs_2_, bf16[12,96,1024]{2,1,0:T(8,128)(2,1)} %get-tuple-element.78.refs_3_, ...), custom_call_target="tpu_custom_call" | custom-call | flops 6039797760 | bytes 23592960 | tf_op jit(solution)/shard_map/attn_bwd/pallas_call | solution.py:201
  821.6 34.5 %mlp_back.12.refs_3_ = bf16[4,384,2048]{2,1,0:T(8,128)(2,1)} custom-call(bf16[3072,2048]{1,0:T(8,128)(2,1)} %get-tuple-element.76.refs_0_, bf16[3072,2048]{1,0:T(8,128)(2,1)} %get-tuple-element.77.refs_1_, bf16[2048,2048]{1,0:T(8,128)(2,1)} %refs_2_.5, bf16[2048,2048]{1,0:T(8,128)(2,1)} %refs_3_.17, ...), custom_call_target="tpu_custom_call" | custom-call | flops 25769803776 | bytes 48234496 | tf_op jit(solution)/shard_map/mlp_back/pallas_call | solution.py:201
  856.2 20.6 %mlp_back.13.refs_7_ = bf16[4,384,2048]{2,1,0:T(8,128)(2,1)} custom-call(bf16[3072,2048]{1,0:T(8,128)(2,1)} %get-tuple-element.75.refs_2_.refs_0_, bf16[2048,2048]{1,0:T(8,128)(2,1)} %refs_1_.4, bf16[4,2,384,2048]{3,2,1,0:T(8,128)(2,1)} %collective-permute-done.12.refs_4_.refs_2_, bf16[4,384,2048]{2,1,0:T(8,128)(2,1)} %mlp_back.12.refs_3_), custom_call_target="tpu_custom_call" | custom-call | flops 12884901888 | bytes 27262976 | tf_op jit(solution)/shard_map/mlp_back/pallas_call | solution.py:201
  876.8 46.0 %wgrad.4.refs_10_.refs_7_ = f32[2048,2048]{1,0:T(8,128)} custom-call(s32[1]{0:T(128)} %bitcast.1.core_s.refs_0_.refs_2_, bf16[4,2,384,2048]{3,2,1,0:T(8,128)(2,1)} %bitcast.137, bf16[4,2,384,2048]{3,2,1,0:T(8,128)(2,1)} %bitcast.143, bf16[4,2,384,2048]{3,2,1,0:T(8,128)(2,1)} %bitcast.149, bf16[8,384,2048]{2,1,0:T(8,128)(2,1)} %bitcast.158, ...), custom_call_target="tpu_custom_call" | custom-call | flops 77309411328 | bytes 92274688 | tf_op jit(solution)/shard_map/wgrad/pallas_call | solution.py:201
  922.9 18.4 %d_resid.3 = (f32[8,2048]{1,0:T(8,128)}, bf16[1152,2048]{1,0:T(8,128)(2,1)}, bf16[1152,1024]{1,0:T(8,128)(2,1)}, bf16[1152,1024]{1,0:T(8,128)(2,1)}) custom-call(bf16[2,384,2048]{2,1,0:T(8,128)(2,1)} %reduce-scatter.9.cloned.1.call-done.refs_0_.refs_2_, ...), custom_call_target="tpu_custom_call", output_to_operand_aliasing={{1}: (7, {}), {2}: (8, {}), {3}: (9, {})} | custom-call | flops 6442450944 | bytes 17825792 | tf_op jit(solution)/shard_map/d_resid/pallas_call | solution.py:201
  941.3 26.6 %attn_bwd.3 = (bf16[12,96,1024]{2,1,0:T(8,128)(2,1)}, bf16[12,96,1024]{2,1,0:T(8,128)(2,1)}, bf16[4,12,96,512]{3,2,1,0:T(8,128)(2,1)}, bf16[4,12,96,512]{3,2,1,0:T(8,128)(2,1)}) custom-call(s32[12]{0:T(128)} %refs_0_.3, s32[12]{0:T(128)} %refs_1_.5, ...), custom_call_target="tpu_custom_call", output_to_operand_aliasing={{0}: (12, {}), {1}: (13, {}), {2}: (14, {}), {3}: (15, {})} | custom-call | flops 12079595520 | bytes 28311552 | tf_op jit(solution)/shard_map/attn_bwd/pallas_call | solution.py:201
  967.9 17.1 %head_wgrad.2.refs_8_ = f32[4,2,256,2048]{3,2,1,0:T(8,128)} custom-call(bf16[1152,1024]{1,0:T(8,128)(2,1)} %bitcast.167, bf16[1152,1024]{1,0:T(8,128)(2,1)} %bitcast.168, bf16[1152,2048]{1,0:T(8,128)(2,1)} %get-tuple-element.94.refs_2_.refs_4_, bf16[1152,2048]{1,0:T(8,128)(2,1)} %bitcast.92, bf16[12,96,1024]{2,1,0:T(8,128)(2,1)} %get-tuple-element.95.refs_4_), custom_call_target="tpu_custom_call" | custom-call | flops 9663676416 | bytes 30932992 | tf_op jit(solution)/shard_map/head_wgrad/pallas_call | solution.py:201
  995.0 46.0 %wgrad.5.refs_5_ = f32[2048,2048]{1,0:T(8,128)} custom-call(s32[1]{0:T(128)} %bitcast.1.core_s.refs_0_.refs_2_, bf16[4,2,384,2048]{3,2,1,0:T(8,128)(2,1)} %bitcast.138, bf16[4,2,384,2048]{3,2,1,0:T(8,128)(2,1)} %bitcast.144, bf16[4,2,384,2048]{3,2,1,0:T(8,128)(2,1)} %bitcast.150, bf16[8,384,2048]{2,1,0:T(8,128)(2,1)} %bitcast.159, ...), custom_call_target="tpu_custom_call", output_to_operand_aliasing={{}: (7, {})} | custom-call | flops 77309411328 | bytes 92274688 | tf_op jit(solution)/shard_map/wgrad/pallas_call | solution.py:201
  1041.0 21.8 %head_wgrad.3.refs_9_ = f32[4,2,256,2048]{3,2,1,0:T(8,128)} custom-call(bf16[1152,1024]{1,0:T(8,128)(2,1)} %bitcast.119, bf16[1152,1024]{1,0:T(8,128)(2,1)} %bitcast.120, bf16[1152,2048]{1,0:T(8,128)(2,1)} %get-tuple-element.94.refs_2_.refs_4_, bf16[1152,2048]{1,0:T(8,128)(2,1)} %bitcast.93, f32[4,2,256,2048]{3,2,1,0:T(8,128)} %collective-permute-done.14.refs_4_, ...), custom_call_target="tpu_custom_call" | custom-call | flops 9663676416 | bytes 47710208 | tf_op jit(solution)/shard_map/head_wgrad/pallas_call | solution.py:201
  1065.6 25.3 %d_hidden.1 = (bf16[1152,2048]{1,0:T(8,128)(2,1)}, f32[8,2048]{1,0:T(8,128)}) custom-call(bf16[1152,1024]{1,0:T(8,128)(2,1)} %bitcast.121, bf16[1152,1024]{1,0:T(8,128)(2,1)} %bitcast.169, bf16[1152,512]{1,0:T(8,128)(2,1)} %bitcast.114, bf16[1152,2048]{1,0:T(8,128)(2,1)} %bitcast.104, bf16[1152,2048]{1,0:T(8,128)(2,1)} %get-tuple-element.94.refs_2_.refs_4_, ...), custom_call_target="tpu_custom_call" | custom-call | flops 14495514624 | bytes 27328512 | tf_op jit(solution)/shard_map/d_hidden/pallas_call | solution.py:201
  1098.0 15.5 %reduce-scatter.11.cloned.1.call-done.refs_3_ = bf16[384,2048]{1,0:T(8,128)(2,1)} async-done(((bf16[1536,2048]{1,0:T(8,128)(2,1)}), bf16[384,2048]{1,0:T(8,128)(2,1)}) %reduce-scatter.11.cloned.1.call-update) | async-done | bytes 1572880 | tf_op jit(solution)/shard_map/reduce_scatter | solution.py:638
  1122.1 86.8 %wgrad.6.refs_7_ = f32[2048,2048]{1,0:T(8,128)} custom-call(s32[1]{0:T(128)} %bitcast.1.core_s.refs_0_.refs_2_, bf16[4,2,384,2048]{3,2,1,0:T(8,128)(2,1)} %bitcast.139, bf16[4,2,384,2048]{3,2,1,0:T(8,128)(2,1)} %bitcast.145, bf16[4,2,384,2048]{3,2,1,0:T(8,128)(2,1)} %bitcast.151, bf16[8,384,2048]{2,1,0:T(8,128)(2,1)} %bitcast.153, ...), custom_call_target="tpu_custom_call" | custom-call | flops 77309411328 | bytes 92274688 | tf_op jit(solution)/shard_map/wgrad/pallas_call | solution.py:201
  1208.9 87.0 %wgrad.7 = f32[2048,2048]{1,0:T(8,128)} custom-call(s32[1]{0:T(128)} %bitcast.1.core_s.refs_0_.refs_2_, bf16[8,384,2048]{2,1,0:T(8,128)(2,1)} %bitcast.152, bf16[8,384,2048]{2,1,0:T(8,128)(2,1)} %bitcast.154, bf16[8,384,2048]{2,1,0:T(8,128)(2,1)} %bitcast.156, bf16[4,2,384,2048]{3,2,1,0:T(8,128)(2,1)} %bitcast.135, bf16[4,2,384,2048]{3,2,1,0:T(8,128)(2,1)} %bitcast.141, ...), custom_call_target="tpu_custom_call" | custom-call | flops 77309411328 | bytes 92274688 | tf_op jit(solution)/shard_map/wgrad/pallas_call | solution.py:201
  1302.5 44.0 %reduce-scatter.17.cloned.1.call-done = f32[2,256,2048]{2,1,0:T(8,128)} async-done(((f32[8,256,2048]{2,1,0:T(8,128)}), f32[2,256,2048]{2,1,0:T(8,128)}) %reduce-scatter.17.cloned.1.call-update) | async-done | bytes 4194320 | tf_op jit(solution)/shard_map/reduce_scatter | solution.py:638
  (176 shorter events, 128.4 us)
Async XLA Ops:
  7.2 132.1 %all-gather.11.cloned.1.call-start = ((), (), s32[]{:S(2)}) async-start(), calls=%async_computation.6 | async-start | bytes 10616832 | tf_op jit(solution)/shard_map/all_gather | solution.py:641
  17.8 182.6 %all-gather.13.cloned.1.call-start = ((), (), s32[]{:S(2)}) async-start(), calls=%async_computation.7 | async-start | bytes 14155776 | tf_op jit(solution)/shard_map/all_gather | solution.py:641
  22.6 242.7 %all-gather.19.cloned.1.call-start = ((), (), s32[]{:S(2)}) async-start(), calls=%async_computation.17 | async-start | bytes 14155776 | tf_op jit(solution)/shard_map/all_gather | solution.py:641
  22.9 43.4 %collective-permute-start = (bf16[256,2048]{0,1:T(8,128)(2,1)}, bf16[256,2048]{0,1:T(8,128)(2,1)S(1)}, u32[]{:S(2)}, u32[]{:S(2)}) collective-permute-start(bf16[256,2048]{0,1:T(8,128)(2,1)} %bitcast.3), channel_id=1, source_target_pairs={{0,2},{1,3},{2,0},{3,1},{4,6},{5,7},{6,4},{7,5}} | collective-permute-start | bytes 3145736 | tf_op jit(solution)/shard_map/ppermute | solution.py:647
  26.3 42.9 %collective-permute-start.1 = (bf16[256,2048]{0,1:T(8,128)(2,1)}, bf16[256,2048]{0,1:T(8,128)(2,1)S(1)}, u32[]{:S(2)}, u32[]{:S(2)}) collective-permute-start(bf16[256,2048]{0,1:T(8,128)(2,1)} %bitcast.3), channel_id=1, source_target_pairs={{0,4},{1,5},{2,6},{3,7},{4,0},{5,1},{6,2},{7,3}} | collective-permute-start | bytes 3145736 | tf_op jit(solution)/shard_map/ppermute | solution.py:647
  67.2 25.7 %collective-permute-start.2 = (bf16[128,2048]{0,1:T(8,128)(2,1)}, bf16[128,2048]{0,1:T(8,128)(2,1)}, u32[]{:S(2)}, u32[]{:S(2)}) collective-permute-start(bf16[128,2048]{0,1:T(8,128)(2,1)} %slice.76), channel_id=1, source_target_pairs={{0,4},{1,5},{2,6},{3,7},{4,0},{5,1},{6,2},{7,3}} | collective-permute-start | bytes 1572872 | tf_op jit(solution)/shard_map/ppermute | solution.py:647
  70.0 25.6 %collective-permute-start.3 = (bf16[128,2048]{0,1:T(8,128)(2,1)}, bf16[128,2048]{0,1:T(8,128)(2,1)}, u32[]{:S(2)}, u32[]{:S(2)}) collective-permute-start(bf16[128,2048]{0,1:T(8,128)(2,1)} %slice.77), channel_id=1, source_target_pairs={{0,2},{1,3},{2,0},{3,1},{4,6},{5,7},{6,4},{7,5}} | collective-permute-start | bytes 1572872 | tf_op jit(solution)/shard_map/ppermute | solution.py:647
  98.5 14.3 %collective-permute-start.4 = (bf16[1024,2048]{1,0:T(8,128)(2,1)}, bf16[1024,2048]{1,0:T(8,128)(2,1)}, u32[]{:S(2)}, u32[]{:S(2)}) collective-permute-start(bf16[1024,2048]{1,0:T(8,128)(2,1)} %bitcast.9.refs_6_), channel_id=1, source_target_pairs={{0,1},{1,0},{2,3},{3,2},{4,5},{5,4},{6,7},{7,6}} | collective-permute-start | bytes 12582920 | tf_op jit(solution)/shard_map/ppermute | solution.py:644
  98.5 37.6 %collective-permute-start.5 = (bf16[256,2048]{1,0:T(8,128)(2,1)}, bf16[256,2048]{1,0:T(8,128)(2,1)S(1)}, u32[]{:S(2)}, u32[]{:S(2)}) collective-permute-start(bf16[256,2048]{1,0:T(8,128)(2,1)} %param.21), channel_id=1, source_target_pairs={{0,2},{1,3},{2,0},{3,1},{4,6},{5,7},{6,4},{7,5}} | collective-permute-start | bytes 3145736 | tf_op jit(solution)/shard_map/ppermute | solution.py:647
  100.3 37.7 %collective-permute-start.6 = (bf16[256,2048]{1,0:T(8,128)(2,1)}, bf16[256,2048]{1,0:T(8,128)(2,1)S(1)}, u32[]{:S(2)}, u32[]{:S(2)}) collective-permute-start(bf16[256,2048]{1,0:T(8,128)(2,1)} %param.21), channel_id=1, source_target_pairs={{0,4},{1,5},{2,6},{3,7},{4,0},{5,1},{6,2},{7,3}} | collective-permute-start | bytes 3145736 | tf_op jit(solution)/shard_map/ppermute | solution.py:647
  138.1 23.5 %collective-permute-start.8 = (bf16[128,2048]{1,0:T(8,128)(2,1)S(1)}, bf16[128,2048]{1,0:T(8,128)(2,1)}, u32[]{:S(2)}, u32[]{:S(2)}) collective-permute-start(bf16[128,2048]{1,0:T(8,128)(2,1)S(1)} %slice.66), channel_id=1, source_target_pairs={{0,2},{1,3},{2,0},{3,1},{4,6},{5,7},{6,4},{7,5}} | collective-permute-start | bytes 1572872 | tf_op jit(solution)/shard_map/ppermute | solution.py:647
  138.6 23.0 %collective-permute-start.7 = (bf16[128,2048]{1,0:T(8,128)(2,1)S(1)}, bf16[128,2048]{1,0:T(8,128)(2,1)}, u32[]{:S(2)}, u32[]{:S(2)}) collective-permute-start(bf16[128,2048]{1,0:T(8,128)(2,1)S(1)} %slice.65), channel_id=1, source_target_pairs={{0,4},{1,5},{2,6},{3,7},{4,0},{5,1},{6,2},{7,3}} | collective-permute-start | bytes 1572872 | tf_op jit(solution)/shard_map/ppermute | solution.py:647
  167.9 8.0 collective-permute-start.9
  197.8 185.8 %all-gather.15.cloned.1.call-start = ((), (), s32[]{:S(2)}) async-start(), calls=%async_computation.8 | async-start | bytes 14155776 | tf_op jit(solution)/shard_map/all_gather | solution.py:641
  198.4 217.8 %all-gather.21.cloned.1.call-start = ((), (), s32[]{:S(2)}) async-start(), calls=%async_computation.18 | async-start | bytes 14155776 | tf_op jit(solution)/shard_map/all_gather | solution.py:641
  199.0 454.6 %all-gather.17.cloned.1.call-start = ((), (), s32[]{:S(2)}) async-start(), calls=%async_computation.11 | async-start | bytes 14155776 | tf_op jit(solution)/shard_map/all_gather | solution.py:641
  199.6 454.1 %all-gather.23.cloned.1.call-start = ((), (), s32[]{:S(2)}) async-start(), calls=%async_computation.19 | async-start | bytes 14155776 | tf_op jit(solution)/shard_map/all_gather | solution.py:641
  200.3 595.5 %reduce-scatter.7.cloned.1.call-start = ((), (), s32[]{:S(2)}) async-start(), calls=%async_computation.9 | async-start | bytes 15728640 | tf_op jit(solution)/shard_map/reduce_scatter | solution.py:638
  383.4 151.2 %collective-permute-start.10 = (bf16[4,2,384,2048]{3,2,1,0:T(8,128)(2,1)}, bf16[4,2,384,2048]{3,2,1,0:T(8,128)(2,1)}, u32[]{:S(2)}, u32[]{:S(2)}) collective-permute-start(bf16[4,2,384,2048]{3,2,1,0:T(8,128)(2,1)} %mlp_back.7.refs_3_), channel_id=1, source_target_pairs={{0,1},{1,0},{2,3},{3,2},{4,5},{5,4},{6,7},{7,6}} | collective-permute-start | bytes 37748744 | tf_op jit(solution)/shard_map/ppermute | solution.py:644
  584.2 338.6 %reduce-scatter.9.cloned.1.call-start = ((), (), s32[]{:S(2)}) async-start(), calls=%async_computation.10 | async-start | bytes 15728640 | tf_op jit(solution)/shard_map/reduce_scatter | solution.py:638
  584.3 19.5 %collective-permute-start.11 = (bf16[4,2,384,2048]{3,2,1,0:T(8,128)(2,1)}, bf16[4,2,384,2048]{3,2,1,0:T(8,128)(2,1)}, u32[]{:S(2)}, u32[]{:S(2)}) collective-permute-start(bf16[4,2,384,2048]{3,2,1,0:T(8,128)(2,1)} %mlp_back.8.refs_7_), channel_id=1, source_target_pairs={{0,1},{1,0},{2,3},{3,2},{4,5},{5,4},{6,7},{7,6}} | collective-permute-start | bytes 37748744 | tf_op jit(solution)/shard_map/ppermute | solution.py:644
  653.5 269.3 %reduce-scatter.13.cloned.1.call-start = ((), (), s32[]{:S(2)}) async-start(), calls=%async_computation.13 | async-start | bytes 7864320 | tf_op jit(solution)/shard_map/reduce_scatter | solution.py:638
  746.0 48.2 %copy-start.13 = (s32[4,96]{1,0:T(4,128)S(1)}, s32[4,96]{1,0:T(4,128)}, u32[]{:S(2)}) copy-start(s32[4,96]{1,0:T(4,128)} %copy-done.12) | copy-start | bytes 4612
  746.0 48.9 %copy-start.15 = (s32[768]{0:T(1024)S(1)}, s32[768]{0:T(1024)}, u32[]{:S(2)}) copy-start(s32[768]{0:T(1024)} %copy-done.14) | copy-start | bytes 9220
  793.6 28.0 %collective-permute-start.12 = (bf16[4,2,384,2048]{3,2,1,0:T(8,128)(2,1)}, bf16[4,2,384,2048]{3,2,1,0:T(8,128)(2,1)}, u32[]{:S(2)}, u32[]{:S(2)}) collective-permute-start(bf16[4,2,384,2048]{3,2,1,0:T(8,128)(2,1)} %mlp_back.11.refs_6_), channel_id=1, source_target_pairs={{0,1},{1,0},{2,3},{3,2},{4,5},{5,4},{6,7},{7,6}} | collective-permute-start | bytes 37748744 | tf_op jit(solution)/shard_map/ppermute | solution.py:644
  856.2 206.7 %reduce-scatter.15.cloned.1.call-start = ((), (), s32[]{:S(2)}) async-start(), calls=%async_computation.14 | async-start | bytes 5898240 | tf_op jit(solution)/shard_map/reduce_scatter | solution.py:638
  967.9 17.1 %collective-permute-start.13 = (bf16[4,12,96,512]{3,2,1,0:T(8,128)(2,1)}, bf16[4,12,96,512]{3,2,1,0:T(8,128)(2,1)}, u32[]{:S(2)}, u32[]{:S(2)}) collective-permute-start(bf16[4,12,96,512]{3,2,1,0:T(8,128)(2,1)} %get-tuple-element.91), channel_id=1, source_target_pairs={{0,1},{1,0},{2,3},{3,2},{4,5},{5,4},{6,7},{7,6}} | collective-permute-start | bytes 14155784 | tf_op jit(solution)/shard_map/ppermute | solution.py:644
  993.1 120.4 %reduce-scatter.11.cloned.1.call-start = ((), (), s32[]{:S(2)}) async-start(), calls=%async_computation.12 | async-start | bytes 7864320 | tf_op jit(solution)/shard_map/reduce_scatter | solution.py:638
  993.1 47.8 %collective-permute-start.14 = (f32[4,2,256,2048]{3,2,1,0:T(8,128)}, f32[4,2,256,2048]{3,2,1,0:T(8,128)}, u32[]{:S(2)}, u32[]{:S(2)}) collective-permute-start(f32[4,2,256,2048]{3,2,1,0:T(8,128)} %head_wgrad.2.refs_8_), channel_id=1, source_target_pairs={{0,1},{1,0},{2,3},{3,2},{4,5},{5,4},{6,7},{7,6}} | collective-permute-start | bytes 50331656 | tf_op jit(solution)/shard_map/ppermute | solution.py:644
  1041.0 23.3 %copy-start.7 = (f32[96,128]{1,0:T(8,128)S(1)}, f32[96,128]{1,0:T(8,128)}, u32[]{:S(2)}) copy-start(f32[96,128]{1,0:T(8,128)} %copy-done.6) | copy-start | bytes 147460
  1120.8 175.1 %all-reduce.4.cloned.1.call-start = ((), (), s32[]{:S(2)}) async-start(), calls=%async_computation.15 | async-start | bytes 8421376 | tf_op jit(solution)/shard_map/psum | solution.py:780
  1121.5 225.0 %reduce-scatter.17.cloned.1.call-start = ((), (), s32[]{:S(2)}) async-start(), calls=%async_computation.16 | async-start | bytes 20971520 | tf_op jit(solution)/shard_map/reduce_scatter | solution.py:638
  (19 other events, 107.6 us)
Sparse Core Ops, SparseCore 0:
  17.9 84.9 all-gather.10
  105.3 84.4 all-gather.12
  197.9 67.2 all-gather.18
  267.5 66.4 all-gather.14
  336.2 67.2 all-gather.20
  405.2 66.4 all-gather.16
  474.0 66.4 all-gather.22
  584.4 115.3 reduce-scatter.6
  702.8 115.0 reduce-scatter.8
  856.3 65.0 reduce-scatter.12
  993.1 53.0 reduce-scatter.14
  1049.0 64.4 reduce-scatter.10
  1124.9 70.5 all-reduce.3
  1198.3 148.1 reduce-scatter.16
